TPU v7x, 128 devices: a whole 4x4x4 slice. The times are simulated.
128 devices in a mesh: grp: 4 (over y), row: 32 (over z, x, core).
Axes of the slice: x: 4, y: 4, z: 4, core: 2. Of those that a mesh axis runs over, the one named last changes fastest.
Arguments:
- tiles: bfloat16 [4, 32, 32, 256, 256], P('grp', 'row'), may hold values from -0.046875 to 0.046875
- tile_rows: int32 [4, 32, 32], P('grp', 'row'), may hold values from 0 to 3, as said below
- tile_cols: int32 [4, 32, 32], P('grp', 'row'), may hold values from 0 to 31, as said below
- live_tiles: int32 [4, 32], P('grp', 'row'), may hold values from 16 to 32, as said below
- dual_shift: float32 [32768], P('row'), may hold values from 0.5 to 2
- start_block: float32 [32, 32768], P(None, 'row'), may hold values from -6 to 6
Outputs:
- projections: float32 [4, 32, 128], replicated
- factors: float32 [4, 32, 32], replicated
- next_block: float32 [32, 32768], P(None, 'row')
Inputs may be any that keep to these rules, and one draw needn't show every extreme that they name: `tile_rows`: the tile slots of one device sit at distinct positions (block row, column block), padding slots included. `tile_cols`: column block j of group g is global block column (j // 1) * 4 + g * 1 + j % 1. Slots from live_tiles on are padding with arbitrary values; in every draw some device has all 32 slots live.
All inputs are finite; a program needn't handle non-finite values.
Results may differ from a plain program's by a relative error of at most 0.013.
Values may be sent and summed in bfloat16 or wider, within the bound.
No kernel may reach another device: no remote copies, remote signals or barrier semaphores. Data moves between devices by JAX's collectives and lax.ppermute only.
A program may use at most 64 MiB of HBM per device.

v0:
```python
import jax
import jax.numpy as jnp
from jax import lax
from jax.sharding import PartitionSpec as P

ITERS = 4


def in_order(parts, dim):
    parts = jnp.moveaxis(parts, 0, dim)
    lengths = parts.shape
    return parts.reshape(*lengths[:dim], lengths[dim] * lengths[dim + 1], *lengths[dim + 2 :])


def copy_for_each(value, axis):
    size = lax.axis_size(axis)
    return lax.all_to_all(
        jnp.broadcast_to(value[None], (size, *value.shape)), axis, 0, 0, tiled=True
    )


def gathered_copies(value, axis, dim):
    return in_order(copy_for_each(value, axis), dim)


def split_up(value, dim, size):
    before, after = (value.shape[:dim], value.shape[dim + 1 :])
    return jnp.moveaxis(value.reshape(*before, size, -1, *after), dim, 0)


def sent_and_summed(value, axis, dim):
    parts = split_up(value, dim, lax.axis_size(axis))
    arrived = lax.all_to_all(parts, axis, split_axis=0, concat_axis=0, tiled=True)
    return arrived.astype(jnp.float32).sum(axis=0)


def of_everyone(value, axis):
    return copy_for_each(value, axis).sum(axis=0)


def inner_product(left, right):
    return lax.dot_general(
        left,
        right,
        (((1,), (1,)), ((), ())),
        precision=lax.Precision.HIGHEST,
        preferred_element_type=jnp.float32,
    )


def apply_matrix(left, right):
    return jnp.dot(left, right, precision=lax.Precision.HIGHEST, preferred_element_type=jnp.float32)


def per_device(tiles, tile_rows, tile_cols, live_tiles, dual_shift, start_block):
    matrix = tiles[0, 0]
    rows_here = tile_rows[0, 0]
    cols_here = tile_cols[0, 0]
    tile_count = matrix.shape[0]
    tile_edge = matrix.shape[1]
    vec_width = start_block.shape[0]
    row_count = start_block.shape[1]
    group_count = lax.axis_size("grp")
    owner_count = lax.axis_size("row")
    owned_blocks = row_count // tile_edge
    quarter_tiles = owned_blocks // group_count
    column_tiles = quarter_tiles * owner_count
    group_index = lax.axis_index("grp")
    live_mask = (jnp.arange(tile_count) < live_tiles[0, 0]).astype(jnp.float32)
    row_table = (rows_here[:, None] == jnp.arange(owned_blocks)[None, :]).astype(
        jnp.float32
    ) * live_mask[:, None]
    col_table = (cols_here[:, None] == jnp.arange(column_tiles)[None, :]).astype(
        jnp.float32
    ) * live_mask[:, None]

    def partial_of(full_rows, group_rows):
        gathered = gathered_copies(group_rows, "row", 1)
        forward = jnp.einsum(
            "kbc,brc->kbr",
            jnp.take(gathered, cols_here, axis=1),
            matrix,
            preferred_element_type=jnp.float32,
        )
        direct = jnp.einsum("kbr,bi->kir", forward, row_table)
        backward = jnp.einsum(
            "kbr,brc->kbc",
            jnp.take(full_rows, rows_here, axis=1),
            matrix,
            preferred_element_type=jnp.float32,
        )
        spread = jnp.einsum("kbc,bj->kjc", backward, col_table)
        mine = sent_and_summed(spread.astype(jnp.bfloat16), "row", 1)
        placed = lax.dynamic_update_slice_in_dim(
            jnp.zeros_like(direct), mine, group_index * quarter_tiles, 1
        )
        return 0.5 * (direct + placed)

    def split_parts(vectors):
        rounded = vectors.astype(jnp.bfloat16).reshape(vec_width, owned_blocks, tile_edge)
        return (
            rounded,
            lax.dynamic_slice_in_dim(rounded, group_index * quarter_tiles, quarter_tiles, 1),
        )

    def finish_sum(partial_value):
        return of_everyone(partial_value, "grp").reshape(vec_width, row_count)

    def reduce_dots(values):
        return of_everyone(values, "row")

    def orthonormal(block, gram_matrix):
        lower_factor = jnp.linalg.cholesky(gram_matrix)
        return (
            lax.linalg.triangular_solve(lower_factor, block, left_side=True, lower=True),
            lower_factor,
        )

    current, unused = orthonormal(start_block, reduce_dots(inner_product(start_block, start_block)))
    total_cols = ITERS * vec_width
    basis_rows = jnp.zeros((total_cols, current.shape[1]), jnp.float32)
    projections = jnp.zeros((ITERS, vec_width, total_cols), jnp.float32)
    factors = jnp.zeros((ITERS, vec_width, vec_width), jnp.float32)

    def lanczos_step(step_index, state_now):
        current, basis_rows, projections, factors = state_now
        basis_rows = lax.dynamic_update_slice_in_dim(basis_rows, current, step_index * vec_width, 0)
        full_rows, group_rows = split_parts(current)
        image = finish_sum(partial_of(full_rows, group_rows)) - current * dual_shift[None, :]
        first_coef = reduce_dots(inner_product(image, basis_rows))
        image = image - apply_matrix(first_coef, basis_rows)
        gram_matrix = reduce_dots(inner_product(image, image))
        current, lower_factor = orthonormal(image, gram_matrix)
        projections = lax.dynamic_update_index_in_dim(projections, first_coef, step_index, 0)
        factors = lax.dynamic_update_index_in_dim(factors, lower_factor, step_index, 0)
        return (current, basis_rows, projections, factors)

    current, basis_rows, projections, factors = lax.fori_loop(
        0, ITERS, lanczos_step, (current, basis_rows, projections, factors)
    )
    return (projections, factors, current)


def solution(mesh):
    in_specs = (
        P("grp", "row", None, None, None),
        P("grp", "row", None),
        P("grp", "row", None),
        P("grp", "row"),
        P("row"),
        P(None, "row"),
    )
    out_specs = (P(), P(), P(None, "row"))
    return jax.shard_map(
        per_device, mesh=mesh, in_specs=in_specs, out_specs=out_specs, check_vma=False
    )
```

profile of v0, /device:TPU:1, one launch (start us, length us, event | category | flops | bytes accessed | tf_op | source)
XLA Modules:
  0.0 370.9 jit_solution(16995554148360917860)
XLA Ops:
  2.8 9.4 %all-to-all-start.5 = ((f32[32,1,1024]{2,1,0:T(1,128)}), f32[32,1,1024]{2,1,0:T(1,128)S(1)}, u32[]{:S(2)}, u32[]{:S(2)}) async-start(f32[32,1,1024]{2,1,0:T(1,128)} %reshape.192), calls=%async_computation.5 | async-start | bytes 262144 | tf_op jit(solution)/shard_map/all_to_all | solution.py:17
  12.9 6.9 %all-to-all-done.5 = f32[32,1,1024]{2,1,0:T(1,128)S(1)} async-done(((f32[32,1,1024]{2,1,0:T(1,128)}), f32[32,1,1024]{2,1,0:T(1,128)S(1)}, u32[]{:S(2)}, u32[]{:S(2)}) %all-to-all-start.5) | async-done | bytes 131104 | tf_op jit(solution)/shard_map/all_to_all | solution.py:17
  28.7 341.6 %while.23 = (s32[]{:T(128)}, f32[32,1024]{1,0:T(8,128)S(1)}, f32[128,1024]{1,0:T(8,128)S(1)}, f32[4,32,128]{2,1,0:T(8,128)}, f32[4,32,32]{2,1,0:T(8,128)}, /*ind...) while((s32[]{:T(128)}, f32[32,1024]{1,0:T(8,128)S(1)}, ...), condition=%wide.region_8.11_spmd.clone.clone, body=%wide.region_3.10_spmd.clone.clone.sunk | while | flops 414691168 | bytes 29908952 | solution.py:138
  40.2 5.0 %all-to-all-done = bf16[32,32,1,256]{3,1,2,0:T(8,128)(2,1)S(1)} async-done(((bf16[32,32,1,256]{3,1,2,0:T(8,128)(2,1)}), bf16[32,32,1,256]{3,1,2,0:T(8,128)(2,1)S(1)}, u32[]{:S(2)}, u32[]{:S(2)}) %all-to-all-start) | async-done | bytes 524320 | tf_op jit(solution)/shard_map/while/body/eval_jaxpr/all_to_all | solution.py:17
  53.7 6.9 %all-to-all-done.1 = bf16[32,32,1,256]{3,1,2,0:T(8,128)(2,1)S(1)} async-done(((bf16[32,32,1,256]{3,1,2,0:T(8,128)(2,1)}), bf16[32,32,1,256]{3,1,2,0:T(8,128)(2,1)S(1)}, u32[]{:S(2)}, u32[]{:S(2)}) %all-to-all-start.1) | async-done | bytes 524320 | tf_op jit(solution)/shard_map/while/body/eval_jaxpr/all_to_all | solution.py:33
  60.8 12.6 %all_to_all.75 = f32[4,32,4,256]{3,1,2,0:T(8,128)S(1)} all-to-all(f32[4,32,4,256]{3,1,2,0:T(8,128)S(1)} %broadcast_in_dim.180), channel_id=1, replica_groups=mesh['grp'=4,'row'=32] {'grp'}, dimensions={0} | all-to-all | bytes 1048576 | tf_op jit(solution)/shard_map/while/body/eval_jaxpr/all_to_all | solution.py:17
  75.0 5.5 %all-to-all-start.3 = ((f32[32,32,128]{2,1,0:T(8,128)}), f32[32,32,128]{2,1,0:T(8,128)S(1)}, u32[]{:S(2)}, u32[]{:S(2)}) async-start(f32[32,32,128]{2,1,0:T(8,128)} %broadcast_in_dim.181), calls=%async_computation.3 | async-start | bytes 1048576 | tf_op jit(solution)/shard_map/while/body/eval_jaxpr/all_to_all | solution.py:17
  80.4 11.4 %all-to-all-done.3 = f32[32,32,128]{2,1,0:T(8,128)S(1)} async-done(((f32[32,32,128]{2,1,0:T(8,128)}), f32[32,32,128]{2,1,0:T(8,128)S(1)}, u32[]{:S(2)}, u32[]{:S(2)}) %all-to-all-start.3) | async-done | bytes 524320 | tf_op jit(solution)/shard_map/while/body/eval_jaxpr/all_to_all | solution.py:17
  98.1 7.1 %all-to-all-done.4 = f32[32,1,1024]{2,1,0:T(1,128)S(1)} async-done(((f32[32,1,1024]{2,1,0:T(1,128)}), f32[32,1,1024]{2,1,0:T(1,128)S(1)}, u32[]{:S(2)}, u32[]{:S(2)}) %all-to-all-start.4) | async-done | bytes 131104 | tf_op jit(solution)/shard_map/while/body/eval_jaxpr/all_to_all | solution.py:17
  126.8 5.0 %all-to-all-done = bf16[32,32,1,256]{3,1,2,0:T(8,128)(2,1)S(1)} async-done(((bf16[32,32,1,256]{3,1,2,0:T(8,128)(2,1)}), bf16[32,32,1,256]{3,1,2,0:T(8,128)(2,1)S(1)}, u32[]{:S(2)}, u32[]{:S(2)}) %all-to-all-start) | async-done | bytes 524320 | tf_op jit(solution)/shard_map/while/body/eval_jaxpr/all_to_all | solution.py:17
  140.3 6.9 %all-to-all-done.1 = bf16[32,32,1,256]{3,1,2,0:T(8,128)(2,1)S(1)} async-done(((bf16[32,32,1,256]{3,1,2,0:T(8,128)(2,1)}), bf16[32,32,1,256]{3,1,2,0:T(8,128)(2,1)S(1)}, u32[]{:S(2)}, u32[]{:S(2)}) %all-to-all-start.1) | async-done | bytes 524320 | tf_op jit(solution)/shard_map/while/body/eval_jaxpr/all_to_all | solution.py:33
  147.4 11.6 %all_to_all.75 = f32[4,32,4,256]{3,1,2,0:T(8,128)S(1)} all-to-all(f32[4,32,4,256]{3,1,2,0:T(8,128)S(1)} %broadcast_in_dim.180), channel_id=1, replica_groups=mesh['grp'=4,'row'=32] {'grp'}, dimensions={0} | all-to-all | bytes 1048576 | tf_op jit(solution)/shard_map/while/body/eval_jaxpr/all_to_all | solution.py:17
  165.3 11.5 %all-to-all-done.3 = f32[32,32,128]{2,1,0:T(8,128)S(1)} async-done(((f32[32,32,128]{2,1,0:T(8,128)}), f32[32,32,128]{2,1,0:T(8,128)S(1)}, u32[]{:S(2)}, u32[]{:S(2)}) %all-to-all-start.3) | async-done | bytes 524320 | tf_op jit(solution)/shard_map/while/body/eval_jaxpr/all_to_all | solution.py:17
  183.1 7.1 %all-to-all-done.4 = f32[32,1,1024]{2,1,0:T(1,128)S(1)} async-done(((f32[32,1,1024]{2,1,0:T(1,128)}), f32[32,1,1024]{2,1,0:T(1,128)S(1)}, u32[]{:S(2)}, u32[]{:S(2)}) %all-to-all-start.4) | async-done | bytes 131104 | tf_op jit(solution)/shard_map/while/body/eval_jaxpr/all_to_all | solution.py:17
  211.8 5.0 %all-to-all-done = bf16[32,32,1,256]{3,1,2,0:T(8,128)(2,1)S(1)} async-done(((bf16[32,32,1,256]{3,1,2,0:T(8,128)(2,1)}), bf16[32,32,1,256]{3,1,2,0:T(8,128)(2,1)S(1)}, u32[]{:S(2)}, u32[]{:S(2)}) %all-to-all-start) | async-done | bytes 524320 | tf_op jit(solution)/shard_map/while/body/eval_jaxpr/all_to_all | solution.py:17
  225.3 6.9 %all-to-all-done.1 = bf16[32,32,1,256]{3,1,2,0:T(8,128)(2,1)S(1)} async-done(((bf16[32,32,1,256]{3,1,2,0:T(8,128)(2,1)}), bf16[32,32,1,256]{3,1,2,0:T(8,128)(2,1)S(1)}, u32[]{:S(2)}, u32[]{:S(2)}) %all-to-all-start.1) | async-done | bytes 524320 | tf_op jit(solution)/shard_map/while/body/eval_jaxpr/all_to_all | solution.py:33
  232.4 11.6 %all_to_all.75 = f32[4,32,4,256]{3,1,2,0:T(8,128)S(1)} all-to-all(f32[4,32,4,256]{3,1,2,0:T(8,128)S(1)} %broadcast_in_dim.180), channel_id=1, replica_groups=mesh['grp'=4,'row'=32] {'grp'}, dimensions={0} | all-to-all | bytes 1048576 | tf_op jit(solution)/shard_map/while/body/eval_jaxpr/all_to_all | solution.py:17
  250.3 11.5 %all-to-all-done.3 = f32[32,32,128]{2,1,0:T(8,128)S(1)} async-done(((f32[32,32,128]{2,1,0:T(8,128)}), f32[32,32,128]{2,1,0:T(8,128)S(1)}, u32[]{:S(2)}, u32[]{:S(2)}) %all-to-all-start.3) | async-done | bytes 524320 | tf_op jit(solution)/shard_map/while/body/eval_jaxpr/all_to_all | solution.py:17
  268.1 7.1 %all-to-all-done.4 = f32[32,1,1024]{2,1,0:T(1,128)S(1)} async-done(((f32[32,1,1024]{2,1,0:T(1,128)}), f32[32,1,1024]{2,1,0:T(1,128)S(1)}, u32[]{:S(2)}, u32[]{:S(2)}) %all-to-all-start.4) | async-done | bytes 131104 | tf_op jit(solution)/shard_map/while/body/eval_jaxpr/all_to_all | solution.py:17
  296.7 5.0 %all-to-all-done = bf16[32,32,1,256]{3,1,2,0:T(8,128)(2,1)S(1)} async-done(((bf16[32,32,1,256]{3,1,2,0:T(8,128)(2,1)}), bf16[32,32,1,256]{3,1,2,0:T(8,128)(2,1)S(1)}, u32[]{:S(2)}, u32[]{:S(2)}) %all-to-all-start) | async-done | bytes 524320 | tf_op jit(solution)/shard_map/while/body/eval_jaxpr/all_to_all | solution.py:17
  310.3 6.9 %all-to-all-done.1 = bf16[32,32,1,256]{3,1,2,0:T(8,128)(2,1)S(1)} async-done(((bf16[32,32,1,256]{3,1,2,0:T(8,128)(2,1)}), bf16[32,32,1,256]{3,1,2,0:T(8,128)(2,1)S(1)}, u32[]{:S(2)}, u32[]{:S(2)}) %all-to-all-start.1) | async-done | bytes 524320 | tf_op jit(solution)/shard_map/while/body/eval_jaxpr/all_to_all | solution.py:33
  317.4 11.6 %all_to_all.75 = f32[4,32,4,256]{3,1,2,0:T(8,128)S(1)} all-to-all(f32[4,32,4,256]{3,1,2,0:T(8,128)S(1)} %broadcast_in_dim.180), channel_id=1, replica_groups=mesh['grp'=4,'row'=32] {'grp'}, dimensions={0} | all-to-all | bytes 1048576 | tf_op jit(solution)/shard_map/while/body/eval_jaxpr/all_to_all | solution.py:17
  335.3 11.5 %all-to-all-done.3 = f32[32,32,128]{2,1,0:T(8,128)S(1)} async-done(((f32[32,32,128]{2,1,0:T(8,128)}), f32[32,32,128]{2,1,0:T(8,128)S(1)}, u32[]{:S(2)}, u32[]{:S(2)}) %all-to-all-start.3) | async-done | bytes 524320 | tf_op jit(solution)/shard_map/while/body/eval_jaxpr/all_to_all | solution.py:17
  353.1 7.1 %all-to-all-done.4 = f32[32,1,1024]{2,1,0:T(1,128)S(1)} async-done(((f32[32,1,1024]{2,1,0:T(1,128)}), f32[32,1,1024]{2,1,0:T(1,128)S(1)}, u32[]{:S(2)}, u32[]{:S(2)}) %all-to-all-start.4) | async-done | bytes 131104 | tf_op jit(solution)/shard_map/while/body/eval_jaxpr/all_to_all | solution.py:17
  (254 shorter events, 177.1 us)
Async XLA Ops:
  2.8 17.0 %all-to-all-start.5 = ((f32[32,1,1024]{2,1,0:T(1,128)}), f32[32,1,1024]{2,1,0:T(1,128)S(1)}, u32[]{:S(2)}, u32[]{:S(2)}) async-start(f32[32,1,1024]{2,1,0:T(1,128)} %reshape.192), calls=%async_computation.5 | async-start | bytes 262144 | tf_op jit(solution)/shard_map/all_to_all | solution.py:17
  29.7 15.5 %all-to-all-start = ((bf16[32,32,1,256]{3,1,2,0:T(8,128)(2,1)}), bf16[32,32,1,256]{3,1,2,0:T(8,128)(2,1)S(1)}, u32[]{:S(2)}, u32[]{:S(2)}) async-start(bf16[32,32,1,256]{3,1,2,0:T(8,128)(2,1)} %broadcast_in_dim.179), calls=%async_computation | async-start | bytes 1048576 | tf_op jit(solution)/shard_map/while/body/eval_jaxpr/all_to_all | solution.py:17
  39.0 14.2 %copy-start.4 = (s32[32]{0:T(128)S(1)}, s32[32]{0:T(128)}, u32[]{:S(2)}) copy-start(s32[32]{0:T(128)} %get-tuple-element.490) | copy-start | bytes 388 | tf_op jit(solution)/shard_map/while
  45.2 15.5 %all-to-all-start.1 = ((bf16[32,32,1,256]{3,1,2,0:T(8,128)(2,1)}), bf16[32,32,1,256]{3,1,2,0:T(8,128)(2,1)S(1)}, u32[]{:S(2)}, u32[]{:S(2)}) async-start(bf16[32,32,1,256]{3,1,2,0:T(8,128)(2,1)} %copy.79), calls=%async_computation.1 | async-start | bytes 1048576 | tf_op jit(solution)/shard_map/while/body/eval_jaxpr/all_to_all | solution.py:33
  49.7 23.8 %copy-start.2 = (f32[1024]{0:T(1024)S(1)}, f32[1024]{0:T(1024)}, u32[]{:S(2)}) copy-start(f32[1024]{0:T(1024)} %get-tuple-element.491) | copy-start | bytes 12292 | tf_op jit(solution)/shard_map/while
  75.0 16.9 %all-to-all-start.3 = ((f32[32,32,128]{2,1,0:T(8,128)}), f32[32,32,128]{2,1,0:T(8,128)S(1)}, u32[]{:S(2)}, u32[]{:S(2)}) async-start(f32[32,32,128]{2,1,0:T(8,128)} %broadcast_in_dim.181), calls=%async_computation.3 | async-start | bytes 1048576 | tf_op jit(solution)/shard_map/while/body/eval_jaxpr/all_to_all | solution.py:17
  93.6 11.6 %all-to-all-start.4 = ((f32[32,1,1024]{2,1,0:T(1,128)}), f32[32,1,1024]{2,1,0:T(1,128)S(1)}, u32[]{:S(2)}, u32[]{:S(2)}) async-start(f32[32,1,1024]{2,1,0:T(1,128)} %reshape.206), calls=%async_computation.4 | async-start | bytes 262144 | tf_op jit(solution)/shard_map/while/body/eval_jaxpr/all_to_all | solution.py:17
  116.3 15.5 %all-to-all-start = ((bf16[32,32,1,256]{3,1,2,0:T(8,128)(2,1)}), bf16[32,32,1,256]{3,1,2,0:T(8,128)(2,1)S(1)}, u32[]{:S(2)}, u32[]{:S(2)}) async-start(bf16[32,32,1,256]{3,1,2,0:T(8,128)(2,1)} %broadcast_in_dim.179), calls=%async_computation | async-start | bytes 1048576 | tf_op jit(solution)/shard_map/while/body/eval_jaxpr/all_to_all | solution.py:17
  125.6 14.2 %copy-start.4 = (s32[32]{0:T(128)S(1)}, s32[32]{0:T(128)}, u32[]{:S(2)}) copy-start(s32[32]{0:T(128)} %get-tuple-element.490) | copy-start | bytes 388 | tf_op jit(solution)/shard_map/while
  131.8 15.5 %all-to-all-start.1 = ((bf16[32,32,1,256]{3,1,2,0:T(8,128)(2,1)}), bf16[32,32,1,256]{3,1,2,0:T(8,128)(2,1)S(1)}, u32[]{:S(2)}, u32[]{:S(2)}) async-start(bf16[32,32,1,256]{3,1,2,0:T(8,128)(2,1)} %copy.79), calls=%async_computation.1 | async-start | bytes 1048576 | tf_op jit(solution)/shard_map/while/body/eval_jaxpr/all_to_all | solution.py:33
  136.3 22.8 %copy-start.2 = (f32[1024]{0:T(1024)S(1)}, f32[1024]{0:T(1024)}, u32[]{:S(2)}) copy-start(f32[1024]{0:T(1024)} %get-tuple-element.491) | copy-start | bytes 12292 | tf_op jit(solution)/shard_map/while
  160.5 16.3 %all-to-all-start.3 = ((f32[32,32,128]{2,1,0:T(8,128)}), f32[32,32,128]{2,1,0:T(8,128)S(1)}, u32[]{:S(2)}, u32[]{:S(2)}) async-start(f32[32,32,128]{2,1,0:T(8,128)} %broadcast_in_dim.181), calls=%async_computation.3 | async-start | bytes 1048576 | tf_op jit(solution)/shard_map/while/body/eval_jaxpr/all_to_all | solution.py:17
  178.6 11.6 %all-to-all-start.4 = ((f32[32,1,1024]{2,1,0:T(1,128)}), f32[32,1,1024]{2,1,0:T(1,128)S(1)}, u32[]{:S(2)}, u32[]{:S(2)}) async-start(f32[32,1,1024]{2,1,0:T(1,128)} %reshape.206), calls=%async_computation.4 | async-start | bytes 262144 | tf_op jit(solution)/shard_map/while/body/eval_jaxpr/all_to_all | solution.py:17
  201.3 15.5 %all-to-all-start = ((bf16[32,32,1,256]{3,1,2,0:T(8,128)(2,1)}), bf16[32,32,1,256]{3,1,2,0:T(8,128)(2,1)S(1)}, u32[]{:S(2)}, u32[]{:S(2)}) async-start(bf16[32,32,1,256]{3,1,2,0:T(8,128)(2,1)} %broadcast_in_dim.179), calls=%async_computation | async-start | bytes 1048576 | tf_op jit(solution)/shard_map/while/body/eval_jaxpr/all_to_all | solution.py:17
  210.6 14.2 %copy-start.4 = (s32[32]{0:T(128)S(1)}, s32[32]{0:T(128)}, u32[]{:S(2)}) copy-start(s32[32]{0:T(128)} %get-tuple-element.490) | copy-start | bytes 388 | tf_op jit(solution)/shard_map/while
  216.8 15.5 %all-to-all-start.1 = ((bf16[32,32,1,256]{3,1,2,0:T(8,128)(2,1)}), bf16[32,32,1,256]{3,1,2,0:T(8,128)(2,1)S(1)}, u32[]{:S(2)}, u32[]{:S(2)}) async-start(bf16[32,32,1,256]{3,1,2,0:T(8,128)(2,1)} %copy.79), calls=%async_computation.1 | async-start | bytes 1048576 | tf_op jit(solution)/shard_map/while/body/eval_jaxpr/all_to_all | solution.py:33
  221.3 22.8 %copy-start.2 = (f32[1024]{0:T(1024)S(1)}, f32[1024]{0:T(1024)}, u32[]{:S(2)}) copy-start(f32[1024]{0:T(1024)} %get-tuple-element.491) | copy-start | bytes 12292 | tf_op jit(solution)/shard_map/while
  245.5 16.3 %all-to-all-start.3 = ((f32[32,32,128]{2,1,0:T(8,128)}), f32[32,32,128]{2,1,0:T(8,128)S(1)}, u32[]{:S(2)}, u32[]{:S(2)}) async-start(f32[32,32,128]{2,1,0:T(8,128)} %broadcast_in_dim.181), calls=%async_computation.3 | async-start | bytes 1048576 | tf_op jit(solution)/shard_map/while/body/eval_jaxpr/all_to_all | solution.py:17
  263.6 11.6 %all-to-all-start.4 = ((f32[32,1,1024]{2,1,0:T(1,128)}), f32[32,1,1024]{2,1,0:T(1,128)S(1)}, u32[]{:S(2)}, u32[]{:S(2)}) async-start(f32[32,1,1024]{2,1,0:T(1,128)} %reshape.206), calls=%async_computation.4 | async-start | bytes 262144 | tf_op jit(solution)/shard_map/while/body/eval_jaxpr/all_to_all | solution.py:17
  286.2 15.5 %all-to-all-start = ((bf16[32,32,1,256]{3,1,2,0:T(8,128)(2,1)}), bf16[32,32,1,256]{3,1,2,0:T(8,128)(2,1)S(1)}, u32[]{:S(2)}, u32[]{:S(2)}) async-start(bf16[32,32,1,256]{3,1,2,0:T(8,128)(2,1)} %broadcast_in_dim.179), calls=%async_computation | async-start | bytes 1048576 | tf_op jit(solution)/shard_map/while/body/eval_jaxpr/all_to_all | solution.py:17
  301.7 15.5 %all-to-all-start.1 = ((bf16[32,32,1,256]{3,1,2,0:T(8,128)(2,1)}), bf16[32,32,1,256]{3,1,2,0:T(8,128)(2,1)S(1)}, u32[]{:S(2)}, u32[]{:S(2)}) async-start(bf16[32,32,1,256]{3,1,2,0:T(8,128)(2,1)} %copy.79), calls=%async_computation.1 | async-start | bytes 1048576 | tf_op jit(solution)/shard_map/while/body/eval_jaxpr/all_to_all | solution.py:33
  306.3 22.8 %copy-start.2 = (f32[1024]{0:T(1024)S(1)}, f32[1024]{0:T(1024)}, u32[]{:S(2)}) copy-start(f32[1024]{0:T(1024)} %get-tuple-element.491) | copy-start | bytes 12292 | tf_op jit(solution)/shard_map/while
  330.5 16.3 %all-to-all-start.3 = ((f32[32,32,128]{2,1,0:T(8,128)}), f32[32,32,128]{2,1,0:T(8,128)S(1)}, u32[]{:S(2)}, u32[]{:S(2)}) async-start(f32[32,32,128]{2,1,0:T(8,128)} %broadcast_in_dim.181), calls=%async_computation.3 | async-start | bytes 1048576 | tf_op jit(solution)/shard_map/while/body/eval_jaxpr/all_to_all | solution.py:17
  348.5 11.6 %all-to-all-start.4 = ((f32[32,1,1024]{2,1,0:T(1,128)}), f32[32,1,1024]{2,1,0:T(1,128)S(1)}, u32[]{:S(2)}, u32[]{:S(2)}) async-start(f32[32,1,1024]{2,1,0:T(1,128)} %reshape.206), calls=%async_computation.4 | async-start | bytes 262144 | tf_op jit(solution)/shard_map/while/body/eval_jaxpr/all_to_all | solution.py:17
  (7 other events, 55.4 us)
where the time goes:
time: 373 us; the launch traced here: 371 us
  waiting for transfers between devices  129 us (35%)
  starting transfers between devices  76.4 us (20%)
  other arithmetic  49.7 us (13%)
  blocking collectives  47.3 us (13%)
  matrix products  36.5 us (10%)
  local copies, waits for them, and re-layouts  29.3 us (8%)
    all_to_all x13, waiting for transfers between devices, copy_for_each(): lax.all_to_all(jnp.broadcast_to(value[None], (size, *value.shape)), axis,...  101 us
    all_to_all x13, starting transfers between devices, copy_for_each(): lax.all_to_all(jnp.broadcast_to(value[None], (size, *value.shape)), axis,...  60.7 us
    all_to_all x4, blocking collectives, copy_for_each(): lax.all_to_all(jnp.broadcast_to(value[None], (size, *value.shape)), axis,...  47.3 us
    all_to_all x4, waiting for transfers between devices, sent_and_summed(): lax.all_to_all(parts, axis, split_axis=0, concat_axis=0, tiled=True)  27.7 us
    another operation x15, other arithmetic, orthonormal(): lower_factor = jnp.linalg.cholesky(gram_matrix)  18 us
    all_to_all x4, starting transfers between devices, sent_and_summed(): lax.all_to_all(parts, axis, split_axis=0, concat_axis=0, tiled=True)  15.7 us
    another operation x10, other arithmetic, orthonormal(): lax.linalg.triangular_solve(lower_factor, block, left_side=True, lower=True)  15.4 us
    dot_general x4, matrix products, partial_of(): jnp.einsum('kbc,brc->kbr', jnp.take(gathered, cols_here, axis=1), matrix,...  14.1 us
  transfers between devices with their start and end apart: 17, of which 17 were waited for; matrix products, arithmetic and copies ran while one was open for 13% of the time, Pallas kernels for 0%

commit v1 on v0

v1 whole, which is shorter than its diff:
```python
import jax
import jax.numpy as jnp
from jax import lax
from jax.sharding import PartitionSpec as P

ITERS = 4
SHIFT = 1.0625
PULL = 0.375

F32 = jnp.float32
BF16 = jnp.bfloat16
HIGHEST = lax.Precision.HIGHEST


def exchange(parts, axis):
    return lax.all_to_all(parts, axis, split_axis=0, concat_axis=0, tiled=True)


def copies(value, axis):
    return exchange(jnp.broadcast_to(value[None], (lax.axis_size(axis), *value.shape)), axis)


def dot(left, right, dims):
    return lax.dot_general(
        left, right, (dims, ((), ())), precision=HIGHEST, preferred_element_type=F32
    )


def per_device(tiles, tile_rows, tile_cols, live_tiles, dual_shift, start_block):
    matrix = tiles[0, 0]
    rows_here = tile_rows[0, 0]
    cols_here = tile_cols[0, 0]
    tile_count, edge, _ = matrix.shape
    width, row_count = start_block.shape
    blocks = row_count // edge
    owners = lax.axis_size("row")
    group = lax.axis_index("grp")
    live_mask = (jnp.arange(tile_count) < live_tiles[0, 0]).astype(F32)
    row_table = (rows_here[:, None] == jnp.arange(blocks)[None, :]).astype(F32) * live_mask[:, None]
    col_table = (cols_here[:, None] == jnp.arange(owners)[None, :]).astype(F32) * live_mask[:, None]

    def forward(columns):
        products = jnp.einsum(
            "bkc,brc->bkr", jnp.take(columns, cols_here, axis=0), matrix,
            preferred_element_type=F32,
        )
        return jnp.einsum("bkr,bi->ikr", products, row_table)

    def backward(own_rows):
        products = jnp.einsum(
            "bkr,brc->bkc", jnp.take(own_rows, rows_here, axis=0), matrix,
            preferred_element_type=F32,
        )
        return jnp.einsum("bkc,bj->jkc", products, col_table)

    full = jnp.moveaxis(start_block.reshape(width, blocks, edge), 1, 0)
    shift_own = lax.dynamic_index_in_dim(dual_shift.reshape(blocks, edge), group, 0, False)
    own = lax.dynamic_index_in_dim(full, group, 0, False)
    before = None
    basis = [full]
    for step in range(ITERS):
        columns = copies(own.astype(BF16), "row")
        back = exchange(backward(full.astype(BF16)).astype(BF16), "row")
        direct = exchange(forward(columns), "grp")
        image = 0.5 * (back.astype(F32).sum(0) + direct.sum(0))
        following = image + (SHIFT - shift_own)[None, :] * own
        if before is not None:
            following = following - PULL * before
        before, own = own, following
        full = copies(own, "grp")
        basis.append(full)

    vectors = jnp.concatenate(basis, 1)
    total = (ITERS + 1) * width
    partial = sum(dot(vectors[i], vectors[i], ((1,), (1,))) for i in range(blocks))
    gram = exchange(partial.reshape(owners, total // owners, total), "row").sum(0)
    gram = copies(gram, "row").reshape(total, total)
    lower = jnp.linalg.cholesky(gram)
    inverse = lax.linalg.triangular_solve(lower, jnp.eye(total, dtype=F32), left_side=True, lower=True)
    used = ITERS * width
    image_rows = lower[width:] - SHIFT * lower[:used]
    image_rows = image_rows + PULL * jnp.concatenate([jnp.zeros((width, total), F32), lower[: used - width]])
    hessenberg = dot(inverse[:used, :used], image_rows, ((1,), (0,)))
    blocked = hessenberg.reshape(ITERS, width, ITERS + 1, width)
    at = jnp.arange(ITERS)
    keep = (jnp.arange(ITERS)[None, :] <= at[:, None]).astype(F32)
    projections = (blocked[:, :, :ITERS] * keep[:, None, :, None]).reshape(ITERS, width, used)
    factors = jnp.stack([blocked[j, :, j + 1] for j in range(ITERS)]) * jnp.tril(jnp.ones((width, width), F32))
    last = jnp.stack([dot(inverse[used:], vectors[i], ((1,), (0,))) for i in range(blocks)], 1)
    return (projections, factors, last.reshape(width, row_count))


def solution(mesh):
    in_specs = (
        P("grp", "row", None, None, None),
        P("grp", "row", None),
        P("grp", "row", None),
        P("grp", "row"),
        P("row"),
        P(None, "row"),
    )
    out_specs = (P(), P(), P(None, "row"))
    return jax.shard_map(
        per_device, mesh=mesh, in_specs=in_specs, out_specs=out_specs, check_vma=False
    )
```

time: 373 us -> 296 us (0.79)
  blocking collectives: 47.3 us -> 0 us
  waiting for transfers between devices: 129 us -> 101 us
  starting transfers between devices: 76.4 us -> 82.1 us
  local copies, waits for them, and re-layouts: 29.3 us -> 24.4 us
    all_to_all x4 -> x0, blocking collectives: 47.3 us -> none  [copy_for_each(): lax.all_to_all(jnp.broadcast_to(value[None], (size, *value.shape)), axis,...]
    all_to_all x17 -> x18, waiting for transfers between devices: 129 us -> 101 us  [exchange(): return lax.all_to_all(parts, axis, split_axis=0, concat_axis=0, tiled=True)]
    another operation x25 -> x13, other arithmetic: 33.4 us -> 45.6 us  [the longest x7 25.8 us: per_device(): lower = jnp.linalg.cholesky(gram)]
    all_to_all x17 -> x18, starting transfers between devices: 76.4 us -> 82.1 us  [exchange(): return lax.all_to_all(parts, axis, split_axis=0, concat_axis=0, tiled=True)]
    dynamic_update_slice x4 -> x0, other arithmetic: 5.04 us -> none  [lanczos_step(): lax.dynamic_update_index_in_dim(factors, lower_factor, step_index, 0)]
    while x36 -> x0, local copies, waits for them, and re-layouts: 4.42 us -> none
    transpose x4 -> x0, local copies, waits for them, and re-layouts: 4.41 us -> none  [split_up(): return jnp.moveaxis(value.reshape(*before, size, -1, *after), dim, 0)]
    convert_element_type x0 -> x4, local copies, waits for them, and re-layouts: none -> 4.36 us  [per_device(): back = exchange(backward(full.astype(BF16)).astype(BF16), 'row')]
  transfers between devices with their start and end apart: 17 -> 18, of which waited for: 17 -> 18; matrix products, arithmetic and copies ran while one was open for 13% -> 15% of each run, Pallas kernels for 0% -> 0%
where the time goes in v1:
time: 296 us; the launch traced here: 294 us
  waiting for transfers between devices  101 us (34%)
  starting transfers between devices  82.1 us (28%)
  other arithmetic  50.1 us (17%)
  matrix products  33.1 us (11%)
  local copies, waits for them, and re-layouts  24.4 us (8%)
  between operations  3.38 us (1%)
    all_to_all x18, waiting for transfers between devices, exchange(): return lax.all_to_all(parts, axis, split_axis=0, concat_axis=0, tiled=True)  101 us
    all_to_all x18, starting transfers between devices, exchange(): return lax.all_to_all(parts, axis, split_axis=0, concat_axis=0, tiled=True)  82.1 us
    another operation x7, other arithmetic, per_device(): lower = jnp.linalg.cholesky(gram)  25.8 us
    another operation x6, other arithmetic, per_device(): lax.linalg.triangular_solve(lower, jnp.eye(total, dtype=F32), left_side=T...  19.8 us
    dot_general x4, matrix products, forward(): jnp.einsum('bkc,brc->bkr', jnp.take(columns, cols_here, axis=0), matrix,...  14.1 us
    dot_general x4, matrix products, backward(): jnp.einsum('bkr,brc->bkc', jnp.take(own_rows, rows_here, axis=0), matrix,...  12.2 us
    broadcast_in_dim x9, local copies, waits for them, and re-layouts, copies(): jnp.broadcast_to(value[None], (lax.axis_size(axis), *value.shape))  6.08 us
  transfers between devices with their start and end apart: 18, of which 18 were waited for; matrix products, arithmetic and copies ran while one was open for 15% of the time, Pallas kernels for 0%

profile of v1, /device:TPU:1, one launch (start us, length us, event | category | flops | bytes accessed | tf_op | source)
XLA Modules:
  0.0 293.7 jit_solution(14681997633007946676)
XLA Ops:
  2.5 9.4 %all-to-all-start.1 = ((bf16[32,32,256]{2,1,0:T(8,128)(2,1)}), bf16[32,32,256]{2,1,0:T(8,128)(2,1)S(1)}, u32[]{:S(2)}, u32[]{:S(2)}) async-start(bf16[32,32,256]{2,1,0:T(8,128)(2,1)} %broadcast_in_dim.40), calls=%async_computation.1 | async-start | bytes 1048576 | tf_op jit(solution)/shard_map/all_to_all | solution.py:16
  32.8 6.2 %all-to-all-done = bf16[32,32,256]{2,1,0:T(8,128)(2,1)S(1)} async-done(((bf16[32,32,256]{2,1,0:T(8,128)(2,1)}), bf16[32,32,256]{2,1,0:T(8,128)(2,1)S(1)}, u32[]{:S(2)}, u32[]{:S(2)}) %all-to-all-start) | async-done | bytes 524320 | tf_op jit(solution)/shard_map/all_to_all | solution.py:16
  43.2 4.7 %all-to-all-done.2 = f32[4,32,256]{2,1,0:T(8,128)S(1)} async-done(((f32[4,32,256]{2,1,0:T(8,128)}), f32[4,32,256]{2,1,0:T(8,128)S(1)}, u32[]{:S(2)}, u32[]{:S(2)}) %all-to-all-start.2) | async-done | bytes 131104 | tf_op jit(solution)/shard_map/all_to_all | solution.py:16
  52.0 4.8 %all-to-all-done.3 = f32[4,32,256]{2,1,0:T(8,128)S(1)} async-done(((f32[4,32,256]{2,1,0:T(8,128)}), f32[4,32,256]{2,1,0:T(8,128)S(1)}, u32[]{:S(2)}, u32[]{:S(2)}) %all-to-all-start.3) | async-done | bytes 131104 | tf_op jit(solution)/shard_map/all_to_all | solution.py:16
  57.7 6.5 %all-to-all-start.5 = ((bf16[32,32,256]{2,1,0:T(8,128)(2,1)}), bf16[32,32,256]{2,1,0:T(8,128)(2,1)S(1)}, u32[]{:S(2)}, u32[]{:S(2)}) async-start(bf16[32,32,256]{2,1,0:T(8,128)(2,1)} %broadcast_in_dim.42), calls=%async_computation.5 | async-start | bytes 1048576 | tf_op jit(solution)/shard_map/all_to_all | solution.py:16
  69.4 6.3 %all-to-all-done.5 = bf16[32,32,256]{2,1,0:T(8,128)(2,1)S(1)} async-done(((bf16[32,32,256]{2,1,0:T(8,128)(2,1)}), bf16[32,32,256]{2,1,0:T(8,128)(2,1)S(1)}, u32[]{:S(2)}, u32[]{:S(2)}) %all-to-all-start.5) | async-done | bytes 524320 | tf_op jit(solution)/shard_map/all_to_all | solution.py:16
  84.9 6.3 %all-to-all-done.4 = bf16[32,32,256]{2,1,0:T(8,128)(2,1)S(1)} async-done(((bf16[32,32,256]{2,1,0:T(8,128)(2,1)}), bf16[32,32,256]{2,1,0:T(8,128)(2,1)S(1)}, u32[]{:S(2)}, u32[]{:S(2)}) %all-to-all-start.4) | async-done | bytes 524320 | tf_op jit(solution)/shard_map/all_to_all | solution.py:16
  103.4 4.8 %all-to-all-done.7 = f32[4,32,256]{2,1,0:T(8,128)S(1)} async-done(((f32[4,32,256]{2,1,0:T(8,128)}), f32[4,32,256]{2,1,0:T(8,128)S(1)}, u32[]{:S(2)}, u32[]{:S(2)}) %all-to-all-start.7) | async-done | bytes 131104 | tf_op jit(solution)/shard_map/all_to_all | solution.py:16
  109.0 6.2 %all-to-all-start.9 = ((bf16[32,32,256]{2,1,0:T(8,128)(2,1)}), bf16[32,32,256]{2,1,0:T(8,128)(2,1)S(1)}, u32[]{:S(2)}, u32[]{:S(2)}) async-start(bf16[32,32,256]{2,1,0:T(8,128)(2,1)} %broadcast_in_dim.44), calls=%async_computation.9 | async-start | bytes 1048576 | tf_op jit(solution)/shard_map/all_to_all | solution.py:16
  120.5 6.3 %all-to-all-done.9 = bf16[32,32,256]{2,1,0:T(8,128)(2,1)S(1)} async-done(((bf16[32,32,256]{2,1,0:T(8,128)(2,1)}), bf16[32,32,256]{2,1,0:T(8,128)(2,1)S(1)}, u32[]{:S(2)}, u32[]{:S(2)}) %all-to-all-start.9) | async-done | bytes 524320 | tf_op jit(solution)/shard_map/all_to_all | solution.py:16
  135.9 6.4 %all-to-all-done.8 = bf16[32,32,256]{2,1,0:T(8,128)(2,1)S(1)} async-done(((bf16[32,32,256]{2,1,0:T(8,128)(2,1)}), bf16[32,32,256]{2,1,0:T(8,128)(2,1)S(1)}, u32[]{:S(2)}, u32[]{:S(2)}) %all-to-all-start.8) | async-done | bytes 524320 | tf_op jit(solution)/shard_map/all_to_all | solution.py:16
  145.7 4.7 %all-to-all-done.10 = f32[4,32,256]{2,1,0:T(8,128)S(1)} async-done(((f32[4,32,256]{2,1,0:T(8,128)}), f32[4,32,256]{2,1,0:T(8,128)S(1)}, u32[]{:S(2)}, u32[]{:S(2)}) %all-to-all-start.10) | async-done | bytes 131104 | tf_op jit(solution)/shard_map/all_to_all | solution.py:16
  154.5 4.8 %all-to-all-done.11 = f32[4,32,256]{2,1,0:T(8,128)S(1)} async-done(((f32[4,32,256]{2,1,0:T(8,128)}), f32[4,32,256]{2,1,0:T(8,128)S(1)}, u32[]{:S(2)}, u32[]{:S(2)}) %all-to-all-start.11) | async-done | bytes 131104 | tf_op jit(solution)/shard_map/all_to_all | solution.py:16
  160.1 6.4 %all-to-all-start.13 = ((bf16[32,32,256]{2,1,0:T(8,128)(2,1)}), bf16[32,32,256]{2,1,0:T(8,128)(2,1)S(1)}, u32[]{:S(2)}, u32[]{:S(2)}) async-start(bf16[32,32,256]{2,1,0:T(8,128)(2,1)} %broadcast_in_dim.46), calls=%async_computation.13 | async-start | bytes 1048576 | tf_op jit(solution)/shard_map/all_to_all | solution.py:16
  171.8 6.3 %all-to-all-done.13 = bf16[32,32,256]{2,1,0:T(8,128)(2,1)S(1)} async-done(((bf16[32,32,256]{2,1,0:T(8,128)(2,1)}), bf16[32,32,256]{2,1,0:T(8,128)(2,1)S(1)}, u32[]{:S(2)}, u32[]{:S(2)}) %all-to-all-start.13) | async-done | bytes 524320 | tf_op jit(solution)/shard_map/all_to_all | solution.py:16
  187.2 6.3 %all-to-all-done.12 = bf16[32,32,256]{2,1,0:T(8,128)(2,1)S(1)} async-done(((bf16[32,32,256]{2,1,0:T(8,128)(2,1)}), bf16[32,32,256]{2,1,0:T(8,128)(2,1)S(1)}, u32[]{:S(2)}, u32[]{:S(2)}) %all-to-all-start.12) | async-done | bytes 524320 | tf_op jit(solution)/shard_map/all_to_all | solution.py:16
  197.0 4.7 %all-to-all-done.14 = f32[4,32,256]{2,1,0:T(8,128)S(1)} async-done(((f32[4,32,256]{2,1,0:T(8,128)}), f32[4,32,256]{2,1,0:T(8,128)S(1)}, u32[]{:S(2)}, u32[]{:S(2)}) %all-to-all-start.14) | async-done | bytes 131104 | tf_op jit(solution)/shard_map/all_to_all | solution.py:16
  205.8 4.8 %all-to-all-done.15 = f32[4,32,256]{2,1,0:T(8,128)S(1)} async-done(((f32[4,32,256]{2,1,0:T(8,128)}), f32[4,32,256]{2,1,0:T(8,128)S(1)}, u32[]{:S(2)}, u32[]{:S(2)}) %all-to-all-start.15) | async-done | bytes 131104 | tf_op jit(solution)/shard_map/all_to_all | solution.py:16
  212.7 6.2 %all-to-all-start.16 = ((f32[32,1,800]{2,1,0:T(1,128)}), f32[32,1,800]{2,1,0:T(1,128)S(1)}, u32[]{:S(2)}, u32[]{:S(2)}) async-start(f32[32,1,800]{2,1,0:T(1,128)} %reshape.591), calls=%async_computation.16 | async-start | bytes 229376 | tf_op jit(solution)/shard_map/all_to_all | solution.py:16
  218.9 7.6 %all-to-all-done.16 = f32[32,1,800]{2,1,0:T(1,128)S(1)} async-done(((f32[32,1,800]{2,1,0:T(1,128)}), f32[32,1,800]{2,1,0:T(1,128)S(1)}, u32[]{:S(2)}, u32[]{:S(2)}) %all-to-all-start.16) | async-done | bytes 102432 | tf_op jit(solution)/shard_map/all_to_all | solution.py:16
  232.9 7.6 %all-to-all-done.17 = f32[32,1,800]{2,1,0:T(1,128)S(1)} async-done(((f32[32,1,800]{2,1,0:T(1,128)}), f32[32,1,800]{2,1,0:T(1,128)S(1)}, u32[]{:S(2)}, u32[]{:S(2)}) %all-to-all-start.17) | async-done | bytes 102432 | tf_op jit(solution)/shard_map/all_to_all | solution.py:16
  241.7 11.7 %cholesky.51 = f32[128,128]{1,0:T(8,128)S(1)} custom-call(f32[128,128]{1,0:T(8,128)S(1)} %cholesky.124), custom_call_target="Cholesky" | custom-call | tf_op jit(solution)/shard_map/jit(cholesky)/cholesky | solution.py:78
  253.5 9.8 %custom-call.14 = f32[1,128,128]{1,2,0:T(8,128)S(1)} custom-call(f32[1,128,128]{2,1,0:T(8,128)S(1)} %get-tuple-element.44), custom_call_target="InvertDiagBlocksLowerTriangular" | custom-call | tf_op jit(solution)/shard_map/jit(cholesky)/cholesky | solution.py:78
  269.3 19.7 %custom-call.15 = f32[2,128,128]{1,2,0:T(8,128)S(1)} custom-call(f32[2,128,128]{2,1,0:T(8,128)S(1)} %pad_maximum_fusion), custom_call_target="InvertDiagBlocksLowerTriangular" | custom-call | tf_op jit(solution)/shard_map/triangular_solve | solution.py:79
  (148 shorter events, 121.7 us)
Async XLA Ops:
  0.6 17.9 %copy-start.1 = (s32[1,1,32]{2,1,0:T(1,128)S(1)}, s32[1,1,32]{2,1,0:T(1,128)}, u32[]{:S(2)}) copy-start(s32[1,1,32]{2,1,0:T(1,128)} %param.12) | copy-start | bytes 388
  2.5 20.9 %all-to-all-start.1 = ((bf16[32,32,256]{2,1,0:T(8,128)(2,1)}), bf16[32,32,256]{2,1,0:T(8,128)(2,1)S(1)}, u32[]{:S(2)}, u32[]{:S(2)}) async-start(bf16[32,32,256]{2,1,0:T(8,128)(2,1)} %broadcast_in_dim.40), calls=%async_computation.1 | async-start | bytes 1048576 | tf_op jit(solution)/shard_map/all_to_all | solution.py:16
  14.9 5.2 %copy-start.3 = (f32[1024]{0:T(1024)S(1)}, f32[1024]{0:T(1024)}, u32[]{:S(2)}) copy-start(f32[1024]{0:T(1024)} %param.14) | copy-start | bytes 12292
  19.0 12.7 %copy-start.2 = (s32[1,1,32]{2,1,0:T(1,128)S(1)}, s32[1,1,32]{2,1,0:T(1,128)}, u32[]{:S(2)}) copy-start(s32[1,1,32]{2,1,0:T(1,128)} %param.11) | copy-start | bytes 388
  23.4 15.6 %all-to-all-start = ((bf16[32,32,256]{2,1,0:T(8,128)(2,1)}), bf16[32,32,256]{2,1,0:T(8,128)(2,1)S(1)}, u32[]{:S(2)}, u32[]{:S(2)}) async-start(bf16[32,32,256]{2,1,0:T(8,128)(2,1)} %copy.53), calls=%async_computation | async-start | bytes 1048576 | tf_op jit(solution)/shard_map/all_to_all | solution.py:16
  27.5 24.5 %copy-start = (f32[32,1024]{1,0:T(8,128)S(1)}, f32[32,1024]{1,0:T(8,128)}, u32[]{:S(2)}) copy-start(f32[32,1024]{1,0:T(8,128)} %param.15) | copy-start | bytes 393220
  39.0 9.0 %all-to-all-start.2 = ((f32[4,32,256]{2,1,0:T(8,128)}), f32[4,32,256]{2,1,0:T(8,128)S(1)}, u32[]{:S(2)}, u32[]{:S(2)}) async-start(f32[4,32,256]{2,1,0:T(8,128)} %copy.55), calls=%async_computation.2 | async-start | bytes 262144 | tf_op jit(solution)/shard_map/all_to_all | solution.py:16
  48.7 8.1 %all-to-all-start.3 = ((f32[4,32,256]{2,1,0:T(8,128)}), f32[4,32,256]{2,1,0:T(8,128)S(1)}, u32[]{:S(2)}, u32[]{:S(2)}) async-start(f32[4,32,256]{2,1,0:T(8,128)} %broadcast_in_dim.41), calls=%async_computation.3 | async-start | bytes 262144 | tf_op jit(solution)/shard_map/all_to_all | solution.py:16
  57.7 18.1 %all-to-all-start.5 = ((bf16[32,32,256]{2,1,0:T(8,128)(2,1)}), bf16[32,32,256]{2,1,0:T(8,128)(2,1)S(1)}, u32[]{:S(2)}, u32[]{:S(2)}) async-start(bf16[32,32,256]{2,1,0:T(8,128)(2,1)} %broadcast_in_dim.42), calls=%async_computation.5 | async-start | bytes 1048576 | tf_op jit(solution)/shard_map/all_to_all | solution.py:16
  75.7 15.5 %all-to-all-start.4 = ((bf16[32,32,256]{2,1,0:T(8,128)(2,1)}), bf16[32,32,256]{2,1,0:T(8,128)(2,1)S(1)}, u32[]{:S(2)}, u32[]{:S(2)}) async-start(bf16[32,32,256]{2,1,0:T(8,128)(2,1)} %copy.58), calls=%async_computation.4 | async-start | bytes 1048576 | tf_op jit(solution)/shard_map/all_to_all | solution.py:16
  91.2 8.1 %all-to-all-start.6 = ((f32[4,32,256]{2,1,0:T(8,128)}), f32[4,32,256]{2,1,0:T(8,128)S(1)}, u32[]{:S(2)}, u32[]{:S(2)}) async-start(f32[4,32,256]{2,1,0:T(8,128)} %copy.60), calls=%async_computation.6 | async-start | bytes 262144 | tf_op jit(solution)/shard_map/all_to_all | solution.py:16
  100.1 8.1 %all-to-all-start.7 = ((f32[4,32,256]{2,1,0:T(8,128)}), f32[4,32,256]{2,1,0:T(8,128)S(1)}, u32[]{:S(2)}, u32[]{:S(2)}) async-start(f32[4,32,256]{2,1,0:T(8,128)} %broadcast_in_dim.43), calls=%async_computation.7 | async-start | bytes 262144 | tf_op jit(solution)/shard_map/all_to_all | solution.py:16
  109.0 17.8 %all-to-all-start.9 = ((bf16[32,32,256]{2,1,0:T(8,128)(2,1)}), bf16[32,32,256]{2,1,0:T(8,128)(2,1)S(1)}, u32[]{:S(2)}, u32[]{:S(2)}) async-start(bf16[32,32,256]{2,1,0:T(8,128)(2,1)} %broadcast_in_dim.44), calls=%async_computation.9 | async-start | bytes 1048576 | tf_op jit(solution)/shard_map/all_to_all | solution.py:16
  126.8 15.5 %all-to-all-start.8 = ((bf16[32,32,256]{2,1,0:T(8,128)(2,1)}), bf16[32,32,256]{2,1,0:T(8,128)(2,1)S(1)}, u32[]{:S(2)}, u32[]{:S(2)}) async-start(bf16[32,32,256]{2,1,0:T(8,128)(2,1)} %copy.63), calls=%async_computation.8 | async-start | bytes 1048576 | tf_op jit(solution)/shard_map/all_to_all | solution.py:16
  142.3 8.1 %all-to-all-start.10 = ((f32[4,32,256]{2,1,0:T(8,128)}), f32[4,32,256]{2,1,0:T(8,128)S(1)}, u32[]{:S(2)}, u32[]{:S(2)}) async-start(f32[4,32,256]{2,1,0:T(8,128)} %copy.65), calls=%async_computation.10 | async-start | bytes 262144 | tf_op jit(solution)/shard_map/all_to_all | solution.py:16
  151.1 8.1 %all-to-all-start.11 = ((f32[4,32,256]{2,1,0:T(8,128)}), f32[4,32,256]{2,1,0:T(8,128)S(1)}, u32[]{:S(2)}, u32[]{:S(2)}) async-start(f32[4,32,256]{2,1,0:T(8,128)} %broadcast_in_dim.45), calls=%async_computation.11 | async-start | bytes 262144 | tf_op jit(solution)/shard_map/all_to_all | solution.py:16
  160.1 18.0 %all-to-all-start.13 = ((bf16[32,32,256]{2,1,0:T(8,128)(2,1)}), bf16[32,32,256]{2,1,0:T(8,128)(2,1)S(1)}, u32[]{:S(2)}, u32[]{:S(2)}) async-start(bf16[32,32,256]{2,1,0:T(8,128)(2,1)} %broadcast_in_dim.46), calls=%async_computation.13 | async-start | bytes 1048576 | tf_op jit(solution)/shard_map/all_to_all | solution.py:16
  178.1 15.5 %all-to-all-start.12 = ((bf16[32,32,256]{2,1,0:T(8,128)(2,1)}), bf16[32,32,256]{2,1,0:T(8,128)(2,1)S(1)}, u32[]{:S(2)}, u32[]{:S(2)}) async-start(bf16[32,32,256]{2,1,0:T(8,128)(2,1)} %copy.68), calls=%async_computation.12 | async-start | bytes 1048576 | tf_op jit(solution)/shard_map/all_to_all | solution.py:16
  193.6 8.1 %all-to-all-start.14 = ((f32[4,32,256]{2,1,0:T(8,128)}), f32[4,32,256]{2,1,0:T(8,128)S(1)}, u32[]{:S(2)}, u32[]{:S(2)}) async-start(f32[4,32,256]{2,1,0:T(8,128)} %copy.70), calls=%async_computation.14 | async-start | bytes 262144 | tf_op jit(solution)/shard_map/all_to_all | solution.py:16
  202.4 8.1 %all-to-all-start.15 = ((f32[4,32,256]{2,1,0:T(8,128)}), f32[4,32,256]{2,1,0:T(8,128)S(1)}, u32[]{:S(2)}, u32[]{:S(2)}) async-start(f32[4,32,256]{2,1,0:T(8,128)} %broadcast_in_dim.47), calls=%async_computation.15 | async-start | bytes 262144 | tf_op jit(solution)/shard_map/all_to_all | solution.py:16
  212.7 13.8 %all-to-all-start.16 = ((f32[32,1,800]{2,1,0:T(1,128)}), f32[32,1,800]{2,1,0:T(1,128)S(1)}, u32[]{:S(2)}, u32[]{:S(2)}) async-start(f32[32,1,800]{2,1,0:T(1,128)} %reshape.591), calls=%async_computation.16 | async-start | bytes 229376 | tf_op jit(solution)/shard_map/all_to_all | solution.py:16
  229.0 11.5 %all-to-all-start.17 = ((f32[32,1,800]{2,1,0:T(1,128)}), f32[32,1,800]{2,1,0:T(1,128)S(1)}, u32[]{:S(2)}, u32[]{:S(2)}) async-start(f32[32,1,800]{2,1,0:T(1,128)} %reshape.593), calls=%async_computation.17 | async-start | bytes 229376 | tf_op jit(solution)/shard_map/all_to_all | solution.py:16

commit v2 on v1

v2 whole, which is shorter than its diff:
```python
import functools

import jax
import jax.numpy as jnp
from jax import lax
from jax.experimental import pallas as pl
from jax.experimental.pallas import tpu as pltpu
from jax.sharding import PartitionSpec as P


ITERS = 4
SHIFT = 1.0625
PULL = 0.375
CHUNKS = 4
LANES = 128
EXTRA = 8

F32 = jnp.float32
BF16 = jnp.bfloat16
HIGHEST = lax.Precision.HIGHEST
VMEM = pltpu.VMEM
SMEM = pltpu.SMEM


def spec(space):
    return pl.BlockSpec(memory_space=space)


def call(kernel, out_shape, in_spaces, operands, limit_mib, scratch=(), flops=2_000_000):
    return pl.pallas_call(
        kernel,
        out_shape=out_shape,
        in_specs=[spec(space) for space in in_spaces],
        out_specs=[spec(VMEM)] * len(out_shape),
        scratch_shapes=list(scratch),
        compiler_params=pltpu.CompilerParams(vmem_limit_bytes=limit_mib << 20),
        cost_estimate=pl.CostEstimate(flops=flops, bytes_accessed=1 << 20, transcendentals=0),
    )(*operands)


def shape(*dims, dtype=F32):
    return jax.ShapeDtypeStruct(dims, dtype)


def exchange(parts, axis):
    return lax.all_to_all(parts, axis, split_axis=0, concat_axis=0, tiled=True)


def from_behind(value, axis, distance):
    size = lax.axis_size(axis)
    return lax.ppermute(value, axis, [(i, (i + distance) % size) for i in range(size)])


def dot(left, right, dims):
    return lax.dot_general(
        left, right, (dims, ((), ())), precision=HIGHEST, preferred_element_type=F32
    )


def plain(left, right):
    return dot(left, right, ((1,), (0,)))


def across(left, right):
    return dot(left, right, ((1,), (1,)))


def pieces(value):
    high = value.astype(BF16).astype(F32)
    rest = value - high
    middle = rest.astype(BF16).astype(F32)
    return high, middle, rest - middle


def stacked(high, middle, low):
    line = lax.broadcasted_iota(jnp.int32, (EXTRA, high.shape[1]), 0)
    value = jnp.where(line == 2, low, 0.0)
    value = jnp.where(line == 1, middle, value)
    return jnp.where(line == 0, high, value)


def init_kernel(groups, owners, start_ref, shift_ref, *outs):
    slots, sent_ref, coef_ref = outs[:groups], outs[groups], outs[groups + 1]
    edge = coef_ref.shape[1]
    group = lax.axis_index("grp")
    for s in range(groups):
        block = lax.rem(group - s + groups, groups)
        slots[s][...] = start_ref[:, pl.ds(pl.multiple_of(block * edge, edge), edge)]
    rounded = slots[0][...].astype(BF16)
    for r in range(owners):
        sent_ref[r] = rounded
    coef_ref[...] = SHIFT - shift_ref[:, pl.ds(pl.multiple_of(group * edge, edge), edge)]


def fetches(tiles_ref, held, sems):
    per_chunk = held.shape[0] // CHUNKS
    return [
        pltpu.make_async_copy(
            tiles_ref.at[0, 0, pl.ds(c * per_chunk, per_chunk)],
            held.at[pl.ds(c * per_chunk, per_chunk)],
            sems.at[c],
        )
        for c in range(CHUNKS)
    ]


def back_kernel(groups, steps, rows_ref, cols_ref, live_ref, tiles_ref, *refs):
    count = steps + 1
    vectors = [refs[i * groups : (i + 1) * groups] for i in range(count)]
    out_ref, held, total, rounded, sems = refs[count * groups :]
    copies = fetches(tiles_ref, held, sems)
    for copy in copies:
        copy.start()
    owners, width, edge = total.shape
    group = lax.axis_index("grp")
    live = live_ref[0, 0]
    for s in range(groups):
        rounded[s] = vectors[steps][s][...].astype(BF16)
    total[...] = jnp.zeros_like(total)
    grams = []
    for i in range(count):
        value = across(vectors[steps][0][...], vectors[i][0][...])
        for s in range(1, groups):
            value = value + across(vectors[steps][s][...], vectors[i][s][...])
        grams.append(value)
    if count * width < LANES:
        grams.append(jnp.zeros((width, LANES - count * width), F32))
    high, middle, low = pieces(jnp.concatenate(grams, 1))
    for r in range(owners):
        value = stacked(high[r : r + 1], middle[r : r + 1], low[r : r + 1])
        value = jnp.concatenate([value, jnp.zeros((EXTRA, edge - LANES), F32)], 1)
        out_ref[r, pl.ds(width, EXTRA), :] = value.astype(BF16)
    per_chunk = held.shape[0] // CHUNKS
    for c in range(CHUNKS):
        copies[c].wait()
        for k in range(c * per_chunk, (c + 1) * per_chunk):
            source = lax.rem(group - rows_ref[0, 0, k] + groups, groups)
            product = lax.dot_general(
                rounded[source], held[k], (((1,), (0,)), ((), ())), preferred_element_type=F32
            )
            total[cols_ref[0, 0, k]] += jnp.where(k < live, product, jnp.zeros_like(product))
    for r in range(owners):
        out_ref[r, pl.ds(0, width), :] = total[r].astype(BF16)


def ahead_kernel(groups, rows_ref, cols_ref, live_ref, tiles_ref, columns_ref, *refs):
    outs = refs[:groups]
    held, total, sems = refs[groups:]
    copies = fetches(tiles_ref, held, sems)
    for copy in copies:
        copy.start()
    width = total.shape[1]
    group = lax.axis_index("grp")
    live = live_ref[0, 0]
    total[...] = jnp.zeros_like(total)
    per_chunk = held.shape[0] // CHUNKS
    for c in range(CHUNKS):
        copies[c].wait()
        for k in range(c * per_chunk, (c + 1) * per_chunk):
            target = lax.rem(rows_ref[0, 0, k] - group + groups, groups)
            product = lax.dot_general(
                columns_ref[cols_ref[0, 0, k], pl.ds(0, width), :],
                held[k],
                (((1,), (1,)), ((), ())),
                preferred_element_type=F32,
            )
            total[target] += jnp.where(k < live, product, jnp.zeros_like(product))
    for s in range(groups):
        outs[s][...] = total[s]


def combine_kernel(groups, last, back_ref, *refs):
    direct = refs[:groups]
    now_ref, before_ref, coef_ref = refs[groups : groups + 3]
    outs = refs[groups + 3 :]
    owners = back_ref.shape[0]
    width = now_ref.shape[0]
    edge = now_ref.shape[1]
    image = direct[0][...]
    for s in range(1, groups):
        image = image + direct[s][...]
    for r in range(owners):
        image = image + back_ref[r, pl.ds(0, width), :].astype(F32)
    new = 0.5 * image + coef_ref[...] * now_ref[...] - PULL * before_ref[...]
    outs[0][...] = new
    sums = back_ref[0, pl.ds(width, EXTRA), pl.ds(0, LANES)].astype(F32)
    for r in range(1, owners):
        sums = sums + back_ref[r, pl.ds(width, EXTRA), pl.ds(0, LANES)].astype(F32)
    row = sums[0:1] + (sums[1:2] + sums[2:3])
    if last:
        outs[1][...] = jnp.broadcast_to(row, (EXTRA, LANES))
    else:
        rounded = new.astype(BF16)
        extra = stacked(*pieces(row))
        extra = jnp.concatenate([extra, jnp.zeros((EXTRA, edge - LANES), F32)], 1).astype(BF16)
        for r in range(owners):
            outs[1][r, pl.ds(0, width), :] = rounded
            outs[1][r, pl.ds(width, EXTRA), :] = extra


def factor(block):
    width = block.shape[0]
    row_id = lax.broadcasted_iota(jnp.int32, (width, 2 * width), 0)
    col_id = lax.broadcasted_iota(jnp.int32, (width, 2 * width), 1)
    work = jnp.concatenate([block, jnp.zeros_like(block)], 1) + jnp.where(
        col_id == row_id + width, 1.0, 0.0
    )
    result = jnp.zeros_like(work)
    for k in range(width):
        row = work[k : k + 1, :]
        scale = lax.rsqrt(row[:, k : k + 1])
        row = row * scale
        column = work[:, k : k + 1] * scale
        result = jnp.where(row_id == k, jnp.broadcast_to(row, work.shape), result)
        if k + 1 < width:
            work = work - jnp.where(row_id > k, column, 0.0) * row
    return result[:, :width], result[:, width:]


def next_rows(j, gram_row, low, inv):
    width = gram_row.shape[0]
    here, done = pl.ds(j * width, width), pl.ds(0, j * width)
    low[here, :] = jnp.zeros((width, low.shape[1]), F32)
    inv[here, :] = jnp.zeros((width, inv.shape[1]), F32)
    schur = gram_row[:, j * width : (j + 1) * width]
    if j > 0:
        left = across(gram_row[:, : j * width], inv[done, done])
        schur = schur - across(left, left)
        back = plain(left, inv[done, done])
    upper, own_inverse = factor(schur)
    low[here, here] = upper.T
    inv[here, here] = own_inverse
    if j > 0:
        low[here, done] = left
        inv[here, done] = -plain(own_inverse, back)


def step_results(j, low, inv, width):
    used = (j + 1) * width
    value = low[pl.ds(width, used), :] - SHIFT * low[pl.ds(0, used), :]
    if j > 0:
        value = value + PULL * jnp.concatenate(
            [jnp.zeros((width, value.shape[1]), F32), low[pl.ds(0, j * width), :]], 0
        )
    image = plain(inv[pl.ds(j * width, width), pl.ds(0, used)], value)
    lane = lax.broadcasted_iota(jnp.int32, (width, ITERS * width), 1)
    square = (width, width)
    keep = lax.broadcasted_iota(jnp.int32, square, 0) >= lax.broadcasted_iota(jnp.int32, square, 1)
    return (
        jnp.where(lane < used, image[:, : ITERS * width], 0.0),
        jnp.where(keep, image[:, used : used + width], 0.0),
    )


def block_kernel(j, columns_ref, *refs):
    olds, (low_ref, inv_ref) = refs[:-2], refs[-2:]
    owners = columns_ref.shape[0]
    width = low_ref.shape[0] // (ITERS + 1)
    if j > 0:
        low_ref[...] = olds[0][...]
        inv_ref[...] = olds[1][...]
    rows = []
    for r in range(owners):
        three = columns_ref[r, pl.ds(width, EXTRA), pl.ds(0, LANES)].astype(F32)
        rows.append(three[0:1] + (three[1:2] + three[2:3]))
    next_rows(j, jnp.concatenate(rows, 0), low_ref, inv_ref)


def gram_kernel(groups, chunk_ref, *refs):
    out_ref = refs[-1]
    vectors = [refs[i * groups : (i + 1) * groups] for i in range(ITERS + 1)]
    owners = out_ref.shape[0]
    width = vectors[0][0].shape[0]
    grams = []
    for i in range(ITERS + 1):
        value = across(vectors[ITERS][0][...], vectors[i][0][...])
        for s in range(1, groups):
            value = value + across(vectors[ITERS][s][...], vectors[i][s][...])
        grams.append(value)
    parts = LANES // width
    rows = width // parts
    packed = jnp.concatenate([grams[ITERS][p * rows : (p + 1) * rows] for p in range(parts)], 1)
    value = jnp.concatenate(
        [jnp.concatenate(grams[:ITERS], 1), packed, jnp.broadcast_to(chunk_ref[0:1], (EXTRA, LANES))], 0
    )
    for r in range(owners):
        out_ref[r] = value


def finish_kernel(groups, parts_ref, old_low, old_inv, *refs):
    vectors = [refs[i * groups : (i + 1) * groups] for i in range(ITERS + 1)]
    proj_ref, fact_ref, out_ref, low, inv = refs[(ITERS + 1) * groups :]
    owners = parts_ref.shape[0]
    width, edge = vectors[0][0].shape
    group = lax.axis_index("grp")
    low[...] = old_low[...]
    inv[...] = old_inv[...]
    last = parts_ref.shape[1] - EXTRA
    rows = [parts_ref[r, pl.ds(last, EXTRA), :][0:1] for r in range(owners)]
    next_rows(ITERS - 1, jnp.concatenate(rows, 0), low, inv)
    sums = parts_ref[0, pl.ds(0, last), :]
    for r in range(1, owners):
        sums = sums + parts_ref[r, pl.ds(0, last), :]
    count = LANES // width
    corner = jnp.concatenate([sums[width:, p * width : (p + 1) * width] for p in range(count)], 0)
    next_rows(ITERS, jnp.concatenate([sums[:width], corner], 1), low, inv)
    for j in range(ITERS):
        proj_ref[j], fact_ref[j] = step_results(j, low, inv, width)
    for s in range(groups):
        value = plain(inv[pl.ds(ITERS * width, width), pl.ds(0, width)], vectors[0][s][...])
        for i in range(1, ITERS + 1):
            value = value + plain(
                inv[pl.ds(ITERS * width, width), pl.ds(i * width, width)], vectors[i][s][...]
            )
        block = lax.rem(group - s + groups, groups)
        out_ref[:, pl.ds(pl.multiple_of(block * edge, edge), edge)] = value


def per_device(tiles, tile_rows, tile_cols, live_tiles, dual_shift, start_block):
    count, edge = tiles.shape[2], tiles.shape[3]
    width, row_count = start_block.shape
    groups = lax.axis_size("grp")
    owners = lax.axis_size("row")
    total = (ITERS + 1) * width
    tables = (tile_rows, tile_cols, live_tiles, tiles)
    spaces = [SMEM, SMEM, SMEM, pl.ANY]
    held = pltpu.VMEM((count, edge, edge), BF16)
    flops = 2 * count * width * edge * edge

    *slots, sent, coef = call(
        functools.partial(init_kernel, groups, owners),
        [shape(width, edge)] * groups + [shape(owners, width, edge, dtype=BF16), shape(1, edge)],
        [VMEM, VMEM],
        (start_block, dual_shift[None, :]),
        4,
    )
    before = jnp.zeros((width, edge), F32)
    basis = [slots]
    state = ()
    for step in range(ITERS):
        own = basis[step][0]
        columns = exchange(sent, "row")
        flat = [slot for slots in basis for slot in slots]
        (parts,) = call(
            functools.partial(back_kernel, groups, step),
            [shape(owners, width + EXTRA, edge, dtype=BF16)],
            spaces + [VMEM] * len(flat),
            (*tables, *flat),
            12,
            [
                held,
                pltpu.VMEM((owners, width, edge), F32),
                pltpu.VMEM((groups, width, edge), BF16),
                pltpu.SemaphoreType.DMA((CHUNKS,)),
            ],
            flops,
        )
        arrived = exchange(parts, "row")
        direct = call(
            functools.partial(ahead_kernel, groups),
            [shape(width, edge)] * groups,
            spaces + [VMEM],
            (*tables, columns),
            12,
            [held, pltpu.VMEM((groups, width, edge), F32), pltpu.SemaphoreType.DMA((CHUNKS,))],
            flops,
        )
        direct = [direct[0]] + [from_behind(direct[k], "grp", k) for k in range(1, groups)]
        if step > 0:
            state = call(
                functools.partial(block_kernel, step - 1),
                [shape(total, total)] * 2,
                [VMEM] * (1 + len(state)),
                (columns, *state),
                4,
            )
        last = step == ITERS - 1
        second = shape(EXTRA, LANES) if last else shape(owners, width + EXTRA, edge, dtype=BF16)
        new, sent = call(
            functools.partial(combine_kernel, groups, last),
            [shape(width, edge), second],
            [VMEM] * (groups + 4),
            (arrived, *direct, own, before, coef),
            4,
        )
        before = own
        basis.append([new] + [from_behind(new, "grp", k) for k in range(1, groups)])

    flat = [slot for slots in basis for slot in slots]
    (parts,) = call(
        functools.partial(gram_kernel, groups),
        [shape(owners, width + width * width // LANES + EXTRA, LANES)],
        [VMEM] * (1 + len(flat)),
        (sent, *flat),
        6,
    )
    parts = exchange(parts, "row")
    return call(
        functools.partial(finish_kernel, groups),
        [shape(ITERS, width, ITERS * width), shape(ITERS, width, width), shape(width, row_count)],
        [VMEM] * (3 + len(flat)),
        (parts, *state, *flat),
        8,
        [pltpu.VMEM((total, total), F32), pltpu.VMEM((total, total), F32)],
    )


def solution(mesh):
    in_specs = (
        P("grp", "row", None, None, None),
        P("grp", "row", None),
        P("grp", "row", None),
        P("grp", "row"),
        P("row"),
        P(None, "row"),
    )
    out_specs = (P(), P(), P(None, "row"))
    return jax.shard_map(
        per_device, mesh=mesh, in_specs=in_specs, out_specs=out_specs, check_vma=False
    )
```

time: 296 us -> 208 us (0.70)
  waiting for transfers between devices: 101 us -> 40.5 us
  other arithmetic: 50.1 us -> 0 us
  Pallas kernels: 0 us -> 47.9 us
  matrix products: 33.1 us -> 0 us
  starting transfers between devices: 82.1 us -> 96.2 us
  local copies, waits for them, and re-layouts: 24.4 us -> 20.4 us
    all_to_all x18 -> x9, waiting for transfers between devices: 101 us -> 18.3 us  [exchange(): return lax.all_to_all(parts, axis, split_axis=0, concat_axis=0, tiled=True)]
    pallas_call x0 -> x18, Pallas kernels: none -> 47.9 us  [call(): pl.pallas_call(kernel, out_shape=out_shape, in_specs=[spec(space) for spa...]
    another operation x13 -> x0, other arithmetic: 45.6 us -> none  [the longest x7 25.8 us: per_device(): lower = jnp.linalg.cholesky(gram)]
    dot_general x25 -> x0, matrix products: 32.1 us -> none  [the longest x4 14.1 us: forward(): jnp.einsum('bkc,brc->bkr', jnp.take(columns, cols_here, axis=0), matrix,...]
    ppermute x0 -> x24, starting transfers between devices: none -> 28.6 us  [from_behind(): lax.ppermute(value, axis, [(i, (i + distance) % size) for i in range(size)])]
    ppermute x0 -> x24, waiting for transfers between devices: none -> 22.3 us  [from_behind(): lax.ppermute(value, axis, [(i, (i + distance) % size) for i in range(size)])]
    unnamed x18 -> x28, local copies, waits for them, and re-layouts: 2.24 us -> 20.4 us
    all_to_all x18 -> x9, starting transfers between devices: 82.1 us -> 67.5 us  [exchange(): return lax.all_to_all(parts, axis, split_axis=0, concat_axis=0, tiled=True)]
  transfers between devices with their start and end apart: 18 -> 33, of which waited for: 18 -> 29; matrix products, arithmetic and copies ran while one was open for 15% -> 0% of each run, Pallas kernels for 0% -> 17%
where the time goes in v2:
time: 208 us; the launch traced here: 207 us
  starting transfers between devices  96.2 us (46%)
  Pallas kernels  47.9 us (23%)
  waiting for transfers between devices  40.5 us (19%)
  local copies, waits for them, and re-layouts  20.4 us (10%)
    all_to_all x9, starting transfers between devices, exchange(): return lax.all_to_all(parts, axis, split_axis=0, concat_axis=0, tiled=True)  67.5 us
    pallas_call x18, Pallas kernels, call(): pl.pallas_call(kernel, out_shape=out_shape, in_specs=[spec(space) for spa...  47.9 us
    ppermute x24, starting transfers between devices, from_behind(): lax.ppermute(value, axis, [(i, (i + distance) % size) for i in range(size)])  28.6 us
    ppermute x24, waiting for transfers between devices, from_behind(): lax.ppermute(value, axis, [(i, (i + distance) % size) for i in range(size)])  22.3 us
    unnamed x28, local copies, waits for them, and re-layouts  20.4 us
    all_to_all x9, waiting for transfers between devices, exchange(): return lax.all_to_all(parts, axis, split_axis=0, concat_axis=0, tiled=True)  18.3 us
  transfers between devices with their start and end apart: 33, of which 29 were waited for; matrix products, arithmetic and copies ran while one was open for 0% of the time, Pallas kernels for 17%

profile of v2, /device:TPU:1, one launch (start us, length us, event | category | flops | bytes accessed | tf_op | source)
XLA Modules:
  0.0 206.5 jit_solution(10396441166942353111)
XLA Ops:
  3.1 9.4 %all-to-all-start.1 = ((bf16[32,32,256]{2,1,0:T(8,128)(2,1)}), bf16[32,32,256]{2,1,0:T(8,128)(2,1)S(1)}, u32[]{:S(2)}, u32[]{:S(2)}) async-start(bf16[32,32,256]{2,1,0:T(8,128)(2,1)} %get-tuple-element.43), calls=%async_computation.1 | async-start | bytes 1048576 | tf_op jit(solution)/shard_map/all_to_all | solution.py:46
  16.7 3.4 %shard_map.86 = bf16[32,40,256]{2,1,0:T(8,128)(2,1)} custom-call(s32[1,1,32]{2,1,0:T(1,128)S(1)} %copy-done.9, s32[1,1,32]{2,1,0:T(1,128)S(1)} %copy-done.11, s32[1,1]{1,0:T(1,128)S(6)} %copy.9.live_ref, bf16[1,1,32,256,256]{4,3,2,1,0:T(8,128)(2,1)S(1)} %copy-done, f32[32,256]{1,0:T(8,128)S(1)} %get-tuple-element.39.refs_0_.refs_4_.refs_5_, ...), custom_call_target="tpu_custom_call" | custom-call | flops 134217728 | bytes 1048576 | tf_op jit(solution)/shard_map/pallas_call | solution.py:30
  20.1 3.8 %all-to-all-done.1.columns_ref = bf16[32,32,256]{2,1,0:T(8,128)(2,1)S(1)} async-done(((bf16[32,32,256]{2,1,0:T(8,128)(2,1)}), bf16[32,32,256]{2,1,0:T(8,128)(2,1)S(1)}, u32[]{:S(2)}, u32[]{:S(2)}) %all-to-all-start.1) | async-done | bytes 524320 | tf_op jit(solution)/shard_map/all_to_all | solution.py:46
  23.9 4.0 %all-to-all-start = ((bf16[32,40,256]{2,1,0:T(8,128)(2,1)}), bf16[32,40,256]{2,1,0:T(8,128)(2,1)S(1)}, u32[]{:S(2)}, u32[]{:S(2)}) async-start(bf16[32,40,256]{2,1,0:T(8,128)(2,1)} %shard_map.86), calls=%async_computation | async-start | bytes 1310720 | tf_op jit(solution)/shard_map/all_to_all | solution.py:46
  41.8 7.8 %all-to-all-start.3 = ((bf16[32,40,256]{2,1,0:T(8,128)(2,1)}), bf16[32,40,256]{2,1,0:T(8,128)(2,1)S(1)}, u32[]{:S(2)}, u32[]{:S(2)}) async-start(bf16[32,40,256]{2,1,0:T(8,128)(2,1)} %get-tuple-element.50), calls=%async_computation.3 | async-start | bytes 1310720 | tf_op jit(solution)/shard_map/all_to_all | solution.py:46
  53.0 3.5 %collective-permute-done.4.refs_6_ = f32[32,256]{1,0:T(8,128)S(1)} collective-permute-done((f32[32,256]{1,0:T(8,128)S(1)}, f32[32,256]{1,0:T(8,128)S(1)}, u32[]{:S(2)}, u32[]{:S(2)}) %collective-permute-start.4) | collective-permute-done | bytes 32800 | tf_op jit(solution)/shard_map/ppermute | solution.py:51
  58.8 3.5 %shard_map.89 = bf16[32,40,256]{2,1,0:T(8,128)(2,1)} custom-call(s32[1,1,32]{2,1,0:T(1,128)S(1)} %copy-done.10, s32[1,1,32]{2,1,0:T(1,128)S(1)} %copy-done.12, s32[1,1]{1,0:T(1,128)S(6)} %copy.9.live_ref, bf16[1,1,32,256,256]{4,3,2,1,0:T(8,128)(2,1)S(1)} %copy-done.2, f32[32,256]{1,0:T(8,128)S(1)} %get-tuple-element.39.refs_0_.refs_4_.refs_5_, ...), custom_call_target="tpu_custom_call" | custom-call | flops 134217728 | bytes 1048576 | tf_op jit(solution)/shard_map/pallas_call | solution.py:30
  62.5 8.3 %all-to-all-start.2 = ((bf16[32,40,256]{2,1,0:T(8,128)(2,1)}), bf16[32,40,256]{2,1,0:T(8,128)(2,1)S(1)}, u32[]{:S(2)}, u32[]{:S(2)}) async-start(bf16[32,40,256]{2,1,0:T(8,128)(2,1)} %shard_map.89), calls=%async_computation.2 | async-start | bytes 1310720 | tf_op jit(solution)/shard_map/all_to_all | solution.py:46
  84.7 5.8 %all-to-all-start.5 = ((bf16[32,40,256]{2,1,0:T(8,128)(2,1)}), bf16[32,40,256]{2,1,0:T(8,128)(2,1)S(1)}, u32[]{:S(2)}, u32[]{:S(2)}) async-start(bf16[32,40,256]{2,1,0:T(8,128)(2,1)} %get-tuple-element.56), calls=%async_computation.5 | async-start | bytes 1310720 | tf_op jit(solution)/shard_map/all_to_all | solution.py:46
  90.5 3.2 %collective-permute-start.11 = (f32[32,256]{1,0:T(8,128)S(1)}, f32[32,256]{1,0:T(8,128)S(1)}, u32[]{:S(2)}, u32[]{:S(2)}) collective-permute-start(f32[32,256]{1,0:T(8,128)S(1)} %get-tuple-element.55.refs_8_.refs_4_.refs_5_), channel_id=1, source_target_pairs={{0,96},{32,0},{64,32},{96,64},{1,97},{33,1},{65,33},{97,65},{2,98}... | collective-permute-start | bytes 98312 | tf_op jit(solution)/shard_map/ppermute | solution.py:51
  94.7 3.3 %collective-permute-done.10.refs_10_ = f32[32,256]{1,0:T(8,128)S(1)} collective-permute-done((f32[32,256]{1,0:T(8,128)S(1)}, f32[32,256]{1,0:T(8,128)S(1)}, u32[]{:S(2)}, u32[]{:S(2)}) %collective-permute-start.10) | collective-permute-done | bytes 32800 | tf_op jit(solution)/shard_map/ppermute | solution.py:51
  100.5 3.7 %shard_map.92 = bf16[32,40,256]{2,1,0:T(8,128)(2,1)} custom-call(s32[1,1,32]{2,1,0:T(1,128)S(1)} %copy-done.10, s32[1,1,32]{2,1,0:T(1,128)S(1)} %copy-done.12, s32[1,1]{1,0:T(1,128)S(6)} %copy.9.live_ref, bf16[1,1,32,256,256]{4,3,2,1,0:T(8,128)(2,1)S(1)} %copy-done.4, f32[32,256]{1,0:T(8,128)S(1)} %get-tuple-element.39.refs_0_.refs_4_.refs_5_, ...), custom_call_target="tpu_custom_call" | custom-call | flops 134217728 | bytes 1048576 | tf_op jit(solution)/shard_map/pallas_call | solution.py:30
  104.3 8.7 %all-to-all-start.4 = ((bf16[32,40,256]{2,1,0:T(8,128)(2,1)}), bf16[32,40,256]{2,1,0:T(8,128)(2,1)S(1)}, u32[]{:S(2)}, u32[]{:S(2)}) async-start(bf16[32,40,256]{2,1,0:T(8,128)(2,1)} %shard_map.92), calls=%async_computation.4 | async-start | bytes 1310720 | tf_op jit(solution)/shard_map/all_to_all | solution.py:46
  123.1 2.8 %all-to-all-done.4.back_ref = bf16[32,40,256]{2,1,0:T(8,128)(2,1)S(1)} async-done(((bf16[32,40,256]{2,1,0:T(8,128)(2,1)}), bf16[32,40,256]{2,1,0:T(8,128)(2,1)S(1)}, u32[]{:S(2)}, u32[]{:S(2)}) %all-to-all-start.4) | async-done | bytes 655392 | tf_op jit(solution)/shard_map/all_to_all | solution.py:46
  126.9 5.8 %all-to-all-start.7 = ((bf16[32,40,256]{2,1,0:T(8,128)(2,1)}), bf16[32,40,256]{2,1,0:T(8,128)(2,1)S(1)}, u32[]{:S(2)}, u32[]{:S(2)}) async-start(bf16[32,40,256]{2,1,0:T(8,128)(2,1)} %get-tuple-element.62), calls=%async_computation.7 | async-start | bytes 1310720 | tf_op jit(solution)/shard_map/all_to_all | solution.py:46
  132.7 2.9 %collective-permute-start.17 = (f32[32,256]{1,0:T(8,128)S(1)}, f32[32,256]{1,0:T(8,128)S(1)}, u32[]{:S(2)}, u32[]{:S(2)}) collective-permute-start(f32[32,256]{1,0:T(8,128)S(1)} %get-tuple-element.61.refs_12_.refs_4_), channel_id=1, source_target_pairs={{0,96},{32,0},{64,32},{96,64},{1,97},{33,1},{65,33},{97,65},{2,98}... | collective-permute-start | bytes 98312 | tf_op jit(solution)/shard_map/ppermute | solution.py:51
  136.6 3.5 %collective-permute-done.16.refs_14_ = f32[32,256]{1,0:T(8,128)S(1)} collective-permute-done((f32[32,256]{1,0:T(8,128)S(1)}, f32[32,256]{1,0:T(8,128)S(1)}, u32[]{:S(2)}, u32[]{:S(2)}) %collective-permute-start.16) | collective-permute-done | bytes 32800 | tf_op jit(solution)/shard_map/ppermute | solution.py:51
  142.6 3.7 %shard_map.95 = bf16[32,40,256]{2,1,0:T(8,128)(2,1)} custom-call(s32[1,1,32]{2,1,0:T(1,128)S(1)} %copy-done.10, s32[1,1,32]{2,1,0:T(1,128)S(1)} %copy-done.12, s32[1,1]{1,0:T(1,128)S(6)} %copy.9.live_ref, bf16[1,1,32,256,256]{4,3,2,1,0:T(8,128)(2,1)S(1)} %copy-done.6, f32[32,256]{1,0:T(8,128)S(1)} %get-tuple-element.39.refs_0_.refs_4_.refs_5_, ...), custom_call_target="tpu_custom_call" | custom-call | flops 134217728 | bytes 1048576 | tf_op jit(solution)/shard_map/pallas_call | solution.py:30
  146.4 8.5 %all-to-all-start.6 = ((bf16[32,40,256]{2,1,0:T(8,128)(2,1)}), bf16[32,40,256]{2,1,0:T(8,128)(2,1)S(1)}, u32[]{:S(2)}, u32[]{:S(2)}) async-start(bf16[32,40,256]{2,1,0:T(8,128)(2,1)} %shard_map.95), calls=%async_computation.6 | async-start | bytes 1310720 | tf_op jit(solution)/shard_map/all_to_all | solution.py:46
  175.0 9.2 %all-to-all-start.8 = ((f32[32,48,128]{2,1,0:T(8,128)}), f32[32,48,128]{2,1,0:T(8,128)S(1)}, u32[]{:S(2)}, u32[]{:S(2)}) async-start(f32[32,48,128]{2,1,0:T(8,128)} %shard_map.98), calls=%async_computation.8 | async-start | bytes 1572864 | tf_op jit(solution)/shard_map/all_to_all | solution.py:46
  186.8 3.4 %shard_map.100 = (f32[160,160]{1,0:T(8,128)S(1)}, f32[160,160]{1,0:T(8,128)S(1)}) custom-call(bf16[32,40,256]{2,1,0:T(8,128)(2,1)S(1)} %all-to-all-done.5.columns_ref, f32[160,160]{1,0:T(8,128)S(1)} %get-tuple-element.69.refs_0_, f32[160,160]{1,0:T(8,128)S(1)} %get-tuple-element.70.refs_1_), custom_call_target="tpu_custom_call" | custom-call | flops 2000000 | bytes 1048576 | tf_op jit(solution)/shard_map/pallas_call | solution.py:30
  190.2 3.4 %shard_map.101 = (f32[160,160]{1,0:T(8,128)S(1)}, f32[160,160]{1,0:T(8,128)S(1)}) custom-call(bf16[32,40,256]{2,1,0:T(8,128)(2,1)S(1)} %all-to-all-done.7.columns_ref, f32[160,160]{1,0:T(8,128)S(1)} %get-tuple-element.71.refs_0_, f32[160,160]{1,0:T(8,128)S(1)} %get-tuple-element.72.refs_1_), custom_call_target="tpu_custom_call" | custom-call | flops 2000000 | bytes 1048576 | tf_op jit(solution)/shard_map/pallas_call | solution.py:30
  193.6 4.9 %all-to-all-done.8.parts_ref = f32[32,48,128]{2,1,0:T(8,128)S(1)} async-done(((f32[32,48,128]{2,1,0:T(8,128)}), f32[32,48,128]{2,1,0:T(8,128)S(1)}, u32[]{:S(2)}, u32[]{:S(2)}) %all-to-all-start.8) | async-done | bytes 786464 | tf_op jit(solution)/shard_map/all_to_all | solution.py:46
  198.4 8.1 %shard_map.102 = (f32[4,32,128]{2,1,0:T(8,128)}, f32[4,32,32]{2,1,0:T(8,128)}, f32[32,1024]{1,0:T(8,128)}) custom-call(f32[32,48,128]{2,1,0:T(8,128)S(1)} %all-to-all-done.8.parts_ref, f32[160,160]{1,0:T(8,128)S(1)} %get-tuple-element.73.old_low, f32[160,160]{1,0:T(8,128)S(1)} %get-tuple-element.74.old_inv, ...), custom_call_target="tpu_custom_call" | custom-call | flops 2000000 | bytes 1048576 | tf_op jit(solution)/shard_map/pallas_call | solution.py:30
  (89 shorter events, 80.4 us)
Async XLA Ops:
  3.1 20.9 %all-to-all-start.1 = ((bf16[32,32,256]{2,1,0:T(8,128)(2,1)}), bf16[32,32,256]{2,1,0:T(8,128)(2,1)S(1)}, u32[]{:S(2)}, u32[]{:S(2)}) async-start(bf16[32,32,256]{2,1,0:T(8,128)(2,1)} %get-tuple-element.43), calls=%async_computation.1 | async-start | bytes 1048576 | tf_op jit(solution)/shard_map/all_to_all | solution.py:46
  23.9 16.9 %all-to-all-start = ((bf16[32,40,256]{2,1,0:T(8,128)(2,1)}), bf16[32,40,256]{2,1,0:T(8,128)(2,1)S(1)}, u32[]{:S(2)}, u32[]{:S(2)}) async-start(bf16[32,40,256]{2,1,0:T(8,128)(2,1)} %shard_map.86), calls=%async_computation | async-start | bytes 1310720 | tf_op jit(solution)/shard_map/all_to_all | solution.py:46
  32.7 5.1 %collective-permute-start = (f32[32,256]{1,0:T(8,128)S(1)}, f32[32,256]{1,0:T(8,128)S(1)}, u32[]{:S(2)}, u32[]{:S(2)}) collective-permute-start(f32[32,256]{1,0:T(8,128)S(1)} %get-tuple-element.45), channel_id=1, source_target_pairs={{0,32},{32,64},{64,96},{96,0},{1,33},{33,65},{65,97},{97,1},{2,34}... | collective-permute-start | bytes 98312 | tf_op jit(solution)/shard_map/ppermute | solution.py:51
  34.1 4.6 %collective-permute-start.1 = (f32[32,256]{1,0:T(8,128)S(1)}, f32[32,256]{1,0:T(8,128)S(1)}, u32[]{:S(2)}, u32[]{:S(2)}) collective-permute-start(f32[32,256]{1,0:T(8,128)S(1)} %get-tuple-element.46), channel_id=1, source_target_pairs={{0,64},{32,96},{64,0},{96,32},{1,65},{33,97},{65,1},{97,33},{2,66}... | collective-permute-start | bytes 98312 | tf_op jit(solution)/shard_map/ppermute | solution.py:51
  41.8 20.7 %all-to-all-start.3 = ((bf16[32,40,256]{2,1,0:T(8,128)(2,1)}), bf16[32,40,256]{2,1,0:T(8,128)(2,1)S(1)}, u32[]{:S(2)}, u32[]{:S(2)}) async-start(bf16[32,40,256]{2,1,0:T(8,128)(2,1)} %get-tuple-element.50), calls=%async_computation.3 | async-start | bytes 1310720 | tf_op jit(solution)/shard_map/all_to_all | solution.py:46
  52.0 4.6 %collective-permute-start.4 = (f32[32,256]{1,0:T(8,128)S(1)}, f32[32,256]{1,0:T(8,128)S(1)}, u32[]{:S(2)}, u32[]{:S(2)}) collective-permute-start(f32[32,256]{1,0:T(8,128)S(1)} %get-tuple-element.49.refs_4_.refs_5_), channel_id=1, source_target_pairs={{0,64},{32,96},{64,0},{96,32},{1,65},{33,97},{65,1},{97,33},{2,66}... | collective-permute-start | bytes 98312 | tf_op jit(solution)/shard_map/ppermute | solution.py:51
  52.0 4.6 %collective-permute-start.3 = (f32[32,256]{1,0:T(8,128)S(1)}, f32[32,256]{1,0:T(8,128)S(1)}, u32[]{:S(2)}, u32[]{:S(2)}) collective-permute-start(f32[32,256]{1,0:T(8,128)S(1)} %get-tuple-element.49.refs_4_.refs_5_), channel_id=1, source_target_pairs={{0,32},{32,64},{64,96},{96,0},{1,33},{33,65},{65,97},{97,1},{2,34}... | collective-permute-start | bytes 98312 | tf_op jit(solution)/shard_map/ppermute | solution.py:51
  62.5 21.2 %all-to-all-start.2 = ((bf16[32,40,256]{2,1,0:T(8,128)(2,1)}), bf16[32,40,256]{2,1,0:T(8,128)(2,1)S(1)}, u32[]{:S(2)}, u32[]{:S(2)}) async-start(bf16[32,40,256]{2,1,0:T(8,128)(2,1)} %shard_map.89), calls=%async_computation.2 | async-start | bytes 1310720 | tf_op jit(solution)/shard_map/all_to_all | solution.py:46
  75.7 4.3 %collective-permute-start.6 = (f32[32,256]{1,0:T(8,128)S(1)}, f32[32,256]{1,0:T(8,128)S(1)}, u32[]{:S(2)}, u32[]{:S(2)}) collective-permute-start(f32[32,256]{1,0:T(8,128)S(1)} %get-tuple-element.52), channel_id=1, source_target_pairs={{0,32},{32,64},{64,96},{96,0},{1,33},{33,65},{65,97},{97,1},{2,34}... | collective-permute-start | bytes 98312 | tf_op jit(solution)/shard_map/ppermute | solution.py:51
  75.8 4.6 %collective-permute-start.7 = (f32[32,256]{1,0:T(8,128)S(1)}, f32[32,256]{1,0:T(8,128)S(1)}, u32[]{:S(2)}, u32[]{:S(2)}) collective-permute-start(f32[32,256]{1,0:T(8,128)S(1)} %get-tuple-element.53), channel_id=1, source_target_pairs={{0,64},{32,96},{64,0},{96,32},{1,65},{33,97},{65,1},{97,33},{2,66}... | collective-permute-start | bytes 98312 | tf_op jit(solution)/shard_map/ppermute | solution.py:51
  84.7 19.6 %all-to-all-start.5 = ((bf16[32,40,256]{2,1,0:T(8,128)(2,1)}), bf16[32,40,256]{2,1,0:T(8,128)(2,1)S(1)}, u32[]{:S(2)}, u32[]{:S(2)}) async-start(bf16[32,40,256]{2,1,0:T(8,128)(2,1)} %get-tuple-element.56), calls=%async_computation.5 | async-start | bytes 1310720 | tf_op jit(solution)/shard_map/all_to_all | solution.py:46
  93.6 4.4 %collective-permute-start.10 = (f32[32,256]{1,0:T(8,128)S(1)}, f32[32,256]{1,0:T(8,128)S(1)}, u32[]{:S(2)}, u32[]{:S(2)}) collective-permute-start(f32[32,256]{1,0:T(8,128)S(1)} %get-tuple-element.55.refs_8_.refs_4_.refs_5_), channel_id=1, source_target_pairs={{0,64},{32,96},{64,0},{96,32},{1,65},{33,97},{65,1},{97,33},{2,66}... | collective-permute-start | bytes 98312 | tf_op jit(solution)/shard_map/ppermute | solution.py:51
  93.7 4.6 %collective-permute-start.9 = (f32[32,256]{1,0:T(8,128)S(1)}, f32[32,256]{1,0:T(8,128)S(1)}, u32[]{:S(2)}, u32[]{:S(2)}) collective-permute-start(f32[32,256]{1,0:T(8,128)S(1)} %get-tuple-element.55.refs_8_.refs_4_.refs_5_), channel_id=1, source_target_pairs={{0,32},{32,64},{64,96},{96,0},{1,33},{33,65},{65,97},{97,1},{2,34}... | collective-permute-start | bytes 98312 | tf_op jit(solution)/shard_map/ppermute | solution.py:51
  104.3 21.6 %all-to-all-start.4 = ((bf16[32,40,256]{2,1,0:T(8,128)(2,1)}), bf16[32,40,256]{2,1,0:T(8,128)(2,1)S(1)}, u32[]{:S(2)}, u32[]{:S(2)}) async-start(bf16[32,40,256]{2,1,0:T(8,128)(2,1)} %shard_map.92), calls=%async_computation.4 | async-start | bytes 1310720 | tf_op jit(solution)/shard_map/all_to_all | solution.py:46
  117.9 4.3 %collective-permute-start.12 = (f32[32,256]{1,0:T(8,128)S(1)}, f32[32,256]{1,0:T(8,128)S(1)}, u32[]{:S(2)}, u32[]{:S(2)}) collective-permute-start(f32[32,256]{1,0:T(8,128)S(1)} %get-tuple-element.58), channel_id=1, source_target_pairs={{0,32},{32,64},{64,96},{96,0},{1,33},{33,65},{65,97},{97,1},{2,34}... | collective-permute-start | bytes 98312 | tf_op jit(solution)/shard_map/ppermute | solution.py:51
  117.9 4.6 %collective-permute-start.13 = (f32[32,256]{1,0:T(8,128)S(1)}, f32[32,256]{1,0:T(8,128)S(1)}, u32[]{:S(2)}, u32[]{:S(2)}) collective-permute-start(f32[32,256]{1,0:T(8,128)S(1)} %get-tuple-element.59), channel_id=1, source_target_pairs={{0,64},{32,96},{64,0},{96,32},{1,65},{33,97},{65,1},{97,33},{2,66}... | collective-permute-start | bytes 98312 | tf_op jit(solution)/shard_map/ppermute | solution.py:51
  126.9 19.5 %all-to-all-start.7 = ((bf16[32,40,256]{2,1,0:T(8,128)(2,1)}), bf16[32,40,256]{2,1,0:T(8,128)(2,1)S(1)}, u32[]{:S(2)}, u32[]{:S(2)}) async-start(bf16[32,40,256]{2,1,0:T(8,128)(2,1)} %get-tuple-element.62), calls=%async_computation.7 | async-start | bytes 1310720 | tf_op jit(solution)/shard_map/all_to_all | solution.py:46
  135.5 4.5 %collective-permute-start.16 = (f32[32,256]{1,0:T(8,128)S(1)}, f32[32,256]{1,0:T(8,128)S(1)}, u32[]{:S(2)}, u32[]{:S(2)}) collective-permute-start(f32[32,256]{1,0:T(8,128)S(1)} %get-tuple-element.61.refs_12_.refs_4_), channel_id=1, source_target_pairs={{0,64},{32,96},{64,0},{96,32},{1,65},{33,97},{65,1},{97,33},{2,66}... | collective-permute-start | bytes 98312 | tf_op jit(solution)/shard_map/ppermute | solution.py:51
  135.9 4.5 %collective-permute-start.15 = (f32[32,256]{1,0:T(8,128)S(1)}, f32[32,256]{1,0:T(8,128)S(1)}, u32[]{:S(2)}, u32[]{:S(2)}) collective-permute-start(f32[32,256]{1,0:T(8,128)S(1)} %get-tuple-element.61.refs_12_.refs_4_), channel_id=1, source_target_pairs={{0,32},{32,64},{64,96},{96,0},{1,33},{33,65},{65,97},{97,1},{2,34}... | collective-permute-start | bytes 98312 | tf_op jit(solution)/shard_map/ppermute | solution.py:51
  146.4 21.4 %all-to-all-start.6 = ((bf16[32,40,256]{2,1,0:T(8,128)(2,1)}), bf16[32,40,256]{2,1,0:T(8,128)(2,1)S(1)}, u32[]{:S(2)}, u32[]{:S(2)}) async-start(bf16[32,40,256]{2,1,0:T(8,128)(2,1)} %shard_map.95), calls=%async_computation.6 | async-start | bytes 1310720 | tf_op jit(solution)/shard_map/all_to_all | solution.py:46
  159.7 4.3 %collective-permute-start.18 = (f32[32,256]{1,0:T(8,128)S(1)}, f32[32,256]{1,0:T(8,128)S(1)}, u32[]{:S(2)}, u32[]{:S(2)}) collective-permute-start(f32[32,256]{1,0:T(8,128)S(1)} %get-tuple-element.64), channel_id=1, source_target_pairs={{0,32},{32,64},{64,96},{96,0},{1,33},{33,65},{65,97},{97,1},{2,34}... | collective-permute-start | bytes 98312 | tf_op jit(solution)/shard_map/ppermute | solution.py:51
  159.8 4.6 %collective-permute-start.19 = (f32[32,256]{1,0:T(8,128)S(1)}, f32[32,256]{1,0:T(8,128)S(1)}, u32[]{:S(2)}, u32[]{:S(2)}) collective-permute-start(f32[32,256]{1,0:T(8,128)S(1)} %get-tuple-element.65), channel_id=1, source_target_pairs={{0,64},{32,96},{64,0},{96,32},{1,65},{33,97},{65,1},{97,33},{2,66}... | collective-permute-start | bytes 98312 | tf_op jit(solution)/shard_map/ppermute | solution.py:51
  168.2 4.3 %collective-permute-start.22 = (f32[32,256]{1,0:T(8,128)S(1)}, f32[32,256]{1,0:T(8,128)S(1)}, u32[]{:S(2)}, u32[]{:S(2)}) collective-permute-start(f32[32,256]{1,0:T(8,128)S(1)} %get-tuple-element.68.refs_16_), channel_id=1, source_target_pairs={{0,64},{32,96},{64,0},{96,32},{1,65},{33,97},{65,1},{97,33},{2,66}... | collective-permute-start | bytes 98312 | tf_op jit(solution)/shard_map/ppermute | solution.py:51
  175.0 23.4 %all-to-all-start.8 = ((f32[32,48,128]{2,1,0:T(8,128)}), f32[32,48,128]{2,1,0:T(8,128)S(1)}, u32[]{:S(2)}, u32[]{:S(2)}) async-start(f32[32,48,128]{2,1,0:T(8,128)} %shard_map.98), calls=%async_computation.8 | async-start | bytes 1572864 | tf_op jit(solution)/shard_map/all_to_all | solution.py:46
  (23 other events, 125.5 us)

commit v3 on v2

--- a/solution.py
+++ b/solution.py
@@ -65,6 +65,14 @@
     return dot(left, right, ((1,), (1,)))
 
 
+def halves(value):
+    return jnp.concatenate([value[:, :LANES], value[:, LANES:]], 0)
+
+
+def whole(ref, r, width):
+    return jnp.concatenate([ref[r, pl.ds(0, width), :], ref[r, pl.ds(width, width), :]], 1)
+
+
 def pieces(value):
     high = value.astype(BF16).astype(F32)
     rest = value - high
@@ -86,7 +94,7 @@
     for s in range(groups):
         block = lax.rem(group - s + groups, groups)
         slots[s][...] = start_ref[:, pl.ds(pl.multiple_of(block * edge, edge), edge)]
-    rounded = slots[0][...].astype(BF16)
+    rounded = halves(slots[0][...]).astype(BF16)
     for r in range(owners):
         sent_ref[r] = rounded
     coef_ref[...] = SHIFT - shift_ref[:, pl.ds(pl.multiple_of(group * edge, edge), edge)]
@@ -111,7 +119,7 @@
     copies = fetches(tiles_ref, held, sems)
     for copy in copies:
         copy.start()
-    owners, width, edge = total.shape
+    owners, width, _ = total.shape
     group = lax.axis_index("grp")
     live = live_ref[0, 0]
     for s in range(groups):
@@ -128,8 +136,7 @@
     high, middle, low = pieces(jnp.concatenate(grams, 1))
     for r in range(owners):
         value = stacked(high[r : r + 1], middle[r : r + 1], low[r : r + 1])
-        value = jnp.concatenate([value, jnp.zeros((EXTRA, edge - LANES), F32)], 1)
-        out_ref[r, pl.ds(width, EXTRA), :] = value.astype(BF16)
+        out_ref[r, pl.ds(2 * width, EXTRA), :] = value.astype(BF16)
     per_chunk = held.shape[0] // CHUNKS
     for c in range(CHUNKS):
         copies[c].wait()
@@ -140,7 +147,7 @@
             )
             total[cols_ref[0, 0, k]] += jnp.where(k < live, product, jnp.zeros_like(product))
     for r in range(owners):
-        out_ref[r, pl.ds(0, width), :] = total[r].astype(BF16)
+        out_ref[r, pl.ds(0, 2 * width), :] = halves(total[r]).astype(BF16)
 
 
 def ahead_kernel(groups, rows_ref, cols_ref, live_ref, tiles_ref, columns_ref, *refs):
@@ -159,14 +166,14 @@
         for k in range(c * per_chunk, (c + 1) * per_chunk):
             target = lax.rem(rows_ref[0, 0, k] - group + groups, groups)
             product = lax.dot_general(
-                columns_ref[cols_ref[0, 0, k], pl.ds(0, width), :],
+                whole(columns_ref, cols_ref[0, 0, k], width),
                 held[k],
                 (((1,), (1,)), ((), ())),
                 preferred_element_type=F32,
             )
             total[target] += jnp.where(k < live, product, jnp.zeros_like(product))
     for s in range(groups):
-        outs[s][...] = total[s]
+        outs[s][...] = total[s].astype(outs[s].dtype)
 
 
 def combine_kernel(groups, last, back_ref, *refs):
@@ -175,27 +182,25 @@
     outs = refs[groups + 3 :]
     owners = back_ref.shape[0]
     width = now_ref.shape[0]
-    edge = now_ref.shape[1]
     image = direct[0][...]
     for s in range(1, groups):
-        image = image + direct[s][...]
-    for r in range(owners):
-        image = image + back_ref[r, pl.ds(0, width), :].astype(F32)
+        image = image + direct[s][...].astype(F32)
+    for r in range(owners):
+        image = image + whole(back_ref, r, width).astype(F32)
     new = 0.5 * image + coef_ref[...] * now_ref[...] - PULL * before_ref[...]
     outs[0][...] = new
-    sums = back_ref[0, pl.ds(width, EXTRA), pl.ds(0, LANES)].astype(F32)
+    sums = back_ref[0, pl.ds(2 * width, EXTRA), :].astype(F32)
     for r in range(1, owners):
-        sums = sums + back_ref[r, pl.ds(width, EXTRA), pl.ds(0, LANES)].astype(F32)
+        sums = sums + back_ref[r, pl.ds(2 * width, EXTRA), :].astype(F32)
     row = sums[0:1] + (sums[1:2] + sums[2:3])
     if last:
         outs[1][...] = jnp.broadcast_to(row, (EXTRA, LANES))
     else:
-        rounded = new.astype(BF16)
-        extra = stacked(*pieces(row))
-        extra = jnp.concatenate([extra, jnp.zeros((EXTRA, edge - LANES), F32)], 1).astype(BF16)
+        rounded = halves(new).astype(BF16)
+        extra = stacked(*pieces(row)).astype(BF16)
         for r in range(owners):
-            outs[1][r, pl.ds(0, width), :] = rounded
-            outs[1][r, pl.ds(width, EXTRA), :] = extra
+            outs[1][r, pl.ds(0, 2 * width), :] = rounded
+            outs[1][r, pl.ds(2 * width, EXTRA), :] = extra
 
 
 def factor(block):
@@ -261,7 +266,7 @@
         inv_ref[...] = olds[1][...]
     rows = []
     for r in range(owners):
-        three = columns_ref[r, pl.ds(width, EXTRA), pl.ds(0, LANES)].astype(F32)
+        three = columns_ref[r, pl.ds(2 * width, EXTRA), :].astype(F32)
         rows.append(three[0:1] + (three[1:2] + three[2:3]))
     next_rows(j, jnp.concatenate(rows, 0), low_ref, inv_ref)
 
@@ -323,13 +328,13 @@
     owners = lax.axis_size("row")
     total = (ITERS + 1) * width
     tables = (tile_rows, tile_cols, live_tiles, tiles)
-    spaces = [SMEM, SMEM, SMEM, pl.ANY]
+    spaces = [SMEM, SMEM, SMEM, pltpu.HBM]
     held = pltpu.VMEM((count, edge, edge), BF16)
     flops = 2 * count * width * edge * edge
 
     *slots, sent, coef = call(
         functools.partial(init_kernel, groups, owners),
-        [shape(width, edge)] * groups + [shape(owners, width, edge, dtype=BF16), shape(1, edge)],
+        [shape(width, edge)] * groups + [shape(owners, 2 * width, LANES, dtype=BF16), shape(1, edge)],
         [VMEM, VMEM],
         (start_block, dual_shift[None, :]),
         4,
@@ -343,10 +348,10 @@
         flat = [slot for slots in basis for slot in slots]
         (parts,) = call(
             functools.partial(back_kernel, groups, step),
-            [shape(owners, width + EXTRA, edge, dtype=BF16)],
+            [shape(owners, 2 * width + EXTRA, LANES, dtype=BF16)],
             spaces + [VMEM] * len(flat),
             (*tables, *flat),
-            12,
+            50,
             [
                 held,
                 pltpu.VMEM((owners, width, edge), F32),
@@ -358,10 +363,10 @@
         arrived = exchange(parts, "row")
         direct = call(
             functools.partial(ahead_kernel, groups),
-            [shape(width, edge)] * groups,
+            [shape(width, edge)] + [shape(width, edge, dtype=BF16)] * (groups - 1),
             spaces + [VMEM],
             (*tables, columns),
-            12,
+            50,
             [held, pltpu.VMEM((groups, width, edge), F32), pltpu.SemaphoreType.DMA((CHUNKS,))],
             flops,
         )
@@ -375,7 +380,7 @@
                 4,
             )
         last = step == ITERS - 1
-        second = shape(EXTRA, LANES) if last else shape(owners, width + EXTRA, edge, dtype=BF16)
+        second = shape(EXTRA, LANES) if last else shape(owners, 2 * width + EXTRA, LANES, dtype=BF16)
         new, sent = call(
             functools.partial(combine_kernel, groups, last),
             [shape(width, edge), second],

time: 208 us -> 197 us (0.947)
  local copies, waits for them, and re-layouts: 20.4 us -> 2.9 us
  Pallas kernels: 47.9 us -> 53.6 us
  waiting for transfers between devices: 40.5 us -> 45.7 us
  starting transfers between devices: 96.2 us -> 91.9 us
    unnamed x28 -> x12, local copies, waits for them, and re-layouts: 20.4 us -> 2.9 us
    all_to_all x9, waiting for transfers between devices: 18.3 us -> 24.3 us  [exchange(): return lax.all_to_all(parts, axis, split_axis=0, concat_axis=0, tiled=True)]
    pallas_call x18, Pallas kernels: 47.9 us -> 53.6 us  [call(): pl.pallas_call(kernel, out_shape=out_shape, in_specs=[spec(space) for spa...]
    all_to_all x9, starting transfers between devices: 67.5 us -> 63 us  [exchange(): return lax.all_to_all(parts, axis, split_axis=0, concat_axis=0, tiled=True)]
  transfers between devices with their start and end apart: 33 -> 33, of which waited for: 29 -> 29; matrix products, arithmetic and copies ran while one was open for 0% -> 0% of each run, Pallas kernels for 17% -> 20%
where the time goes in v3:
time: 197 us; the launch traced here: 196 us
  starting transfers between devices  91.9 us (47%)
  Pallas kernels  53.6 us (27%)
  waiting for transfers between devices  45.7 us (23%)
  local copies, waits for them, and re-layouts  2.9 us (1%)
    all_to_all x9, starting transfers between devices, exchange(): return lax.all_to_all(parts, axis, split_axis=0, concat_axis=0, tiled=True)  63 us
    pallas_call x18, Pallas kernels, call(): pl.pallas_call(kernel, out_shape=out_shape, in_specs=[spec(space) for spa...  53.6 us
    ppermute x24, starting transfers between devices, from_behind(): lax.ppermute(value, axis, [(i, (i + distance) % size) for i in range(size)])  28.9 us
    all_to_all x9, waiting for transfers between devices, exchange(): return lax.all_to_all(parts, axis, split_axis=0, concat_axis=0, tiled=True)  24.3 us
    ppermute x24, waiting for transfers between devices, from_behind(): lax.ppermute(value, axis, [(i, (i + distance) % size) for i in range(size)])  21.4 us
  transfers between devices with their start and end apart: 33, of which 29 were waited for; matrix products, arithmetic and copies ran while one was open for 0% of the time, Pallas kernels for 20%

profile of v3, /device:TPU:1, one launch (start us, length us, event | category | flops | bytes accessed | tf_op | source)
XLA Modules:
  0.0 195.6 jit_solution(11515460169475583979)
XLA Ops:
  3.1 9.4 %all-to-all-start.1 = ((bf16[32,64,128]{2,1,0:T(8,128)(2,1)}), bf16[32,64,128]{2,1,0:T(8,128)(2,1)S(1)}, u32[]{:S(2)}, u32[]{:S(2)}) async-start(bf16[32,64,128]{2,1,0:T(8,128)(2,1)} %get-tuple-element.43), calls=%async_computation.1 | async-start | bytes 1048576 | tf_op jit(solution)/shard_map/all_to_all | solution.py:46
  14.5 4.1 %shard_map.86 = bf16[32,72,128]{2,1,0:T(8,128)(2,1)} custom-call(s32[1,1,32]{2,1,0:T(1,128)S(1)} %copy-done.1, s32[1,1,32]{2,1,0:T(1,128)S(1)} %copy-done.3, s32[1,1]{1,0:T(1,128)S(6)} %copy.9.live_ref, bf16[1,1,32,256,256]{4,3,2,1,0:T(8,128)(2,1)} %tiles_ref.15, f32[32,256]{1,0:T(8,128)S(1)} %get-tuple-element.39.refs_0_.refs_4_.refs_5_, ...), custom_call_target="tpu_custom_call" | custom-call | flops 134217728 | bytes 1048576 | tf_op jit(solution)/shard_map/pallas_call | solution.py:30
  18.7 5.3 %all-to-all-done.1.columns_ref = bf16[32,64,128]{2,1,0:T(8,128)(2,1)S(1)} async-done(((bf16[32,64,128]{2,1,0:T(8,128)(2,1)}), bf16[32,64,128]{2,1,0:T(8,128)(2,1)S(1)}, u32[]{:S(2)}, u32[]{:S(2)}) %all-to-all-start.1) | async-done | bytes 524320 | tf_op jit(solution)/shard_map/all_to_all | solution.py:46
  24.0 3.9 %all-to-all-start = ((bf16[32,72,128]{2,1,0:T(8,128)(2,1)}), bf16[32,72,128]{2,1,0:T(8,128)(2,1)S(1)}, u32[]{:S(2)}, u32[]{:S(2)}) async-start(bf16[32,72,128]{2,1,0:T(8,128)(2,1)} %shard_map.86), calls=%async_computation | async-start | bytes 1179648 | tf_op jit(solution)/shard_map/all_to_all | solution.py:46
  27.9 3.5 %shard_map.87 = (f32[32,256]{1,0:T(8,128)S(1)}, bf16[32,256]{1,0:T(8,128)(2,1)S(1)}, bf16[32,256]{1,0:T(8,128)(2,1)S(1)}, bf16[32,256]{1,0:T(8,128)(2,1)S(1)}) custom-call(s32[1,1,32]{2,1,0:T(1,128)S(1)} %copy-done.1, s32[1,1,32]{2,1,0:T(1,128)S(1)} %copy-done.3, s32[1,1]{1,0:T(1,128)S(6)} %copy.9.live_ref, bf16[1,1,32,256,256]{4,3,2,1,0:T(8,128)(2,1)} %tiles_ref.15, ...), custom_call_target="tpu_custom_call" | custom-call | flops 134217728 | bytes 1048576 | tf_op jit(solution)/shard_map/pallas_call | solution.py:30
  41.1 7.1 %all-to-all-start.3 = ((bf16[32,72,128]{2,1,0:T(8,128)(2,1)}), bf16[32,72,128]{2,1,0:T(8,128)(2,1)S(1)}, u32[]{:S(2)}, u32[]{:S(2)}) async-start(bf16[32,72,128]{2,1,0:T(8,128)(2,1)} %get-tuple-element.50), calls=%async_computation.3 | async-start | bytes 1179648 | tf_op jit(solution)/shard_map/all_to_all | solution.py:46
  51.6 3.5 %collective-permute-done.4.refs_6_ = f32[32,256]{1,0:T(8,128)S(1)} collective-permute-done((f32[32,256]{1,0:T(8,128)S(1)}, f32[32,256]{1,0:T(8,128)S(1)}, u32[]{:S(2)}, u32[]{:S(2)}) %collective-permute-start.4) | collective-permute-done | bytes 32800 | tf_op jit(solution)/shard_map/ppermute | solution.py:51
  55.1 3.9 %shard_map.89 = bf16[32,72,128]{2,1,0:T(8,128)(2,1)} custom-call(s32[1,1,32]{2,1,0:T(1,128)S(1)} %copy-done.2, s32[1,1,32]{2,1,0:T(1,128)S(1)} %copy-done.4, s32[1,1]{1,0:T(1,128)S(6)} %copy.9.live_ref, bf16[1,1,32,256,256]{4,3,2,1,0:T(8,128)(2,1)} %tiles_ref.15, f32[32,256]{1,0:T(8,128)S(1)} %get-tuple-element.39.refs_0_.refs_4_.refs_5_, ...), custom_call_target="tpu_custom_call" | custom-call | flops 134217728 | bytes 1048576 | tf_op jit(solution)/shard_map/pallas_call | solution.py:30
  60.4 7.3 %all-to-all-start.2 = ((bf16[32,72,128]{2,1,0:T(8,128)(2,1)}), bf16[32,72,128]{2,1,0:T(8,128)(2,1)S(1)}, u32[]{:S(2)}, u32[]{:S(2)}) async-start(bf16[32,72,128]{2,1,0:T(8,128)(2,1)} %shard_map.89), calls=%async_computation.2 | async-start | bytes 1179648 | tf_op jit(solution)/shard_map/all_to_all | solution.py:46
  67.7 3.6 %shard_map.90 = (f32[32,256]{1,0:T(8,128)S(1)}, bf16[32,256]{1,0:T(8,128)(2,1)S(1)}, bf16[32,256]{1,0:T(8,128)(2,1)S(1)}, bf16[32,256]{1,0:T(8,128)(2,1)S(1)}) custom-call(s32[1,1,32]{2,1,0:T(1,128)S(1)} %copy-done.2, s32[1,1,32]{2,1,0:T(1,128)S(1)} %copy-done.4, s32[1,1]{1,0:T(1,128)S(6)} %copy.9.live_ref, bf16[1,1,32,256,256]{4,3,2,1,0:T(8,128)(2,1)} %tiles_ref.15, ...), custom_call_target="tpu_custom_call" | custom-call | flops 134217728 | bytes 1048576 | tf_op jit(solution)/shard_map/pallas_call | solution.py:30
  76.1 3.7 %all-to-all-done.2.back_ref = bf16[32,72,128]{2,1,0:T(8,128)(2,1)S(1)} async-done(((bf16[32,72,128]{2,1,0:T(8,128)(2,1)}), bf16[32,72,128]{2,1,0:T(8,128)(2,1)S(1)}, u32[]{:S(2)}, u32[]{:S(2)}) %all-to-all-start.2) | async-done | bytes 589856 | tf_op jit(solution)/shard_map/all_to_all | solution.py:46
  80.8 4.9 %all-to-all-start.5 = ((bf16[32,72,128]{2,1,0:T(8,128)(2,1)}), bf16[32,72,128]{2,1,0:T(8,128)(2,1)S(1)}, u32[]{:S(2)}, u32[]{:S(2)}) async-start(bf16[32,72,128]{2,1,0:T(8,128)(2,1)} %get-tuple-element.56), calls=%async_computation.5 | async-start | bytes 1179648 | tf_op jit(solution)/shard_map/all_to_all | solution.py:46
  93.7 4.1 %shard_map.92 = bf16[32,72,128]{2,1,0:T(8,128)(2,1)} custom-call(s32[1,1,32]{2,1,0:T(1,128)S(1)} %copy-done.2, s32[1,1,32]{2,1,0:T(1,128)S(1)} %copy-done.4, s32[1,1]{1,0:T(1,128)S(6)} %copy.9.live_ref, bf16[1,1,32,256,256]{4,3,2,1,0:T(8,128)(2,1)} %tiles_ref.15, f32[32,256]{1,0:T(8,128)S(1)} %get-tuple-element.39.refs_0_.refs_4_.refs_5_, ...), custom_call_target="tpu_custom_call" | custom-call | flops 134217728 | bytes 1048576 | tf_op jit(solution)/shard_map/pallas_call | solution.py:30
  97.9 8.7 %all-to-all-start.4 = ((bf16[32,72,128]{2,1,0:T(8,128)(2,1)}), bf16[32,72,128]{2,1,0:T(8,128)(2,1)S(1)}, u32[]{:S(2)}, u32[]{:S(2)}) async-start(bf16[32,72,128]{2,1,0:T(8,128)(2,1)} %shard_map.92), calls=%async_computation.4 | async-start | bytes 1179648 | tf_op jit(solution)/shard_map/all_to_all | solution.py:46
  106.6 3.6 %shard_map.93 = (f32[32,256]{1,0:T(8,128)S(1)}, bf16[32,256]{1,0:T(8,128)(2,1)S(1)}, bf16[32,256]{1,0:T(8,128)(2,1)S(1)}, bf16[32,256]{1,0:T(8,128)(2,1)S(1)}) custom-call(s32[1,1,32]{2,1,0:T(1,128)S(1)} %copy-done.2, s32[1,1,32]{2,1,0:T(1,128)S(1)} %copy-done.4, s32[1,1]{1,0:T(1,128)S(6)} %copy.9.live_ref, bf16[1,1,32,256,256]{4,3,2,1,0:T(8,128)(2,1)} %tiles_ref.15, ...), custom_call_target="tpu_custom_call" | custom-call | flops 134217728 | bytes 1048576 | tf_op jit(solution)/shard_map/pallas_call | solution.py:30
  115.1 3.7 %all-to-all-done.4.back_ref = bf16[32,72,128]{2,1,0:T(8,128)(2,1)S(1)} async-done(((bf16[32,72,128]{2,1,0:T(8,128)(2,1)}), bf16[32,72,128]{2,1,0:T(8,128)(2,1)S(1)}, u32[]{:S(2)}, u32[]{:S(2)}) %all-to-all-start.4) | async-done | bytes 589856 | tf_op jit(solution)/shard_map/all_to_all | solution.py:46
  119.7 4.9 %all-to-all-start.7 = ((bf16[32,72,128]{2,1,0:T(8,128)(2,1)}), bf16[32,72,128]{2,1,0:T(8,128)(2,1)S(1)}, u32[]{:S(2)}, u32[]{:S(2)}) async-start(bf16[32,72,128]{2,1,0:T(8,128)(2,1)} %get-tuple-element.62), calls=%async_computation.7 | async-start | bytes 1179648 | tf_op jit(solution)/shard_map/all_to_all | solution.py:46
  132.6 4.2 %shard_map.95 = bf16[32,72,128]{2,1,0:T(8,128)(2,1)} custom-call(s32[1,1,32]{2,1,0:T(1,128)S(1)} %copy-done.2, s32[1,1,32]{2,1,0:T(1,128)S(1)} %copy-done.4, s32[1,1]{1,0:T(1,128)S(6)} %copy.9.live_ref, bf16[1,1,32,256,256]{4,3,2,1,0:T(8,128)(2,1)} %tiles_ref.15, f32[32,256]{1,0:T(8,128)S(1)} %get-tuple-element.39.refs_0_.refs_4_.refs_5_, ...), custom_call_target="tpu_custom_call" | custom-call | flops 134217728 | bytes 1048576 | tf_op jit(solution)/shard_map/pallas_call | solution.py:30
  136.8 8.5 %all-to-all-start.6 = ((bf16[32,72,128]{2,1,0:T(8,128)(2,1)}), bf16[32,72,128]{2,1,0:T(8,128)(2,1)S(1)}, u32[]{:S(2)}, u32[]{:S(2)}) async-start(bf16[32,72,128]{2,1,0:T(8,128)(2,1)} %shard_map.95), calls=%async_computation.6 | async-start | bytes 1179648 | tf_op jit(solution)/shard_map/all_to_all | solution.py:46
  145.3 3.6 %shard_map.96 = (f32[32,256]{1,0:T(8,128)S(1)}, bf16[32,256]{1,0:T(8,128)(2,1)S(1)}, bf16[32,256]{1,0:T(8,128)(2,1)S(1)}, bf16[32,256]{1,0:T(8,128)(2,1)S(1)}) custom-call(s32[1,1,32]{2,1,0:T(1,128)S(1)} %copy-done.2, s32[1,1,32]{2,1,0:T(1,128)S(1)} %copy-done.4, s32[1,1]{1,0:T(1,128)S(6)} %copy.9.live_ref, bf16[1,1,32,256,256]{4,3,2,1,0:T(8,128)(2,1)} %tiles_ref.15, ...), custom_call_target="tpu_custom_call" | custom-call | flops 134217728 | bytes 1048576 | tf_op jit(solution)/shard_map/pallas_call | solution.py:30
  153.8 3.7 %all-to-all-done.6.back_ref = bf16[32,72,128]{2,1,0:T(8,128)(2,1)S(1)} async-done(((bf16[32,72,128]{2,1,0:T(8,128)(2,1)}), bf16[32,72,128]{2,1,0:T(8,128)(2,1)S(1)}, u32[]{:S(2)}, u32[]{:S(2)}) %all-to-all-start.6) | async-done | bytes 589856 | tf_op jit(solution)/shard_map/all_to_all | solution.py:46
  165.1 8.2 %all-to-all-start.8 = ((f32[32,48,128]{2,1,0:T(8,128)}), f32[32,48,128]{2,1,0:T(8,128)S(1)}, u32[]{:S(2)}, u32[]{:S(2)}) async-start(f32[32,48,128]{2,1,0:T(8,128)} %shard_map.98), calls=%async_computation.8 | async-start | bytes 1572864 | tf_op jit(solution)/shard_map/all_to_all | solution.py:46
  182.6 4.9 %all-to-all-done.8.parts_ref = f32[32,48,128]{2,1,0:T(8,128)S(1)} async-done(((f32[32,48,128]{2,1,0:T(8,128)}), f32[32,48,128]{2,1,0:T(8,128)S(1)}, u32[]{:S(2)}, u32[]{:S(2)}) %all-to-all-start.8) | async-done | bytes 786464 | tf_op jit(solution)/shard_map/all_to_all | solution.py:46
  187.5 8.1 %shard_map.102 = (f32[4,32,128]{2,1,0:T(8,128)}, f32[4,32,32]{2,1,0:T(8,128)}, f32[32,1024]{1,0:T(8,128)}) custom-call(f32[32,48,128]{2,1,0:T(8,128)S(1)} %all-to-all-done.8.parts_ref, f32[160,160]{1,0:T(8,128)S(1)} %get-tuple-element.73.old_low, f32[160,160]{1,0:T(8,128)S(1)} %get-tuple-element.74.old_inv, ...), custom_call_target="tpu_custom_call" | custom-call | flops 2000000 | bytes 1048576 | tf_op jit(solution)/shard_map/pallas_call | solution.py:30
  (73 shorter events, 67.7 us)
Async XLA Ops:
  3.1 20.9 %all-to-all-start.1 = ((bf16[32,64,128]{2,1,0:T(8,128)(2,1)}), bf16[32,64,128]{2,1,0:T(8,128)(2,1)S(1)}, u32[]{:S(2)}, u32[]{:S(2)}) async-start(bf16[32,64,128]{2,1,0:T(8,128)(2,1)} %get-tuple-element.43), calls=%async_computation.1 | async-start | bytes 1048576 | tf_op jit(solution)/shard_map/all_to_all | solution.py:46
  24.0 16.2 %all-to-all-start = ((bf16[32,72,128]{2,1,0:T(8,128)(2,1)}), bf16[32,72,128]{2,1,0:T(8,128)(2,1)S(1)}, u32[]{:S(2)}, u32[]{:S(2)}) async-start(bf16[32,72,128]{2,1,0:T(8,128)(2,1)} %shard_map.86), calls=%async_computation | async-start | bytes 1179648 | tf_op jit(solution)/shard_map/all_to_all | solution.py:46
  31.5 5.0 %collective-permute-start = (bf16[32,256]{1,0:T(8,128)(2,1)S(1)}, bf16[32,256]{1,0:T(8,128)(2,1)S(1)}, u32[]{:S(2)}, u32[]{:S(2)}) collective-permute-start(bf16[32,256]{1,0:T(8,128)(2,1)S(1)} %get-tuple-element.45), channel_id=1, source_target_pairs={{0,32},{32,64},{64,96},{96,0},{1,33},{33,65},{65,97},{97,1},{2,34}... | collective-permute-start | bytes 49160 | tf_op jit(solution)/shard_map/ppermute | solution.py:51
  32.8 4.4 %collective-permute-start.1 = (bf16[32,256]{1,0:T(8,128)(2,1)S(1)}, bf16[32,256]{1,0:T(8,128)(2,1)S(1)}, u32[]{:S(2)}, u32[]{:S(2)}) collective-permute-start(bf16[32,256]{1,0:T(8,128)(2,1)S(1)} %get-tuple-element.46), channel_id=1, source_target_pairs={{0,64},{32,96},{64,0},{96,32},{1,65},{33,97},{65,1},{97,33},{2,66}... | collective-permute-start | bytes 49160 | tf_op jit(solution)/shard_map/ppermute | solution.py:51
  41.1 19.2 %all-to-all-start.3 = ((bf16[32,72,128]{2,1,0:T(8,128)(2,1)}), bf16[32,72,128]{2,1,0:T(8,128)(2,1)S(1)}, u32[]{:S(2)}, u32[]{:S(2)}) async-start(bf16[32,72,128]{2,1,0:T(8,128)(2,1)} %get-tuple-element.50), calls=%async_computation.3 | async-start | bytes 1179648 | tf_op jit(solution)/shard_map/all_to_all | solution.py:46
  50.6 4.6 %collective-permute-start.4 = (f32[32,256]{1,0:T(8,128)S(1)}, f32[32,256]{1,0:T(8,128)S(1)}, u32[]{:S(2)}, u32[]{:S(2)}) collective-permute-start(f32[32,256]{1,0:T(8,128)S(1)} %get-tuple-element.49.refs_4_.refs_5_), channel_id=1, source_target_pairs={{0,64},{32,96},{64,0},{96,32},{1,65},{33,97},{65,1},{97,33},{2,66}... | collective-permute-start | bytes 98312 | tf_op jit(solution)/shard_map/ppermute | solution.py:51
  50.6 4.6 %collective-permute-start.3 = (f32[32,256]{1,0:T(8,128)S(1)}, f32[32,256]{1,0:T(8,128)S(1)}, u32[]{:S(2)}, u32[]{:S(2)}) collective-permute-start(f32[32,256]{1,0:T(8,128)S(1)} %get-tuple-element.49.refs_4_.refs_5_), channel_id=1, source_target_pairs={{0,32},{32,64},{64,96},{96,0},{1,33},{33,65},{65,97},{97,1},{2,34}... | collective-permute-start | bytes 98312 | tf_op jit(solution)/shard_map/ppermute | solution.py:51
  60.4 19.4 %all-to-all-start.2 = ((bf16[32,72,128]{2,1,0:T(8,128)(2,1)}), bf16[32,72,128]{2,1,0:T(8,128)(2,1)S(1)}, u32[]{:S(2)}, u32[]{:S(2)}) async-start(bf16[32,72,128]{2,1,0:T(8,128)(2,1)} %shard_map.89), calls=%async_computation.2 | async-start | bytes 1179648 | tf_op jit(solution)/shard_map/all_to_all | solution.py:46
  71.2 4.2 %collective-permute-start.6 = (bf16[32,256]{1,0:T(8,128)(2,1)S(1)}, bf16[32,256]{1,0:T(8,128)(2,1)S(1)}, u32[]{:S(2)}, u32[]{:S(2)}) collective-permute-start(bf16[32,256]{1,0:T(8,128)(2,1)S(1)} %get-tuple-element.52), channel_id=1, source_target_pairs={{0,32},{32,64},{64,96},{96,0},{1,33},{33,65},{65,97},{97,1},{2,34}... | collective-permute-start | bytes 49160 | tf_op jit(solution)/shard_map/ppermute | solution.py:51
  71.3 4.5 %collective-permute-start.7 = (bf16[32,256]{1,0:T(8,128)(2,1)S(1)}, bf16[32,256]{1,0:T(8,128)(2,1)S(1)}, u32[]{:S(2)}, u32[]{:S(2)}) collective-permute-start(bf16[32,256]{1,0:T(8,128)(2,1)S(1)} %get-tuple-element.53), channel_id=1, source_target_pairs={{0,64},{32,96},{64,0},{96,32},{1,65},{33,97},{65,1},{97,33},{2,66}... | collective-permute-start | bytes 49160 | tf_op jit(solution)/shard_map/ppermute | solution.py:51
  80.8 17.1 %all-to-all-start.5 = ((bf16[32,72,128]{2,1,0:T(8,128)(2,1)}), bf16[32,72,128]{2,1,0:T(8,128)(2,1)S(1)}, u32[]{:S(2)}, u32[]{:S(2)}) async-start(bf16[32,72,128]{2,1,0:T(8,128)(2,1)} %get-tuple-element.56), calls=%async_computation.5 | async-start | bytes 1179648 | tf_op jit(solution)/shard_map/all_to_all | solution.py:46
  85.7 4.3 %collective-permute-start.11 = (f32[32,256]{1,0:T(8,128)S(1)}, f32[32,256]{1,0:T(8,128)S(1)}, u32[]{:S(2)}, u32[]{:S(2)}) collective-permute-start(f32[32,256]{1,0:T(8,128)S(1)} %get-tuple-element.55.refs_8_.refs_4_.refs_5_), channel_id=1, source_target_pairs={{0,96},{32,0},{64,32},{96,64},{1,97},{33,1},{65,33},{97,65},{2,98}... | collective-permute-start | bytes 98312 | tf_op jit(solution)/shard_map/ppermute | solution.py:51
  89.0 4.4 %collective-permute-start.10 = (f32[32,256]{1,0:T(8,128)S(1)}, f32[32,256]{1,0:T(8,128)S(1)}, u32[]{:S(2)}, u32[]{:S(2)}) collective-permute-start(f32[32,256]{1,0:T(8,128)S(1)} %get-tuple-element.55.refs_8_.refs_4_.refs_5_), channel_id=1, source_target_pairs={{0,64},{32,96},{64,0},{96,32},{1,65},{33,97},{65,1},{97,33},{2,66}... | collective-permute-start | bytes 98312 | tf_op jit(solution)/shard_map/ppermute | solution.py:51
  89.1 4.6 %collective-permute-start.9 = (f32[32,256]{1,0:T(8,128)S(1)}, f32[32,256]{1,0:T(8,128)S(1)}, u32[]{:S(2)}, u32[]{:S(2)}) collective-permute-start(f32[32,256]{1,0:T(8,128)S(1)} %get-tuple-element.55.refs_8_.refs_4_.refs_5_), channel_id=1, source_target_pairs={{0,32},{32,64},{64,96},{96,0},{1,33},{33,65},{65,97},{97,1},{2,34}... | collective-permute-start | bytes 98312 | tf_op jit(solution)/shard_map/ppermute | solution.py:51
  97.9 20.9 %all-to-all-start.4 = ((bf16[32,72,128]{2,1,0:T(8,128)(2,1)}), bf16[32,72,128]{2,1,0:T(8,128)(2,1)S(1)}, u32[]{:S(2)}, u32[]{:S(2)}) async-start(bf16[32,72,128]{2,1,0:T(8,128)(2,1)} %shard_map.92), calls=%async_computation.4 | async-start | bytes 1179648 | tf_op jit(solution)/shard_map/all_to_all | solution.py:46
  110.2 4.5 %collective-permute-start.13 = (bf16[32,256]{1,0:T(8,128)(2,1)S(1)}, bf16[32,256]{1,0:T(8,128)(2,1)S(1)}, u32[]{:S(2)}, u32[]{:S(2)}) collective-permute-start(bf16[32,256]{1,0:T(8,128)(2,1)S(1)} %get-tuple-element.59), channel_id=1, source_target_pairs={{0,64},{32,96},{64,0},{96,32},{1,65},{33,97},{65,1},{97,33},{2,66}... | collective-permute-start | bytes 49160 | tf_op jit(solution)/shard_map/ppermute | solution.py:51
  119.7 17.1 %all-to-all-start.7 = ((bf16[32,72,128]{2,1,0:T(8,128)(2,1)}), bf16[32,72,128]{2,1,0:T(8,128)(2,1)S(1)}, u32[]{:S(2)}, u32[]{:S(2)}) async-start(bf16[32,72,128]{2,1,0:T(8,128)(2,1)} %get-tuple-element.62), calls=%async_computation.7 | async-start | bytes 1179648 | tf_op jit(solution)/shard_map/all_to_all | solution.py:46
  127.6 4.3 %collective-permute-start.16 = (f32[32,256]{1,0:T(8,128)S(1)}, f32[32,256]{1,0:T(8,128)S(1)}, u32[]{:S(2)}, u32[]{:S(2)}) collective-permute-start(f32[32,256]{1,0:T(8,128)S(1)} %get-tuple-element.61.refs_12_.refs_4_), channel_id=1, source_target_pairs={{0,64},{32,96},{64,0},{96,32},{1,65},{33,97},{65,1},{97,33},{2,66}... | collective-permute-start | bytes 98312 | tf_op jit(solution)/shard_map/ppermute | solution.py:51
  128.0 4.5 %collective-permute-start.15 = (f32[32,256]{1,0:T(8,128)S(1)}, f32[32,256]{1,0:T(8,128)S(1)}, u32[]{:S(2)}, u32[]{:S(2)}) collective-permute-start(f32[32,256]{1,0:T(8,128)S(1)} %get-tuple-element.61.refs_12_.refs_4_), channel_id=1, source_target_pairs={{0,32},{32,64},{64,96},{96,0},{1,33},{33,65},{65,97},{97,1},{2,34}... | collective-permute-start | bytes 98312 | tf_op jit(solution)/shard_map/ppermute | solution.py:51
  136.8 20.7 %all-to-all-start.6 = ((bf16[32,72,128]{2,1,0:T(8,128)(2,1)}), bf16[32,72,128]{2,1,0:T(8,128)(2,1)S(1)}, u32[]{:S(2)}, u32[]{:S(2)}) async-start(bf16[32,72,128]{2,1,0:T(8,128)(2,1)} %shard_map.95), calls=%async_computation.6 | async-start | bytes 1179648 | tf_op jit(solution)/shard_map/all_to_all | solution.py:46
  149.0 4.5 %collective-permute-start.19 = (bf16[32,256]{1,0:T(8,128)(2,1)S(1)}, bf16[32,256]{1,0:T(8,128)(2,1)S(1)}, u32[]{:S(2)}, u32[]{:S(2)}) collective-permute-start(bf16[32,256]{1,0:T(8,128)(2,1)S(1)} %get-tuple-element.65), channel_id=1, source_target_pairs={{0,64},{32,96},{64,0},{96,32},{1,65},{33,97},{65,1},{97,33},{2,66}... | collective-permute-start | bytes 49160 | tf_op jit(solution)/shard_map/ppermute | solution.py:51
  157.9 4.3 %collective-permute-start.22 = (f32[32,256]{1,0:T(8,128)S(1)}, f32[32,256]{1,0:T(8,128)S(1)}, u32[]{:S(2)}, u32[]{:S(2)}) collective-permute-start(f32[32,256]{1,0:T(8,128)S(1)} %get-tuple-element.68.refs_16_), channel_id=1, source_target_pairs={{0,64},{32,96},{64,0},{96,32},{1,65},{33,97},{65,1},{97,33},{2,66}... | collective-permute-start | bytes 98312 | tf_op jit(solution)/shard_map/ppermute | solution.py:51
  159.1 4.3 %collective-permute-start.21 = (f32[32,256]{1,0:T(8,128)S(1)}, f32[32,256]{1,0:T(8,128)S(1)}, u32[]{:S(2)}, u32[]{:S(2)}) collective-permute-start(f32[32,256]{1,0:T(8,128)S(1)} %get-tuple-element.68.refs_16_), channel_id=1, source_target_pairs={{0,32},{32,64},{64,96},{96,0},{1,33},{33,65},{65,97},{97,1},{2,34}... | collective-permute-start | bytes 98312 | tf_op jit(solution)/shard_map/ppermute | solution.py:51
  165.1 22.4 %all-to-all-start.8 = ((f32[32,48,128]{2,1,0:T(8,128)}), f32[32,48,128]{2,1,0:T(8,128)S(1)}, u32[]{:S(2)}, u32[]{:S(2)}) async-start(f32[32,48,128]{2,1,0:T(8,128)} %shard_map.98), calls=%async_computation.8 | async-start | bytes 1572864 | tf_op jit(solution)/shard_map/all_to_all | solution.py:46
  (15 other events, 107.3 us)

commit v4 on v3

--- a/solution.py
+++ b/solution.py
@@ -11,7 +11,9 @@
 ITERS = 4
 SHIFT = 1.0625
 PULL = 0.375
-CHUNKS = 4
+KEEP = 8
+CHUNKS = 6
+GRANT = 50
 LANES = 128
 EXTRA = 8
 
@@ -44,6 +46,14 @@
 
 def exchange(parts, axis):
     return lax.all_to_all(parts, axis, split_axis=0, concat_axis=0, tiled=True)
+
+
+def gather_same_core(parts):
+    owners = lax.axis_size("row")
+    groups = [list(range(core, owners, 2)) for core in range(2)]
+    same = lax.all_to_all(parts, "row", 0, 0, axis_index_groups=groups, tiled=True)
+    other = lax.ppermute(same, "row", [(i, i ^ 1) for i in range(owners)])
+    return same, other
 
 
 def from_behind(value, axis, distance):
@@ -100,25 +110,42 @@
     coef_ref[...] = SHIFT - shift_ref[:, pl.ds(pl.multiple_of(group * edge, edge), edge)]
 
 
-def fetches(tiles_ref, held, sems):
-    per_chunk = held.shape[0] // CHUNKS
-    return [
+def load_kernel(tiles_ref, out_ref, sem):
+    copy = pltpu.make_async_copy(tiles_ref.at[0, 0, pl.ds(0, out_ref.shape[0])], out_ref, sem)
+    copy.start()
+    copy.wait()
+
+
+def fetch(tiles_ref, rest, sems):
+    per_chunk = rest.shape[0] // CHUNKS
+    copies = [
         pltpu.make_async_copy(
-            tiles_ref.at[0, 0, pl.ds(c * per_chunk, per_chunk)],
-            held.at[pl.ds(c * per_chunk, per_chunk)],
+            tiles_ref.at[0, 0, pl.ds(KEEP + c * per_chunk, per_chunk)],
+            rest.at[pl.ds(c * per_chunk, per_chunk)],
             sems.at[c],
         )
         for c in range(CHUNKS)
     ]
-
-
-def back_kernel(groups, steps, rows_ref, cols_ref, live_ref, tiles_ref, *refs):
+    for copy in copies:
+        copy.start()
+    return copies
+
+
+def each_tile(kept_ref, rest, copies):
+    per_chunk = rest.shape[0] // CHUNKS
+    for k in range(KEEP):
+        yield k, kept_ref[k]
+    for c in range(CHUNKS):
+        copies[c].wait()
+        for k in range(c * per_chunk, (c + 1) * per_chunk):
+            yield KEEP + k, rest[k]
+
+
+def back_kernel(groups, steps, rows_ref, cols_ref, live_ref, kept_ref, tiles_ref, *refs):
     count = steps + 1
     vectors = [refs[i * groups : (i + 1) * groups] for i in range(count)]
-    out_ref, held, total, rounded, sems = refs[count * groups :]
-    copies = fetches(tiles_ref, held, sems)
-    for copy in copies:
-        copy.start()
+    out_ref, total, rounded, rest, sems = refs[count * groups :]
+    copies = fetch(tiles_ref, rest, sems)
     owners, width, _ = total.shape
     group = lax.axis_index("grp")
     live = live_ref[0, 0]
@@ -137,41 +164,37 @@
     for r in range(owners):
         value = stacked(high[r : r + 1], middle[r : r + 1], low[r : r + 1])
         out_ref[r, pl.ds(2 * width, EXTRA), :] = value.astype(BF16)
-    per_chunk = held.shape[0] // CHUNKS
-    for c in range(CHUNKS):
-        copies[c].wait()
-        for k in range(c * per_chunk, (c + 1) * per_chunk):
-            source = lax.rem(group - rows_ref[0, 0, k] + groups, groups)
-            product = lax.dot_general(
-                rounded[source], held[k], (((1,), (0,)), ((), ())), preferred_element_type=F32
-            )
-            total[cols_ref[0, 0, k]] += jnp.where(k < live, product, jnp.zeros_like(product))
+    for k, tile in each_tile(kept_ref, rest, copies):
+        source = lax.rem(group - rows_ref[0, 0, k] + groups, groups)
+        product = lax.dot_general(
+            rounded[source], tile, (((1,), (0,)), ((), ())), preferred_element_type=F32
+        )
+        total[cols_ref[0, 0, k]] += jnp.where(k < live, product, jnp.zeros_like(product))
     for r in range(owners):
         out_ref[r, pl.ds(0, 2 * width), :] = halves(total[r]).astype(BF16)
 
 
-def ahead_kernel(groups, rows_ref, cols_ref, live_ref, tiles_ref, columns_ref, *refs):
-    outs = refs[:groups]
-    held, total, sems = refs[groups:]
-    copies = fetches(tiles_ref, held, sems)
-    for copy in copies:
-        copy.start()
+def ahead_kernel(
+    groups, rows_ref, cols_ref, live_ref, kept_ref, tiles_ref, same_ref, other_ref, *refs
+):
+    outs, (total, rest, sems) = refs[:groups], refs[groups:]
+    copies = fetch(tiles_ref, rest, sems)
     width = total.shape[1]
     group = lax.axis_index("grp")
+    core = lax.rem(lax.axis_index("row"), 2)
     live = live_ref[0, 0]
     total[...] = jnp.zeros_like(total)
-    per_chunk = held.shape[0] // CHUNKS
-    for c in range(CHUNKS):
-        copies[c].wait()
-        for k in range(c * per_chunk, (c + 1) * per_chunk):
-            target = lax.rem(rows_ref[0, 0, k] - group + groups, groups)
-            product = lax.dot_general(
-                whole(columns_ref, cols_ref[0, 0, k], width),
-                held[k],
-                (((1,), (1,)), ((), ())),
-                preferred_element_type=F32,
-            )
-            total[target] += jnp.where(k < live, product, jnp.zeros_like(product))
+    for k, tile in each_tile(kept_ref, rest, copies):
+        target = lax.rem(rows_ref[0, 0, k] - group + groups, groups)
+        col = cols_ref[0, 0, k]
+        place = lax.div(col, 2)
+        vectors = jnp.where(
+            lax.rem(col, 2) == core, whole(same_ref, place, width), whole(other_ref, place, width)
+        )
+        product = lax.dot_general(
+            vectors, tile, (((1,), (1,)), ((), ())), preferred_element_type=F32
+        )
+        total[target] += jnp.where(k < live, product, jnp.zeros_like(product))
     for s in range(groups):
         outs[s][...] = total[s].astype(outs[s].dtype)
 
@@ -198,7 +221,7 @@
     else:
         rounded = halves(new).astype(BF16)
         extra = stacked(*pieces(row)).astype(BF16)
-        for r in range(owners):
+        for r in range(outs[1].shape[0]):
             outs[1][r, pl.ds(0, 2 * width), :] = rounded
             outs[1][r, pl.ds(2 * width, EXTRA), :] = extra
 
@@ -257,17 +280,20 @@
     )
 
 
-def block_kernel(j, columns_ref, *refs):
+def block_kernel(j, same_ref, other_ref, *refs):
     olds, (low_ref, inv_ref) = refs[:-2], refs[-2:]
-    owners = columns_ref.shape[0]
+    pairs = same_ref.shape[0]
     width = low_ref.shape[0] // (ITERS + 1)
+    core = lax.rem(lax.axis_index("row"), 2)
     if j > 0:
         low_ref[...] = olds[0][...]
         inv_ref[...] = olds[1][...]
     rows = []
-    for r in range(owners):
-        three = columns_ref[r, pl.ds(2 * width, EXTRA), :].astype(F32)
-        rows.append(three[0:1] + (three[1:2] + three[2:3]))
+    for r in range(pairs):
+        mine = same_ref[r, pl.ds(2 * width, EXTRA), :].astype(F32)
+        theirs = other_ref[r, pl.ds(2 * width, EXTRA), :].astype(F32)
+        for three in (jnp.where(core == 0, mine, theirs), jnp.where(core == 0, theirs, mine)):
+            rows.append(three[0:1] + (three[1:2] + three[2:3]))
     next_rows(j, jnp.concatenate(rows, 0), low_ref, inv_ref)
 
 
@@ -327,60 +353,67 @@
     groups = lax.axis_size("grp")
     owners = lax.axis_size("row")
     total = (ITERS + 1) * width
-    tables = (tile_rows, tile_cols, live_tiles, tiles)
-    spaces = [SMEM, SMEM, SMEM, pltpu.HBM]
-    held = pltpu.VMEM((count, edge, edge), BF16)
+    (kept,) = call(
+        load_kernel,
+        [shape(KEEP, edge, edge, dtype=BF16)],
+        [pltpu.HBM],
+        (tiles,),
+        GRANT,
+        [pltpu.SemaphoreType.DMA],
+    )
+    tables = (tile_rows, tile_cols, live_tiles, kept, tiles)
+    spaces = [SMEM, SMEM, SMEM, VMEM, pltpu.HBM]
+    rest = [pltpu.VMEM((count - KEEP, edge, edge), BF16), pltpu.SemaphoreType.DMA((CHUNKS,))]
     flops = 2 * count * width * edge * edge
 
     *slots, sent, coef = call(
-        functools.partial(init_kernel, groups, owners),
-        [shape(width, edge)] * groups + [shape(owners, 2 * width, LANES, dtype=BF16), shape(1, edge)],
+        functools.partial(init_kernel, groups, owners // 2),
+        [shape(width, edge)] * groups + [shape(owners // 2, 2 * width, LANES, dtype=BF16), shape(1, edge)],
         [VMEM, VMEM],
         (start_block, dual_shift[None, :]),
         4,
     )
+    def block(j, gathered, state):
+        return call(
+            functools.partial(block_kernel, j),
+            [shape(total, total)] * 2,
+            [VMEM] * (2 + len(state)),
+            (*gathered, *state),
+            4,
+        )
+
     before = jnp.zeros((width, edge), F32)
     basis = [slots]
-    state = ()
+    state = gathered = ()
     for step in range(ITERS):
         own = basis[step][0]
-        columns = exchange(sent, "row")
+        same, other = gather_same_core(sent)
         flat = [slot for slots in basis for slot in slots]
         (parts,) = call(
             functools.partial(back_kernel, groups, step),
             [shape(owners, 2 * width + EXTRA, LANES, dtype=BF16)],
             spaces + [VMEM] * len(flat),
             (*tables, *flat),
-            50,
-            [
-                held,
-                pltpu.VMEM((owners, width, edge), F32),
-                pltpu.VMEM((groups, width, edge), BF16),
-                pltpu.SemaphoreType.DMA((CHUNKS,)),
-            ],
+            GRANT,
+            [pltpu.VMEM((owners, width, edge), F32), pltpu.VMEM((groups, width, edge), BF16), *rest],
             flops,
         )
         arrived = exchange(parts, "row")
         direct = call(
             functools.partial(ahead_kernel, groups),
             [shape(width, edge)] + [shape(width, edge, dtype=BF16)] * (groups - 1),
-            spaces + [VMEM],
-            (*tables, columns),
-            50,
-            [held, pltpu.VMEM((groups, width, edge), F32), pltpu.SemaphoreType.DMA((CHUNKS,))],
+            spaces + [VMEM, VMEM],
+            (*tables, same, other),
+            GRANT,
+            [pltpu.VMEM((groups, width, edge), F32), *rest],
             flops,
         )
         direct = [direct[0]] + [from_behind(direct[k], "grp", k) for k in range(1, groups)]
-        if step > 0:
-            state = call(
-                functools.partial(block_kernel, step - 1),
-                [shape(total, total)] * 2,
-                [VMEM] * (1 + len(state)),
-                (columns, *state),
-                4,
-            )
+        if step > 1:
+            state = block(step - 2, gathered, state)
+        gathered = (same, other)
         last = step == ITERS - 1
-        second = shape(EXTRA, LANES) if last else shape(owners, 2 * width + EXTRA, LANES, dtype=BF16)
+        second = shape(EXTRA, LANES) if last else shape(owners // 2, 2 * width + EXTRA, LANES, dtype=BF16)
         new, sent = call(
             functools.partial(combine_kernel, groups, last),
             [shape(width, edge), second],
@@ -391,6 +424,7 @@
         before = own
         basis.append([new] + [from_behind(new, "grp", k) for k in range(1, groups)])
 
+    state = block(ITERS - 2, gathered, state)
     flat = [slot for slots in basis for slot in slots]
     (parts,) = call(
         functools.partial(gram_kernel, groups),

time: 197 us -> 207 us (1.051)
  starting transfers between devices: 91.9 us -> 103 us
  waiting for transfers between devices: 45.7 us -> 37 us
  local copies, waits for them, and re-layouts: 2.9 us -> 8.8 us
    all_to_all x0 -> x4, starting transfers between devices: none -> 24.6 us  [gather_same_core(): lax.all_to_all(parts, 'row', 0, 0, axis_index_groups=groups, tiled=True)]
    all_to_all x9 -> x5, waiting for transfers between devices: 24.3 us -> 9.11 us  [exchange(): return lax.all_to_all(parts, axis, split_axis=0, concat_axis=0, tiled=True)]
    all_to_all x9 -> x5, starting transfers between devices: 63 us -> 49.6 us  [exchange(): return lax.all_to_all(parts, axis, split_axis=0, concat_axis=0, tiled=True)]
    unnamed x12 -> x36, local copies, waits for them, and re-layouts: 2.9 us -> 8.8 us
    ppermute x0 -> x4, waiting for transfers between devices: none -> 5.34 us  [gather_same_core(): other = lax.ppermute(same, 'row', [(i, i ^ 1) for i in range(owners)])]
    pallas_call x18 -> x19, Pallas kernels: 53.6 us -> 54.9 us  [call(): pl.pallas_call(kernel, out_shape=out_shape, in_specs=[spec(space) for spa...]
  transfers between devices with their start and end apart: 33 -> 37, of which waited for: 29 -> 30; matrix products, arithmetic and copies ran while one was open for 0% -> 0% of each run, Pallas kernels for 20% -> 20%
where the time goes in v4:
time: 207 us; the launch traced here: 205 us
  starting transfers between devices  103 us (50%)
  Pallas kernels  54.9 us (27%)
  waiting for transfers between devices  37 us (18%)
  local copies, waits for them, and re-layouts  8.8 us (4%)
    pallas_call x19, Pallas kernels, call(): pl.pallas_call(kernel, out_shape=out_shape, in_specs=[spec(space) for spa...  54.9 us
    all_to_all x5, starting transfers between devices, exchange(): return lax.all_to_all(parts, axis, split_axis=0, concat_axis=0, tiled=True)  49.6 us
    ppermute x24, starting transfers between devices, from_behind(): lax.ppermute(value, axis, [(i, (i + distance) % size) for i in range(size)])  27.8 us
    all_to_all x4, starting transfers between devices, gather_same_core(): lax.all_to_all(parts, 'row', 0, 0, axis_index_groups=groups, tiled=True)  24.6 us
    ppermute x24, waiting for transfers between devices, from_behind(): lax.ppermute(value, axis, [(i, (i + distance) % size) for i in range(size)])  20.9 us
    all_to_all x5, waiting for transfers between devices, exchange(): return lax.all_to_all(parts, axis, split_axis=0, concat_axis=0, tiled=True)  9.11 us
    unnamed x36, local copies, waits for them, and re-layouts  8.8 us
    ppermute x4, waiting for transfers between devices, gather_same_core(): other = lax.ppermute(same, 'row', [(i, i ^ 1) for i in range(owners)])  5.34 us
  transfers between devices with their start and end apart: 37, of which 30 were waited for; matrix products, arithmetic and copies ran while one was open for 0% of the time, Pallas kernels for 20%

profile of v4, /device:TPU:1, one launch (start us, length us, event | category | flops | bytes accessed | tf_op | source)
XLA Modules:
  0.0 205.5 jit_solution(2067198846251789829)
XLA Ops:
  3.0 8.4 %all-to-all-start.1 = ((bf16[16,64,128]{2,1,0:T(8,128)(2,1)}), bf16[16,64,128]{2,1,0:T(8,128)(2,1)S(1)}, u32[]{:S(2)}, u32[]{:S(2)}) async-start(bf16[16,64,128]{2,1,0:T(8,128)(2,1)} %get-tuple-element.43), calls=%async_computation.1 | async-start | bytes 524288 | tf_op jit(solution)/shard_map/all_to_all | solution.py:54
  13.3 4.0 %shard_map.87 = bf16[32,72,128]{2,1,0:T(8,128)(2,1)} custom-call(s32[1,1,32]{2,1,0:T(1,128)S(1)} %copy-done.15, s32[1,1,32]{2,1,0:T(1,128)S(1)} %copy-done.16, s32[1,1]{1,0:T(1,128)S(6)} %copy.9.live_ref, bf16[8,256,256]{2,1,0:T(8,128)(2,1)S(1)} %shard_map.85.kept_ref, bf16[1,1,32,256,256]{4,3,2,1,0:T(8,128)(2,1)} %tiles_ref.17, ...), custom_call_target="tpu_custom_call" | custom-call | flops 134217728 | bytes 1048576 | tf_op jit(solution)/shard_map/pallas_call | solution.py:32
  19.0 6.6 %all-to-all-start = ((bf16[32,72,128]{2,1,0:T(8,128)(2,1)}), bf16[32,72,128]{2,1,0:T(8,128)(2,1)S(1)}, u32[]{:S(2)}, u32[]{:S(2)}) async-start(bf16[32,72,128]{2,1,0:T(8,128)(2,1)} %shard_map.87), calls=%async_computation | async-start | bytes 1179648 | tf_op jit(solution)/shard_map/all_to_all | solution.py:48
  27.2 3.6 %shard_map.88 = (f32[32,256]{1,0:T(8,128)S(1)}, bf16[32,256]{1,0:T(8,128)(2,1)S(1)}, bf16[32,256]{1,0:T(8,128)(2,1)S(1)}, bf16[32,256]{1,0:T(8,128)(2,1)S(1)}) custom-call(s32[1,1,32]{2,1,0:T(1,128)S(1)} %copy-done.15, s32[1,1,32]{2,1,0:T(1,128)S(1)} %copy-done.16, s32[1,1]{1,0:T(1,128)S(6)} %copy.9.live_ref, bf16[8,256,256]{2,1,0:T(8,128)(2,1)S(1)} %shard_map.85.kept_ref, ...), custom_call_target="tpu_custom_call" | custom-call | flops 134217728 | bytes 1048576 | tf_op jit(solution)/shard_map/pallas_call | solution.py:32
  38.6 6.7 %all-to-all-start.3 = ((bf16[16,72,128]{2,1,0:T(8,128)(2,1)}), bf16[16,72,128]{2,1,0:T(8,128)(2,1)S(1)}, u32[]{:S(2)}, u32[]{:S(2)}) async-start(bf16[16,72,128]{2,1,0:T(8,128)(2,1)} %get-tuple-element.50), calls=%async_computation.3 | async-start | bytes 589824 | tf_op jit(solution)/shard_map/all_to_all | solution.py:54
  48.3 3.3 %collective-permute-done.5.refs_6_ = f32[32,256]{1,0:T(8,128)S(1)} collective-permute-done((f32[32,256]{1,0:T(8,128)S(1)}, f32[32,256]{1,0:T(8,128)S(1)}, u32[]{:S(2)}, u32[]{:S(2)}) %collective-permute-start.5) | collective-permute-done | bytes 32800 | tf_op jit(solution)/shard_map/ppermute | solution.py:61
  51.6 4.0 %shard_map.90 = bf16[32,72,128]{2,1,0:T(8,128)(2,1)} custom-call(s32[1,1,32]{2,1,0:T(1,128)S(1)} %copy-done.15, s32[1,1,32]{2,1,0:T(1,128)S(1)} %copy-done.16, s32[1,1]{1,0:T(1,128)S(6)} %copy.9.live_ref, bf16[8,256,256]{2,1,0:T(8,128)(2,1)S(1)} %shard_map.85.kept_ref, bf16[1,1,32,256,256]{4,3,2,1,0:T(8,128)(2,1)} %tiles_ref.17, ...), custom_call_target="tpu_custom_call" | custom-call | flops 134217728 | bytes 1048576 | tf_op jit(solution)/shard_map/pallas_call | solution.py:32
  55.7 11.0 %all-to-all-start.2 = ((bf16[32,72,128]{2,1,0:T(8,128)(2,1)}), bf16[32,72,128]{2,1,0:T(8,128)(2,1)S(1)}, u32[]{:S(2)}, u32[]{:S(2)}) async-start(bf16[32,72,128]{2,1,0:T(8,128)(2,1)} %shard_map.90), calls=%async_computation.2 | async-start | bytes 1179648 | tf_op jit(solution)/shard_map/all_to_all | solution.py:48
  68.4 3.6 %shard_map.91 = (f32[32,256]{1,0:T(8,128)S(1)}, bf16[32,256]{1,0:T(8,128)(2,1)S(1)}, bf16[32,256]{1,0:T(8,128)(2,1)S(1)}, bf16[32,256]{1,0:T(8,128)(2,1)S(1)}) custom-call(s32[1,1,32]{2,1,0:T(1,128)S(1)} %copy-done.15, s32[1,1,32]{2,1,0:T(1,128)S(1)} %copy-done.16, s32[1,1]{1,0:T(1,128)S(6)} %copy.9.live_ref, bf16[8,256,256]{2,1,0:T(8,128)(2,1)S(1)} %shard_map.85.kept_ref, ...), custom_call_target="tpu_custom_call" | custom-call | flops 134217728 | bytes 1048576 | tf_op jit(solution)/shard_map/pallas_call | solution.py:32
  79.7 4.8 %all-to-all-start.5 = ((bf16[16,72,128]{2,1,0:T(8,128)(2,1)}), bf16[16,72,128]{2,1,0:T(8,128)(2,1)S(1)}, u32[]{:S(2)}, u32[]{:S(2)}) async-start(bf16[16,72,128]{2,1,0:T(8,128)(2,1)} %get-tuple-element.56), calls=%async_computation.5 | async-start | bytes 589824 | tf_op jit(solution)/shard_map/all_to_all | solution.py:54
  88.6 3.5 %collective-permute-done.12.refs_10_ = f32[32,256]{1,0:T(8,128)S(1)} collective-permute-done((f32[32,256]{1,0:T(8,128)S(1)}, f32[32,256]{1,0:T(8,128)S(1)}, u32[]{:S(2)}, u32[]{:S(2)}) %collective-permute-start.12) | collective-permute-done | bytes 32800 | tf_op jit(solution)/shard_map/ppermute | solution.py:61
  92.1 4.3 %shard_map.93 = bf16[32,72,128]{2,1,0:T(8,128)(2,1)} custom-call(s32[1,1,32]{2,1,0:T(1,128)S(1)} %copy-done.15, s32[1,1,32]{2,1,0:T(1,128)S(1)} %copy-done.16, s32[1,1]{1,0:T(1,128)S(6)} %copy.9.live_ref, bf16[8,256,256]{2,1,0:T(8,128)(2,1)S(1)} %shard_map.85.kept_ref, bf16[1,1,32,256,256]{4,3,2,1,0:T(8,128)(2,1)} %tiles_ref.17, ...), custom_call_target="tpu_custom_call" | custom-call | flops 134217728 | bytes 1048576 | tf_op jit(solution)/shard_map/pallas_call | solution.py:32
  96.4 10.8 %all-to-all-start.4 = ((bf16[32,72,128]{2,1,0:T(8,128)(2,1)}), bf16[32,72,128]{2,1,0:T(8,128)(2,1)S(1)}, u32[]{:S(2)}, u32[]{:S(2)}) async-start(bf16[32,72,128]{2,1,0:T(8,128)(2,1)} %shard_map.93), calls=%async_computation.4 | async-start | bytes 1179648 | tf_op jit(solution)/shard_map/all_to_all | solution.py:48
  108.8 3.6 %shard_map.94 = (f32[32,256]{1,0:T(8,128)S(1)}, bf16[32,256]{1,0:T(8,128)(2,1)S(1)}, bf16[32,256]{1,0:T(8,128)(2,1)S(1)}, bf16[32,256]{1,0:T(8,128)(2,1)S(1)}) custom-call(s32[1,1,32]{2,1,0:T(1,128)S(1)} %copy-done.15, s32[1,1,32]{2,1,0:T(1,128)S(1)} %copy-done.16, s32[1,1]{1,0:T(1,128)S(6)} %copy.9.live_ref, bf16[8,256,256]{2,1,0:T(8,128)(2,1)S(1)} %shard_map.85.kept_ref, ...), custom_call_target="tpu_custom_call" | custom-call | flops 134217728 | bytes 1048576 | tf_op jit(solution)/shard_map/pallas_call | solution.py:32
  120.1 4.8 %all-to-all-start.7 = ((bf16[16,72,128]{2,1,0:T(8,128)(2,1)}), bf16[16,72,128]{2,1,0:T(8,128)(2,1)S(1)}, u32[]{:S(2)}, u32[]{:S(2)}) async-start(bf16[16,72,128]{2,1,0:T(8,128)(2,1)} %get-tuple-element.62), calls=%async_computation.7 | async-start | bytes 589824 | tf_op jit(solution)/shard_map/all_to_all | solution.py:54
  128.4 3.5 %collective-permute-done.19.refs_14_ = f32[32,256]{1,0:T(8,128)S(1)} collective-permute-done((f32[32,256]{1,0:T(8,128)S(1)}, f32[32,256]{1,0:T(8,128)S(1)}, u32[]{:S(2)}, u32[]{:S(2)}) %collective-permute-start.19) | collective-permute-done | bytes 32800 | tf_op jit(solution)/shard_map/ppermute | solution.py:61
  132.3 4.3 %shard_map.96 = bf16[32,72,128]{2,1,0:T(8,128)(2,1)} custom-call(s32[1,1,32]{2,1,0:T(1,128)S(1)} %copy-done.15, s32[1,1,32]{2,1,0:T(1,128)S(1)} %copy-done.16, s32[1,1]{1,0:T(1,128)S(6)} %copy.9.live_ref, bf16[8,256,256]{2,1,0:T(8,128)(2,1)S(1)} %shard_map.85.kept_ref, bf16[1,1,32,256,256]{4,3,2,1,0:T(8,128)(2,1)} %tiles_ref.17, ...), custom_call_target="tpu_custom_call" | custom-call | flops 134217728 | bytes 1048576 | tf_op jit(solution)/shard_map/pallas_call | solution.py:32
  138.5 10.7 %all-to-all-start.6 = ((bf16[32,72,128]{2,1,0:T(8,128)(2,1)}), bf16[32,72,128]{2,1,0:T(8,128)(2,1)S(1)}, u32[]{:S(2)}, u32[]{:S(2)}) async-start(bf16[32,72,128]{2,1,0:T(8,128)(2,1)} %shard_map.96), calls=%async_computation.6 | async-start | bytes 1179648 | tf_op jit(solution)/shard_map/all_to_all | solution.py:48
  150.8 3.6 %shard_map.97 = (f32[32,256]{1,0:T(8,128)S(1)}, bf16[32,256]{1,0:T(8,128)(2,1)S(1)}, bf16[32,256]{1,0:T(8,128)(2,1)S(1)}, bf16[32,256]{1,0:T(8,128)(2,1)S(1)}) custom-call(s32[1,1,32]{2,1,0:T(1,128)S(1)} %copy-done.15, s32[1,1,32]{2,1,0:T(1,128)S(1)} %copy-done.16, s32[1,1]{1,0:T(1,128)S(6)} %copy.9.live_ref, bf16[8,256,256]{2,1,0:T(8,128)(2,1)S(1)} %shard_map.85.kept_ref, ...), custom_call_target="tpu_custom_call" | custom-call | flops 134217728 | bytes 1048576 | tf_op jit(solution)/shard_map/pallas_call | solution.py:32
  171.9 10.5 %all-to-all-start.8 = ((f32[32,48,128]{2,1,0:T(8,128)}), f32[32,48,128]{2,1,0:T(8,128)S(1)}, u32[]{:S(2)}, u32[]{:S(2)}) async-start(f32[32,48,128]{2,1,0:T(8,128)} %shard_map.99), calls=%async_computation.8 | async-start | bytes 1572864 | tf_op jit(solution)/shard_map/all_to_all | solution.py:48
  186.0 3.4 %shard_map.101 = (f32[160,160]{1,0:T(8,128)S(1)}, f32[160,160]{1,0:T(8,128)S(1)}) custom-call(bf16[16,72,128]{2,1,0:T(8,128)(2,1)S(1)} %all-to-all-done.5.same_ref, bf16[16,72,128]{2,1,0:T(8,128)(2,1)S(1)} %collective-permute-done.14.other_ref, f32[160,160]{1,0:T(8,128)S(1)} %get-tuple-element.69.refs_0_, f32[160,160]{1,0:T(8,128)S(1)} %get-tuple-element.70.refs_1_), custom_call_target="tpu_custom_call" | custom-call | flops 2000000 | bytes 1048576 | tf_op jit(solution)/shard_map/pallas_call | solution.py:32
  189.4 3.4 %shard_map.102 = (f32[160,160]{1,0:T(8,128)S(1)}, f32[160,160]{1,0:T(8,128)S(1)}) custom-call(bf16[16,72,128]{2,1,0:T(8,128)(2,1)S(1)} %all-to-all-done.7.same_ref, bf16[16,72,128]{2,1,0:T(8,128)(2,1)S(1)} %collective-permute-done.21.other_ref, f32[160,160]{1,0:T(8,128)S(1)} %get-tuple-element.71.refs_0_, f32[160,160]{1,0:T(8,128)S(1)} %get-tuple-element.72.refs_1_), custom_call_target="tpu_custom_call" | custom-call | flops 2000000 | bytes 1048576 | tf_op jit(solution)/shard_map/pallas_call | solution.py:32
  192.8 3.9 %all-to-all-done.8.parts_ref = f32[32,48,128]{2,1,0:T(8,128)S(1)} async-done(((f32[32,48,128]{2,1,0:T(8,128)}), f32[32,48,128]{2,1,0:T(8,128)S(1)}, u32[]{:S(2)}, u32[]{:S(2)}) %all-to-all-start.8) | async-done | bytes 786464 | tf_op jit(solution)/shard_map/all_to_all | solution.py:48
  197.4 8.1 %shard_map.103 = (f32[4,32,128]{2,1,0:T(8,128)}, f32[4,32,32]{2,1,0:T(8,128)}, f32[32,1024]{1,0:T(8,128)}) custom-call(f32[32,48,128]{2,1,0:T(8,128)S(1)} %all-to-all-done.8.parts_ref, f32[160,160]{1,0:T(8,128)S(1)} %get-tuple-element.73.old_low, f32[160,160]{1,0:T(8,128)S(1)} %get-tuple-element.74.old_inv, ...), custom_call_target="tpu_custom_call" | custom-call | flops 2000000 | bytes 1048576 | tf_op jit(solution)/shard_map/pallas_call | solution.py:32
  (106 shorter events, 69.5 us)
Async XLA Ops:
  3.0 16.0 %all-to-all-start.1 = ((bf16[16,64,128]{2,1,0:T(8,128)(2,1)}), bf16[16,64,128]{2,1,0:T(8,128)(2,1)S(1)}, u32[]{:S(2)}, u32[]{:S(2)}) async-start(bf16[16,64,128]{2,1,0:T(8,128)(2,1)} %get-tuple-element.43), calls=%async_computation.1 | async-start | bytes 524288 | tf_op jit(solution)/shard_map/all_to_all | solution.py:54
  19.0 18.8 %all-to-all-start = ((bf16[32,72,128]{2,1,0:T(8,128)(2,1)}), bf16[32,72,128]{2,1,0:T(8,128)(2,1)S(1)}, u32[]{:S(2)}, u32[]{:S(2)}) async-start(bf16[32,72,128]{2,1,0:T(8,128)(2,1)} %shard_map.87), calls=%async_computation | async-start | bytes 1179648 | tf_op jit(solution)/shard_map/all_to_all | solution.py:48
  30.8 5.0 %collective-permute-start.1 = (bf16[32,256]{1,0:T(8,128)(2,1)S(1)}, bf16[32,256]{1,0:T(8,128)(2,1)S(1)}, u32[]{:S(2)}, u32[]{:S(2)}) collective-permute-start(bf16[32,256]{1,0:T(8,128)(2,1)S(1)} %get-tuple-element.45), channel_id=1, source_target_pairs={{0,32},{32,64},{64,96},{96,0},{1,33},{33,65},{65,97},{97,1},{2,34}... | collective-permute-start | bytes 49160 | tf_op jit(solution)/shard_map/ppermute | solution.py:61
  32.2 4.4 %collective-permute-start.2 = (bf16[32,256]{1,0:T(8,128)(2,1)S(1)}, bf16[32,256]{1,0:T(8,128)(2,1)S(1)}, u32[]{:S(2)}, u32[]{:S(2)}) collective-permute-start(bf16[32,256]{1,0:T(8,128)(2,1)S(1)} %get-tuple-element.46), channel_id=1, source_target_pairs={{0,64},{32,96},{64,0},{96,32},{1,65},{33,97},{65,1},{97,33},{2,66}... | collective-permute-start | bytes 49160 | tf_op jit(solution)/shard_map/ppermute | solution.py:61
  38.6 17.1 %all-to-all-start.3 = ((bf16[16,72,128]{2,1,0:T(8,128)(2,1)}), bf16[16,72,128]{2,1,0:T(8,128)(2,1)S(1)}, u32[]{:S(2)}, u32[]{:S(2)}) async-start(bf16[16,72,128]{2,1,0:T(8,128)(2,1)} %get-tuple-element.50), calls=%async_computation.3 | async-start | bytes 589824 | tf_op jit(solution)/shard_map/all_to_all | solution.py:54
  47.3 4.3 %collective-permute-start.5 = (f32[32,256]{1,0:T(8,128)S(1)}, f32[32,256]{1,0:T(8,128)S(1)}, u32[]{:S(2)}, u32[]{:S(2)}) collective-permute-start(f32[32,256]{1,0:T(8,128)S(1)} %get-tuple-element.49.refs_4_.refs_5_), channel_id=1, source_target_pairs={{0,64},{32,96},{64,0},{96,32},{1,65},{33,97},{65,1},{97,33},{2,66}... | collective-permute-start | bytes 98312 | tf_op jit(solution)/shard_map/ppermute | solution.py:61
  47.3 4.3 %collective-permute-start.4 = (f32[32,256]{1,0:T(8,128)S(1)}, f32[32,256]{1,0:T(8,128)S(1)}, u32[]{:S(2)}, u32[]{:S(2)}) collective-permute-start(f32[32,256]{1,0:T(8,128)S(1)} %get-tuple-element.49.refs_4_.refs_5_), channel_id=1, source_target_pairs={{0,32},{32,64},{64,96},{96,0},{1,33},{33,65},{65,97},{97,1},{2,34}... | collective-permute-start | bytes 98312 | tf_op jit(solution)/shard_map/ppermute | solution.py:61
  55.7 23.1 %all-to-all-start.2 = ((bf16[32,72,128]{2,1,0:T(8,128)(2,1)}), bf16[32,72,128]{2,1,0:T(8,128)(2,1)S(1)}, u32[]{:S(2)}, u32[]{:S(2)}) async-start(bf16[32,72,128]{2,1,0:T(8,128)(2,1)} %shard_map.90), calls=%async_computation.2 | async-start | bytes 1179648 | tf_op jit(solution)/shard_map/all_to_all | solution.py:48
  72.0 4.2 %collective-permute-start.8 = (bf16[32,256]{1,0:T(8,128)(2,1)S(1)}, bf16[32,256]{1,0:T(8,128)(2,1)S(1)}, u32[]{:S(2)}, u32[]{:S(2)}) collective-permute-start(bf16[32,256]{1,0:T(8,128)(2,1)S(1)} %get-tuple-element.52), channel_id=1, source_target_pairs={{0,32},{32,64},{64,96},{96,0},{1,33},{33,65},{65,97},{97,1},{2,34}... | collective-permute-start | bytes 49160 | tf_op jit(solution)/shard_map/ppermute | solution.py:61
  72.1 4.5 %collective-permute-start.9 = (bf16[32,256]{1,0:T(8,128)(2,1)S(1)}, bf16[32,256]{1,0:T(8,128)(2,1)S(1)}, u32[]{:S(2)}, u32[]{:S(2)}) collective-permute-start(bf16[32,256]{1,0:T(8,128)(2,1)S(1)} %get-tuple-element.53), channel_id=1, source_target_pairs={{0,64},{32,96},{64,0},{96,32},{1,65},{33,97},{65,1},{97,33},{2,66}... | collective-permute-start | bytes 49160 | tf_op jit(solution)/shard_map/ppermute | solution.py:61
  79.7 16.7 %all-to-all-start.5 = ((bf16[16,72,128]{2,1,0:T(8,128)(2,1)}), bf16[16,72,128]{2,1,0:T(8,128)(2,1)S(1)}, u32[]{:S(2)}, u32[]{:S(2)}) async-start(bf16[16,72,128]{2,1,0:T(8,128)(2,1)} %get-tuple-element.56), calls=%async_computation.5 | async-start | bytes 589824 | tf_op jit(solution)/shard_map/all_to_all | solution.py:54
  87.5 4.6 %collective-permute-start.12 = (f32[32,256]{1,0:T(8,128)S(1)}, f32[32,256]{1,0:T(8,128)S(1)}, u32[]{:S(2)}, u32[]{:S(2)}) collective-permute-start(f32[32,256]{1,0:T(8,128)S(1)} %get-tuple-element.55.refs_8_.refs_4_.refs_5_), channel_id=1, source_target_pairs={{0,64},{32,96},{64,0},{96,32},{1,65},{33,97},{65,1},{97,33},{2,66}... | collective-permute-start | bytes 98312 | tf_op jit(solution)/shard_map/ppermute | solution.py:61
  87.5 4.6 %collective-permute-start.11 = (f32[32,256]{1,0:T(8,128)S(1)}, f32[32,256]{1,0:T(8,128)S(1)}, u32[]{:S(2)}, u32[]{:S(2)}) collective-permute-start(f32[32,256]{1,0:T(8,128)S(1)} %get-tuple-element.55.refs_8_.refs_4_.refs_5_), channel_id=1, source_target_pairs={{0,32},{32,64},{64,96},{96,0},{1,33},{33,65},{65,97},{97,1},{2,34}... | collective-permute-start | bytes 98312 | tf_op jit(solution)/shard_map/ppermute | solution.py:61
  96.4 22.9 %all-to-all-start.4 = ((bf16[32,72,128]{2,1,0:T(8,128)(2,1)}), bf16[32,72,128]{2,1,0:T(8,128)(2,1)S(1)}, u32[]{:S(2)}, u32[]{:S(2)}) async-start(bf16[32,72,128]{2,1,0:T(8,128)(2,1)} %shard_map.93), calls=%async_computation.4 | async-start | bytes 1179648 | tf_op jit(solution)/shard_map/all_to_all | solution.py:48
  112.4 4.2 %collective-permute-start.15 = (bf16[32,256]{1,0:T(8,128)(2,1)S(1)}, bf16[32,256]{1,0:T(8,128)(2,1)S(1)}, u32[]{:S(2)}, u32[]{:S(2)}) collective-permute-start(bf16[32,256]{1,0:T(8,128)(2,1)S(1)} %get-tuple-element.58), channel_id=1, source_target_pairs={{0,32},{32,64},{64,96},{96,0},{1,33},{33,65},{65,97},{97,1},{2,34}... | collective-permute-start | bytes 49160 | tf_op jit(solution)/shard_map/ppermute | solution.py:61
  112.5 4.5 %collective-permute-start.16 = (bf16[32,256]{1,0:T(8,128)(2,1)S(1)}, bf16[32,256]{1,0:T(8,128)(2,1)S(1)}, u32[]{:S(2)}, u32[]{:S(2)}) collective-permute-start(bf16[32,256]{1,0:T(8,128)(2,1)S(1)} %get-tuple-element.59), channel_id=1, source_target_pairs={{0,64},{32,96},{64,0},{96,32},{1,65},{33,97},{65,1},{97,33},{2,66}... | collective-permute-start | bytes 49160 | tf_op jit(solution)/shard_map/ppermute | solution.py:61
  120.1 18.4 %all-to-all-start.7 = ((bf16[16,72,128]{2,1,0:T(8,128)(2,1)}), bf16[16,72,128]{2,1,0:T(8,128)(2,1)S(1)}, u32[]{:S(2)}, u32[]{:S(2)}) async-start(bf16[16,72,128]{2,1,0:T(8,128)(2,1)} %get-tuple-element.62), calls=%async_computation.7 | async-start | bytes 589824 | tf_op jit(solution)/shard_map/all_to_all | solution.py:54
  127.4 4.6 %collective-permute-start.19 = (f32[32,256]{1,0:T(8,128)S(1)}, f32[32,256]{1,0:T(8,128)S(1)}, u32[]{:S(2)}, u32[]{:S(2)}) collective-permute-start(f32[32,256]{1,0:T(8,128)S(1)} %get-tuple-element.61.refs_12_.refs_4_), channel_id=1, source_target_pairs={{0,64},{32,96},{64,0},{96,32},{1,65},{33,97},{65,1},{97,33},{2,66}... | collective-permute-start | bytes 98312 | tf_op jit(solution)/shard_map/ppermute | solution.py:61
  128.0 4.3 %collective-permute-start.18 = (f32[32,256]{1,0:T(8,128)S(1)}, f32[32,256]{1,0:T(8,128)S(1)}, u32[]{:S(2)}, u32[]{:S(2)}) collective-permute-start(f32[32,256]{1,0:T(8,128)S(1)} %get-tuple-element.61.refs_12_.refs_4_), channel_id=1, source_target_pairs={{0,32},{32,64},{64,96},{96,0},{1,33},{33,65},{65,97},{97,1},{2,34}... | collective-permute-start | bytes 98312 | tf_op jit(solution)/shard_map/ppermute | solution.py:61
  138.5 22.8 %all-to-all-start.6 = ((bf16[32,72,128]{2,1,0:T(8,128)(2,1)}), bf16[32,72,128]{2,1,0:T(8,128)(2,1)S(1)}, u32[]{:S(2)}, u32[]{:S(2)}) async-start(bf16[32,72,128]{2,1,0:T(8,128)(2,1)} %shard_map.96), calls=%async_computation.6 | async-start | bytes 1179648 | tf_op jit(solution)/shard_map/all_to_all | solution.py:48
  155.1 4.1 %collective-permute-start.22 = (bf16[32,256]{1,0:T(8,128)(2,1)S(1)}, bf16[32,256]{1,0:T(8,128)(2,1)S(1)}, u32[]{:S(2)}, u32[]{:S(2)}) collective-permute-start(bf16[32,256]{1,0:T(8,128)(2,1)S(1)} %get-tuple-element.64), channel_id=1, source_target_pairs={{0,32},{32,64},{64,96},{96,0},{1,33},{33,65},{65,97},{97,1},{2,34}... | collective-permute-start | bytes 49160 | tf_op jit(solution)/shard_map/ppermute | solution.py:61
  155.1 4.4 %collective-permute-start.23 = (bf16[32,256]{1,0:T(8,128)(2,1)S(1)}, bf16[32,256]{1,0:T(8,128)(2,1)S(1)}, u32[]{:S(2)}, u32[]{:S(2)}) collective-permute-start(bf16[32,256]{1,0:T(8,128)(2,1)S(1)} %get-tuple-element.65), channel_id=1, source_target_pairs={{0,64},{32,96},{64,0},{96,32},{1,65},{33,97},{65,1},{97,33},{2,66}... | collective-permute-start | bytes 49160 | tf_op jit(solution)/shard_map/ppermute | solution.py:61
  163.3 4.3 %collective-permute-start.26 = (f32[32,256]{1,0:T(8,128)S(1)}, f32[32,256]{1,0:T(8,128)S(1)}, u32[]{:S(2)}, u32[]{:S(2)}) collective-permute-start(f32[32,256]{1,0:T(8,128)S(1)} %get-tuple-element.68.refs_16_), channel_id=1, source_target_pairs={{0,64},{32,96},{64,0},{96,32},{1,65},{33,97},{65,1},{97,33},{2,66}... | collective-permute-start | bytes 98312 | tf_op jit(solution)/shard_map/ppermute | solution.py:61
  171.9 24.7 %all-to-all-start.8 = ((f32[32,48,128]{2,1,0:T(8,128)}), f32[32,48,128]{2,1,0:T(8,128)S(1)}, u32[]{:S(2)}, u32[]{:S(2)}) async-start(f32[32,48,128]{2,1,0:T(8,128)} %shard_map.99), calls=%async_computation.8 | async-start | bytes 1572864 | tf_op jit(solution)/shard_map/all_to_all | solution.py:48
  (31 other events, 172.0 us)

commit v5 on v4

--- a/solution.py
+++ b/solution.py
@@ -177,9 +177,9 @@
 def ahead_kernel(
     groups, rows_ref, cols_ref, live_ref, kept_ref, tiles_ref, same_ref, other_ref, *refs
 ):
-    outs, (total, rest, sems) = refs[:groups], refs[groups:]
+    outs, (total, rest, sems) = refs[:groups], refs[-3:]
     copies = fetch(tiles_ref, rest, sems)
-    width = total.shape[1]
+    width = outs[0].shape[0]
     group = lax.axis_index("grp")
     core = lax.rem(lax.axis_index("row"), 2)
     live = live_ref[0, 0]
@@ -192,11 +192,19 @@
             lax.rem(col, 2) == core, whole(same_ref, place, width), whole(other_ref, place, width)
         )
         product = lax.dot_general(
-            vectors, tile, (((1,), (1,)), ((), ())), preferred_element_type=F32
+            tile, vectors, (((1,), (1,)), ((), ())), preferred_element_type=F32
         )
         total[target] += jnp.where(k < live, product, jnp.zeros_like(product))
     for s in range(groups):
-        outs[s][...] = total[s].astype(outs[s].dtype)
+        outs[s][...] = total[s].T.astype(outs[s].dtype)
+    if same_ref.shape[1] > 2 * width:
+        rows = []
+        for r in range(same_ref.shape[0]):
+            mine = same_ref[r, pl.ds(2 * width, EXTRA), :].astype(F32)
+            theirs = other_ref[r, pl.ds(2 * width, EXTRA), :].astype(F32)
+            for three in (jnp.where(core == 0, mine, theirs), jnp.where(core == 0, theirs, mine)):
+                rows.append(three[0:1] + (three[1:2] + three[2:3]))
+        refs[groups][...] = jnp.concatenate(rows, 0)
 
 
 def combine_kernel(groups, last, back_ref, *refs):
@@ -280,21 +288,12 @@
     )
 
 
-def block_kernel(j, same_ref, other_ref, *refs):
+def block_kernel(j, gram_ref, *refs):
     olds, (low_ref, inv_ref) = refs[:-2], refs[-2:]
-    pairs = same_ref.shape[0]
-    width = low_ref.shape[0] // (ITERS + 1)
-    core = lax.rem(lax.axis_index("row"), 2)
     if j > 0:
         low_ref[...] = olds[0][...]
         inv_ref[...] = olds[1][...]
-    rows = []
-    for r in range(pairs):
-        mine = same_ref[r, pl.ds(2 * width, EXTRA), :].astype(F32)
-        theirs = other_ref[r, pl.ds(2 * width, EXTRA), :].astype(F32)
-        for three in (jnp.where(core == 0, mine, theirs), jnp.where(core == 0, theirs, mine)):
-            rows.append(three[0:1] + (three[1:2] + three[2:3]))
-    next_rows(j, jnp.concatenate(rows, 0), low_ref, inv_ref)
+    next_rows(j, gram_ref[...], low_ref, inv_ref)
 
 
 def gram_kernel(groups, chunk_ref, *refs):
@@ -373,18 +372,18 @@
         (start_block, dual_shift[None, :]),
         4,
     )
-    def block(j, gathered, state):
+    def block(j, rows, state):
         return call(
             functools.partial(block_kernel, j),
             [shape(total, total)] * 2,
-            [VMEM] * (2 + len(state)),
-            (*gathered, *state),
+            [VMEM] * (1 + len(state)),
+            (rows, *state),
             4,
         )
 
     before = jnp.zeros((width, edge), F32)
     basis = [slots]
-    state = gathered = ()
+    grams = []
     for step in range(ITERS):
         own = basis[step][0]
         same, other = gather_same_core(sent)
@@ -401,17 +400,17 @@
         arrived = exchange(parts, "row")
         direct = call(
             functools.partial(ahead_kernel, groups),
-            [shape(width, edge)] + [shape(width, edge, dtype=BF16)] * (groups - 1),
+            [shape(width, edge)]
+            + [shape(width, edge, dtype=BF16)] * (groups - 1)
+            + [shape(width, LANES)] * (step > 0),
             spaces + [VMEM, VMEM],
             (*tables, same, other),
             GRANT,
-            [pltpu.VMEM((groups, width, edge), F32), *rest],
+            [pltpu.VMEM((groups, edge, width), F32), *rest],
             flops,
         )
+        grams += direct[groups:]
         direct = [direct[0]] + [from_behind(direct[k], "grp", k) for k in range(1, groups)]
-        if step > 1:
-            state = block(step - 2, gathered, state)
-        gathered = (same, other)
         last = step == ITERS - 1
         second = shape(EXTRA, LANES) if last else shape(owners // 2, 2 * width + EXTRA, LANES, dtype=BF16)
         new, sent = call(
@@ -424,7 +423,6 @@
         before = own
         basis.append([new] + [from_behind(new, "grp", k) for k in range(1, groups)])
 
-    state = block(ITERS - 2, gathered, state)
     flat = [slot for slots in basis for slot in slots]
     (parts,) = call(
         functools.partial(gram_kernel, groups),
@@ -433,7 +431,10 @@
         (sent, *flat),
         6,
     )
+    state = ()
     parts = exchange(parts, "row")
+    for j, rows in enumerate(grams):
+        state = block(j, rows, state)
     return call(
         functools.partial(finish_kernel, groups),
         [shape(ITERS, width, ITERS * width), shape(ITERS, width, width), shape(width, row_count)],

time: 207 us -> 204 us (0.986)
  local copies, waits for them, and re-layouts: 8.8 us -> 1.61 us
  Pallas kernels: 54.9 us -> 57.8 us
    unnamed x36 -> x8, local copies, waits for them, and re-layouts: 8.8 us -> 1.6 us
    pallas_call x19, Pallas kernels: 54.9 us -> 57.8 us  [call(): pl.pallas_call(kernel, out_shape=out_shape, in_specs=[spec(space) for spa...]
  transfers between devices with their start and end apart: 37 -> 37, of which waited for: 30 -> 30; matrix products, arithmetic and copies ran while one was open for 0% -> 0% of each run, Pallas kernels for 20% -> 22%
where the time goes in v5:
time: 204 us; the launch traced here: 203 us
  starting transfers between devices  105 us (51%)
  Pallas kernels  57.8 us (28%)
  waiting for transfers between devices  36.6 us (18%)
    pallas_call x19, Pallas kernels, call(): pl.pallas_call(kernel, out_shape=out_shape, in_specs=[spec(space) for spa...  57.8 us
    all_to_all x5, starting transfers between devices, exchange(): return lax.all_to_all(parts, axis, split_axis=0, concat_axis=0, tiled=True)  49.5 us
    ppermute x24, starting transfers between devices, from_behind(): lax.ppermute(value, axis, [(i, (i + distance) % size) for i in range(size)])  27.7 us
    all_to_all x4, starting transfers between devices, gather_same_core(): lax.all_to_all(parts, 'row', 0, 0, axis_index_groups=groups, tiled=True)  26.3 us
    ppermute x24, waiting for transfers between devices, from_behind(): lax.ppermute(value, axis, [(i, (i + distance) % size) for i in range(size)])  21.4 us
    all_to_all x5, waiting for transfers between devices, exchange(): return lax.all_to_all(parts, axis, split_axis=0, concat_axis=0, tiled=True)  8.22 us
    ppermute x4, waiting for transfers between devices, gather_same_core(): other = lax.ppermute(same, 'row', [(i, i ^ 1) for i in range(owners)])  5.34 us
  transfers between devices with their start and end apart: 37, of which 30 were waited for; matrix products, arithmetic and copies ran while one was open for 0% of the time, Pallas kernels for 22%

profile of v5, /device:TPU:1, one launch (start us, length us, event | category | flops | bytes accessed | tf_op | source)
XLA Modules:
  0.0 202.6 jit_solution(8675924453355275095)
XLA Ops:
  3.0 8.4 %all-to-all-start.1 = ((bf16[16,64,128]{2,1,0:T(8,128)(2,1)}), bf16[16,64,128]{2,1,0:T(8,128)(2,1)S(1)}, u32[]{:S(2)}, u32[]{:S(2)}) async-start(bf16[16,64,128]{2,1,0:T(8,128)(2,1)} %get-tuple-element.46), calls=%async_computation.1 | async-start | bytes 524288 | tf_op jit(solution)/shard_map/all_to_all | solution.py:54
  13.3 4.0 %shard_map.87 = bf16[32,72,128]{2,1,0:T(8,128)(2,1)} custom-call(s32[1,1,32]{2,1,0:T(1,128)S(1)} %copy-done.1, s32[1,1,32]{2,1,0:T(1,128)S(1)} %copy-done.2, s32[1,1]{1,0:T(1,128)S(6)} %copy.9.live_ref, bf16[8,256,256]{2,1,0:T(8,128)(2,1)S(1)} %shard_map.85.kept_ref, bf16[1,1,32,256,256]{4,3,2,1,0:T(8,128)(2,1)} %tiles_ref.17, ...), custom_call_target="tpu_custom_call" | custom-call | flops 134217728 | bytes 1048576 | tf_op jit(solution)/shard_map/pallas_call | solution.py:32
  19.0 6.6 %all-to-all-start = ((bf16[32,72,128]{2,1,0:T(8,128)(2,1)}), bf16[32,72,128]{2,1,0:T(8,128)(2,1)S(1)}, u32[]{:S(2)}, u32[]{:S(2)}) async-start(bf16[32,72,128]{2,1,0:T(8,128)(2,1)} %shard_map.87), calls=%async_computation | async-start | bytes 1179648 | tf_op jit(solution)/shard_map/all_to_all | solution.py:48
  27.2 4.3 %shard_map.88 = (f32[32,256]{1,0:T(8,128)S(1)}, bf16[32,256]{1,0:T(8,128)(2,1)S(1)}, bf16[32,256]{1,0:T(8,128)(2,1)S(1)}, bf16[32,256]{1,0:T(8,128)(2,1)S(1)}) custom-call(s32[1,1,32]{2,1,0:T(1,128)S(1)} %copy-done.1, s32[1,1,32]{2,1,0:T(1,128)S(1)} %copy-done.2, s32[1,1]{1,0:T(1,128)S(6)} %copy.9.live_ref, bf16[8,256,256]{2,1,0:T(8,128)(2,1)S(1)} %shard_map.85.kept_ref, ...), custom_call_target="tpu_custom_call" | custom-call | flops 134217728 | bytes 1048576 | tf_op jit(solution)/shard_map/pallas_call | solution.py:32
  39.1 6.8 %all-to-all-start.3 = ((bf16[16,72,128]{2,1,0:T(8,128)(2,1)}), bf16[16,72,128]{2,1,0:T(8,128)(2,1)S(1)}, u32[]{:S(2)}, u32[]{:S(2)}) async-start(bf16[16,72,128]{2,1,0:T(8,128)(2,1)} %get-tuple-element.53), calls=%async_computation.3 | async-start | bytes 589824 | tf_op jit(solution)/shard_map/all_to_all | solution.py:54
  49.1 3.3 %collective-permute-done.5.refs_6_ = f32[32,256]{1,0:T(8,128)S(1)} collective-permute-done((f32[32,256]{1,0:T(8,128)S(1)}, f32[32,256]{1,0:T(8,128)S(1)}, u32[]{:S(2)}, u32[]{:S(2)}) %collective-permute-start.5) | collective-permute-done | bytes 32800 | tf_op jit(solution)/shard_map/ppermute | solution.py:61
  52.4 4.0 %shard_map.90 = bf16[32,72,128]{2,1,0:T(8,128)(2,1)} custom-call(s32[1,1,32]{2,1,0:T(1,128)S(1)} %copy-done.1, s32[1,1,32]{2,1,0:T(1,128)S(1)} %copy-done.2, s32[1,1]{1,0:T(1,128)S(6)} %copy.9.live_ref, bf16[8,256,256]{2,1,0:T(8,128)(2,1)S(1)} %shard_map.85.kept_ref, bf16[1,1,32,256,256]{4,3,2,1,0:T(8,128)(2,1)} %tiles_ref.17, ...), custom_call_target="tpu_custom_call" | custom-call | flops 134217728 | bytes 1048576 | tf_op jit(solution)/shard_map/pallas_call | solution.py:32
  56.4 11.0 %all-to-all-start.2 = ((bf16[32,72,128]{2,1,0:T(8,128)(2,1)}), bf16[32,72,128]{2,1,0:T(8,128)(2,1)S(1)}, u32[]{:S(2)}, u32[]{:S(2)}) async-start(bf16[32,72,128]{2,1,0:T(8,128)(2,1)} %shard_map.90), calls=%async_computation.2 | async-start | bytes 1179648 | tf_op jit(solution)/shard_map/all_to_all | solution.py:48
  69.1 4.4 %shard_map.91 = (f32[32,256]{1,0:T(8,128)S(1)}, bf16[32,256]{1,0:T(8,128)(2,1)S(1)}, bf16[32,256]{1,0:T(8,128)(2,1)S(1)}, bf16[32,256]{1,0:T(8,128)(2,1)S(1)}, f32[32,128]{1,0:T(8,128)S(1)}) custom-call(s32[1,1,32]{2,1,0:T(1,128)S(1)} %copy-done.1, s32[1,1,32]{2,1,0:T(1,128)S(1)} %copy-done.2, s32[1,1]{1,0:T(1,128)S(6)} %copy.9.live_ref, ...), custom_call_target="tpu_custom_call" | custom-call | flops 134217728 | bytes 1048576 | tf_op jit(solution)/shard_map/pallas_call | solution.py:32
  80.4 5.5 %all-to-all-start.5 = ((bf16[16,72,128]{2,1,0:T(8,128)(2,1)}), bf16[16,72,128]{2,1,0:T(8,128)(2,1)S(1)}, u32[]{:S(2)}, u32[]{:S(2)}) async-start(bf16[16,72,128]{2,1,0:T(8,128)(2,1)} %get-tuple-element.59), calls=%async_computation.5 | async-start | bytes 589824 | tf_op jit(solution)/shard_map/all_to_all | solution.py:54
  90.0 3.5 %collective-permute-done.12.refs_10_ = f32[32,256]{1,0:T(8,128)S(1)} collective-permute-done((f32[32,256]{1,0:T(8,128)S(1)}, f32[32,256]{1,0:T(8,128)S(1)}, u32[]{:S(2)}, u32[]{:S(2)}) %collective-permute-start.12) | collective-permute-done | bytes 32800 | tf_op jit(solution)/shard_map/ppermute | solution.py:61
  93.6 4.3 %shard_map.93 = bf16[32,72,128]{2,1,0:T(8,128)(2,1)} custom-call(s32[1,1,32]{2,1,0:T(1,128)S(1)} %copy-done.1, s32[1,1,32]{2,1,0:T(1,128)S(1)} %copy-done.2, s32[1,1]{1,0:T(1,128)S(6)} %copy.9.live_ref, bf16[8,256,256]{2,1,0:T(8,128)(2,1)S(1)} %shard_map.85.kept_ref, bf16[1,1,32,256,256]{4,3,2,1,0:T(8,128)(2,1)} %tiles_ref.17, ...), custom_call_target="tpu_custom_call" | custom-call | flops 134217728 | bytes 1048576 | tf_op jit(solution)/shard_map/pallas_call | solution.py:32
  97.9 10.7 %all-to-all-start.4 = ((bf16[32,72,128]{2,1,0:T(8,128)(2,1)}), bf16[32,72,128]{2,1,0:T(8,128)(2,1)S(1)}, u32[]{:S(2)}, u32[]{:S(2)}) async-start(bf16[32,72,128]{2,1,0:T(8,128)(2,1)} %shard_map.93), calls=%async_computation.4 | async-start | bytes 1179648 | tf_op jit(solution)/shard_map/all_to_all | solution.py:48
  110.3 4.4 %shard_map.94 = (f32[32,256]{1,0:T(8,128)S(1)}, bf16[32,256]{1,0:T(8,128)(2,1)S(1)}, bf16[32,256]{1,0:T(8,128)(2,1)S(1)}, bf16[32,256]{1,0:T(8,128)(2,1)S(1)}, f32[32,128]{1,0:T(8,128)S(1)}) custom-call(s32[1,1,32]{2,1,0:T(1,128)S(1)} %copy-done.1, s32[1,1,32]{2,1,0:T(1,128)S(1)} %copy-done.2, s32[1,1]{1,0:T(1,128)S(6)} %copy.9.live_ref, ...), custom_call_target="tpu_custom_call" | custom-call | flops 134217728 | bytes 1048576 | tf_op jit(solution)/shard_map/pallas_call | solution.py:32
  121.6 5.5 %all-to-all-start.7 = ((bf16[16,72,128]{2,1,0:T(8,128)(2,1)}), bf16[16,72,128]{2,1,0:T(8,128)(2,1)S(1)}, u32[]{:S(2)}, u32[]{:S(2)}) async-start(bf16[16,72,128]{2,1,0:T(8,128)(2,1)} %get-tuple-element.65), calls=%async_computation.7 | async-start | bytes 589824 | tf_op jit(solution)/shard_map/all_to_all | solution.py:54
  130.7 3.5 %collective-permute-done.19.refs_14_ = f32[32,256]{1,0:T(8,128)S(1)} collective-permute-done((f32[32,256]{1,0:T(8,128)S(1)}, f32[32,256]{1,0:T(8,128)S(1)}, u32[]{:S(2)}, u32[]{:S(2)}) %collective-permute-start.19) | collective-permute-done | bytes 32800 | tf_op jit(solution)/shard_map/ppermute | solution.py:61
  134.6 4.3 %shard_map.96 = bf16[32,72,128]{2,1,0:T(8,128)(2,1)} custom-call(s32[1,1,32]{2,1,0:T(1,128)S(1)} %copy-done.1, s32[1,1,32]{2,1,0:T(1,128)S(1)} %copy-done.2, s32[1,1]{1,0:T(1,128)S(6)} %copy.9.live_ref, bf16[8,256,256]{2,1,0:T(8,128)(2,1)S(1)} %shard_map.85.kept_ref, bf16[1,1,32,256,256]{4,3,2,1,0:T(8,128)(2,1)} %tiles_ref.17, ...), custom_call_target="tpu_custom_call" | custom-call | flops 134217728 | bytes 1048576 | tf_op jit(solution)/shard_map/pallas_call | solution.py:32
  138.9 10.7 %all-to-all-start.6 = ((bf16[32,72,128]{2,1,0:T(8,128)(2,1)}), bf16[32,72,128]{2,1,0:T(8,128)(2,1)S(1)}, u32[]{:S(2)}, u32[]{:S(2)}) async-start(bf16[32,72,128]{2,1,0:T(8,128)(2,1)} %shard_map.96), calls=%async_computation.6 | async-start | bytes 1179648 | tf_op jit(solution)/shard_map/all_to_all | solution.py:48
  151.5 4.4 %shard_map.97 = (f32[32,256]{1,0:T(8,128)S(1)}, bf16[32,256]{1,0:T(8,128)(2,1)S(1)}, bf16[32,256]{1,0:T(8,128)(2,1)S(1)}, bf16[32,256]{1,0:T(8,128)(2,1)S(1)}, f32[32,128]{1,0:T(8,128)S(1)}) custom-call(s32[1,1,32]{2,1,0:T(1,128)S(1)} %copy-done.1, s32[1,1,32]{2,1,0:T(1,128)S(1)} %copy-done.2, s32[1,1]{1,0:T(1,128)S(6)} %copy.9.live_ref, ...), custom_call_target="tpu_custom_call" | custom-call | flops 134217728 | bytes 1048576 | tf_op jit(solution)/shard_map/pallas_call | solution.py:32
  169.7 10.5 %all-to-all-start.8 = ((f32[32,48,128]{2,1,0:T(8,128)}), f32[32,48,128]{2,1,0:T(8,128)S(1)}, u32[]{:S(2)}, u32[]{:S(2)}) async-start(f32[32,48,128]{2,1,0:T(8,128)} %shard_map.99), calls=%async_computation.8 | async-start | bytes 1572864 | tf_op jit(solution)/shard_map/all_to_all | solution.py:48
  182.8 3.4 %shard_map.101 = (f32[160,160]{1,0:T(8,128)S(1)}, f32[160,160]{1,0:T(8,128)S(1)}) custom-call(f32[32,128]{1,0:T(8,128)S(1)} %get-tuple-element.73.gram_ref, f32[160,160]{1,0:T(8,128)S(1)} %get-tuple-element.75.refs_0_, f32[160,160]{1,0:T(8,128)S(1)} %get-tuple-element.76.refs_1_), custom_call_target="tpu_custom_call" | custom-call | flops 2000000 | bytes 1048576 | tf_op jit(solution)/shard_map/pallas_call | solution.py:32
  186.2 3.4 %shard_map.102 = (f32[160,160]{1,0:T(8,128)S(1)}, f32[160,160]{1,0:T(8,128)S(1)}) custom-call(f32[32,128]{1,0:T(8,128)S(1)} %get-tuple-element.72.gram_ref, f32[160,160]{1,0:T(8,128)S(1)} %get-tuple-element.77.refs_0_, f32[160,160]{1,0:T(8,128)S(1)} %get-tuple-element.78.refs_1_), custom_call_target="tpu_custom_call" | custom-call | flops 2000000 | bytes 1048576 | tf_op jit(solution)/shard_map/pallas_call | solution.py:32
  189.6 4.9 %all-to-all-done.8.parts_ref = f32[32,48,128]{2,1,0:T(8,128)S(1)} async-done(((f32[32,48,128]{2,1,0:T(8,128)}), f32[32,48,128]{2,1,0:T(8,128)S(1)}, u32[]{:S(2)}, u32[]{:S(2)}) %all-to-all-start.8) | async-done | bytes 786464 | tf_op jit(solution)/shard_map/all_to_all | solution.py:48
  194.5 8.1 %shard_map.103 = (f32[4,32,128]{2,1,0:T(8,128)}, f32[4,32,32]{2,1,0:T(8,128)}, f32[32,1024]{1,0:T(8,128)}) custom-call(f32[32,48,128]{2,1,0:T(8,128)S(1)} %all-to-all-done.8.parts_ref, f32[160,160]{1,0:T(8,128)S(1)} %get-tuple-element.79.old_low, f32[160,160]{1,0:T(8,128)S(1)} %get-tuple-element.80.old_inv, ...), custom_call_target="tpu_custom_call" | custom-call | flops 2000000 | bytes 1048576 | tf_op jit(solution)/shard_map/pallas_call | solution.py:32
  (78 shorter events, 61.0 us)
Async XLA Ops:
  3.0 16.0 %all-to-all-start.1 = ((bf16[16,64,128]{2,1,0:T(8,128)(2,1)}), bf16[16,64,128]{2,1,0:T(8,128)(2,1)S(1)}, u32[]{:S(2)}, u32[]{:S(2)}) async-start(bf16[16,64,128]{2,1,0:T(8,128)(2,1)} %get-tuple-element.46), calls=%async_computation.1 | async-start | bytes 524288 | tf_op jit(solution)/shard_map/all_to_all | solution.py:54
  19.0 19.3 %all-to-all-start = ((bf16[32,72,128]{2,1,0:T(8,128)(2,1)}), bf16[32,72,128]{2,1,0:T(8,128)(2,1)S(1)}, u32[]{:S(2)}, u32[]{:S(2)}) async-start(bf16[32,72,128]{2,1,0:T(8,128)(2,1)} %shard_map.87), calls=%async_computation | async-start | bytes 1179648 | tf_op jit(solution)/shard_map/all_to_all | solution.py:48
  31.5 5.0 %collective-permute-start.1 = (bf16[32,256]{1,0:T(8,128)(2,1)S(1)}, bf16[32,256]{1,0:T(8,128)(2,1)S(1)}, u32[]{:S(2)}, u32[]{:S(2)}) collective-permute-start(bf16[32,256]{1,0:T(8,128)(2,1)S(1)} %get-tuple-element.48), channel_id=1, source_target_pairs={{0,32},{32,64},{64,96},{96,0},{1,33},{33,65},{65,97},{97,1},{2,34}... | collective-permute-start | bytes 49160 | tf_op jit(solution)/shard_map/ppermute | solution.py:61
  32.9 4.4 %collective-permute-start.2 = (bf16[32,256]{1,0:T(8,128)(2,1)S(1)}, bf16[32,256]{1,0:T(8,128)(2,1)S(1)}, u32[]{:S(2)}, u32[]{:S(2)}) collective-permute-start(bf16[32,256]{1,0:T(8,128)(2,1)S(1)} %get-tuple-element.49), channel_id=1, source_target_pairs={{0,64},{32,96},{64,0},{96,32},{1,65},{33,97},{65,1},{97,33},{2,66}... | collective-permute-start | bytes 49160 | tf_op jit(solution)/shard_map/ppermute | solution.py:61
  39.1 17.3 %all-to-all-start.3 = ((bf16[16,72,128]{2,1,0:T(8,128)(2,1)}), bf16[16,72,128]{2,1,0:T(8,128)(2,1)S(1)}, u32[]{:S(2)}, u32[]{:S(2)}) async-start(bf16[16,72,128]{2,1,0:T(8,128)(2,1)} %get-tuple-element.53), calls=%async_computation.3 | async-start | bytes 589824 | tf_op jit(solution)/shard_map/all_to_all | solution.py:54
  48.0 4.3 %collective-permute-start.5 = (f32[32,256]{1,0:T(8,128)S(1)}, f32[32,256]{1,0:T(8,128)S(1)}, u32[]{:S(2)}, u32[]{:S(2)}) collective-permute-start(f32[32,256]{1,0:T(8,128)S(1)} %get-tuple-element.52.refs_4_.refs_5_), channel_id=1, source_target_pairs={{0,64},{32,96},{64,0},{96,32},{1,65},{33,97},{65,1},{97,33},{2,66}... | collective-permute-start | bytes 98312 | tf_op jit(solution)/shard_map/ppermute | solution.py:61
  48.0 4.3 %collective-permute-start.4 = (f32[32,256]{1,0:T(8,128)S(1)}, f32[32,256]{1,0:T(8,128)S(1)}, u32[]{:S(2)}, u32[]{:S(2)}) collective-permute-start(f32[32,256]{1,0:T(8,128)S(1)} %get-tuple-element.52.refs_4_.refs_5_), channel_id=1, source_target_pairs={{0,32},{32,64},{64,96},{96,0},{1,33},{33,65},{65,97},{97,1},{2,34}... | collective-permute-start | bytes 98312 | tf_op jit(solution)/shard_map/ppermute | solution.py:61
  56.4 23.1 %all-to-all-start.2 = ((bf16[32,72,128]{2,1,0:T(8,128)(2,1)}), bf16[32,72,128]{2,1,0:T(8,128)(2,1)S(1)}, u32[]{:S(2)}, u32[]{:S(2)}) async-start(bf16[32,72,128]{2,1,0:T(8,128)(2,1)} %shard_map.90), calls=%async_computation.2 | async-start | bytes 1179648 | tf_op jit(solution)/shard_map/all_to_all | solution.py:48
  73.5 4.2 %collective-permute-start.8 = (bf16[32,256]{1,0:T(8,128)(2,1)S(1)}, bf16[32,256]{1,0:T(8,128)(2,1)S(1)}, u32[]{:S(2)}, u32[]{:S(2)}) collective-permute-start(bf16[32,256]{1,0:T(8,128)(2,1)S(1)} %get-tuple-element.55), channel_id=1, source_target_pairs={{0,32},{32,64},{64,96},{96,0},{1,33},{33,65},{65,97},{97,1},{2,34}... | collective-permute-start | bytes 49160 | tf_op jit(solution)/shard_map/ppermute | solution.py:61
  73.5 4.6 %collective-permute-start.9 = (bf16[32,256]{1,0:T(8,128)(2,1)S(1)}, bf16[32,256]{1,0:T(8,128)(2,1)S(1)}, u32[]{:S(2)}, u32[]{:S(2)}) collective-permute-start(bf16[32,256]{1,0:T(8,128)(2,1)S(1)} %get-tuple-element.56), channel_id=1, source_target_pairs={{0,64},{32,96},{64,0},{96,32},{1,65},{33,97},{65,1},{97,33},{2,66}... | collective-permute-start | bytes 49160 | tf_op jit(solution)/shard_map/ppermute | solution.py:61
  80.4 17.5 %all-to-all-start.5 = ((bf16[16,72,128]{2,1,0:T(8,128)(2,1)}), bf16[16,72,128]{2,1,0:T(8,128)(2,1)S(1)}, u32[]{:S(2)}, u32[]{:S(2)}) async-start(bf16[16,72,128]{2,1,0:T(8,128)(2,1)} %get-tuple-element.59), calls=%async_computation.5 | async-start | bytes 589824 | tf_op jit(solution)/shard_map/all_to_all | solution.py:54
  89.0 4.6 %collective-permute-start.12 = (f32[32,256]{1,0:T(8,128)S(1)}, f32[32,256]{1,0:T(8,128)S(1)}, u32[]{:S(2)}, u32[]{:S(2)}) collective-permute-start(f32[32,256]{1,0:T(8,128)S(1)} %get-tuple-element.58.refs_8_.refs_4_.refs_5_), channel_id=1, source_target_pairs={{0,64},{32,96},{64,0},{96,32},{1,65},{33,97},{65,1},{97,33},{2,66}... | collective-permute-start | bytes 98312 | tf_op jit(solution)/shard_map/ppermute | solution.py:61
  89.0 4.6 %collective-permute-start.11 = (f32[32,256]{1,0:T(8,128)S(1)}, f32[32,256]{1,0:T(8,128)S(1)}, u32[]{:S(2)}, u32[]{:S(2)}) collective-permute-start(f32[32,256]{1,0:T(8,128)S(1)} %get-tuple-element.58.refs_8_.refs_4_.refs_5_), channel_id=1, source_target_pairs={{0,32},{32,64},{64,96},{96,0},{1,33},{33,65},{65,97},{97,1},{2,34}... | collective-permute-start | bytes 98312 | tf_op jit(solution)/shard_map/ppermute | solution.py:61
  97.9 22.9 %all-to-all-start.4 = ((bf16[32,72,128]{2,1,0:T(8,128)(2,1)}), bf16[32,72,128]{2,1,0:T(8,128)(2,1)S(1)}, u32[]{:S(2)}, u32[]{:S(2)}) async-start(bf16[32,72,128]{2,1,0:T(8,128)(2,1)} %shard_map.93), calls=%async_computation.4 | async-start | bytes 1179648 | tf_op jit(solution)/shard_map/all_to_all | solution.py:48
  114.7 4.2 %collective-permute-start.15 = (bf16[32,256]{1,0:T(8,128)(2,1)S(1)}, bf16[32,256]{1,0:T(8,128)(2,1)S(1)}, u32[]{:S(2)}, u32[]{:S(2)}) collective-permute-start(bf16[32,256]{1,0:T(8,128)(2,1)S(1)} %get-tuple-element.61), channel_id=1, source_target_pairs={{0,32},{32,64},{64,96},{96,0},{1,33},{33,65},{65,97},{97,1},{2,34}... | collective-permute-start | bytes 49160 | tf_op jit(solution)/shard_map/ppermute | solution.py:61
  114.7 4.5 %collective-permute-start.16 = (bf16[32,256]{1,0:T(8,128)(2,1)S(1)}, bf16[32,256]{1,0:T(8,128)(2,1)S(1)}, u32[]{:S(2)}, u32[]{:S(2)}) collective-permute-start(bf16[32,256]{1,0:T(8,128)(2,1)S(1)} %get-tuple-element.62), channel_id=1, source_target_pairs={{0,64},{32,96},{64,0},{96,32},{1,65},{33,97},{65,1},{97,33},{2,66}... | collective-permute-start | bytes 49160 | tf_op jit(solution)/shard_map/ppermute | solution.py:61
  121.6 17.3 %all-to-all-start.7 = ((bf16[16,72,128]{2,1,0:T(8,128)(2,1)}), bf16[16,72,128]{2,1,0:T(8,128)(2,1)S(1)}, u32[]{:S(2)}, u32[]{:S(2)}) async-start(bf16[16,72,128]{2,1,0:T(8,128)(2,1)} %get-tuple-element.65), calls=%async_computation.7 | async-start | bytes 589824 | tf_op jit(solution)/shard_map/all_to_all | solution.py:54
  129.6 4.6 %collective-permute-start.19 = (f32[32,256]{1,0:T(8,128)S(1)}, f32[32,256]{1,0:T(8,128)S(1)}, u32[]{:S(2)}, u32[]{:S(2)}) collective-permute-start(f32[32,256]{1,0:T(8,128)S(1)} %get-tuple-element.64.refs_12_.refs_4_), channel_id=1, source_target_pairs={{0,64},{32,96},{64,0},{96,32},{1,65},{33,97},{65,1},{97,33},{2,66}... | collective-permute-start | bytes 98312 | tf_op jit(solution)/shard_map/ppermute | solution.py:61
  130.3 4.3 %collective-permute-start.18 = (f32[32,256]{1,0:T(8,128)S(1)}, f32[32,256]{1,0:T(8,128)S(1)}, u32[]{:S(2)}, u32[]{:S(2)}) collective-permute-start(f32[32,256]{1,0:T(8,128)S(1)} %get-tuple-element.64.refs_12_.refs_4_), channel_id=1, source_target_pairs={{0,32},{32,64},{64,96},{96,0},{1,33},{33,65},{65,97},{97,1},{2,34}... | collective-permute-start | bytes 98312 | tf_op jit(solution)/shard_map/ppermute | solution.py:61
  138.9 22.8 %all-to-all-start.6 = ((bf16[32,72,128]{2,1,0:T(8,128)(2,1)}), bf16[32,72,128]{2,1,0:T(8,128)(2,1)S(1)}, u32[]{:S(2)}, u32[]{:S(2)}) async-start(bf16[32,72,128]{2,1,0:T(8,128)(2,1)} %shard_map.96), calls=%async_computation.6 | async-start | bytes 1179648 | tf_op jit(solution)/shard_map/all_to_all | solution.py:48
  155.9 4.2 %collective-permute-start.22 = (bf16[32,256]{1,0:T(8,128)(2,1)S(1)}, bf16[32,256]{1,0:T(8,128)(2,1)S(1)}, u32[]{:S(2)}, u32[]{:S(2)}) collective-permute-start(bf16[32,256]{1,0:T(8,128)(2,1)S(1)} %get-tuple-element.67), channel_id=1, source_target_pairs={{0,32},{32,64},{64,96},{96,0},{1,33},{33,65},{65,97},{97,1},{2,34}... | collective-permute-start | bytes 49160 | tf_op jit(solution)/shard_map/ppermute | solution.py:61
  156.0 4.5 %collective-permute-start.23 = (bf16[32,256]{1,0:T(8,128)(2,1)S(1)}, bf16[32,256]{1,0:T(8,128)(2,1)S(1)}, u32[]{:S(2)}, u32[]{:S(2)}) collective-permute-start(bf16[32,256]{1,0:T(8,128)(2,1)S(1)} %get-tuple-element.68), channel_id=1, source_target_pairs={{0,64},{32,96},{64,0},{96,32},{1,65},{33,97},{65,1},{97,33},{2,66}... | collective-permute-start | bytes 49160 | tf_op jit(solution)/shard_map/ppermute | solution.py:61
  163.4 4.3 %collective-permute-start.26 = (f32[32,256]{1,0:T(8,128)S(1)}, f32[32,256]{1,0:T(8,128)S(1)}, u32[]{:S(2)}, u32[]{:S(2)}) collective-permute-start(f32[32,256]{1,0:T(8,128)S(1)} %get-tuple-element.71.refs_16_), channel_id=1, source_target_pairs={{0,64},{32,96},{64,0},{96,32},{1,65},{33,97},{65,1},{97,33},{2,66}... | collective-permute-start | bytes 98312 | tf_op jit(solution)/shard_map/ppermute | solution.py:61
  169.7 24.8 %all-to-all-start.8 = ((f32[32,48,128]{2,1,0:T(8,128)}), f32[32,48,128]{2,1,0:T(8,128)S(1)}, u32[]{:S(2)}, u32[]{:S(2)}) async-start(f32[32,48,128]{2,1,0:T(8,128)} %shard_map.99), calls=%async_computation.8 | async-start | bytes 1572864 | tf_op jit(solution)/shard_map/all_to_all | solution.py:48
  (17 other events, 63.9 us)

commit v6 on v5

--- a/solution.py
+++ b/solution.py
@@ -11,9 +11,9 @@
 ITERS = 4
 SHIFT = 1.0625
 PULL = 0.375
-KEEP = 8
-CHUNKS = 6
-GRANT = 50
+KEEP = 20
+CHUNKS = 4
+GRANT = 52
 LANES = 128
 EXTRA = 8
 
@@ -48,17 +48,27 @@
     return lax.all_to_all(parts, axis, split_axis=0, concat_axis=0, tiled=True)
 
 
-def gather_same_core(parts):
+def same_core(parts):
     owners = lax.axis_size("row")
     groups = [list(range(core, owners, 2)) for core in range(2)]
-    same = lax.all_to_all(parts, "row", 0, 0, axis_index_groups=groups, tiled=True)
-    other = lax.ppermute(same, "row", [(i, i ^ 1) for i in range(owners)])
-    return same, other
-
-
-def from_behind(value, axis, distance):
-    size = lax.axis_size(axis)
-    return lax.ppermute(value, axis, [(i, (i + distance) % size) for i in range(size)])
+    return lax.all_to_all(parts, "row", 0, 0, axis_index_groups=groups, tiled=True)
+
+
+def swapped(value, axis, mask):
+    return lax.ppermute(value, axis, [(i, i ^ mask) for i in range(lax.axis_size(axis))])
+
+
+def all_slots(own):
+    one = swapped(own, "grp", 1)
+    three = swapped(own, "grp", 3)
+    two = swapped(one, "grp", 3)
+    return [own, one, two, three]
+
+
+def to_owners(parts):
+    two = swapped(parts[2], "grp", 2)
+    one, three = swapped(parts[1], "grp", 1), swapped(parts[3], "grp", 3)
+    return [parts[0], one, two, three]
 
 
 def dot(left, right, dims):
@@ -102,7 +112,7 @@
     edge = coef_ref.shape[1]
     group = lax.axis_index("grp")
     for s in range(groups):
-        block = lax.rem(group - s + groups, groups)
+        block = group ^ s
         slots[s][...] = start_ref[:, pl.ds(pl.multiple_of(block * edge, edge), edge)]
     rounded = halves(slots[0][...]).astype(BF16)
     for r in range(owners):
@@ -129,6 +139,12 @@
     for copy in copies:
         copy.start()
     return copies
+
+
+def clear(total):
+    @pl.loop(0, total.shape[0])
+    def _(i):
+        total[i] = jnp.zeros(total.shape[1:], F32)
 
 
 def each_tile(kept_ref, rest, copies):
@@ -149,9 +165,9 @@
     owners, width, _ = total.shape
     group = lax.axis_index("grp")
     live = live_ref[0, 0]
+    clear(total)
     for s in range(groups):
         rounded[s] = vectors[steps][s][...].astype(BF16)
-    total[...] = jnp.zeros_like(total)
     grams = []
     for i in range(count):
         value = across(vectors[steps][0][...], vectors[i][0][...])
@@ -165,7 +181,7 @@
         value = stacked(high[r : r + 1], middle[r : r + 1], low[r : r + 1])
         out_ref[r, pl.ds(2 * width, EXTRA), :] = value.astype(BF16)
     for k, tile in each_tile(kept_ref, rest, copies):
-        source = lax.rem(group - rows_ref[0, 0, k] + groups, groups)
+        source = rows_ref[0, 0, k] ^ group
         product = lax.dot_general(
             rounded[source], tile, (((1,), (0,)), ((), ())), preferred_element_type=F32
         )
@@ -181,22 +197,22 @@
     copies = fetch(tiles_ref, rest, sems)
     width = outs[0].shape[0]
     group = lax.axis_index("grp")
-    core = lax.rem(lax.axis_index("row"), 2)
+    core = lax.axis_index("row") & 1
     live = live_ref[0, 0]
-    total[...] = jnp.zeros_like(total)
+    clear(total)
     for k, tile in each_tile(kept_ref, rest, copies):
-        target = lax.rem(rows_ref[0, 0, k] - group + groups, groups)
+        target = rows_ref[0, 0, k] ^ group
         col = cols_ref[0, 0, k]
-        place = lax.div(col, 2)
+        place = col >> 1
         vectors = jnp.where(
-            lax.rem(col, 2) == core, whole(same_ref, place, width), whole(other_ref, place, width)
+            (col & 1) == core, whole(same_ref, place, width), whole(other_ref, place, width)
         )
         product = lax.dot_general(
-            tile, vectors, (((1,), (1,)), ((), ())), preferred_element_type=F32
+            vectors, tile, (((1,), (1,)), ((), ())), preferred_element_type=F32
         )
         total[target] += jnp.where(k < live, product, jnp.zeros_like(product))
     for s in range(groups):
-        outs[s][...] = total[s].T.astype(outs[s].dtype)
+        outs[s][...] = total[s].astype(outs[s].dtype)
     if same_ref.shape[1] > 2 * width:
         rows = []
         for r in range(same_ref.shape[0]):
@@ -242,14 +258,19 @@
         col_id == row_id + width, 1.0, 0.0
     )
     result = jnp.zeros_like(work)
-    for k in range(width):
-        row = work[k : k + 1, :]
-        scale = lax.rsqrt(row[:, k : k + 1])
-        row = row * scale
-        column = work[:, k : k + 1] * scale
-        result = jnp.where(row_id == k, jnp.broadcast_to(row, work.shape), result)
-        if k + 1 < width:
-            work = work - jnp.where(row_id > k, column, 0.0) * row
+    for k in range(0, width, 2):
+        first = jnp.broadcast_to(work[:, k : k + 1], work.shape)
+        second = jnp.broadcast_to(work[:, k + 1 : k + 2], work.shape)
+        scale = lax.rsqrt(first[k : k + 1])
+        link = first[k + 1 : k + 2] * scale
+        scale2 = lax.rsqrt(second[k + 1 : k + 2] - link * link)
+        row = work[k : k + 1] * scale
+        row2 = (work[k + 1 : k + 2] - link * row) * scale2
+        result = jnp.where(row_id == k, row, jnp.where(row_id == k + 1, row2, result))
+        if k + 2 < width:
+            column = first * scale
+            column2 = (second - column * link) * scale2
+            work = work - jnp.where(row_id > k + 1, column * row + column2 * row2, 0.0)
     return result[:, :width], result[:, width:]
 
 
@@ -299,7 +320,6 @@
 def gram_kernel(groups, chunk_ref, *refs):
     out_ref = refs[-1]
     vectors = [refs[i * groups : (i + 1) * groups] for i in range(ITERS + 1)]
-    owners = out_ref.shape[0]
     width = vectors[0][0].shape[0]
     grams = []
     for i in range(ITERS + 1):
@@ -310,11 +330,20 @@
     parts = LANES // width
     rows = width // parts
     packed = jnp.concatenate([grams[ITERS][p * rows : (p + 1) * rows] for p in range(parts)], 1)
-    value = jnp.concatenate(
+    out_ref[...] = jnp.concatenate(
         [jnp.concatenate(grams[:ITERS], 1), packed, jnp.broadcast_to(chunk_ref[0:1], (EXTRA, LANES))], 0
     )
-    for r in range(owners):
-        out_ref[r] = value
+
+
+def pair_kernel(mine_ref, theirs_ref, out_ref):
+    last = mine_ref.shape[0] - EXTRA
+    core = lax.axis_index("row") & 1
+    line = lax.broadcasted_iota(jnp.int32, (EXTRA, LANES), 0)
+    rows = jnp.where(line == core, mine_ref[pl.ds(last, EXTRA), :], theirs_ref[pl.ds(last, EXTRA), :])
+    value = mine_ref[pl.ds(0, last), :] + theirs_ref[pl.ds(0, last), :]
+    for r in range(out_ref.shape[0]):
+        out_ref[r, pl.ds(0, last), :] = value
+        out_ref[r, pl.ds(last, EXTRA), :] = rows
 
 
 def finish_kernel(groups, parts_ref, old_low, old_inv, *refs):
@@ -326,7 +355,7 @@
     low[...] = old_low[...]
     inv[...] = old_inv[...]
     last = parts_ref.shape[1] - EXTRA
-    rows = [parts_ref[r, pl.ds(last, EXTRA), :][0:1] for r in range(owners)]
+    rows = [parts_ref[r, pl.ds(last, EXTRA), :][0:2] for r in range(owners)]
     next_rows(ITERS - 1, jnp.concatenate(rows, 0), low, inv)
     sums = parts_ref[0, pl.ds(0, last), :]
     for r in range(1, owners):
@@ -342,7 +371,7 @@
             value = value + plain(
                 inv[pl.ds(ITERS * width, width), pl.ds(i * width, width)], vectors[i][s][...]
             )
-        block = lax.rem(group - s + groups, groups)
+        block = group ^ s
         out_ref[:, pl.ds(pl.multiple_of(block * edge, edge), edge)] = value
 
 
@@ -386,7 +415,8 @@
     grams = []
     for step in range(ITERS):
         own = basis[step][0]
-        same, other = gather_same_core(sent)
+        same = same_core(sent)
+        other = swapped(same, "row", 1)
         flat = [slot for slots in basis for slot in slots]
         (parts,) = call(
             functools.partial(back_kernel, groups, step),
@@ -406,11 +436,11 @@
             spaces + [VMEM, VMEM],
             (*tables, same, other),
             GRANT,
-            [pltpu.VMEM((groups, edge, width), F32), *rest],
+            [pltpu.VMEM((groups, width, edge), F32), *rest],
             flops,
         )
         grams += direct[groups:]
-        direct = [direct[0]] + [from_behind(direct[k], "grp", k) for k in range(1, groups)]
+        direct = to_owners(direct)
         last = step == ITERS - 1
         second = shape(EXTRA, LANES) if last else shape(owners // 2, 2 * width + EXTRA, LANES, dtype=BF16)
         new, sent = call(
@@ -421,18 +451,26 @@
             4,
         )
         before = own
-        basis.append([new] + [from_behind(new, "grp", k) for k in range(1, groups)])
+        basis.append(all_slots(new))
 
     flat = [slot for slots in basis for slot in slots]
-    (parts,) = call(
+    lines = width + width * width // LANES + EXTRA
+    (part,) = call(
         functools.partial(gram_kernel, groups),
-        [shape(owners, width + width * width // LANES + EXTRA, LANES)],
+        [shape(lines, LANES)],
         [VMEM] * (1 + len(flat)),
         (sent, *flat),
-        6,
+        4,
+    )
+    (parts,) = call(
+        pair_kernel,
+        [shape(owners // 2, lines, LANES)],
+        [VMEM, VMEM],
+        (part, swapped(part, "row", 1)),
+        4,
     )
     state = ()
-    parts = exchange(parts, "row")
+    parts = same_core(parts)
     for j, rows in enumerate(grams):
         state = block(j, rows, state)
     return call(

time: 204 us -> 206 us (level)
  waiting for transfers between devices: 36.6 us -> 42.3 us
  Pallas kernels: 57.8 us -> 53.5 us
    ppermute x28 -> x29, waiting for transfers between devices: 26.7 us -> 36.4 us  [swapped(): lax.ppermute(value, axis, [(i, i ^ mask) for i in range(lax.axis_size(axi...]
    all_to_all x4 -> x5, starting transfers between devices: 26.3 us -> 34 us  [same_core(): lax.all_to_all(parts, 'row', 0, 0, axis_index_groups=groups, tiled=True)]
    all_to_all x5 -> x4, starting transfers between devices: 49.5 us -> 42.1 us  [exchange(): return lax.all_to_all(parts, axis, split_axis=0, concat_axis=0, tiled=True)]
    all_to_all x5 -> x4, waiting for transfers between devices: 8.22 us -> 2.34 us  [exchange(): return lax.all_to_all(parts, axis, split_axis=0, concat_axis=0, tiled=True)]
    pallas_call x19 -> x20, Pallas kernels: 57.8 us -> 53.5 us  [call(): pl.pallas_call(kernel, out_shape=out_shape, in_specs=[spec(space) for spa...]
    ppermute x28 -> x29, starting transfers between devices: 29.2 us -> 29 us  [swapped(): lax.ppermute(value, axis, [(i, i ^ mask) for i in range(lax.axis_size(axi...]
  transfers between devices with their start and end apart: 37 -> 38, of which waited for: 30 -> 27; matrix products, arithmetic and copies ran while one was open for 0% -> 0% of each run, Pallas kernels for 22% -> 21%
where the time goes in v6:
time: 206 us; the launch traced here: 204 us
  starting transfers between devices  105 us (51%)
  Pallas kernels  53.5 us (26%)
  waiting for transfers between devices  42.3 us (21%)
    pallas_call x20, Pallas kernels, call(): pl.pallas_call(kernel, out_shape=out_shape, in_specs=[spec(space) for spa...  53.5 us
    all_to_all x4, starting transfers between devices, exchange(): return lax.all_to_all(parts, axis, split_axis=0, concat_axis=0, tiled=True)  42.1 us
    ppermute x29, waiting for transfers between devices, swapped(): lax.ppermute(value, axis, [(i, i ^ mask) for i in range(lax.axis_size(axi...  36.4 us
    all_to_all x5, starting transfers between devices, same_core(): lax.all_to_all(parts, 'row', 0, 0, axis_index_groups=groups, tiled=True)  34 us
    ppermute x29, starting transfers between devices, swapped(): lax.ppermute(value, axis, [(i, i ^ mask) for i in range(lax.axis_size(axi...  29 us
  transfers between devices with their start and end apart: 38, of which 27 were waited for; matrix products, arithmetic and copies ran while one was open for 0% of the time, Pallas kernels for 21%

profile of v6, /device:TPU:1, one launch (start us, length us, event | category | flops | bytes accessed | tf_op | source)
XLA Modules:
  0.0 204.0 jit_solution(8530009086240168847)
XLA Ops:
  3.0 8.4 %all-to-all-start.1 = ((bf16[16,64,128]{2,1,0:T(8,128)(2,1)}), bf16[16,64,128]{2,1,0:T(8,128)(2,1)S(1)}, u32[]{:S(2)}, u32[]{:S(2)}) async-start(bf16[16,64,128]{2,1,0:T(8,128)(2,1)} %get-tuple-element.46), calls=%async_computation.1 | async-start | bytes 524288 | tf_op jit(solution)/shard_map/all_to_all | solution.py:54
  12.1 3.2 %shard_map.85.kept_ref = bf16[20,256,256]{2,1,0:T(8,128)(2,1)} custom-call(bf16[1,1,32,256,256]{4,3,2,1,0:T(8,128)(2,1)} %tiles_ref.17), custom_call_target="tpu_custom_call" | custom-call | flops 2000000 | bytes 1048576 | tf_op jit(solution)/shard_map/pallas_call | solution.py:32
  15.3 4.5 %shard_map.87 = bf16[32,72,128]{2,1,0:T(8,128)(2,1)} custom-call(s32[1,1,32]{2,1,0:T(1,128)S(1)} %copy-done.1, s32[1,1,32]{2,1,0:T(1,128)S(1)} %copy-done.2, s32[1,1]{1,0:T(1,128)S(6)} %copy.9.live_ref, bf16[20,256,256]{2,1,0:T(8,128)(2,1)} %shard_map.85.kept_ref, bf16[1,1,32,256,256]{4,3,2,1,0:T(8,128)(2,1)} %tiles_ref.17, ...), custom_call_target="tpu_custom_call" | custom-call | flops 134217728 | bytes 1048576 | tf_op jit(solution)/shard_map/pallas_call | solution.py:32
  19.8 8.2 %all-to-all-start = ((bf16[32,72,128]{2,1,0:T(8,128)(2,1)}), bf16[32,72,128]{2,1,0:T(8,128)(2,1)S(1)}, u32[]{:S(2)}, u32[]{:S(2)}) async-start(bf16[32,72,128]{2,1,0:T(8,128)(2,1)} %shard_map.87), calls=%async_computation | async-start | bytes 1179648 | tf_op jit(solution)/shard_map/all_to_all | solution.py:48
  29.6 3.9 %shard_map.88 = (f32[32,256]{1,0:T(8,128)S(1)}, bf16[32,256]{1,0:T(8,128)(2,1)S(1)}, bf16[32,256]{1,0:T(8,128)(2,1)S(1)}, bf16[32,256]{1,0:T(8,128)(2,1)S(1)}) custom-call(s32[1,1,32]{2,1,0:T(1,128)S(1)} %copy-done.1, s32[1,1,32]{2,1,0:T(1,128)S(1)} %copy-done.2, s32[1,1]{1,0:T(1,128)S(6)} %copy.9.live_ref, bf16[20,256,256]{2,1,0:T(8,128)(2,1)} %shard_map.85.kept_ref, ...), custom_call_target="tpu_custom_call" | custom-call | flops 134217728 | bytes 1048576 | tf_op jit(solution)/shard_map/pallas_call | solution.py:32
  42.1 6.7 %all-to-all-start.3 = ((bf16[16,72,128]{2,1,0:T(8,128)(2,1)}), bf16[16,72,128]{2,1,0:T(8,128)(2,1)S(1)}, u32[]{:S(2)}, u32[]{:S(2)}) async-start(bf16[16,72,128]{2,1,0:T(8,128)(2,1)} %get-tuple-element.53), calls=%async_computation.3 | async-start | bytes 589824 | tf_op jit(solution)/shard_map/all_to_all | solution.py:54
  53.0 3.2 %collective-permute-done.5.refs_6_ = f32[32,256]{1,0:T(8,128)S(1)} collective-permute-done((f32[32,256]{1,0:T(8,128)S(1)}, f32[32,256]{1,0:T(8,128)S(1)}, u32[]{:S(2)}, u32[]{:S(2)}) %collective-permute-start.5) | collective-permute-done | bytes 32800 | tf_op jit(solution)/shard_map/ppermute | solution.py:58
  56.1 4.4 %shard_map.90 = bf16[32,72,128]{2,1,0:T(8,128)(2,1)} custom-call(s32[1,1,32]{2,1,0:T(1,128)S(1)} %copy-done.1, s32[1,1,32]{2,1,0:T(1,128)S(1)} %copy-done.2, s32[1,1]{1,0:T(1,128)S(6)} %copy.9.live_ref, bf16[20,256,256]{2,1,0:T(8,128)(2,1)} %shard_map.85.kept_ref, bf16[1,1,32,256,256]{4,3,2,1,0:T(8,128)(2,1)} %tiles_ref.17, ...), custom_call_target="tpu_custom_call" | custom-call | flops 134217728 | bytes 1048576 | tf_op jit(solution)/shard_map/pallas_call | solution.py:32
  60.6 11.4 %all-to-all-start.2 = ((bf16[32,72,128]{2,1,0:T(8,128)(2,1)}), bf16[32,72,128]{2,1,0:T(8,128)(2,1)S(1)}, u32[]{:S(2)}, u32[]{:S(2)}) async-start(bf16[32,72,128]{2,1,0:T(8,128)(2,1)} %shard_map.90), calls=%async_computation.2 | async-start | bytes 1179648 | tf_op jit(solution)/shard_map/all_to_all | solution.py:48
  73.6 3.9 %shard_map.91 = (f32[32,256]{1,0:T(8,128)S(1)}, bf16[32,256]{1,0:T(8,128)(2,1)S(1)}, bf16[32,256]{1,0:T(8,128)(2,1)S(1)}, bf16[32,256]{1,0:T(8,128)(2,1)S(1)}, f32[32,128]{1,0:T(8,128)S(1)}) custom-call(s32[1,1,32]{2,1,0:T(1,128)S(1)} %copy-done.1, s32[1,1,32]{2,1,0:T(1,128)S(1)} %copy-done.2, s32[1,1]{1,0:T(1,128)S(6)} %copy.9.live_ref, ...), custom_call_target="tpu_custom_call" | custom-call | flops 134217728 | bytes 1048576 | tf_op jit(solution)/shard_map/pallas_call | solution.py:32
  85.0 5.5 %all-to-all-start.5 = ((bf16[16,72,128]{2,1,0:T(8,128)(2,1)}), bf16[16,72,128]{2,1,0:T(8,128)(2,1)S(1)}, u32[]{:S(2)}, u32[]{:S(2)}) async-start(bf16[16,72,128]{2,1,0:T(8,128)(2,1)} %get-tuple-element.59), calls=%async_computation.5 | async-start | bytes 589824 | tf_op jit(solution)/shard_map/all_to_all | solution.py:54
  97.6 4.5 %shard_map.93 = bf16[32,72,128]{2,1,0:T(8,128)(2,1)} custom-call(s32[1,1,32]{2,1,0:T(1,128)S(1)} %copy-done.1, s32[1,1,32]{2,1,0:T(1,128)S(1)} %copy-done.2, s32[1,1]{1,0:T(1,128)S(6)} %copy.9.live_ref, bf16[20,256,256]{2,1,0:T(8,128)(2,1)} %shard_map.85.kept_ref, bf16[1,1,32,256,256]{4,3,2,1,0:T(8,128)(2,1)} %tiles_ref.17, ...), custom_call_target="tpu_custom_call" | custom-call | flops 134217728 | bytes 1048576 | tf_op jit(solution)/shard_map/pallas_call | solution.py:32
  102.1 11.1 %all-to-all-start.4 = ((bf16[32,72,128]{2,1,0:T(8,128)(2,1)}), bf16[32,72,128]{2,1,0:T(8,128)(2,1)S(1)}, u32[]{:S(2)}, u32[]{:S(2)}) async-start(bf16[32,72,128]{2,1,0:T(8,128)(2,1)} %shard_map.93), calls=%async_computation.4 | async-start | bytes 1179648 | tf_op jit(solution)/shard_map/all_to_all | solution.py:48
  115.1 3.9 %shard_map.94 = (f32[32,256]{1,0:T(8,128)S(1)}, bf16[32,256]{1,0:T(8,128)(2,1)S(1)}, bf16[32,256]{1,0:T(8,128)(2,1)S(1)}, bf16[32,256]{1,0:T(8,128)(2,1)S(1)}, f32[32,128]{1,0:T(8,128)S(1)}) custom-call(s32[1,1,32]{2,1,0:T(1,128)S(1)} %copy-done.1, s32[1,1,32]{2,1,0:T(1,128)S(1)} %copy-done.2, s32[1,1]{1,0:T(1,128)S(6)} %copy.9.live_ref, ...), custom_call_target="tpu_custom_call" | custom-call | flops 134217728 | bytes 1048576 | tf_op jit(solution)/shard_map/pallas_call | solution.py:32
  119.1 3.9 %collective-permute-start.16 = (bf16[32,256]{1,0:T(8,128)(2,1)S(1)}, bf16[32,256]{1,0:T(8,128)(2,1)S(1)}, u32[]{:S(2)}, u32[]{:S(2)}) collective-permute-start(bf16[32,256]{1,0:T(8,128)(2,1)S(1)} %get-tuple-element.62), channel_id=1, source_target_pairs={{0,64},{32,96},{64,0},{96,32},{1,65},{33,97},{65,1},{97,33},{2,66}... | collective-permute-start | bytes 49160 | tf_op jit(solution)/shard_map/ppermute | solution.py:58
  127.6 6.7 %all-to-all-start.7 = ((bf16[16,72,128]{2,1,0:T(8,128)(2,1)}), bf16[16,72,128]{2,1,0:T(8,128)(2,1)S(1)}, u32[]{:S(2)}, u32[]{:S(2)}) async-start(bf16[16,72,128]{2,1,0:T(8,128)(2,1)} %get-tuple-element.65), calls=%async_computation.7 | async-start | bytes 589824 | tf_op jit(solution)/shard_map/all_to_all | solution.py:54
  138.5 3.2 %collective-permute-done.19.refs_14_ = f32[32,256]{1,0:T(8,128)S(1)} collective-permute-done((f32[32,256]{1,0:T(8,128)S(1)}, f32[32,256]{1,0:T(8,128)S(1)}, u32[]{:S(2)}, u32[]{:S(2)}) %collective-permute-start.19) | collective-permute-done | bytes 32800 | tf_op jit(solution)/shard_map/ppermute | solution.py:58
  141.6 4.6 %shard_map.96 = bf16[32,72,128]{2,1,0:T(8,128)(2,1)} custom-call(s32[1,1,32]{2,1,0:T(1,128)S(1)} %copy-done.1, s32[1,1,32]{2,1,0:T(1,128)S(1)} %copy-done.2, s32[1,1]{1,0:T(1,128)S(6)} %copy.9.live_ref, bf16[20,256,256]{2,1,0:T(8,128)(2,1)} %shard_map.85.kept_ref, bf16[1,1,32,256,256]{4,3,2,1,0:T(8,128)(2,1)} %tiles_ref.17, ...), custom_call_target="tpu_custom_call" | custom-call | flops 134217728 | bytes 1048576 | tf_op jit(solution)/shard_map/pallas_call | solution.py:32
  146.3 11.4 %all-to-all-start.6 = ((bf16[32,72,128]{2,1,0:T(8,128)(2,1)}), bf16[32,72,128]{2,1,0:T(8,128)(2,1)S(1)}, u32[]{:S(2)}, u32[]{:S(2)}) async-start(bf16[32,72,128]{2,1,0:T(8,128)(2,1)} %shard_map.96), calls=%async_computation.6 | async-start | bytes 1179648 | tf_op jit(solution)/shard_map/all_to_all | solution.py:48
  159.3 3.9 %shard_map.97 = (f32[32,256]{1,0:T(8,128)S(1)}, bf16[32,256]{1,0:T(8,128)(2,1)S(1)}, bf16[32,256]{1,0:T(8,128)(2,1)S(1)}, bf16[32,256]{1,0:T(8,128)(2,1)S(1)}, f32[32,128]{1,0:T(8,128)S(1)}) custom-call(s32[1,1,32]{2,1,0:T(1,128)S(1)} %copy-done.1, s32[1,1,32]{2,1,0:T(1,128)S(1)} %copy-done.2, s32[1,1]{1,0:T(1,128)S(6)} %copy.9.live_ref, ...), custom_call_target="tpu_custom_call" | custom-call | flops 134217728 | bytes 1048576 | tf_op jit(solution)/shard_map/pallas_call | solution.py:32
  177.4 2.7 %collective-permute-start.28 = (f32[48,128]{1,0:T(8,128)S(1)}, f32[48,128]{1,0:T(8,128)S(1)}, u32[]{:S(2)}, u32[]{:S(2)}) collective-permute-start(f32[48,128]{1,0:T(8,128)S(1)} %shard_map.99.mine_ref), channel_id=1, source_target_pairs={{0,1},{1,0},{2,3},{3,2},{4,5},{5,4},{6,7},{7,6},{8,9},{9,8},{10,11... | collective-permute-start | bytes 73736 | tf_op jit(solution)/shard_map/ppermute | solution.py:58
  181.8 6.8 %all-to-all-start.8 = ((f32[16,48,128]{2,1,0:T(8,128)}), f32[16,48,128]{2,1,0:T(8,128)S(1)}, u32[]{:S(2)}, u32[]{:S(2)}) async-start(f32[16,48,128]{2,1,0:T(8,128)} %shard_map.100), calls=%async_computation.8 | async-start | bytes 786432 | tf_op jit(solution)/shard_map/all_to_all | solution.py:54
  194.6 3.5 %all-to-all-done.8.parts_ref = f32[16,48,128]{2,1,0:T(8,128)S(1)} async-done(((f32[16,48,128]{2,1,0:T(8,128)}), f32[16,48,128]{2,1,0:T(8,128)S(1)}, u32[]{:S(2)}, u32[]{:S(2)}) %all-to-all-start.8) | async-done | bytes 393248 | tf_op jit(solution)/shard_map/all_to_all | solution.py:54
  198.1 5.9 %shard_map.104 = (f32[4,32,128]{2,1,0:T(8,128)}, f32[4,32,32]{2,1,0:T(8,128)}, f32[32,1024]{1,0:T(8,128)}) custom-call(f32[16,48,128]{2,1,0:T(8,128)S(1)} %all-to-all-done.8.parts_ref, f32[160,160]{1,0:T(8,128)S(1)} %get-tuple-element.79.old_low, f32[160,160]{1,0:T(8,128)S(1)} %get-tuple-element.80.old_inv, ...), custom_call_target="tpu_custom_call" | custom-call | flops 2000000 | bytes 1048576 | tf_op jit(solution)/shard_map/pallas_call | solution.py:32
  (81 shorter events, 67.3 us)
Async XLA Ops:
  3.0 16.8 %all-to-all-start.1 = ((bf16[16,64,128]{2,1,0:T(8,128)(2,1)}), bf16[16,64,128]{2,1,0:T(8,128)(2,1)S(1)}, u32[]{:S(2)}, u32[]{:S(2)}) async-start(bf16[16,64,128]{2,1,0:T(8,128)(2,1)} %get-tuple-element.46), calls=%async_computation.1 | async-start | bytes 524288 | tf_op jit(solution)/shard_map/all_to_all | solution.py:54
  19.8 21.5 %all-to-all-start = ((bf16[32,72,128]{2,1,0:T(8,128)(2,1)}), bf16[32,72,128]{2,1,0:T(8,128)(2,1)S(1)}, u32[]{:S(2)}, u32[]{:S(2)}) async-start(bf16[32,72,128]{2,1,0:T(8,128)(2,1)} %shard_map.87), calls=%async_computation | async-start | bytes 1179648 | tf_op jit(solution)/shard_map/all_to_all | solution.py:48
  33.5 4.0 %collective-permute-start.1 = (bf16[32,256]{1,0:T(8,128)(2,1)S(1)}, bf16[32,256]{1,0:T(8,128)(2,1)S(1)}, u32[]{:S(2)}, u32[]{:S(2)}) collective-permute-start(bf16[32,256]{1,0:T(8,128)(2,1)S(1)} %get-tuple-element.48), channel_id=1, source_target_pairs={{0,32},{32,0},{64,96},{96,64},{1,33},{33,1},{65,97},{97,65},{2,34}... | collective-permute-start | bytes 49160 | tf_op jit(solution)/shard_map/ppermute | solution.py:58
  34.9 4.4 %collective-permute-start.2 = (bf16[32,256]{1,0:T(8,128)(2,1)S(1)}, bf16[32,256]{1,0:T(8,128)(2,1)S(1)}, u32[]{:S(2)}, u32[]{:S(2)}) collective-permute-start(bf16[32,256]{1,0:T(8,128)(2,1)S(1)} %get-tuple-element.49), channel_id=1, source_target_pairs={{0,64},{32,96},{64,0},{96,32},{1,65},{33,97},{65,1},{97,33},{2,66}... | collective-permute-start | bytes 49160 | tf_op jit(solution)/shard_map/ppermute | solution.py:58
  42.1 18.5 %all-to-all-start.3 = ((bf16[16,72,128]{2,1,0:T(8,128)(2,1)}), bf16[16,72,128]{2,1,0:T(8,128)(2,1)S(1)}, u32[]{:S(2)}, u32[]{:S(2)}) async-start(bf16[16,72,128]{2,1,0:T(8,128)(2,1)} %get-tuple-element.53), calls=%async_computation.3 | async-start | bytes 589824 | tf_op jit(solution)/shard_map/all_to_all | solution.py:54
  48.9 4.1 %collective-permute-start.6 = (f32[32,256]{1,0:T(8,128)S(1)}, f32[32,256]{1,0:T(8,128)S(1)}, u32[]{:S(2)}, u32[]{:S(2)}) collective-permute-start(f32[32,256]{1,0:T(8,128)S(1)} %get-tuple-element.52.refs_4_.refs_5_), channel_id=1, source_target_pairs={{0,96},{32,64},{64,32},{96,0},{1,97},{33,65},{65,33},{97,1},{2,98}... | collective-permute-start | bytes 98312 | tf_op jit(solution)/shard_map/ppermute | solution.py:58
  51.7 4.5 %collective-permute-start.5 = (f32[32,256]{1,0:T(8,128)S(1)}, f32[32,256]{1,0:T(8,128)S(1)}, u32[]{:S(2)}, u32[]{:S(2)}) collective-permute-start(f32[32,256]{1,0:T(8,128)S(1)} %collective-permute-done.4.refs_5_), channel_id=1, source_target_pairs={{0,96},{32,64},{64,32},{96,0},{1,97},{33,65},{65,33},{97,1},{2,98}... | collective-permute-start | bytes 98312 | tf_op jit(solution)/shard_map/ppermute | solution.py:58
  60.6 23.5 %all-to-all-start.2 = ((bf16[32,72,128]{2,1,0:T(8,128)(2,1)}), bf16[32,72,128]{2,1,0:T(8,128)(2,1)S(1)}, u32[]{:S(2)}, u32[]{:S(2)}) async-start(bf16[32,72,128]{2,1,0:T(8,128)(2,1)} %shard_map.90), calls=%async_computation.2 | async-start | bytes 1179648 | tf_op jit(solution)/shard_map/all_to_all | solution.py:48
  77.6 4.5 %collective-permute-start.9 = (bf16[32,256]{1,0:T(8,128)(2,1)S(1)}, bf16[32,256]{1,0:T(8,128)(2,1)S(1)}, u32[]{:S(2)}, u32[]{:S(2)}) collective-permute-start(bf16[32,256]{1,0:T(8,128)(2,1)S(1)} %get-tuple-element.56), channel_id=1, source_target_pairs={{0,64},{32,96},{64,0},{96,32},{1,65},{33,97},{65,1},{97,33},{2,66}... | collective-permute-start | bytes 49160 | tf_op jit(solution)/shard_map/ppermute | solution.py:58
  78.7 4.2 %collective-permute-start.10 = (bf16[32,256]{1,0:T(8,128)(2,1)S(1)}, bf16[32,256]{1,0:T(8,128)(2,1)S(1)}, u32[]{:S(2)}, u32[]{:S(2)}) collective-permute-start(bf16[32,256]{1,0:T(8,128)(2,1)S(1)} %get-tuple-element.57), channel_id=1, source_target_pairs={{0,96},{32,64},{64,32},{96,0},{1,97},{33,65},{65,33},{97,1},{2,98}... | collective-permute-start | bytes 49160 | tf_op jit(solution)/shard_map/ppermute | solution.py:58
  85.0 17.2 %all-to-all-start.5 = ((bf16[16,72,128]{2,1,0:T(8,128)(2,1)}), bf16[16,72,128]{2,1,0:T(8,128)(2,1)S(1)}, u32[]{:S(2)}, u32[]{:S(2)}) async-start(bf16[16,72,128]{2,1,0:T(8,128)(2,1)} %get-tuple-element.59), calls=%async_computation.5 | async-start | bytes 589824 | tf_op jit(solution)/shard_map/all_to_all | solution.py:54
  90.8 4.9 %collective-permute-start.13 = (f32[32,256]{1,0:T(8,128)S(1)}, f32[32,256]{1,0:T(8,128)S(1)}, u32[]{:S(2)}, u32[]{:S(2)}) collective-permute-start(f32[32,256]{1,0:T(8,128)S(1)} %get-tuple-element.58.refs_8_.refs_4_.refs_5_), channel_id=1, source_target_pairs={{0,96},{32,64},{64,32},{96,0},{1,97},{33,65},{65,33},{97,1},{2,98}... | collective-permute-start | bytes 98312 | tf_op jit(solution)/shard_map/ppermute | solution.py:58
  93.3 4.3 %collective-permute-start.12 = (f32[32,256]{1,0:T(8,128)S(1)}, f32[32,256]{1,0:T(8,128)S(1)}, u32[]{:S(2)}, u32[]{:S(2)}) collective-permute-start(f32[32,256]{1,0:T(8,128)S(1)} %collective-permute-done.11.refs_9_), channel_id=1, source_target_pairs={{0,96},{32,64},{64,32},{96,0},{1,97},{33,65},{65,33},{97,1},{2,98}... | collective-permute-start | bytes 98312 | tf_op jit(solution)/shard_map/ppermute | solution.py:58
  102.1 24.7 %all-to-all-start.4 = ((bf16[32,72,128]{2,1,0:T(8,128)(2,1)}), bf16[32,72,128]{2,1,0:T(8,128)(2,1)S(1)}, u32[]{:S(2)}, u32[]{:S(2)}) async-start(bf16[32,72,128]{2,1,0:T(8,128)(2,1)} %shard_map.93), calls=%async_computation.4 | async-start | bytes 1179648 | tf_op jit(solution)/shard_map/all_to_all | solution.py:48
  119.0 4.0 %collective-permute-start.15 = (bf16[32,256]{1,0:T(8,128)(2,1)S(1)}, bf16[32,256]{1,0:T(8,128)(2,1)S(1)}, u32[]{:S(2)}, u32[]{:S(2)}) collective-permute-start(bf16[32,256]{1,0:T(8,128)(2,1)S(1)} %get-tuple-element.61), channel_id=1, source_target_pairs={{0,32},{32,0},{64,96},{96,64},{1,33},{33,1},{65,97},{97,65},{2,34}... | collective-permute-start | bytes 49160 | tf_op jit(solution)/shard_map/ppermute | solution.py:58
  119.1 5.5 %collective-permute-start.16 = (bf16[32,256]{1,0:T(8,128)(2,1)S(1)}, bf16[32,256]{1,0:T(8,128)(2,1)S(1)}, u32[]{:S(2)}, u32[]{:S(2)}) collective-permute-start(bf16[32,256]{1,0:T(8,128)(2,1)S(1)} %get-tuple-element.62), channel_id=1, source_target_pairs={{0,64},{32,96},{64,0},{96,32},{1,65},{33,97},{65,1},{97,33},{2,66}... | collective-permute-start | bytes 49160 | tf_op jit(solution)/shard_map/ppermute | solution.py:58
  127.6 18.7 %all-to-all-start.7 = ((bf16[16,72,128]{2,1,0:T(8,128)(2,1)}), bf16[16,72,128]{2,1,0:T(8,128)(2,1)S(1)}, u32[]{:S(2)}, u32[]{:S(2)}) async-start(bf16[16,72,128]{2,1,0:T(8,128)(2,1)} %get-tuple-element.65), calls=%async_computation.7 | async-start | bytes 589824 | tf_op jit(solution)/shard_map/all_to_all | solution.py:54
  134.4 4.1 %collective-permute-start.20 = (f32[32,256]{1,0:T(8,128)S(1)}, f32[32,256]{1,0:T(8,128)S(1)}, u32[]{:S(2)}, u32[]{:S(2)}) collective-permute-start(f32[32,256]{1,0:T(8,128)S(1)} %get-tuple-element.64.refs_12_.refs_4_), channel_id=1, source_target_pairs={{0,96},{32,64},{64,32},{96,0},{1,97},{33,65},{65,33},{97,1},{2,98}... | collective-permute-start | bytes 98312 | tf_op jit(solution)/shard_map/ppermute | solution.py:58
  137.2 4.5 %collective-permute-start.19 = (f32[32,256]{1,0:T(8,128)S(1)}, f32[32,256]{1,0:T(8,128)S(1)}, u32[]{:S(2)}, u32[]{:S(2)}) collective-permute-start(f32[32,256]{1,0:T(8,128)S(1)} %collective-permute-done.18.refs_13_), channel_id=1, source_target_pairs={{0,96},{32,64},{64,32},{96,0},{1,97},{33,65},{65,33},{97,1},{2,98}... | collective-permute-start | bytes 98312 | tf_op jit(solution)/shard_map/ppermute | solution.py:58
  146.3 23.5 %all-to-all-start.6 = ((bf16[32,72,128]{2,1,0:T(8,128)(2,1)}), bf16[32,72,128]{2,1,0:T(8,128)(2,1)S(1)}, u32[]{:S(2)}, u32[]{:S(2)}) async-start(bf16[32,72,128]{2,1,0:T(8,128)(2,1)} %shard_map.96), calls=%async_computation.6 | async-start | bytes 1179648 | tf_op jit(solution)/shard_map/all_to_all | solution.py:48
  163.3 4.5 %collective-permute-start.23 = (bf16[32,256]{1,0:T(8,128)(2,1)S(1)}, bf16[32,256]{1,0:T(8,128)(2,1)S(1)}, u32[]{:S(2)}, u32[]{:S(2)}) collective-permute-start(bf16[32,256]{1,0:T(8,128)(2,1)S(1)} %get-tuple-element.68), channel_id=1, source_target_pairs={{0,64},{32,96},{64,0},{96,32},{1,65},{33,97},{65,1},{97,33},{2,66}... | collective-permute-start | bytes 49160 | tf_op jit(solution)/shard_map/ppermute | solution.py:58
  164.4 4.2 %collective-permute-start.24 = (bf16[32,256]{1,0:T(8,128)(2,1)S(1)}, bf16[32,256]{1,0:T(8,128)(2,1)S(1)}, u32[]{:S(2)}, u32[]{:S(2)}) collective-permute-start(bf16[32,256]{1,0:T(8,128)(2,1)S(1)} %get-tuple-element.69), channel_id=1, source_target_pairs={{0,96},{32,64},{64,32},{96,0},{1,97},{33,65},{65,33},{97,1},{2,98}... | collective-permute-start | bytes 49160 | tf_op jit(solution)/shard_map/ppermute | solution.py:58
  170.0 4.1 %collective-permute-start.27 = (f32[32,256]{1,0:T(8,128)S(1)}, f32[32,256]{1,0:T(8,128)S(1)}, u32[]{:S(2)}, u32[]{:S(2)}) collective-permute-start(f32[32,256]{1,0:T(8,128)S(1)} %get-tuple-element.71.refs_16_), channel_id=1, source_target_pairs={{0,96},{32,64},{64,32},{96,0},{1,97},{33,65},{65,33},{97,1},{2,98}... | collective-permute-start | bytes 98312 | tf_op jit(solution)/shard_map/ppermute | solution.py:58
  181.8 16.3 %all-to-all-start.8 = ((f32[16,48,128]{2,1,0:T(8,128)}), f32[16,48,128]{2,1,0:T(8,128)S(1)}, u32[]{:S(2)}, u32[]{:S(2)}) async-start(f32[16,48,128]{2,1,0:T(8,128)} %shard_map.100), calls=%async_computation.8 | async-start | bytes 786432 | tf_op jit(solution)/shard_map/all_to_all | solution.py:54
  (18 other events, 72.1 us)

commit v7 on v6

--- a/solution.py
+++ b/solution.py
@@ -11,9 +11,9 @@
 ITERS = 4
 SHIFT = 1.0625
 PULL = 0.375
-KEEP = 20
-CHUNKS = 4
-GRANT = 52
+KEEP = 12
+CHUNKS = 5
+GRANT = 50
 LANES = 128
 EXTRA = 8
 
@@ -58,17 +58,11 @@
     return lax.ppermute(value, axis, [(i, i ^ mask) for i in range(lax.axis_size(axis))])
 
 
-def all_slots(own):
-    one = swapped(own, "grp", 1)
-    three = swapped(own, "grp", 3)
-    two = swapped(one, "grp", 3)
-    return [own, one, two, three]
-
-
-def to_owners(parts):
-    two = swapped(parts[2], "grp", 2)
-    one, three = swapped(parts[1], "grp", 1), swapped(parts[3], "grp", 3)
-    return [parts[0], one, two, three]
+def trade(parts):
+    arrived = [parts[0]]
+    for k in range(1, len(parts)):
+        arrived.append(swapped(parts[k], "grp", k))
+    return arrived
 
 
 def dot(left, right, dims):
@@ -107,17 +101,16 @@
     return jnp.where(line == 0, high, value)
 
 
-def init_kernel(groups, owners, start_ref, shift_ref, *outs):
-    slots, sent_ref, coef_ref = outs[:groups], outs[groups], outs[groups + 1]
-    edge = coef_ref.shape[1]
+def init_kernel(groups, copies, start_ref, *refs):
+    slots, sent_ref = refs[:groups], refs[groups]
+    edge = slots[0].shape[1]
     group = lax.axis_index("grp")
     for s in range(groups):
         block = group ^ s
         slots[s][...] = start_ref[:, pl.ds(pl.multiple_of(block * edge, edge), edge)]
     rounded = halves(slots[0][...]).astype(BF16)
-    for r in range(owners):
+    for r in range(copies):
         sent_ref[r] = rounded
-    coef_ref[...] = SHIFT - shift_ref[:, pl.ds(pl.multiple_of(group * edge, edge), edge)]
 
 
 def load_kernel(tiles_ref, out_ref, sem):
@@ -225,7 +218,7 @@
 
 def combine_kernel(groups, last, back_ref, *refs):
     direct = refs[:groups]
-    now_ref, before_ref, coef_ref = refs[groups : groups + 3]
+    now_ref, before_ref, shift_ref = refs[groups : groups + 3]
     outs = refs[groups + 3 :]
     owners = back_ref.shape[0]
     width = now_ref.shape[0]
@@ -234,7 +227,10 @@
         image = image + direct[s][...].astype(F32)
     for r in range(owners):
         image = image + whole(back_ref, r, width).astype(F32)
-    new = 0.5 * image + coef_ref[...] * now_ref[...] - PULL * before_ref[...]
+    edge = now_ref.shape[1]
+    block = lax.axis_index("grp")
+    shift = shift_ref[:, pl.ds(pl.multiple_of(block * edge, edge), edge)]
+    new = 0.5 * image + (SHIFT - shift) * now_ref[...] - PULL * before_ref[...]
     outs[0][...] = new
     sums = back_ref[0, pl.ds(2 * width, EXTRA), :].astype(F32)
     for r in range(1, owners):
@@ -310,11 +306,14 @@
 
 
 def block_kernel(j, gram_ref, *refs):
-    olds, (low_ref, inv_ref) = refs[:-2], refs[-2:]
+    outs = 2 if j == 0 else 4
+    olds, (low_ref, inv_ref) = refs[:-outs], refs[-outs:][:2]
     if j > 0:
         low_ref[...] = olds[0][...]
         inv_ref[...] = olds[1][...]
     next_rows(j, gram_ref[...], low_ref, inv_ref)
+    if j > 0:
+        refs[-2][...], refs[-1][...] = step_results(j - 1, low_ref, inv_ref, gram_ref.shape[0])
 
 
 def gram_kernel(groups, chunk_ref, *refs):
@@ -347,6 +346,8 @@
 
 
 def finish_kernel(groups, parts_ref, old_low, old_inv, *refs):
+    known = ITERS - 2
+    early, refs = refs[: 2 * known], refs[2 * known :]
     vectors = [refs[i * groups : (i + 1) * groups] for i in range(ITERS + 1)]
     proj_ref, fact_ref, out_ref, low, inv = refs[(ITERS + 1) * groups :]
     owners = parts_ref.shape[0]
@@ -363,7 +364,9 @@
     count = LANES // width
     corner = jnp.concatenate([sums[width:, p * width : (p + 1) * width] for p in range(count)], 0)
     next_rows(ITERS, jnp.concatenate([sums[:width], corner], 1), low, inv)
-    for j in range(ITERS):
+    for j in range(known):
+        proj_ref[j], fact_ref[j] = early[2 * j][...], early[2 * j + 1][...]
+    for j in range(known, ITERS):
         proj_ref[j], fact_ref[j] = step_results(j, low, inv, width)
     for s in range(groups):
         value = plain(inv[pl.ds(ITERS * width, width), pl.ds(0, width)], vectors[0][s][...])
@@ -394,17 +397,19 @@
     rest = [pltpu.VMEM((count - KEEP, edge, edge), BF16), pltpu.SemaphoreType.DMA((CHUNKS,))]
     flops = 2 * count * width * edge * edge
 
-    *slots, sent, coef = call(
+    *slots, sent = call(
         functools.partial(init_kernel, groups, owners // 2),
-        [shape(width, edge)] * groups + [shape(owners // 2, 2 * width, LANES, dtype=BF16), shape(1, edge)],
-        [VMEM, VMEM],
-        (start_block, dual_shift[None, :]),
+        [shape(width, edge)] * groups + [shape(owners // 2, 2 * width, LANES, dtype=BF16)],
+        [VMEM],
+        (start_block,),
         4,
     )
+    shift = dual_shift[None, :]
     def block(j, rows, state):
         return call(
             functools.partial(block_kernel, j),
-            [shape(total, total)] * 2,
+            [shape(total, total)] * 2
+            + [shape(width, ITERS * width), shape(width, width)] * (j > 0),
             [VMEM] * (1 + len(state)),
             (rows, *state),
             4,
@@ -440,18 +445,18 @@
             flops,
         )
         grams += direct[groups:]
-        direct = to_owners(direct)
+        direct = trade(direct[:groups])
         last = step == ITERS - 1
         second = shape(EXTRA, LANES) if last else shape(owners // 2, 2 * width + EXTRA, LANES, dtype=BF16)
         new, sent = call(
             functools.partial(combine_kernel, groups, last),
             [shape(width, edge), second],
             [VMEM] * (groups + 4),
-            (arrived, *direct, own, before, coef),
+            (arrived, *direct, own, before, shift),
             4,
         )
         before = own
-        basis.append(all_slots(new))
+        basis.append(trade([new] * groups))
 
     flat = [slot for slots in basis for slot in slots]
     lines = width + width * width // LANES + EXTRA
@@ -471,13 +476,15 @@
     )
     state = ()
     parts = same_core(parts)
+    early = []
     for j, rows in enumerate(grams):
-        state = block(j, rows, state)
+        *state, proj, fact = [*block(j, rows, state), None, None][:4]
+        early += [proj, fact] * (j > 0)
     return call(
         functools.partial(finish_kernel, groups),
         [shape(ITERS, width, ITERS * width), shape(ITERS, width, width), shape(width, row_count)],
-        [VMEM] * (3 + len(flat)),
-        (parts, *state, *flat),
+        [VMEM] * (3 + len(early) + len(flat)),
+        (parts, *state, *early, *flat),
         8,
         [pltpu.VMEM((total, total), F32), pltpu.VMEM((total, total), F32)],
     )

time: 206 us -> 188 us (0.913)
  Pallas kernels: 53.5 us -> 44.7 us
  waiting for transfers between devices: 42.3 us -> 33.5 us
    pallas_call x20, Pallas kernels: 53.5 us -> 44.7 us  [call(): pl.pallas_call(kernel, out_shape=out_shape, in_specs=[spec(space) for spa...]
    ppermute x29, waiting for transfers between devices: 36.4 us -> 28.3 us  [swapped(): lax.ppermute(value, axis, [(i, i ^ mask) for i in range(lax.axis_size(axi...]
    ppermute x29, starting transfers between devices: 29 us -> 32.4 us  [swapped(): lax.ppermute(value, axis, [(i, i ^ mask) for i in range(lax.axis_size(axi...]
    all_to_all x4, starting transfers between devices: 42.1 us -> 39.3 us  [exchange(): return lax.all_to_all(parts, axis, split_axis=0, concat_axis=0, tiled=True)]
    all_to_all x4, waiting for transfers between devices: 2.34 us -> 0.12 us  [exchange(): return lax.all_to_all(parts, axis, split_axis=0, concat_axis=0, tiled=True)]
  transfers between devices with their start and end apart: 38 -> 38, of which waited for: 27 -> 26; matrix products, arithmetic and copies ran while one was open for 0% -> 0% of each run, Pallas kernels for 21% -> 18%
where the time goes in v7:
time: 188 us; the launch traced here: 187 us
  starting transfers between devices  106 us (56%)
  Pallas kernels  44.7 us (24%)
  waiting for transfers between devices  33.5 us (18%)
    pallas_call x20, Pallas kernels, call(): pl.pallas_call(kernel, out_shape=out_shape, in_specs=[spec(space) for spa...  44.7 us
    all_to_all x4, starting transfers between devices, exchange(): return lax.all_to_all(parts, axis, split_axis=0, concat_axis=0, tiled=True)  39.3 us
    all_to_all x5, starting transfers between devices, same_core(): lax.all_to_all(parts, 'row', 0, 0, axis_index_groups=groups, tiled=True)  34.5 us
    ppermute x29, starting transfers between devices, swapped(): lax.ppermute(value, axis, [(i, i ^ mask) for i in range(lax.axis_size(axi...  32.4 us
    ppermute x29, waiting for transfers between devices, swapped(): lax.ppermute(value, axis, [(i, i ^ mask) for i in range(lax.axis_size(axi...  28.3 us
    all_to_all x5, waiting for transfers between devices, same_core(): lax.all_to_all(parts, 'row', 0, 0, axis_index_groups=groups, tiled=True)  5.06 us
  transfers between devices with their start and end apart: 38, of which 26 were waited for; matrix products, arithmetic and copies ran while one was open for 0% of the time, Pallas kernels for 18%

profile of v7, /device:TPU:1, one launch (start us, length us, event | category | flops | bytes accessed | tf_op | source)
XLA Modules:
  0.0 186.9 jit_solution(14139534595934329621)
XLA Ops:
  2.3 8.4 %all-to-all-start.1 = ((bf16[16,64,128]{2,1,0:T(8,128)(2,1)}), bf16[16,64,128]{2,1,0:T(8,128)(2,1)S(1)}, u32[]{:S(2)}, u32[]{:S(2)}) async-start(bf16[16,64,128]{2,1,0:T(8,128)(2,1)} %get-tuple-element.49), calls=%async_computation.1 | async-start | bytes 524288 | tf_op jit(solution)/shard_map/all_to_all | solution.py:54
  12.8 3.5 %shard_map.87 = bf16[32,72,128]{2,1,0:T(8,128)(2,1)} custom-call(s32[1,1,32]{2,1,0:T(1,128)S(1)} %copy-done.2, s32[1,1,32]{2,1,0:T(1,128)S(1)} %copy-done.3, s32[1,1]{1,0:T(1,128)S(6)} %copy.9.live_ref, bf16[12,256,256]{2,1,0:T(8,128)(2,1)S(1)} %shard_map.85.kept_ref, bf16[1,1,32,256,256]{4,3,2,1,0:T(8,128)(2,1)} %tiles_ref.17, ...), custom_call_target="tpu_custom_call" | custom-call | flops 134217728 | bytes 1048576 | tf_op jit(solution)/shard_map/pallas_call | solution.py:32
  18.2 6.4 %all-to-all-start = ((bf16[32,72,128]{2,1,0:T(8,128)(2,1)}), bf16[32,72,128]{2,1,0:T(8,128)(2,1)S(1)}, u32[]{:S(2)}, u32[]{:S(2)}) async-start(bf16[32,72,128]{2,1,0:T(8,128)(2,1)} %shard_map.87), calls=%async_computation | async-start | bytes 1179648 | tf_op jit(solution)/shard_map/all_to_all | solution.py:48
  26.2 3.0 %shard_map.88 = (f32[32,256]{1,0:T(8,128)S(1)}, bf16[32,256]{1,0:T(8,128)(2,1)S(1)}, bf16[32,256]{1,0:T(8,128)(2,1)S(1)}, bf16[32,256]{1,0:T(8,128)(2,1)S(1)}) custom-call(s32[1,1,32]{2,1,0:T(1,128)S(1)} %copy-done.2, s32[1,1,32]{2,1,0:T(1,128)S(1)} %copy-done.3, s32[1,1]{1,0:T(1,128)S(6)} %copy.9.live_ref, bf16[12,256,256]{2,1,0:T(8,128)(2,1)S(1)} %shard_map.85.kept_ref, ...), custom_call_target="tpu_custom_call" | custom-call | flops 134217728 | bytes 1048576 | tf_op jit(solution)/shard_map/pallas_call | solution.py:32
  30.6 2.6 %collective-permute-start.2 = (bf16[32,256]{1,0:T(8,128)(2,1)S(1)}, bf16[32,256]{1,0:T(8,128)(2,1)S(1)}, u32[]{:S(2)}, u32[]{:S(2)}) collective-permute-start(bf16[32,256]{1,0:T(8,128)(2,1)S(1)} %get-tuple-element.52), channel_id=1, source_target_pairs={{0,64},{32,96},{64,0},{96,32},{1,65},{33,97},{65,1},{97,33},{2,66}... | collective-permute-start | bytes 49160 | tf_op jit(solution)/shard_map/ppermute | solution.py:58
  37.9 6.7 %all-to-all-start.3 = ((bf16[16,72,128]{2,1,0:T(8,128)(2,1)}), bf16[16,72,128]{2,1,0:T(8,128)(2,1)S(1)}, u32[]{:S(2)}, u32[]{:S(2)}) async-start(bf16[16,72,128]{2,1,0:T(8,128)(2,1)} %get-tuple-element.55), calls=%async_computation.3 | async-start | bytes 589824 | tf_op jit(solution)/shard_map/all_to_all | solution.py:54
  45.4 2.5 %collective-permute-start.4 = (f32[32,256]{1,0:T(8,128)S(1)}, f32[32,256]{1,0:T(8,128)S(1)}, u32[]{:S(2)}, u32[]{:S(2)}) collective-permute-start(f32[32,256]{1,0:T(8,128)S(1)} %get-tuple-element.54.refs_4_.refs_5_.refs_8_), channel_id=1, source_target_pairs={{0,32},{32,0},{64,96},{96,64},{1,33},{33,1},{65,97},{97,65},{2,34}... | collective-permute-start | bytes 98312 | tf_op jit(solution)/shard_map/ppermute | solution.py:58
  49.6 3.5 %shard_map.90 = bf16[32,72,128]{2,1,0:T(8,128)(2,1)} custom-call(s32[1,1,32]{2,1,0:T(1,128)S(1)} %copy-done.2, s32[1,1,32]{2,1,0:T(1,128)S(1)} %copy-done.3, s32[1,1]{1,0:T(1,128)S(6)} %copy.9.live_ref, bf16[12,256,256]{2,1,0:T(8,128)(2,1)S(1)} %shard_map.85.kept_ref, bf16[1,1,32,256,256]{4,3,2,1,0:T(8,128)(2,1)} %tiles_ref.17, ...), custom_call_target="tpu_custom_call" | custom-call | flops 134217728 | bytes 1048576 | tf_op jit(solution)/shard_map/pallas_call | solution.py:32
  53.1 11.0 %all-to-all-start.2 = ((bf16[32,72,128]{2,1,0:T(8,128)(2,1)}), bf16[32,72,128]{2,1,0:T(8,128)(2,1)S(1)}, u32[]{:S(2)}, u32[]{:S(2)}) async-start(bf16[32,72,128]{2,1,0:T(8,128)(2,1)} %shard_map.90), calls=%async_computation.2 | async-start | bytes 1179648 | tf_op jit(solution)/shard_map/all_to_all | solution.py:48
  65.8 3.0 %shard_map.91 = (f32[32,256]{1,0:T(8,128)S(1)}, bf16[32,256]{1,0:T(8,128)(2,1)S(1)}, bf16[32,256]{1,0:T(8,128)(2,1)S(1)}, bf16[32,256]{1,0:T(8,128)(2,1)S(1)}, f32[32,128]{1,0:T(8,128)S(1)}) custom-call(s32[1,1,32]{2,1,0:T(1,128)S(1)} %copy-done.2, s32[1,1,32]{2,1,0:T(1,128)S(1)} %copy-done.3, s32[1,1]{1,0:T(1,128)S(6)} %copy.9.live_ref, ...), custom_call_target="tpu_custom_call" | custom-call | flops 134217728 | bytes 1048576 | tf_op jit(solution)/shard_map/pallas_call | solution.py:32
  77.1 6.3 %all-to-all-start.5 = ((bf16[16,72,128]{2,1,0:T(8,128)(2,1)}), bf16[16,72,128]{2,1,0:T(8,128)(2,1)S(1)}, u32[]{:S(2)}, u32[]{:S(2)}) async-start(bf16[16,72,128]{2,1,0:T(8,128)(2,1)} %get-tuple-element.61), calls=%async_computation.5 | async-start | bytes 589824 | tf_op jit(solution)/shard_map/all_to_all | solution.py:54
  84.2 2.6 %collective-permute-start.11 = (f32[32,256]{1,0:T(8,128)S(1)}, f32[32,256]{1,0:T(8,128)S(1)}, u32[]{:S(2)}, u32[]{:S(2)}) collective-permute-start(f32[32,256]{1,0:T(8,128)S(1)} %get-tuple-element.60.refs_8_.refs_4_.refs_5_.refs_12_), channel_id=1, source_target_pairs={{0,32},{32,0},{64,96},{96,64},{1,33},{33,1},{65,97},{97,65},{2,34}... | collective-permute-start | bytes 98312 | tf_op jit(solution)/shard_map/ppermute | solution.py:58
  88.4 3.5 %shard_map.93 = bf16[32,72,128]{2,1,0:T(8,128)(2,1)} custom-call(s32[1,1,32]{2,1,0:T(1,128)S(1)} %copy-done.2, s32[1,1,32]{2,1,0:T(1,128)S(1)} %copy-done.3, s32[1,1]{1,0:T(1,128)S(6)} %copy.9.live_ref, bf16[12,256,256]{2,1,0:T(8,128)(2,1)S(1)} %shard_map.85.kept_ref, bf16[1,1,32,256,256]{4,3,2,1,0:T(8,128)(2,1)} %tiles_ref.17, ...), custom_call_target="tpu_custom_call" | custom-call | flops 134217728 | bytes 1048576 | tf_op jit(solution)/shard_map/pallas_call | solution.py:32
  92.0 11.0 %all-to-all-start.4 = ((bf16[32,72,128]{2,1,0:T(8,128)(2,1)}), bf16[32,72,128]{2,1,0:T(8,128)(2,1)S(1)}, u32[]{:S(2)}, u32[]{:S(2)}) async-start(bf16[32,72,128]{2,1,0:T(8,128)(2,1)} %shard_map.93), calls=%async_computation.4 | async-start | bytes 1179648 | tf_op jit(solution)/shard_map/all_to_all | solution.py:48
  104.8 3.0 %shard_map.94 = (f32[32,256]{1,0:T(8,128)S(1)}, bf16[32,256]{1,0:T(8,128)(2,1)S(1)}, bf16[32,256]{1,0:T(8,128)(2,1)S(1)}, bf16[32,256]{1,0:T(8,128)(2,1)S(1)}, f32[32,128]{1,0:T(8,128)S(1)}) custom-call(s32[1,1,32]{2,1,0:T(1,128)S(1)} %copy-done.2, s32[1,1,32]{2,1,0:T(1,128)S(1)} %copy-done.3, s32[1,1]{1,0:T(1,128)S(6)} %copy.9.live_ref, ...), custom_call_target="tpu_custom_call" | custom-call | flops 134217728 | bytes 1048576 | tf_op jit(solution)/shard_map/pallas_call | solution.py:32
  115.9 6.5 %all-to-all-start.7 = ((bf16[16,72,128]{2,1,0:T(8,128)(2,1)}), bf16[16,72,128]{2,1,0:T(8,128)(2,1)S(1)}, u32[]{:S(2)}, u32[]{:S(2)}) async-start(bf16[16,72,128]{2,1,0:T(8,128)(2,1)} %get-tuple-element.67), calls=%async_computation.7 | async-start | bytes 589824 | tf_op jit(solution)/shard_map/all_to_all | solution.py:54
  123.2 2.6 %collective-permute-start.18 = (f32[32,256]{1,0:T(8,128)S(1)}, f32[32,256]{1,0:T(8,128)S(1)}, u32[]{:S(2)}, u32[]{:S(2)}) collective-permute-start(f32[32,256]{1,0:T(8,128)S(1)} %get-tuple-element.66.refs_12_.refs_4_.refs_16_), channel_id=1, source_target_pairs={{0,32},{32,0},{64,96},{96,64},{1,33},{33,1},{65,97},{97,65},{2,34}... | collective-permute-start | bytes 98312 | tf_op jit(solution)/shard_map/ppermute | solution.py:58
  127.5 3.5 %shard_map.96 = bf16[32,72,128]{2,1,0:T(8,128)(2,1)} custom-call(s32[1,1,32]{2,1,0:T(1,128)S(1)} %copy-done.2, s32[1,1,32]{2,1,0:T(1,128)S(1)} %copy-done.3, s32[1,1]{1,0:T(1,128)S(6)} %copy.9.live_ref, bf16[12,256,256]{2,1,0:T(8,128)(2,1)S(1)} %shard_map.85.kept_ref, bf16[1,1,32,256,256]{4,3,2,1,0:T(8,128)(2,1)} %tiles_ref.17, ...), custom_call_target="tpu_custom_call" | custom-call | flops 134217728 | bytes 1048576 | tf_op jit(solution)/shard_map/pallas_call | solution.py:32
  131.0 11.0 %all-to-all-start.6 = ((bf16[32,72,128]{2,1,0:T(8,128)(2,1)}), bf16[32,72,128]{2,1,0:T(8,128)(2,1)S(1)}, u32[]{:S(2)}, u32[]{:S(2)}) async-start(bf16[32,72,128]{2,1,0:T(8,128)(2,1)} %shard_map.96), calls=%async_computation.6 | async-start | bytes 1179648 | tf_op jit(solution)/shard_map/all_to_all | solution.py:48
  143.7 3.0 %shard_map.97 = (f32[32,256]{1,0:T(8,128)S(1)}, bf16[32,256]{1,0:T(8,128)(2,1)S(1)}, bf16[32,256]{1,0:T(8,128)(2,1)S(1)}, bf16[32,256]{1,0:T(8,128)(2,1)S(1)}, f32[32,128]{1,0:T(8,128)S(1)}) custom-call(s32[1,1,32]{2,1,0:T(1,128)S(1)} %copy-done.2, s32[1,1,32]{2,1,0:T(1,128)S(1)} %copy-done.3, s32[1,1]{1,0:T(1,128)S(6)} %copy.9.live_ref, ...), custom_call_target="tpu_custom_call" | custom-call | flops 134217728 | bytes 1048576 | tf_op jit(solution)/shard_map/pallas_call | solution.py:32
  164.9 6.6 %all-to-all-start.8 = ((f32[16,48,128]{2,1,0:T(8,128)}), f32[16,48,128]{2,1,0:T(8,128)S(1)}, u32[]{:S(2)}, u32[]{:S(2)}) async-start(f32[16,48,128]{2,1,0:T(8,128)} %shard_map.100), calls=%async_computation.8 | async-start | bytes 786432 | tf_op jit(solution)/shard_map/all_to_all | solution.py:54
  175.4 2.4 %shard_map.103 = (f32[160,160]{1,0:T(8,128)S(1)}, f32[160,160]{1,0:T(8,128)S(1)}, f32[32,128]{1,0:T(8,128)S(1)}, f32[32,32]{1,0:T(8,128)S(1)}) custom-call(f32[32,128]{1,0:T(8,128)S(1)} %get-tuple-element.74.gram_ref, f32[160,160]{1,0:T(8,128)S(1)} %get-tuple-element.79.refs_0_, f32[160,160]{1,0:T(8,128)S(1)} %get-tuple-element.80.refs_1_), custom_call_target="tpu_custom_call" | custom-call | flops 2000000 | bytes 1048576 | tf_op jit(solution)/shard_map/pallas_call | solution.py:32
  177.9 3.2 %all-to-all-done.8.parts_ref = f32[16,48,128]{2,1,0:T(8,128)S(1)} async-done(((f32[16,48,128]{2,1,0:T(8,128)}), f32[16,48,128]{2,1,0:T(8,128)S(1)}, u32[]{:S(2)}, u32[]{:S(2)}) %all-to-all-start.8) | async-done | bytes 393248 | tf_op jit(solution)/shard_map/all_to_all | solution.py:54
  181.0 5.9 %shard_map.104 = (f32[4,32,128]{2,1,0:T(8,128)}, f32[4,32,32]{2,1,0:T(8,128)}, f32[32,1024]{1,0:T(8,128)}) custom-call(f32[16,48,128]{2,1,0:T(8,128)S(1)} %all-to-all-done.8.parts_ref, f32[160,160]{1,0:T(8,128)S(1)} %get-tuple-element.81.old_low, f32[160,160]{1,0:T(8,128)S(1)} %get-tuple-element.82.old_inv, f32[32,128]{1,0:T(8,128)S(1)} %get-tuple-element.83.refs_0_, ...), custom_call_target="tpu_custom_call" | custom-call | flops 2000000 | bytes 1048576 | tf_op jit(solution)/shard_map/pallas_call | solution.py:32
  (81 shorter events, 63.6 us)
Async XLA Ops:
  2.3 16.0 %all-to-all-start.1 = ((bf16[16,64,128]{2,1,0:T(8,128)(2,1)}), bf16[16,64,128]{2,1,0:T(8,128)(2,1)S(1)}, u32[]{:S(2)}, u32[]{:S(2)}) async-start(bf16[16,64,128]{2,1,0:T(8,128)(2,1)} %get-tuple-element.49), calls=%async_computation.1 | async-start | bytes 524288 | tf_op jit(solution)/shard_map/all_to_all | solution.py:54
  18.2 18.8 %all-to-all-start = ((bf16[32,72,128]{2,1,0:T(8,128)(2,1)}), bf16[32,72,128]{2,1,0:T(8,128)(2,1)S(1)}, u32[]{:S(2)}, u32[]{:S(2)}) async-start(bf16[32,72,128]{2,1,0:T(8,128)(2,1)} %shard_map.87), calls=%async_computation | async-start | bytes 1179648 | tf_op jit(solution)/shard_map/all_to_all | solution.py:48
  30.6 4.4 %collective-permute-start.2 = (bf16[32,256]{1,0:T(8,128)(2,1)S(1)}, bf16[32,256]{1,0:T(8,128)(2,1)S(1)}, u32[]{:S(2)}, u32[]{:S(2)}) collective-permute-start(bf16[32,256]{1,0:T(8,128)(2,1)S(1)} %get-tuple-element.52), channel_id=1, source_target_pairs={{0,64},{32,96},{64,0},{96,32},{1,65},{33,97},{65,1},{97,33},{2,66}... | collective-permute-start | bytes 49160 | tf_op jit(solution)/shard_map/ppermute | solution.py:58
  37.9 15.2 %all-to-all-start.3 = ((bf16[16,72,128]{2,1,0:T(8,128)(2,1)}), bf16[16,72,128]{2,1,0:T(8,128)(2,1)S(1)}, u32[]{:S(2)}, u32[]{:S(2)}) async-start(bf16[16,72,128]{2,1,0:T(8,128)(2,1)} %get-tuple-element.55), calls=%async_computation.3 | async-start | bytes 589824 | tf_op jit(solution)/shard_map/all_to_all | solution.py:54
  44.6 4.1 %collective-permute-start.6 = (f32[32,256]{1,0:T(8,128)S(1)}, f32[32,256]{1,0:T(8,128)S(1)}, u32[]{:S(2)}, u32[]{:S(2)}) collective-permute-start(f32[32,256]{1,0:T(8,128)S(1)} %get-tuple-element.54.refs_4_.refs_5_.refs_8_), channel_id=1, source_target_pairs={{0,96},{32,64},{64,32},{96,0},{1,97},{33,65},{65,33},{97,1},{2,98}... | collective-permute-start | bytes 98312 | tf_op jit(solution)/shard_map/ppermute | solution.py:58
  44.7 4.3 %collective-permute-start.5 = (f32[32,256]{1,0:T(8,128)S(1)}, f32[32,256]{1,0:T(8,128)S(1)}, u32[]{:S(2)}, u32[]{:S(2)}) collective-permute-start(f32[32,256]{1,0:T(8,128)S(1)} %get-tuple-element.54.refs_4_.refs_5_.refs_8_), channel_id=1, source_target_pairs={{0,64},{32,96},{64,0},{96,32},{1,65},{33,97},{65,1},{97,33},{2,66}... | collective-permute-start | bytes 98312 | tf_op jit(solution)/shard_map/ppermute | solution.py:58
  45.4 4.2 %collective-permute-start.4 = (f32[32,256]{1,0:T(8,128)S(1)}, f32[32,256]{1,0:T(8,128)S(1)}, u32[]{:S(2)}, u32[]{:S(2)}) collective-permute-start(f32[32,256]{1,0:T(8,128)S(1)} %get-tuple-element.54.refs_4_.refs_5_.refs_8_), channel_id=1, source_target_pairs={{0,32},{32,0},{64,96},{96,64},{1,33},{33,1},{65,97},{97,65},{2,34}... | collective-permute-start | bytes 98312 | tf_op jit(solution)/shard_map/ppermute | solution.py:58
  53.1 23.1 %all-to-all-start.2 = ((bf16[32,72,128]{2,1,0:T(8,128)(2,1)}), bf16[32,72,128]{2,1,0:T(8,128)(2,1)S(1)}, u32[]{:S(2)}, u32[]{:S(2)}) async-start(bf16[32,72,128]{2,1,0:T(8,128)(2,1)} %shard_map.90), calls=%async_computation.2 | async-start | bytes 1179648 | tf_op jit(solution)/shard_map/all_to_all | solution.py:48
  70.3 4.4 %collective-permute-start.9 = (bf16[32,256]{1,0:T(8,128)(2,1)S(1)}, bf16[32,256]{1,0:T(8,128)(2,1)S(1)}, u32[]{:S(2)}, u32[]{:S(2)}) collective-permute-start(bf16[32,256]{1,0:T(8,128)(2,1)S(1)} %get-tuple-element.58), channel_id=1, source_target_pairs={{0,64},{32,96},{64,0},{96,32},{1,65},{33,97},{65,1},{97,33},{2,66}... | collective-permute-start | bytes 49160 | tf_op jit(solution)/shard_map/ppermute | solution.py:58
  72.1 4.1 %collective-permute-start.10 = (bf16[32,256]{1,0:T(8,128)(2,1)S(1)}, bf16[32,256]{1,0:T(8,128)(2,1)S(1)}, u32[]{:S(2)}, u32[]{:S(2)}) collective-permute-start(bf16[32,256]{1,0:T(8,128)(2,1)S(1)} %get-tuple-element.59), channel_id=1, source_target_pairs={{0,96},{32,64},{64,32},{96,0},{1,97},{33,65},{65,33},{97,1},{2,98}... | collective-permute-start | bytes 49160 | tf_op jit(solution)/shard_map/ppermute | solution.py:58
  77.1 14.9 %all-to-all-start.5 = ((bf16[16,72,128]{2,1,0:T(8,128)(2,1)}), bf16[16,72,128]{2,1,0:T(8,128)(2,1)S(1)}, u32[]{:S(2)}, u32[]{:S(2)}) async-start(bf16[16,72,128]{2,1,0:T(8,128)(2,1)} %get-tuple-element.61), calls=%async_computation.5 | async-start | bytes 589824 | tf_op jit(solution)/shard_map/all_to_all | solution.py:54
  83.4 4.1 %collective-permute-start.13 = (f32[32,256]{1,0:T(8,128)S(1)}, f32[32,256]{1,0:T(8,128)S(1)}, u32[]{:S(2)}, u32[]{:S(2)}) collective-permute-start(f32[32,256]{1,0:T(8,128)S(1)} %get-tuple-element.60.refs_8_.refs_4_.refs_5_.refs_12_), channel_id=1, source_target_pairs={{0,96},{32,64},{64,32},{96,0},{1,97},{33,65},{65,33},{97,1},{2,98}... | collective-permute-start | bytes 98312 | tf_op jit(solution)/shard_map/ppermute | solution.py:58
  84.2 4.3 %collective-permute-start.12 = (f32[32,256]{1,0:T(8,128)S(1)}, f32[32,256]{1,0:T(8,128)S(1)}, u32[]{:S(2)}, u32[]{:S(2)}) collective-permute-start(f32[32,256]{1,0:T(8,128)S(1)} %get-tuple-element.60.refs_8_.refs_4_.refs_5_.refs_12_), channel_id=1, source_target_pairs={{0,64},{32,96},{64,0},{96,32},{1,65},{33,97},{65,1},{97,33},{2,66}... | collective-permute-start | bytes 98312 | tf_op jit(solution)/shard_map/ppermute | solution.py:58
  84.2 4.3 %collective-permute-start.11 = (f32[32,256]{1,0:T(8,128)S(1)}, f32[32,256]{1,0:T(8,128)S(1)}, u32[]{:S(2)}, u32[]{:S(2)}) collective-permute-start(f32[32,256]{1,0:T(8,128)S(1)} %get-tuple-element.60.refs_8_.refs_4_.refs_5_.refs_12_), channel_id=1, source_target_pairs={{0,32},{32,0},{64,96},{96,64},{1,33},{33,1},{65,97},{97,65},{2,34}... | collective-permute-start | bytes 98312 | tf_op jit(solution)/shard_map/ppermute | solution.py:58
  92.0 23.1 %all-to-all-start.4 = ((bf16[32,72,128]{2,1,0:T(8,128)(2,1)}), bf16[32,72,128]{2,1,0:T(8,128)(2,1)S(1)}, u32[]{:S(2)}, u32[]{:S(2)}) async-start(bf16[32,72,128]{2,1,0:T(8,128)(2,1)} %shard_map.93), calls=%async_computation.4 | async-start | bytes 1179648 | tf_op jit(solution)/shard_map/all_to_all | solution.py:48
  109.3 4.4 %collective-permute-start.16 = (bf16[32,256]{1,0:T(8,128)(2,1)S(1)}, bf16[32,256]{1,0:T(8,128)(2,1)S(1)}, u32[]{:S(2)}, u32[]{:S(2)}) collective-permute-start(bf16[32,256]{1,0:T(8,128)(2,1)S(1)} %get-tuple-element.64), channel_id=1, source_target_pairs={{0,64},{32,96},{64,0},{96,32},{1,65},{33,97},{65,1},{97,33},{2,66}... | collective-permute-start | bytes 49160 | tf_op jit(solution)/shard_map/ppermute | solution.py:58
  115.9 15.1 %all-to-all-start.7 = ((bf16[16,72,128]{2,1,0:T(8,128)(2,1)}), bf16[16,72,128]{2,1,0:T(8,128)(2,1)S(1)}, u32[]{:S(2)}, u32[]{:S(2)}) async-start(bf16[16,72,128]{2,1,0:T(8,128)(2,1)} %get-tuple-element.67), calls=%async_computation.7 | async-start | bytes 589824 | tf_op jit(solution)/shard_map/all_to_all | solution.py:54
  123.2 4.3 %collective-permute-start.19 = (f32[32,256]{1,0:T(8,128)S(1)}, f32[32,256]{1,0:T(8,128)S(1)}, u32[]{:S(2)}, u32[]{:S(2)}) collective-permute-start(f32[32,256]{1,0:T(8,128)S(1)} %get-tuple-element.66.refs_12_.refs_4_.refs_16_), channel_id=1, source_target_pairs={{0,64},{32,96},{64,0},{96,32},{1,65},{33,97},{65,1},{97,33},{2,66}... | collective-permute-start | bytes 98312 | tf_op jit(solution)/shard_map/ppermute | solution.py:58
  123.2 4.3 %collective-permute-start.18 = (f32[32,256]{1,0:T(8,128)S(1)}, f32[32,256]{1,0:T(8,128)S(1)}, u32[]{:S(2)}, u32[]{:S(2)}) collective-permute-start(f32[32,256]{1,0:T(8,128)S(1)} %get-tuple-element.66.refs_12_.refs_4_.refs_16_), channel_id=1, source_target_pairs={{0,32},{32,0},{64,96},{96,64},{1,33},{33,1},{65,97},{97,65},{2,34}... | collective-permute-start | bytes 98312 | tf_op jit(solution)/shard_map/ppermute | solution.py:58
  131.0 23.1 %all-to-all-start.6 = ((bf16[32,72,128]{2,1,0:T(8,128)(2,1)}), bf16[32,72,128]{2,1,0:T(8,128)(2,1)S(1)}, u32[]{:S(2)}, u32[]{:S(2)}) async-start(bf16[32,72,128]{2,1,0:T(8,128)(2,1)} %shard_map.96), calls=%async_computation.6 | async-start | bytes 1179648 | tf_op jit(solution)/shard_map/all_to_all | solution.py:48
  148.2 4.4 %collective-permute-start.23 = (bf16[32,256]{1,0:T(8,128)(2,1)S(1)}, bf16[32,256]{1,0:T(8,128)(2,1)S(1)}, u32[]{:S(2)}, u32[]{:S(2)}) collective-permute-start(bf16[32,256]{1,0:T(8,128)(2,1)S(1)} %get-tuple-element.70), channel_id=1, source_target_pairs={{0,64},{32,96},{64,0},{96,32},{1,65},{33,97},{65,1},{97,33},{2,66}... | collective-permute-start | bytes 49160 | tf_op jit(solution)/shard_map/ppermute | solution.py:58
  150.0 4.1 %collective-permute-start.24 = (bf16[32,256]{1,0:T(8,128)(2,1)S(1)}, bf16[32,256]{1,0:T(8,128)(2,1)S(1)}, u32[]{:S(2)}, u32[]{:S(2)}) collective-permute-start(bf16[32,256]{1,0:T(8,128)(2,1)S(1)} %get-tuple-element.71), channel_id=1, source_target_pairs={{0,96},{32,64},{64,32},{96,0},{1,97},{33,65},{65,33},{97,1},{2,98}... | collective-permute-start | bytes 49160 | tf_op jit(solution)/shard_map/ppermute | solution.py:58
  156.4 4.4 %collective-permute-start.26 = (f32[32,256]{1,0:T(8,128)S(1)}, f32[32,256]{1,0:T(8,128)S(1)}, u32[]{:S(2)}, u32[]{:S(2)}) collective-permute-start(f32[32,256]{1,0:T(8,128)S(1)} %get-tuple-element.73.refs_16_.refs_20_), channel_id=1, source_target_pairs={{0,64},{32,96},{64,0},{96,32},{1,65},{33,97},{65,1},{97,33},{2,66}... | collective-permute-start | bytes 98312 | tf_op jit(solution)/shard_map/ppermute | solution.py:58
  164.9 16.2 %all-to-all-start.8 = ((f32[16,48,128]{2,1,0:T(8,128)}), f32[16,48,128]{2,1,0:T(8,128)S(1)}, u32[]{:S(2)}, u32[]{:S(2)}) async-start(f32[16,48,128]{2,1,0:T(8,128)} %shard_map.100), calls=%async_computation.8 | async-start | bytes 786432 | tf_op jit(solution)/shard_map/all_to_all | solution.py:54
  (18 other events, 88.5 us)

commit v8 on v7

--- a/solution.py
+++ b/solution.py
@@ -9,8 +9,6 @@
 
 
 ITERS = 4
-SHIFT = 1.0625
-PULL = 0.375
 KEEP = 12
 CHUNKS = 5
 GRANT = 50
@@ -94,11 +92,22 @@
     return high, middle, rest - middle
 
 
-def stacked(high, middle, low):
-    line = lax.broadcasted_iota(jnp.int32, (EXTRA, high.shape[1]), 0)
-    value = jnp.where(line == 2, low, 0.0)
-    value = jnp.where(line == 1, middle, value)
-    return jnp.where(line == 0, high, value)
+def stacked(*rows):
+    line = lax.broadcasted_iota(jnp.int32, (EXTRA, rows[0].shape[1]), 0)
+    value = jnp.zeros(line.shape, F32)
+    for i, row in enumerate(rows):
+        value = jnp.where(line == i, row, value)
+    return value
+
+
+def lane_sums(value):
+    value = jnp.sum(value, 0, keepdims=True)
+    parts = [value[:, i : i + LANES] for i in range(0, value.shape[1], LANES)]
+    return sum(parts[1:], parts[0])
+
+
+def squares(slots):
+    return lane_sums(sum(slot[...] * slot[...] for slot in slots))
 
 
 def init_kernel(groups, copies, start_ref, *refs):
@@ -153,7 +162,7 @@
 def back_kernel(groups, steps, rows_ref, cols_ref, live_ref, kept_ref, tiles_ref, *refs):
     count = steps + 1
     vectors = [refs[i * groups : (i + 1) * groups] for i in range(count)]
-    out_ref, total, rounded, rest, sems = refs[count * groups :]
+    *shifts, out_ref, total, rounded, rest, sems = refs[count * groups :]
     copies = fetch(tiles_ref, rest, sems)
     owners, width, _ = total.shape
     group = lax.axis_index("grp")
@@ -170,8 +179,13 @@
     if count * width < LANES:
         grams.append(jnp.zeros((width, LANES - count * width), F32))
     high, middle, low = pieces(jnp.concatenate(grams, 1))
+    scales = []
+    if steps == 0:
+        scales = pieces(lane_sums(shifts[0][...]))[:2]
+    elif steps == 1:
+        scales = pieces(squares(vectors[1]))[:2] + pieces(squares(vectors[0]))[:2]
     for r in range(owners):
-        value = stacked(high[r : r + 1], middle[r : r + 1], low[r : r + 1])
+        value = stacked(high[r : r + 1], middle[r : r + 1], low[r : r + 1], *scales)
         out_ref[r, pl.ds(2 * width, EXTRA), :] = value.astype(BF16)
     for k, tile in each_tile(kept_ref, rest, copies):
         source = rows_ref[0, 0, k] ^ group
@@ -216,34 +230,46 @@
         refs[groups][...] = jnp.concatenate(rows, 0)
 
 
-def combine_kernel(groups, last, back_ref, *refs):
+def combine_kernel(groups, step, back_ref, *refs):
     direct = refs[:groups]
-    now_ref, before_ref, shift_ref = refs[groups : groups + 3]
-    outs = refs[groups + 3 :]
+    now_ref, shift_ref = refs[groups : groups + 2]
+    refs = refs[groups + 2 :]
+    width, edge = now_ref.shape
     owners = back_ref.shape[0]
-    width = now_ref.shape[0]
     image = direct[0][...]
     for s in range(1, groups):
         image = image + direct[s][...].astype(F32)
     for r in range(owners):
         image = image + whole(back_ref, r, width).astype(F32)
-    edge = now_ref.shape[1]
-    block = lax.axis_index("grp")
-    shift = shift_ref[:, pl.ds(pl.multiple_of(block * edge, edge), edge)]
-    new = 0.5 * image + (SHIFT - shift) * now_ref[...] - PULL * before_ref[...]
-    outs[0][...] = new
     sums = back_ref[0, pl.ds(2 * width, EXTRA), :].astype(F32)
     for r in range(1, owners):
         sums = sums + back_ref[r, pl.ds(2 * width, EXTRA), :].astype(F32)
     row = sums[0:1] + (sums[1:2] + sums[2:3])
-    if last:
-        outs[1][...] = jnp.broadcast_to(row, (EXTRA, LANES))
+    total = jnp.sum(sums, 1, keepdims=True)
+    block = lax.axis_index("grp")
+    diagonal = shift_ref[:, pl.ds(pl.multiple_of(block * edge, edge), edge)]
+    line = lax.broadcasted_iota(jnp.int32, (EXTRA, LANES), 0)
+    if step == 0:
+        new_ref, sent_ref, coef_ref = refs
+        shift = (total[3:4] + total[4:5]) * (1.0 / (owners * shift_ref.shape[1]))
+        coef_ref[...] = jnp.broadcast_to(shift, coef_ref.shape)
+        new = 0.5 * image + (shift - diagonal) * now_ref[...]
+    else:
+        before_ref, old_ref, new_ref, sent_ref = refs[:4]
+        shift, pull = old_ref[0:1, 0:1], old_ref[1:2, 0:1]
+        if step == 1:
+            pull = (total[3:4] + total[4:5]) / (total[5:6] + total[6:7])
+            refs[4][...] = jnp.where(line == 0, shift, pull)
+        new = 0.5 * image + (shift - diagonal) * now_ref[...] - pull * before_ref[...]
+    new_ref[...] = new
+    if step == ITERS - 1:
+        sent_ref[...] = jnp.broadcast_to(row, (EXTRA, LANES))
     else:
         rounded = halves(new).astype(BF16)
         extra = stacked(*pieces(row)).astype(BF16)
-        for r in range(outs[1].shape[0]):
-            outs[1][r, pl.ds(0, 2 * width), :] = rounded
-            outs[1][r, pl.ds(2 * width, EXTRA), :] = extra
+        for r in range(sent_ref.shape[0]):
+            sent_ref[r, pl.ds(0, 2 * width), :] = rounded
+            sent_ref[r, pl.ds(2 * width, EXTRA), :] = extra
 
 
 def factor(block):
@@ -288,11 +314,12 @@
         inv[here, done] = -plain(own_inverse, back)
 
 
-def step_results(j, low, inv, width):
+def step_results(j, low, inv, coef_ref, width):
     used = (j + 1) * width
-    value = low[pl.ds(width, used), :] - SHIFT * low[pl.ds(0, used), :]
+    shift, pull = coef_ref[0:1, 0:1], coef_ref[1:2, 0:1]
+    value = low[pl.ds(width, used), :] - shift * low[pl.ds(0, used), :]
     if j > 0:
-        value = value + PULL * jnp.concatenate(
+        value = value + pull * jnp.concatenate(
             [jnp.zeros((width, value.shape[1]), F32), low[pl.ds(0, j * width), :]], 0
         )
     image = plain(inv[pl.ds(j * width, width), pl.ds(0, used)], value)
@@ -305,7 +332,7 @@
     )
 
 
-def block_kernel(j, gram_ref, *refs):
+def block_kernel(j, gram_ref, coef_ref, *refs):
     outs = 2 if j == 0 else 4
     olds, (low_ref, inv_ref) = refs[:-outs], refs[-outs:][:2]
     if j > 0:
@@ -313,7 +340,9 @@
         inv_ref[...] = olds[1][...]
     next_rows(j, gram_ref[...], low_ref, inv_ref)
     if j > 0:
-        refs[-2][...], refs[-1][...] = step_results(j - 1, low_ref, inv_ref, gram_ref.shape[0])
+        refs[-2][...], refs[-1][...] = step_results(
+            j - 1, low_ref, inv_ref, coef_ref, gram_ref.shape[0]
+        )
 
 
 def gram_kernel(groups, chunk_ref, *refs):
@@ -345,7 +374,7 @@
         out_ref[r, pl.ds(last, EXTRA), :] = rows
 
 
-def finish_kernel(groups, parts_ref, old_low, old_inv, *refs):
+def finish_kernel(groups, parts_ref, coef_ref, old_low, old_inv, *refs):
     known = ITERS - 2
     early, refs = refs[: 2 * known], refs[2 * known :]
     vectors = [refs[i * groups : (i + 1) * groups] for i in range(ITERS + 1)]
@@ -367,7 +396,7 @@
     for j in range(known):
         proj_ref[j], fact_ref[j] = early[2 * j][...], early[2 * j + 1][...]
     for j in range(known, ITERS):
-        proj_ref[j], fact_ref[j] = step_results(j, low, inv, width)
+        proj_ref[j], fact_ref[j] = step_results(j, low, inv, coef_ref, width)
     for s in range(groups):
         value = plain(inv[pl.ds(ITERS * width, width), pl.ds(0, width)], vectors[0][s][...])
         for i in range(1, ITERS + 1):
@@ -405,17 +434,17 @@
         4,
     )
     shift = dual_shift[None, :]
-    def block(j, rows, state):
+    def block(j, rows, coef, state):
         return call(
             functools.partial(block_kernel, j),
             [shape(total, total)] * 2
             + [shape(width, ITERS * width), shape(width, width)] * (j > 0),
-            [VMEM] * (1 + len(state)),
-            (rows, *state),
+            [VMEM] * (2 + len(state)),
+            (rows, coef, *state),
             4,
         )
 
-    before = jnp.zeros((width, edge), F32)
+    before = coef = None
     basis = [slots]
     grams = []
     for step in range(ITERS):
@@ -426,8 +455,8 @@
         (parts,) = call(
             functools.partial(back_kernel, groups, step),
             [shape(owners, 2 * width + EXTRA, LANES, dtype=BF16)],
-            spaces + [VMEM] * len(flat),
-            (*tables, *flat),
+            spaces + [VMEM] * (len(flat) + (step == 0)),
+            (*tables, *flat, *[shift] * (step == 0)),
             GRANT,
             [pltpu.VMEM((owners, width, edge), F32), pltpu.VMEM((groups, width, edge), BF16), *rest],
             flops,
@@ -448,13 +477,14 @@
         direct = trade(direct[:groups])
         last = step == ITERS - 1
         second = shape(EXTRA, LANES) if last else shape(owners // 2, 2 * width + EXTRA, LANES, dtype=BF16)
-        new, sent = call(
-            functools.partial(combine_kernel, groups, last),
-            [shape(width, edge), second],
-            [VMEM] * (groups + 4),
-            (arrived, *direct, own, before, shift),
+        new, sent, *fresh = call(
+            functools.partial(combine_kernel, groups, step),
+            [shape(width, edge), second] + [shape(EXTRA, LANES)] * (step < 2),
+            [VMEM] * (groups + 3 + 2 * (step > 0)),
+            (arrived, *direct, own, shift, *[before, coef] * (step > 0)),
             4,
         )
+        coef = fresh[0] if fresh else coef
         before = own
         basis.append(trade([new] * groups))
 
@@ -478,13 +508,13 @@
     parts = same_core(parts)
     early = []
     for j, rows in enumerate(grams):
-        *state, proj, fact = [*block(j, rows, state), None, None][:4]
+        *state, proj, fact = [*block(j, rows, coef, state), None, None][:4]
         early += [proj, fact] * (j > 0)
     return call(
         functools.partial(finish_kernel, groups),
         [shape(ITERS, width, ITERS * width), shape(ITERS, width, width), shape(width, row_count)],
-        [VMEM] * (3 + len(early) + len(flat)),
-        (parts, *state, *early, *flat),
+        [VMEM] * (4 + len(early) + len(flat)),
+        (parts, coef, *state, *early, *flat),
         8,
         [pltpu.VMEM((total, total), F32), pltpu.VMEM((total, total), F32)],
     )

time: 188 us -> 188 us (level)
  no operation moved by 1% of the time
where the time goes in v8:
time: 188 us; the launch traced here: 187 us
  starting transfers between devices  106 us (56%)
  Pallas kernels  44.8 us (24%)
  waiting for transfers between devices  33.5 us (18%)
    pallas_call x20, Pallas kernels, call(): pl.pallas_call(kernel, out_shape=out_shape, in_specs=[spec(space) for spa...  44.8 us
    all_to_all x4, starting transfers between devices, exchange(): return lax.all_to_all(parts, axis, split_axis=0, concat_axis=0, tiled=True)  39.3 us
    all_to_all x5, starting transfers between devices, same_core(): lax.all_to_all(parts, 'row', 0, 0, axis_index_groups=groups, tiled=True)  34.5 us
    ppermute x29, starting transfers between devices, swapped(): lax.ppermute(value, axis, [(i, i ^ mask) for i in range(lax.axis_size(axi...  32.4 us
    ppermute x29, waiting for transfers between devices, swapped(): lax.ppermute(value, axis, [(i, i ^ mask) for i in range(lax.axis_size(axi...  28.3 us
    all_to_all x5, waiting for transfers between devices, same_core(): lax.all_to_all(parts, 'row', 0, 0, axis_index_groups=groups, tiled=True)  5.06 us
  transfers between devices with their start and end apart: 38, of which 26 were waited for; matrix products, arithmetic and copies ran while one was open for 0% of the time, Pallas kernels for 18%

profile of v8, /device:TPU:1, one launch (start us, length us, event | category | flops | bytes accessed | tf_op | source)
XLA Modules:
  0.0 187.0 jit_solution(116397506494275153)
XLA Ops:
  2.3 8.4 %all-to-all-start.1 = ((bf16[16,64,128]{2,1,0:T(8,128)(2,1)}), bf16[16,64,128]{2,1,0:T(8,128)(2,1)S(1)}, u32[]{:S(2)}, u32[]{:S(2)}) async-start(bf16[16,64,128]{2,1,0:T(8,128)(2,1)} %get-tuple-element.51), calls=%async_computation.1 | async-start | bytes 524288 | tf_op jit(solution)/shard_map/all_to_all | solution.py:52
  12.8 3.5 %shard_map.87 = bf16[32,72,128]{2,1,0:T(8,128)(2,1)} custom-call(s32[1,1,32]{2,1,0:T(1,128)S(1)} %copy-done.2, s32[1,1,32]{2,1,0:T(1,128)S(1)} %copy-done.3, s32[1,1]{1,0:T(1,128)S(6)} %copy.9.live_ref, bf16[12,256,256]{2,1,0:T(8,128)(2,1)S(1)} %shard_map.85.kept_ref, bf16[1,1,32,256,256]{4,3,2,1,0:T(8,128)(2,1)} %tiles_ref.17, ...), custom_call_target="tpu_custom_call" | custom-call | flops 134217728 | bytes 1048576 | tf_op jit(solution)/shard_map/pallas_call | solution.py:30
  18.2 6.4 %all-to-all-start = ((bf16[32,72,128]{2,1,0:T(8,128)(2,1)}), bf16[32,72,128]{2,1,0:T(8,128)(2,1)S(1)}, u32[]{:S(2)}, u32[]{:S(2)}) async-start(bf16[32,72,128]{2,1,0:T(8,128)(2,1)} %shard_map.87), calls=%async_computation | async-start | bytes 1179648 | tf_op jit(solution)/shard_map/all_to_all | solution.py:46
  26.2 3.0 %shard_map.88 = (f32[32,256]{1,0:T(8,128)S(1)}, bf16[32,256]{1,0:T(8,128)(2,1)S(1)}, bf16[32,256]{1,0:T(8,128)(2,1)S(1)}, bf16[32,256]{1,0:T(8,128)(2,1)S(1)}) custom-call(s32[1,1,32]{2,1,0:T(1,128)S(1)} %copy-done.2, s32[1,1,32]{2,1,0:T(1,128)S(1)} %copy-done.3, s32[1,1]{1,0:T(1,128)S(6)} %copy.9.live_ref, bf16[12,256,256]{2,1,0:T(8,128)(2,1)S(1)} %shard_map.85.kept_ref, ...), custom_call_target="tpu_custom_call" | custom-call | flops 134217728 | bytes 1048576 | tf_op jit(solution)/shard_map/pallas_call | solution.py:30
  30.6 2.6 %collective-permute-start.2 = (bf16[32,256]{1,0:T(8,128)(2,1)S(1)}, bf16[32,256]{1,0:T(8,128)(2,1)S(1)}, u32[]{:S(2)}, u32[]{:S(2)}) collective-permute-start(bf16[32,256]{1,0:T(8,128)(2,1)S(1)} %get-tuple-element.54), channel_id=1, source_target_pairs={{0,64},{32,96},{64,0},{96,32},{1,65},{33,97},{65,1},{97,33},{2,66}... | collective-permute-start | bytes 49160 | tf_op jit(solution)/shard_map/ppermute | solution.py:56
  37.9 6.7 %all-to-all-start.3 = ((bf16[16,72,128]{2,1,0:T(8,128)(2,1)}), bf16[16,72,128]{2,1,0:T(8,128)(2,1)S(1)}, u32[]{:S(2)}, u32[]{:S(2)}) async-start(bf16[16,72,128]{2,1,0:T(8,128)(2,1)} %get-tuple-element.57), calls=%async_computation.3 | async-start | bytes 589824 | tf_op jit(solution)/shard_map/all_to_all | solution.py:52
  45.4 2.5 %collective-permute-start.4 = (f32[32,256]{1,0:T(8,128)S(1)}, f32[32,256]{1,0:T(8,128)S(1)}, u32[]{:S(2)}, u32[]{:S(2)}) collective-permute-start(f32[32,256]{1,0:T(8,128)S(1)} %get-tuple-element.56.refs_4_.refs_6_.refs_8_), channel_id=1, source_target_pairs={{0,32},{32,0},{64,96},{96,64},{1,33},{33,1},{65,97},{97,65},{2,34}... | collective-permute-start | bytes 98312 | tf_op jit(solution)/shard_map/ppermute | solution.py:56
  49.6 3.5 %shard_map.90 = bf16[32,72,128]{2,1,0:T(8,128)(2,1)} custom-call(s32[1,1,32]{2,1,0:T(1,128)S(1)} %copy-done.2, s32[1,1,32]{2,1,0:T(1,128)S(1)} %copy-done.3, s32[1,1]{1,0:T(1,128)S(6)} %copy.9.live_ref, bf16[12,256,256]{2,1,0:T(8,128)(2,1)S(1)} %shard_map.85.kept_ref, bf16[1,1,32,256,256]{4,3,2,1,0:T(8,128)(2,1)} %tiles_ref.17, ...), custom_call_target="tpu_custom_call" | custom-call | flops 134217728 | bytes 1048576 | tf_op jit(solution)/shard_map/pallas_call | solution.py:30
  53.2 11.0 %all-to-all-start.2 = ((bf16[32,72,128]{2,1,0:T(8,128)(2,1)}), bf16[32,72,128]{2,1,0:T(8,128)(2,1)S(1)}, u32[]{:S(2)}, u32[]{:S(2)}) async-start(bf16[32,72,128]{2,1,0:T(8,128)(2,1)} %shard_map.90), calls=%async_computation.2 | async-start | bytes 1179648 | tf_op jit(solution)/shard_map/all_to_all | solution.py:46
  65.8 3.0 %shard_map.91 = (f32[32,256]{1,0:T(8,128)S(1)}, bf16[32,256]{1,0:T(8,128)(2,1)S(1)}, bf16[32,256]{1,0:T(8,128)(2,1)S(1)}, bf16[32,256]{1,0:T(8,128)(2,1)S(1)}, f32[32,128]{1,0:T(8,128)S(1)}) custom-call(s32[1,1,32]{2,1,0:T(1,128)S(1)} %copy-done.2, s32[1,1,32]{2,1,0:T(1,128)S(1)} %copy-done.3, s32[1,1]{1,0:T(1,128)S(6)} %copy.9.live_ref, ...), custom_call_target="tpu_custom_call" | custom-call | flops 134217728 | bytes 1048576 | tf_op jit(solution)/shard_map/pallas_call | solution.py:30
  77.2 6.3 %all-to-all-start.5 = ((bf16[16,72,128]{2,1,0:T(8,128)(2,1)}), bf16[16,72,128]{2,1,0:T(8,128)(2,1)S(1)}, u32[]{:S(2)}, u32[]{:S(2)}) async-start(bf16[16,72,128]{2,1,0:T(8,128)(2,1)} %get-tuple-element.64), calls=%async_computation.5 | async-start | bytes 589824 | tf_op jit(solution)/shard_map/all_to_all | solution.py:52
  84.3 2.6 %collective-permute-start.11 = (f32[32,256]{1,0:T(8,128)S(1)}, f32[32,256]{1,0:T(8,128)S(1)}, u32[]{:S(2)}, u32[]{:S(2)}) collective-permute-start(f32[32,256]{1,0:T(8,128)S(1)} %get-tuple-element.63.refs_8_.refs_4_.refs_6_.refs_12_), channel_id=1, source_target_pairs={{0,32},{32,0},{64,96},{96,64},{1,33},{33,1},{65,97},{97,65},{2,34}... | collective-permute-start | bytes 98312 | tf_op jit(solution)/shard_map/ppermute | solution.py:56
  88.5 3.5 %shard_map.93 = bf16[32,72,128]{2,1,0:T(8,128)(2,1)} custom-call(s32[1,1,32]{2,1,0:T(1,128)S(1)} %copy-done.2, s32[1,1,32]{2,1,0:T(1,128)S(1)} %copy-done.3, s32[1,1]{1,0:T(1,128)S(6)} %copy.9.live_ref, bf16[12,256,256]{2,1,0:T(8,128)(2,1)S(1)} %shard_map.85.kept_ref, bf16[1,1,32,256,256]{4,3,2,1,0:T(8,128)(2,1)} %tiles_ref.17, ...), custom_call_target="tpu_custom_call" | custom-call | flops 134217728 | bytes 1048576 | tf_op jit(solution)/shard_map/pallas_call | solution.py:30
  92.1 11.0 %all-to-all-start.4 = ((bf16[32,72,128]{2,1,0:T(8,128)(2,1)}), bf16[32,72,128]{2,1,0:T(8,128)(2,1)S(1)}, u32[]{:S(2)}, u32[]{:S(2)}) async-start(bf16[32,72,128]{2,1,0:T(8,128)(2,1)} %shard_map.93), calls=%async_computation.4 | async-start | bytes 1179648 | tf_op jit(solution)/shard_map/all_to_all | solution.py:46
  104.9 3.0 %shard_map.94 = (f32[32,256]{1,0:T(8,128)S(1)}, bf16[32,256]{1,0:T(8,128)(2,1)S(1)}, bf16[32,256]{1,0:T(8,128)(2,1)S(1)}, bf16[32,256]{1,0:T(8,128)(2,1)S(1)}, f32[32,128]{1,0:T(8,128)S(1)}) custom-call(s32[1,1,32]{2,1,0:T(1,128)S(1)} %copy-done.2, s32[1,1,32]{2,1,0:T(1,128)S(1)} %copy-done.3, s32[1,1]{1,0:T(1,128)S(6)} %copy.9.live_ref, ...), custom_call_target="tpu_custom_call" | custom-call | flops 134217728 | bytes 1048576 | tf_op jit(solution)/shard_map/pallas_call | solution.py:30
  116.0 6.5 %all-to-all-start.7 = ((bf16[16,72,128]{2,1,0:T(8,128)(2,1)}), bf16[16,72,128]{2,1,0:T(8,128)(2,1)S(1)}, u32[]{:S(2)}, u32[]{:S(2)}) async-start(bf16[16,72,128]{2,1,0:T(8,128)(2,1)} %get-tuple-element.71), calls=%async_computation.7 | async-start | bytes 589824 | tf_op jit(solution)/shard_map/all_to_all | solution.py:52
  123.3 2.6 %collective-permute-start.18 = (f32[32,256]{1,0:T(8,128)S(1)}, f32[32,256]{1,0:T(8,128)S(1)}, u32[]{:S(2)}, u32[]{:S(2)}) collective-permute-start(f32[32,256]{1,0:T(8,128)S(1)} %get-tuple-element.70.refs_12_.refs_4_.refs_16_), channel_id=1, source_target_pairs={{0,32},{32,0},{64,96},{96,64},{1,33},{33,1},{65,97},{97,65},{2,34}... | collective-permute-start | bytes 98312 | tf_op jit(solution)/shard_map/ppermute | solution.py:56
  127.6 3.5 %shard_map.96 = bf16[32,72,128]{2,1,0:T(8,128)(2,1)} custom-call(s32[1,1,32]{2,1,0:T(1,128)S(1)} %copy-done.2, s32[1,1,32]{2,1,0:T(1,128)S(1)} %copy-done.3, s32[1,1]{1,0:T(1,128)S(6)} %copy.9.live_ref, bf16[12,256,256]{2,1,0:T(8,128)(2,1)S(1)} %shard_map.85.kept_ref, bf16[1,1,32,256,256]{4,3,2,1,0:T(8,128)(2,1)} %tiles_ref.17, ...), custom_call_target="tpu_custom_call" | custom-call | flops 134217728 | bytes 1048576 | tf_op jit(solution)/shard_map/pallas_call | solution.py:30
  131.1 11.0 %all-to-all-start.6 = ((bf16[32,72,128]{2,1,0:T(8,128)(2,1)}), bf16[32,72,128]{2,1,0:T(8,128)(2,1)S(1)}, u32[]{:S(2)}, u32[]{:S(2)}) async-start(bf16[32,72,128]{2,1,0:T(8,128)(2,1)} %shard_map.96), calls=%async_computation.6 | async-start | bytes 1179648 | tf_op jit(solution)/shard_map/all_to_all | solution.py:46
  143.8 3.0 %shard_map.97 = (f32[32,256]{1,0:T(8,128)S(1)}, bf16[32,256]{1,0:T(8,128)(2,1)S(1)}, bf16[32,256]{1,0:T(8,128)(2,1)S(1)}, bf16[32,256]{1,0:T(8,128)(2,1)S(1)}, f32[32,128]{1,0:T(8,128)S(1)}) custom-call(s32[1,1,32]{2,1,0:T(1,128)S(1)} %copy-done.2, s32[1,1,32]{2,1,0:T(1,128)S(1)} %copy-done.3, s32[1,1]{1,0:T(1,128)S(6)} %copy.9.live_ref, ...), custom_call_target="tpu_custom_call" | custom-call | flops 134217728 | bytes 1048576 | tf_op jit(solution)/shard_map/pallas_call | solution.py:30
  165.0 6.6 %all-to-all-start.8 = ((f32[16,48,128]{2,1,0:T(8,128)}), f32[16,48,128]{2,1,0:T(8,128)S(1)}, u32[]{:S(2)}, u32[]{:S(2)}) async-start(f32[16,48,128]{2,1,0:T(8,128)} %shard_map.100), calls=%async_computation.8 | async-start | bytes 786432 | tf_op jit(solution)/shard_map/all_to_all | solution.py:52
  175.5 2.4 %shard_map.103 = (f32[160,160]{1,0:T(8,128)S(1)}, f32[160,160]{1,0:T(8,128)S(1)}, f32[32,128]{1,0:T(8,128)S(1)}, f32[32,32]{1,0:T(8,128)S(1)}) custom-call(f32[32,128]{1,0:T(8,128)S(1)} %get-tuple-element.78.gram_ref, f32[8,128]{1,0:T(8,128)S(1)} %get-tuple-element.69.refs_7_.coef_ref, f32[160,160]{1,0:T(8,128)S(1)} %get-tuple-element.83.refs_0_, ...), custom_call_target="tpu_custom_call" | custom-call | flops 2000000 | bytes 1048576 | tf_op jit(solution)/shard_map/pallas_call | solution.py:30
  178.0 3.2 %all-to-all-done.8.parts_ref = f32[16,48,128]{2,1,0:T(8,128)S(1)} async-done(((f32[16,48,128]{2,1,0:T(8,128)}), f32[16,48,128]{2,1,0:T(8,128)S(1)}, u32[]{:S(2)}, u32[]{:S(2)}) %all-to-all-start.8) | async-done | bytes 393248 | tf_op jit(solution)/shard_map/all_to_all | solution.py:52
  181.1 5.9 %shard_map.104 = (f32[4,32,128]{2,1,0:T(8,128)}, f32[4,32,32]{2,1,0:T(8,128)}, f32[32,1024]{1,0:T(8,128)}) custom-call(f32[16,48,128]{2,1,0:T(8,128)S(1)} %all-to-all-done.8.parts_ref, f32[8,128]{1,0:T(8,128)S(1)} %get-tuple-element.69.refs_7_.coef_ref, f32[160,160]{1,0:T(8,128)S(1)} %get-tuple-element.85.old_low, f32[160,160]{1,0:T(8,128)S(1)} %get-tuple-element.86.old_inv, ...), custom_call_target="tpu_custom_call" | custom-call | flops 2000000 | bytes 1048576 | tf_op jit(solution)/shard_map/pallas_call | solution.py:30
  (80 shorter events, 63.7 us)
Async XLA Ops:
  2.3 16.0 %all-to-all-start.1 = ((bf16[16,64,128]{2,1,0:T(8,128)(2,1)}), bf16[16,64,128]{2,1,0:T(8,128)(2,1)S(1)}, u32[]{:S(2)}, u32[]{:S(2)}) async-start(bf16[16,64,128]{2,1,0:T(8,128)(2,1)} %get-tuple-element.51), calls=%async_computation.1 | async-start | bytes 524288 | tf_op jit(solution)/shard_map/all_to_all | solution.py:52
  18.2 18.8 %all-to-all-start = ((bf16[32,72,128]{2,1,0:T(8,128)(2,1)}), bf16[32,72,128]{2,1,0:T(8,128)(2,1)S(1)}, u32[]{:S(2)}, u32[]{:S(2)}) async-start(bf16[32,72,128]{2,1,0:T(8,128)(2,1)} %shard_map.87), calls=%async_computation | async-start | bytes 1179648 | tf_op jit(solution)/shard_map/all_to_all | solution.py:46
  30.6 4.4 %collective-permute-start.2 = (bf16[32,256]{1,0:T(8,128)(2,1)S(1)}, bf16[32,256]{1,0:T(8,128)(2,1)S(1)}, u32[]{:S(2)}, u32[]{:S(2)}) collective-permute-start(bf16[32,256]{1,0:T(8,128)(2,1)S(1)} %get-tuple-element.54), channel_id=1, source_target_pairs={{0,64},{32,96},{64,0},{96,32},{1,65},{33,97},{65,1},{97,33},{2,66}... | collective-permute-start | bytes 49160 | tf_op jit(solution)/shard_map/ppermute | solution.py:56
  37.9 15.2 %all-to-all-start.3 = ((bf16[16,72,128]{2,1,0:T(8,128)(2,1)}), bf16[16,72,128]{2,1,0:T(8,128)(2,1)S(1)}, u32[]{:S(2)}, u32[]{:S(2)}) async-start(bf16[16,72,128]{2,1,0:T(8,128)(2,1)} %get-tuple-element.57), calls=%async_computation.3 | async-start | bytes 589824 | tf_op jit(solution)/shard_map/all_to_all | solution.py:52
  44.6 4.1 %collective-permute-start.6 = (f32[32,256]{1,0:T(8,128)S(1)}, f32[32,256]{1,0:T(8,128)S(1)}, u32[]{:S(2)}, u32[]{:S(2)}) collective-permute-start(f32[32,256]{1,0:T(8,128)S(1)} %get-tuple-element.56.refs_4_.refs_6_.refs_8_), channel_id=1, source_target_pairs={{0,96},{32,64},{64,32},{96,0},{1,97},{33,65},{65,33},{97,1},{2,98}... | collective-permute-start | bytes 98312 | tf_op jit(solution)/shard_map/ppermute | solution.py:56
  44.7 4.3 %collective-permute-start.5 = (f32[32,256]{1,0:T(8,128)S(1)}, f32[32,256]{1,0:T(8,128)S(1)}, u32[]{:S(2)}, u32[]{:S(2)}) collective-permute-start(f32[32,256]{1,0:T(8,128)S(1)} %get-tuple-element.56.refs_4_.refs_6_.refs_8_), channel_id=1, source_target_pairs={{0,64},{32,96},{64,0},{96,32},{1,65},{33,97},{65,1},{97,33},{2,66}... | collective-permute-start | bytes 98312 | tf_op jit(solution)/shard_map/ppermute | solution.py:56
  45.4 4.2 %collective-permute-start.4 = (f32[32,256]{1,0:T(8,128)S(1)}, f32[32,256]{1,0:T(8,128)S(1)}, u32[]{:S(2)}, u32[]{:S(2)}) collective-permute-start(f32[32,256]{1,0:T(8,128)S(1)} %get-tuple-element.56.refs_4_.refs_6_.refs_8_), channel_id=1, source_target_pairs={{0,32},{32,0},{64,96},{96,64},{1,33},{33,1},{65,97},{97,65},{2,34}... | collective-permute-start | bytes 98312 | tf_op jit(solution)/shard_map/ppermute | solution.py:56
  53.2 23.1 %all-to-all-start.2 = ((bf16[32,72,128]{2,1,0:T(8,128)(2,1)}), bf16[32,72,128]{2,1,0:T(8,128)(2,1)S(1)}, u32[]{:S(2)}, u32[]{:S(2)}) async-start(bf16[32,72,128]{2,1,0:T(8,128)(2,1)} %shard_map.90), calls=%async_computation.2 | async-start | bytes 1179648 | tf_op jit(solution)/shard_map/all_to_all | solution.py:46
  70.3 4.4 %collective-permute-start.9 = (bf16[32,256]{1,0:T(8,128)(2,1)S(1)}, bf16[32,256]{1,0:T(8,128)(2,1)S(1)}, u32[]{:S(2)}, u32[]{:S(2)}) collective-permute-start(bf16[32,256]{1,0:T(8,128)(2,1)S(1)} %get-tuple-element.60), channel_id=1, source_target_pairs={{0,64},{32,96},{64,0},{96,32},{1,65},{33,97},{65,1},{97,33},{2,66}... | collective-permute-start | bytes 49160 | tf_op jit(solution)/shard_map/ppermute | solution.py:56
  72.1 4.1 %collective-permute-start.10 = (bf16[32,256]{1,0:T(8,128)(2,1)S(1)}, bf16[32,256]{1,0:T(8,128)(2,1)S(1)}, u32[]{:S(2)}, u32[]{:S(2)}) collective-permute-start(bf16[32,256]{1,0:T(8,128)(2,1)S(1)} %get-tuple-element.61), channel_id=1, source_target_pairs={{0,96},{32,64},{64,32},{96,0},{1,97},{33,65},{65,33},{97,1},{2,98}... | collective-permute-start | bytes 49160 | tf_op jit(solution)/shard_map/ppermute | solution.py:56
  77.2 14.9 %all-to-all-start.5 = ((bf16[16,72,128]{2,1,0:T(8,128)(2,1)}), bf16[16,72,128]{2,1,0:T(8,128)(2,1)S(1)}, u32[]{:S(2)}, u32[]{:S(2)}) async-start(bf16[16,72,128]{2,1,0:T(8,128)(2,1)} %get-tuple-element.64), calls=%async_computation.5 | async-start | bytes 589824 | tf_op jit(solution)/shard_map/all_to_all | solution.py:52
  83.5 4.1 %collective-permute-start.13 = (f32[32,256]{1,0:T(8,128)S(1)}, f32[32,256]{1,0:T(8,128)S(1)}, u32[]{:S(2)}, u32[]{:S(2)}) collective-permute-start(f32[32,256]{1,0:T(8,128)S(1)} %get-tuple-element.63.refs_8_.refs_4_.refs_6_.refs_12_), channel_id=1, source_target_pairs={{0,96},{32,64},{64,32},{96,0},{1,97},{33,65},{65,33},{97,1},{2,98}... | collective-permute-start | bytes 98312 | tf_op jit(solution)/shard_map/ppermute | solution.py:56
  84.3 4.3 %collective-permute-start.12 = (f32[32,256]{1,0:T(8,128)S(1)}, f32[32,256]{1,0:T(8,128)S(1)}, u32[]{:S(2)}, u32[]{:S(2)}) collective-permute-start(f32[32,256]{1,0:T(8,128)S(1)} %get-tuple-element.63.refs_8_.refs_4_.refs_6_.refs_12_), channel_id=1, source_target_pairs={{0,64},{32,96},{64,0},{96,32},{1,65},{33,97},{65,1},{97,33},{2,66}... | collective-permute-start | bytes 98312 | tf_op jit(solution)/shard_map/ppermute | solution.py:56
  84.3 4.3 %collective-permute-start.11 = (f32[32,256]{1,0:T(8,128)S(1)}, f32[32,256]{1,0:T(8,128)S(1)}, u32[]{:S(2)}, u32[]{:S(2)}) collective-permute-start(f32[32,256]{1,0:T(8,128)S(1)} %get-tuple-element.63.refs_8_.refs_4_.refs_6_.refs_12_), channel_id=1, source_target_pairs={{0,32},{32,0},{64,96},{96,64},{1,33},{33,1},{65,97},{97,65},{2,34}... | collective-permute-start | bytes 98312 | tf_op jit(solution)/shard_map/ppermute | solution.py:56
  92.1 23.1 %all-to-all-start.4 = ((bf16[32,72,128]{2,1,0:T(8,128)(2,1)}), bf16[32,72,128]{2,1,0:T(8,128)(2,1)S(1)}, u32[]{:S(2)}, u32[]{:S(2)}) async-start(bf16[32,72,128]{2,1,0:T(8,128)(2,1)} %shard_map.93), calls=%async_computation.4 | async-start | bytes 1179648 | tf_op jit(solution)/shard_map/all_to_all | solution.py:46
  109.4 4.4 %collective-permute-start.16 = (bf16[32,256]{1,0:T(8,128)(2,1)S(1)}, bf16[32,256]{1,0:T(8,128)(2,1)S(1)}, u32[]{:S(2)}, u32[]{:S(2)}) collective-permute-start(bf16[32,256]{1,0:T(8,128)(2,1)S(1)} %get-tuple-element.67), channel_id=1, source_target_pairs={{0,64},{32,96},{64,0},{96,32},{1,65},{33,97},{65,1},{97,33},{2,66}... | collective-permute-start | bytes 49160 | tf_op jit(solution)/shard_map/ppermute | solution.py:56
  116.0 15.1 %all-to-all-start.7 = ((bf16[16,72,128]{2,1,0:T(8,128)(2,1)}), bf16[16,72,128]{2,1,0:T(8,128)(2,1)S(1)}, u32[]{:S(2)}, u32[]{:S(2)}) async-start(bf16[16,72,128]{2,1,0:T(8,128)(2,1)} %get-tuple-element.71), calls=%async_computation.7 | async-start | bytes 589824 | tf_op jit(solution)/shard_map/all_to_all | solution.py:52
  123.3 4.3 %collective-permute-start.19 = (f32[32,256]{1,0:T(8,128)S(1)}, f32[32,256]{1,0:T(8,128)S(1)}, u32[]{:S(2)}, u32[]{:S(2)}) collective-permute-start(f32[32,256]{1,0:T(8,128)S(1)} %get-tuple-element.70.refs_12_.refs_4_.refs_16_), channel_id=1, source_target_pairs={{0,64},{32,96},{64,0},{96,32},{1,65},{33,97},{65,1},{97,33},{2,66}... | collective-permute-start | bytes 98312 | tf_op jit(solution)/shard_map/ppermute | solution.py:56
  123.3 4.3 %collective-permute-start.18 = (f32[32,256]{1,0:T(8,128)S(1)}, f32[32,256]{1,0:T(8,128)S(1)}, u32[]{:S(2)}, u32[]{:S(2)}) collective-permute-start(f32[32,256]{1,0:T(8,128)S(1)} %get-tuple-element.70.refs_12_.refs_4_.refs_16_), channel_id=1, source_target_pairs={{0,32},{32,0},{64,96},{96,64},{1,33},{33,1},{65,97},{97,65},{2,34}... | collective-permute-start | bytes 98312 | tf_op jit(solution)/shard_map/ppermute | solution.py:56
  131.1 23.1 %all-to-all-start.6 = ((bf16[32,72,128]{2,1,0:T(8,128)(2,1)}), bf16[32,72,128]{2,1,0:T(8,128)(2,1)S(1)}, u32[]{:S(2)}, u32[]{:S(2)}) async-start(bf16[32,72,128]{2,1,0:T(8,128)(2,1)} %shard_map.96), calls=%async_computation.6 | async-start | bytes 1179648 | tf_op jit(solution)/shard_map/all_to_all | solution.py:46
  148.3 4.4 %collective-permute-start.23 = (bf16[32,256]{1,0:T(8,128)(2,1)S(1)}, bf16[32,256]{1,0:T(8,128)(2,1)S(1)}, u32[]{:S(2)}, u32[]{:S(2)}) collective-permute-start(bf16[32,256]{1,0:T(8,128)(2,1)S(1)} %get-tuple-element.74), channel_id=1, source_target_pairs={{0,64},{32,96},{64,0},{96,32},{1,65},{33,97},{65,1},{97,33},{2,66}... | collective-permute-start | bytes 49160 | tf_op jit(solution)/shard_map/ppermute | solution.py:56
  150.1 4.1 %collective-permute-start.24 = (bf16[32,256]{1,0:T(8,128)(2,1)S(1)}, bf16[32,256]{1,0:T(8,128)(2,1)S(1)}, u32[]{:S(2)}, u32[]{:S(2)}) collective-permute-start(bf16[32,256]{1,0:T(8,128)(2,1)S(1)} %get-tuple-element.75), channel_id=1, source_target_pairs={{0,96},{32,64},{64,32},{96,0},{1,97},{33,65},{65,33},{97,1},{2,98}... | collective-permute-start | bytes 49160 | tf_op jit(solution)/shard_map/ppermute | solution.py:56
  156.5 4.4 %collective-permute-start.26 = (f32[32,256]{1,0:T(8,128)S(1)}, f32[32,256]{1,0:T(8,128)S(1)}, u32[]{:S(2)}, u32[]{:S(2)}) collective-permute-start(f32[32,256]{1,0:T(8,128)S(1)} %get-tuple-element.77.refs_16_.refs_20_), channel_id=1, source_target_pairs={{0,64},{32,96},{64,0},{96,32},{1,65},{33,97},{65,1},{97,33},{2,66}... | collective-permute-start | bytes 98312 | tf_op jit(solution)/shard_map/ppermute | solution.py:56
  165.0 16.2 %all-to-all-start.8 = ((f32[16,48,128]{2,1,0:T(8,128)}), f32[16,48,128]{2,1,0:T(8,128)S(1)}, u32[]{:S(2)}, u32[]{:S(2)}) async-start(f32[16,48,128]{2,1,0:T(8,128)} %shard_map.100), calls=%async_computation.8 | async-start | bytes 786432 | tf_op jit(solution)/shard_map/all_to_all | solution.py:52
  (18 other events, 79.0 us)

commit v9 on v8

--- a/solution.py
+++ b/solution.py
@@ -9,6 +9,8 @@
 
 
 ITERS = 4
+FRESH = 0.1
+
 KEEP = 12
 CHUNKS = 5
 GRANT = 50
@@ -107,7 +109,8 @@
 
 
 def squares(slots):
-    return lane_sums(sum(slot[...] * slot[...] for slot in slots))
+    parts = [slot[...] * slot[...] for slot in slots]
+    return lane_sums((parts[0] + parts[1]) + (parts[2] + parts[3]))
 
 
 def init_kernel(groups, copies, start_ref, *refs):
@@ -128,19 +131,18 @@
     copy.wait()
 
 
+def fetched(tiles_ref, rest, sems, c):
+    per_chunk = rest.shape[0] // CHUNKS
+    return pltpu.make_async_copy(
+        tiles_ref.at[0, 0, pl.ds(KEEP + c * per_chunk, per_chunk)],
+        rest.at[pl.ds(c * per_chunk, per_chunk)],
+        sems.at[c],
+    )
+
+
 def fetch(tiles_ref, rest, sems):
-    per_chunk = rest.shape[0] // CHUNKS
-    copies = [
-        pltpu.make_async_copy(
-            tiles_ref.at[0, 0, pl.ds(KEEP + c * per_chunk, per_chunk)],
-            rest.at[pl.ds(c * per_chunk, per_chunk)],
-            sems.at[c],
-        )
-        for c in range(CHUNKS)
-    ]
-    for copy in copies:
-        copy.start()
-    return copies
+    for c in range(CHUNKS):
+        fetched(tiles_ref, rest, sems, c).start()
 
 
 def clear(total):
@@ -149,33 +151,44 @@
         total[i] = jnp.zeros(total.shape[1:], F32)
 
 
-def each_tile(kept_ref, rest, copies):
+def each_tile(kept_ref, tiles_ref, rest, sems, visit):
     per_chunk = rest.shape[0] // CHUNKS
     for k in range(KEEP):
-        yield k, kept_ref[k]
-    for c in range(CHUNKS):
-        copies[c].wait()
-        for k in range(c * per_chunk, (c + 1) * per_chunk):
-            yield KEEP + k, rest[k]
+        visit(k, kept_ref[k])
+
+    @pl.loop(0, CHUNKS)
+    def _(c):
+        fetched(tiles_ref, rest, sems, c).wait()
+        for i in range(per_chunk):
+            k = c * per_chunk + i
+            visit(KEEP + k, rest[k])
+
+
+def gram_blocks(vectors, group, ordered):
+    groups = len(vectors[0])
+    width = vectors[0][0].shape[0]
+    for i, slots in enumerate(vectors):
+        for s in range(groups):
+            ordered[group ^ s, pl.ds(i * width, width), :] = slots[s][...]
+    last = pl.ds((len(vectors) - 1) * width, width)
+    value = across(ordered[0, last, :], ordered[0])
+    for s in range(1, groups):
+        value = value + across(ordered[s, last, :], ordered[s])
+    return [value[:, i * width : (i + 1) * width] for i in range(len(vectors))]
 
 
 def back_kernel(groups, steps, rows_ref, cols_ref, live_ref, kept_ref, tiles_ref, *refs):
     count = steps + 1
     vectors = [refs[i * groups : (i + 1) * groups] for i in range(count)]
-    *shifts, out_ref, total, rounded, rest, sems = refs[count * groups :]
-    copies = fetch(tiles_ref, rest, sems)
+    *shifts, out_ref, total, rounded, ordered, rest, sems = refs[count * groups :]
+    fetch(tiles_ref, rest, sems)
     owners, width, _ = total.shape
     group = lax.axis_index("grp")
     live = live_ref[0, 0]
     clear(total)
     for s in range(groups):
         rounded[s] = vectors[steps][s][...].astype(BF16)
-    grams = []
-    for i in range(count):
-        value = across(vectors[steps][0][...], vectors[i][0][...])
-        for s in range(1, groups):
-            value = value + across(vectors[steps][s][...], vectors[i][s][...])
-        grams.append(value)
+    grams = gram_blocks(vectors, group, ordered)
     if count * width < LANES:
         grams.append(jnp.zeros((width, LANES - count * width), F32))
     high, middle, low = pieces(jnp.concatenate(grams, 1))
@@ -187,12 +200,15 @@
     for r in range(owners):
         value = stacked(high[r : r + 1], middle[r : r + 1], low[r : r + 1], *scales)
         out_ref[r, pl.ds(2 * width, EXTRA), :] = value.astype(BF16)
-    for k, tile in each_tile(kept_ref, rest, copies):
+
+    def visit(k, tile):
         source = rows_ref[0, 0, k] ^ group
         product = lax.dot_general(
             rounded[source], tile, (((1,), (0,)), ((), ())), preferred_element_type=F32
         )
         total[cols_ref[0, 0, k]] += jnp.where(k < live, product, jnp.zeros_like(product))
+
+    each_tile(kept_ref, tiles_ref, rest, sems, visit)
     for r in range(owners):
         out_ref[r, pl.ds(0, 2 * width), :] = halves(total[r]).astype(BF16)
 
@@ -201,13 +217,14 @@
     groups, rows_ref, cols_ref, live_ref, kept_ref, tiles_ref, same_ref, other_ref, *refs
 ):
     outs, (total, rest, sems) = refs[:groups], refs[-3:]
-    copies = fetch(tiles_ref, rest, sems)
+    fetch(tiles_ref, rest, sems)
     width = outs[0].shape[0]
     group = lax.axis_index("grp")
     core = lax.axis_index("row") & 1
     live = live_ref[0, 0]
     clear(total)
-    for k, tile in each_tile(kept_ref, rest, copies):
+
+    def visit(k, tile):
         target = rows_ref[0, 0, k] ^ group
         col = cols_ref[0, 0, k]
         place = col >> 1
@@ -218,6 +235,8 @@
             vectors, tile, (((1,), (1,)), ((), ())), preferred_element_type=F32
         )
         total[target] += jnp.where(k < live, product, jnp.zeros_like(product))
+
+    each_tile(kept_ref, tiles_ref, rest, sems, visit)
     for s in range(groups):
         outs[s][...] = total[s].astype(outs[s].dtype)
     if same_ref.shape[1] > 2 * width:
@@ -346,15 +365,10 @@
 
 
 def gram_kernel(groups, chunk_ref, *refs):
-    out_ref = refs[-1]
+    out_ref, ordered = refs[-2:]
     vectors = [refs[i * groups : (i + 1) * groups] for i in range(ITERS + 1)]
     width = vectors[0][0].shape[0]
-    grams = []
-    for i in range(ITERS + 1):
-        value = across(vectors[ITERS][0][...], vectors[i][0][...])
-        for s in range(1, groups):
-            value = value + across(vectors[ITERS][s][...], vectors[i][s][...])
-        grams.append(value)
+    grams = gram_blocks(vectors, lax.axis_index("grp"), ordered)
     parts = LANES // width
     rows = width // parts
     packed = jnp.concatenate([grams[ITERS][p * rows : (p + 1) * rows] for p in range(parts)], 1)
@@ -378,7 +392,7 @@
     known = ITERS - 2
     early, refs = refs[: 2 * known], refs[2 * known :]
     vectors = [refs[i * groups : (i + 1) * groups] for i in range(ITERS + 1)]
-    proj_ref, fact_ref, out_ref, low, inv = refs[(ITERS + 1) * groups :]
+    proj_ref, fact_ref, out_ref, fresh_ref, low, inv = refs[(ITERS + 1) * groups :]
     owners = parts_ref.shape[0]
     width, edge = vectors[0][0].shape
     group = lax.axis_index("grp")
@@ -393,6 +407,13 @@
     count = LANES // width
     corner = jnp.concatenate([sums[width:, p * width : (p + 1) * width] for p in range(count)], 0)
     next_rows(ITERS, jnp.concatenate([sums[:width], corner], 1), low, inv)
+    square = low[...] * low[...]
+    on_diagonal = lax.broadcasted_iota(jnp.int32, square.shape, 0) == lax.broadcasted_iota(
+        jnp.int32, square.shape, 1
+    )
+    kept = jnp.sum(jnp.where(on_diagonal, square, 0.0), 1, keepdims=True)
+    bad = jnp.where(kept > FRESH * jnp.sum(square, 1, keepdims=True), 0.0, 1.0)
+    fresh_ref[...] = jnp.broadcast_to(jnp.max(bad, 0, keepdims=True), fresh_ref.shape)
     for j in range(known):
         proj_ref[j], fact_ref[j] = early[2 * j][...], early[2 * j + 1][...]
     for j in range(known, ITERS):
@@ -405,6 +426,141 @@
             )
         block = group ^ s
         out_ref[:, pl.ds(pl.multiple_of(block * edge, edge), edge)] = value
+
+
+def in_order(parts, dim):
+    parts = jnp.moveaxis(parts, 0, dim)
+    lengths = parts.shape
+    return parts.reshape(*lengths[:dim], lengths[dim] * lengths[dim + 1], *lengths[dim + 2 :])
+
+
+def copy_for_each(value, axis):
+    size = lax.axis_size(axis)
+    return lax.all_to_all(
+        jnp.broadcast_to(value[None], (size, *value.shape)), axis, 0, 0, tiled=True
+    )
+
+
+def gathered_copies(value, axis, dim):
+    return in_order(lax.all_gather(value, axis), dim)
+
+
+def split_up(value, dim, size):
+    before, after = (value.shape[:dim], value.shape[dim + 1 :])
+    return jnp.moveaxis(value.reshape(*before, size, -1, *after), dim, 0)
+
+
+def sent_and_summed(value, axis, dim):
+    parts = split_up(value, dim, lax.axis_size(axis))
+    arrived = lax.all_to_all(parts, axis, split_axis=0, concat_axis=0, tiled=True)
+    return arrived.astype(jnp.float32).sum(axis=0)
+
+
+def of_everyone(value, axis):
+    return copy_for_each(value, axis).sum(axis=0)
+
+
+def inner_product(left, right):
+    return lax.dot_general(
+        left,
+        right,
+        (((1,), (1,)), ((), ())),
+        precision=lax.Precision.HIGHEST,
+        preferred_element_type=jnp.float32,
+    )
+
+
+def apply_matrix(left, right):
+    return jnp.dot(left, right, precision=lax.Precision.HIGHEST, preferred_element_type=jnp.float32)
+
+
+def step_by_step(tiles, tile_rows, tile_cols, live_tiles, dual_shift, start_block):
+    matrix = tiles[0, 0]
+    rows_here = tile_rows[0, 0]
+    cols_here = tile_cols[0, 0]
+    tile_count = matrix.shape[0]
+    tile_edge = matrix.shape[1]
+    vec_width = start_block.shape[0]
+    row_count = start_block.shape[1]
+    group_count = lax.axis_size("grp")
+    owner_count = lax.axis_size("row")
+    owned_blocks = row_count // tile_edge
+    quarter_tiles = owned_blocks // group_count
+    column_tiles = quarter_tiles * owner_count
+    group_index = lax.axis_index("grp")
+    live_mask = (jnp.arange(tile_count) < live_tiles[0, 0]).astype(jnp.float32)
+    row_table = (rows_here[:, None] == jnp.arange(owned_blocks)[None, :]).astype(
+        jnp.float32
+    ) * live_mask[:, None]
+    col_table = (cols_here[:, None] == jnp.arange(column_tiles)[None, :]).astype(
+        jnp.float32
+    ) * live_mask[:, None]
+
+    def partial_of(full_rows, group_rows):
+        gathered = gathered_copies(group_rows, "row", 1)
+        forward = jnp.einsum(
+            "kbc,brc->kbr",
+            jnp.take(gathered, cols_here, axis=1),
+            matrix,
+            preferred_element_type=jnp.float32,
+        )
+        direct = jnp.einsum("kbr,bi->kir", forward, row_table)
+        backward = jnp.einsum(
+            "kbr,brc->kbc",
+            jnp.take(full_rows, rows_here, axis=1),
+            matrix,
+            preferred_element_type=jnp.float32,
+        )
+        spread = jnp.einsum("kbc,bj->kjc", backward, col_table)
+        mine = sent_and_summed(spread.astype(jnp.bfloat16), "row", 1)
+        placed = lax.dynamic_update_slice_in_dim(
+            jnp.zeros_like(direct), mine, group_index * quarter_tiles, 1
+        )
+        return 0.5 * (direct + placed)
+
+    def split_parts(vectors):
+        rounded = vectors.astype(jnp.bfloat16).reshape(vec_width, owned_blocks, tile_edge)
+        return (
+            rounded,
+            lax.dynamic_slice_in_dim(rounded, group_index * quarter_tiles, quarter_tiles, 1),
+        )
+
+    def finish_sum(partial_value):
+        return of_everyone(partial_value, "grp").reshape(vec_width, row_count)
+
+    def reduce_dots(values):
+        return lax.psum(values, "row")
+
+    def orthonormal(block, gram_matrix):
+        lower_factor = jnp.linalg.cholesky(gram_matrix)
+        return (
+            lax.linalg.triangular_solve(lower_factor, block, left_side=True, lower=True),
+            lower_factor,
+        )
+
+    current, _ = orthonormal(start_block, reduce_dots(inner_product(start_block, start_block)))
+    total_cols = ITERS * vec_width
+    basis_rows = jnp.zeros((total_cols, current.shape[1]), jnp.float32)
+    projections = jnp.zeros((ITERS, vec_width, total_cols), jnp.float32)
+    factors = jnp.zeros((ITERS, vec_width, vec_width), jnp.float32)
+
+    def lanczos_step(step_index, state_now):
+        current, basis_rows, projections, factors = state_now
+        basis_rows = lax.dynamic_update_slice_in_dim(basis_rows, current, step_index * vec_width, 0)
+        full_rows, group_rows = split_parts(current)
+        image = finish_sum(partial_of(full_rows, group_rows)) - current * dual_shift[None, :]
+        first_coef = reduce_dots(inner_product(image, basis_rows))
+        image = image - apply_matrix(first_coef, basis_rows)
+        gram_matrix = reduce_dots(inner_product(image, image))
+        current, lower_factor = orthonormal(image, gram_matrix)
+        projections = lax.dynamic_update_index_in_dim(projections, first_coef, step_index, 0)
+        factors = lax.dynamic_update_index_in_dim(factors, lower_factor, step_index, 0)
+        return (current, basis_rows, projections, factors)
+
+    current, basis_rows, projections, factors = lax.fori_loop(
+        0, ITERS, lanczos_step, (current, basis_rows, projections, factors)
+    )
+    return (projections, factors, current)
 
 
 def per_device(tiles, tile_rows, tile_cols, live_tiles, dual_shift, start_block):
@@ -434,6 +590,7 @@
         4,
     )
     shift = dual_shift[None, :]
+
     def block(j, rows, coef, state):
         return call(
             functools.partial(block_kernel, j),
@@ -458,7 +615,12 @@
             spaces + [VMEM] * (len(flat) + (step == 0)),
             (*tables, *flat, *[shift] * (step == 0)),
             GRANT,
-            [pltpu.VMEM((owners, width, edge), F32), pltpu.VMEM((groups, width, edge), BF16), *rest],
+            [
+                pltpu.VMEM((owners, width, edge), F32),
+                pltpu.VMEM((groups, width, edge), BF16),
+                pltpu.VMEM((groups, (step + 1) * width, edge), F32),
+                *rest,
+            ],
             flops,
         )
         arrived = exchange(parts, "row")
@@ -496,6 +658,7 @@
         [VMEM] * (1 + len(flat)),
         (sent, *flat),
         4,
+        [pltpu.VMEM((groups, total, edge), F32)],
     )
     (parts,) = call(
         pair_kernel,
@@ -510,14 +673,21 @@
     for j, rows in enumerate(grams):
         *state, proj, fact = [*block(j, rows, coef, state), None, None][:4]
         early += [proj, fact] * (j > 0)
-    return call(
+    *results, bad = call(
         functools.partial(finish_kernel, groups),
-        [shape(ITERS, width, ITERS * width), shape(ITERS, width, width), shape(width, row_count)],
+        [
+            shape(ITERS, width, ITERS * width),
+            shape(ITERS, width, width),
+            shape(width, row_count),
+            shape(EXTRA, LANES),
+        ],
         [VMEM] * (4 + len(early) + len(flat)),
         (parts, coef, *state, *early, *flat),
         8,
         [pltpu.VMEM((total, total), F32), pltpu.VMEM((total, total), F32)],
     )
+    inputs = (tiles, tile_rows, tile_cols, live_tiles, dual_shift, start_block)
+    return lax.cond(bad[0, 0] < 0.5, lambda: tuple(results), lambda: step_by_step(*inputs))
 
 
 def solution(mesh):

time: 188 us -> 190 us (1.011)
  transfers between devices with their start and end apart: 38 -> 38, of which waited for: 26 -> 24; matrix products, arithmetic and copies ran while one was open for 0% -> 0% of each run, Pallas kernels for 18% -> 18%
where the time goes in v9:
time: 190 us; the launch traced here: 189 us
  starting transfers between devices  106 us (56%)
  Pallas kernels  46 us (24%)
  waiting for transfers between devices  33.2 us (17%)
  between operations  2.47 us (1%)
    pallas_call x20, Pallas kernels, call(): pl.pallas_call(kernel, out_shape=out_shape, in_specs=[spec(space) for spa...  46 us
    all_to_all x4, starting transfers between devices, exchange(): return lax.all_to_all(parts, axis, split_axis=0, concat_axis=0, tiled=True)  39.7 us
    all_to_all x5, starting transfers between devices, same_core(): lax.all_to_all(parts, 'row', 0, 0, axis_index_groups=groups, tiled=True)  34.5 us
    ppermute x29, starting transfers between devices, swapped(): lax.ppermute(value, axis, [(i, i ^ mask) for i in range(lax.axis_size(axi...  32.2 us
    ppermute x29, waiting for transfers between devices, swapped(): lax.ppermute(value, axis, [(i, i ^ mask) for i in range(lax.axis_size(axi...  28.5 us
    all_to_all x5, waiting for transfers between devices, same_core(): lax.all_to_all(parts, 'row', 0, 0, axis_index_groups=groups, tiled=True)  4.71 us
  transfers between devices with their start and end apart: 38, of which 24 were waited for; matrix products, arithmetic and copies ran while one was open for 0% of the time, Pallas kernels for 18%

profile of v9, /device:TPU:1, one launch (start us, length us, event | category | flops | bytes accessed | tf_op | source)
XLA Modules:
  0.0 189.1 jit_solution(11317096371356086690)
XLA Ops:
  2.3 8.4 %all-to-all-start.3 = ((bf16[16,64,128]{2,1,0:T(8,128)(2,1)}), bf16[16,64,128]{2,1,0:T(8,128)(2,1)S(1)}, u32[]{:S(2)}, u32[]{:S(2)}) async-start(bf16[16,64,128]{2,1,0:T(8,128)(2,1)} %get-tuple-element.360), calls=%async_computation.3 | async-start | bytes 524288 | tf_op jit(solution)/shard_map/all_to_all | solution.py:54
  13.4 3.3 %shard_map.87 = bf16[32,72,128]{2,1,0:T(8,128)(2,1)} custom-call(s32[1,1,32]{2,1,0:T(1,128)S(1)} %copy-done.4, s32[1,1,32]{2,1,0:T(1,128)S(1)} %copy-done.3, s32[1,1]{1,0:T(1,128)S(6)} %copy.112.live_ref, bf16[12,256,256]{2,1,0:T(8,128)(2,1)S(1)} %shard_map.85.kept_ref, bf16[1,1,32,256,256]{4,3,2,1,0:T(8,128)(2,1)S(1)} %copy-done, ...), custom_call_target="tpu_custom_call" | custom-call | flops 134217728 | bytes 1048576 | tf_op jit(solution)/shard_map/pallas_call | solution.py:32
  18.3 6.7 %all-to-all-start.2 = ((bf16[32,72,128]{2,1,0:T(8,128)(2,1)}), bf16[32,72,128]{2,1,0:T(8,128)(2,1)S(1)}, u32[]{:S(2)}, u32[]{:S(2)}) async-start(bf16[32,72,128]{2,1,0:T(8,128)(2,1)} %shard_map.87), calls=%async_computation.2 | async-start | bytes 1179648 | tf_op jit(solution)/shard_map/all_to_all | solution.py:48
  26.6 3.0 %shard_map.88 = (f32[32,256]{1,0:T(8,128)S(1)}, bf16[32,256]{1,0:T(8,128)(2,1)S(1)}, bf16[32,256]{1,0:T(8,128)(2,1)S(1)}, bf16[32,256]{1,0:T(8,128)(2,1)S(1)}) custom-call(s32[1,1,32]{2,1,0:T(1,128)S(1)} %copy-done.4, s32[1,1,32]{2,1,0:T(1,128)S(1)} %copy-done.3, s32[1,1]{1,0:T(1,128)S(6)} %copy.112.live_ref, bf16[12,256,256]{2,1,0:T(8,128)(2,1)S(1)} %shard_map.85.kept_ref, ...), custom_call_target="tpu_custom_call" | custom-call | flops 134217728 | bytes 1048576 | tf_op jit(solution)/shard_map/pallas_call | solution.py:32
  31.0 2.6 %collective-permute-start.2 = (bf16[32,256]{1,0:T(8,128)(2,1)S(1)}, bf16[32,256]{1,0:T(8,128)(2,1)S(1)}, u32[]{:S(2)}, u32[]{:S(2)}) collective-permute-start(bf16[32,256]{1,0:T(8,128)(2,1)S(1)} %get-tuple-element.363), channel_id=1, source_target_pairs={{0,64},{32,96},{64,0},{96,32},{1,65},{33,97},{65,1},{97,33},{2,66}... | collective-permute-start | bytes 49160 | tf_op jit(solution)/shard_map/ppermute | solution.py:58
  38.4 6.7 %all-to-all-start.5 = ((bf16[16,72,128]{2,1,0:T(8,128)(2,1)}), bf16[16,72,128]{2,1,0:T(8,128)(2,1)S(1)}, u32[]{:S(2)}, u32[]{:S(2)}) async-start(bf16[16,72,128]{2,1,0:T(8,128)(2,1)} %get-tuple-element.366), calls=%async_computation.5 | async-start | bytes 589824 | tf_op jit(solution)/shard_map/all_to_all | solution.py:54
  45.9 2.5 %collective-permute-start.4 = (f32[32,256]{1,0:T(8,128)S(1)}, f32[32,256]{1,0:T(8,128)S(1)}, u32[]{:S(2)}, u32[]{:S(2)}) collective-permute-start(f32[32,256]{1,0:T(8,128)S(1)} %get-tuple-element.365.refs_4_.refs_6_.refs_8_), channel_id=1, source_target_pairs={{0,32},{32,0},{64,96},{96,64},{1,33},{33,1},{65,97},{97,65},{2,34}... | collective-permute-start | bytes 98312 | tf_op jit(solution)/shard_map/ppermute | solution.py:58
  50.0 3.5 %shard_map.90 = bf16[32,72,128]{2,1,0:T(8,128)(2,1)} custom-call(s32[1,1,32]{2,1,0:T(1,128)S(1)} %copy-done.4, s32[1,1,32]{2,1,0:T(1,128)S(1)} %copy-done.3, s32[1,1]{1,0:T(1,128)S(6)} %copy.112.live_ref, bf16[12,256,256]{2,1,0:T(8,128)(2,1)S(1)} %shard_map.85.kept_ref, bf16[1,1,32,256,256]{4,3,2,1,0:T(8,128)(2,1)} %tiles_ref.17, ...), custom_call_target="tpu_custom_call" | custom-call | flops 134217728 | bytes 1048576 | tf_op jit(solution)/shard_map/pallas_call | solution.py:32
  53.6 11.0 %all-to-all-start.4 = ((bf16[32,72,128]{2,1,0:T(8,128)(2,1)}), bf16[32,72,128]{2,1,0:T(8,128)(2,1)S(1)}, u32[]{:S(2)}, u32[]{:S(2)}) async-start(bf16[32,72,128]{2,1,0:T(8,128)(2,1)} %shard_map.90), calls=%async_computation.4 | async-start | bytes 1179648 | tf_op jit(solution)/shard_map/all_to_all | solution.py:48
  66.2 3.0 %shard_map.91 = (f32[32,256]{1,0:T(8,128)S(1)}, bf16[32,256]{1,0:T(8,128)(2,1)S(1)}, bf16[32,256]{1,0:T(8,128)(2,1)S(1)}, bf16[32,256]{1,0:T(8,128)(2,1)S(1)}, f32[32,128]{1,0:T(8,128)S(1)}) custom-call(s32[1,1,32]{2,1,0:T(1,128)S(1)} %copy-done.4, s32[1,1,32]{2,1,0:T(1,128)S(1)} %copy-done.3, s32[1,1]{1,0:T(1,128)S(6)} %copy.112.live_ref, ...), custom_call_target="tpu_custom_call" | custom-call | flops 134217728 | bytes 1048576 | tf_op jit(solution)/shard_map/pallas_call | solution.py:32
  77.6 6.4 %all-to-all-start.7 = ((bf16[16,72,128]{2,1,0:T(8,128)(2,1)}), bf16[16,72,128]{2,1,0:T(8,128)(2,1)S(1)}, u32[]{:S(2)}, u32[]{:S(2)}) async-start(bf16[16,72,128]{2,1,0:T(8,128)(2,1)} %get-tuple-element.373), calls=%async_computation.7 | async-start | bytes 589824 | tf_op jit(solution)/shard_map/all_to_all | solution.py:54
  84.7 2.6 %collective-permute-start.11 = (f32[32,256]{1,0:T(8,128)S(1)}, f32[32,256]{1,0:T(8,128)S(1)}, u32[]{:S(2)}, u32[]{:S(2)}) collective-permute-start(f32[32,256]{1,0:T(8,128)S(1)} %get-tuple-element.372.refs_8_.refs_4_.refs_6_.refs_12_), channel_id=1, source_target_pairs={{0,32},{32,0},{64,96},{96,64},{1,33},{33,1},{65,97},{97,65},{2,34}... | collective-permute-start | bytes 98312 | tf_op jit(solution)/shard_map/ppermute | solution.py:58
  89.0 3.5 %shard_map.93 = bf16[32,72,128]{2,1,0:T(8,128)(2,1)} custom-call(s32[1,1,32]{2,1,0:T(1,128)S(1)} %copy-done.4, s32[1,1,32]{2,1,0:T(1,128)S(1)} %copy-done.3, s32[1,1]{1,0:T(1,128)S(6)} %copy.112.live_ref, bf16[12,256,256]{2,1,0:T(8,128)(2,1)S(1)} %shard_map.85.kept_ref, bf16[1,1,32,256,256]{4,3,2,1,0:T(8,128)(2,1)} %tiles_ref.17, ...), custom_call_target="tpu_custom_call" | custom-call | flops 134217728 | bytes 1048576 | tf_op jit(solution)/shard_map/pallas_call | solution.py:32
  92.6 11.0 %all-to-all-start.6 = ((bf16[32,72,128]{2,1,0:T(8,128)(2,1)}), bf16[32,72,128]{2,1,0:T(8,128)(2,1)S(1)}, u32[]{:S(2)}, u32[]{:S(2)}) async-start(bf16[32,72,128]{2,1,0:T(8,128)(2,1)} %shard_map.93), calls=%async_computation.6 | async-start | bytes 1179648 | tf_op jit(solution)/shard_map/all_to_all | solution.py:48
  105.2 3.0 %shard_map.94 = (f32[32,256]{1,0:T(8,128)S(1)}, bf16[32,256]{1,0:T(8,128)(2,1)S(1)}, bf16[32,256]{1,0:T(8,128)(2,1)S(1)}, bf16[32,256]{1,0:T(8,128)(2,1)S(1)}, f32[32,128]{1,0:T(8,128)S(1)}) custom-call(s32[1,1,32]{2,1,0:T(1,128)S(1)} %copy-done.4, s32[1,1,32]{2,1,0:T(1,128)S(1)} %copy-done.3, s32[1,1]{1,0:T(1,128)S(6)} %copy.112.live_ref, ...), custom_call_target="tpu_custom_call" | custom-call | flops 134217728 | bytes 1048576 | tf_op jit(solution)/shard_map/pallas_call | solution.py:32
  116.5 6.4 %all-to-all-start.9 = ((bf16[16,72,128]{2,1,0:T(8,128)(2,1)}), bf16[16,72,128]{2,1,0:T(8,128)(2,1)S(1)}, u32[]{:S(2)}, u32[]{:S(2)}) async-start(bf16[16,72,128]{2,1,0:T(8,128)(2,1)} %get-tuple-element.380), calls=%async_computation.9 | async-start | bytes 589824 | tf_op jit(solution)/shard_map/all_to_all | solution.py:54
  123.6 2.6 %collective-permute-start.18 = (f32[32,256]{1,0:T(8,128)S(1)}, f32[32,256]{1,0:T(8,128)S(1)}, u32[]{:S(2)}, u32[]{:S(2)}) collective-permute-start(f32[32,256]{1,0:T(8,128)S(1)} %get-tuple-element.379.refs_12_.refs_4_.refs_16_), channel_id=1, source_target_pairs={{0,32},{32,0},{64,96},{96,64},{1,33},{33,1},{65,97},{97,65},{2,34}... | collective-permute-start | bytes 98312 | tf_op jit(solution)/shard_map/ppermute | solution.py:58
  127.9 3.6 %shard_map.96 = bf16[32,72,128]{2,1,0:T(8,128)(2,1)} custom-call(s32[1,1,32]{2,1,0:T(1,128)S(1)} %copy-done.4, s32[1,1,32]{2,1,0:T(1,128)S(1)} %copy-done.3, s32[1,1]{1,0:T(1,128)S(6)} %copy.112.live_ref, bf16[12,256,256]{2,1,0:T(8,128)(2,1)S(1)} %shard_map.85.kept_ref, bf16[1,1,32,256,256]{4,3,2,1,0:T(8,128)(2,1)} %tiles_ref.17, ...), custom_call_target="tpu_custom_call" | custom-call | flops 134217728 | bytes 1048576 | tf_op jit(solution)/shard_map/pallas_call | solution.py:32
  131.5 11.0 %all-to-all-start.8 = ((bf16[32,72,128]{2,1,0:T(8,128)(2,1)}), bf16[32,72,128]{2,1,0:T(8,128)(2,1)S(1)}, u32[]{:S(2)}, u32[]{:S(2)}) async-start(bf16[32,72,128]{2,1,0:T(8,128)(2,1)} %shard_map.96), calls=%async_computation.8 | async-start | bytes 1179648 | tf_op jit(solution)/shard_map/all_to_all | solution.py:48
  144.2 3.0 %shard_map.97 = (f32[32,256]{1,0:T(8,128)S(1)}, bf16[32,256]{1,0:T(8,128)(2,1)S(1)}, bf16[32,256]{1,0:T(8,128)(2,1)S(1)}, bf16[32,256]{1,0:T(8,128)(2,1)S(1)}, f32[32,128]{1,0:T(8,128)S(1)}) custom-call(s32[1,1,32]{2,1,0:T(1,128)S(1)} %copy-done.4, s32[1,1,32]{2,1,0:T(1,128)S(1)} %copy-done.3, s32[1,1]{1,0:T(1,128)S(6)} %copy.112.live_ref, ...), custom_call_target="tpu_custom_call" | custom-call | flops 134217728 | bytes 1048576 | tf_op jit(solution)/shard_map/pallas_call | solution.py:32
  158.8 2.4 %collective-permute-done.26.refs_18_.refs_22_ = f32[32,256]{1,0:T(8,128)S(1)} collective-permute-done((f32[32,256]{1,0:T(8,128)S(1)}, f32[32,256]{1,0:T(8,128)S(1)}, u32[]{:S(2)}, u32[]{:S(2)}) %collective-permute-start.26) | collective-permute-done | bytes 32800 | tf_op jit(solution)/shard_map/ppermute | solution.py:58
  165.5 6.6 %all-to-all-start.10 = ((f32[16,48,128]{2,1,0:T(8,128)}), f32[16,48,128]{2,1,0:T(8,128)S(1)}, u32[]{:S(2)}, u32[]{:S(2)}) async-start(f32[16,48,128]{2,1,0:T(8,128)} %shard_map.100), calls=%async_computation.10 | async-start | bytes 786432 | tf_op jit(solution)/shard_map/all_to_all | solution.py:54
  178.5 3.2 %all-to-all-done.10.parts_ref = f32[16,48,128]{2,1,0:T(8,128)S(1)} async-done(((f32[16,48,128]{2,1,0:T(8,128)}), f32[16,48,128]{2,1,0:T(8,128)S(1)}, u32[]{:S(2)}, u32[]{:S(2)}) %all-to-all-start.10) | async-done | bytes 393248 | tf_op jit(solution)/shard_map/all_to_all | solution.py:54
  181.7 5.9 %shard_map.104 = (f32[4,32,128]{2,1,0:T(8,128)}, f32[4,32,32]{2,1,0:T(8,128)}, f32[32,1024]{1,0:T(8,128)}, f32[8,128]{1,0:T(8,128)S(1)}) custom-call(f32[16,48,128]{2,1,0:T(8,128)S(1)} %all-to-all-done.10.parts_ref, f32[8,128]{1,0:T(8,128)S(1)} %get-tuple-element.378.refs_7_.coef_ref, f32[160,160]{1,0:T(8,128)S(1)} %get-tuple-element.394.old_low, ...), custom_call_target="tpu_custom_call" | custom-call | flops 2000000 | bytes 1048576 | tf_op jit(solution)/shard_map/pallas_call | solution.py:32
  (84 shorter events, 64.6 us)
Async XLA Ops:
  2.3 16.0 %all-to-all-start.3 = ((bf16[16,64,128]{2,1,0:T(8,128)(2,1)}), bf16[16,64,128]{2,1,0:T(8,128)(2,1)S(1)}, u32[]{:S(2)}, u32[]{:S(2)}) async-start(bf16[16,64,128]{2,1,0:T(8,128)(2,1)} %get-tuple-element.360), calls=%async_computation.3 | async-start | bytes 524288 | tf_op jit(solution)/shard_map/all_to_all | solution.py:54
  18.3 19.1 %all-to-all-start.2 = ((bf16[32,72,128]{2,1,0:T(8,128)(2,1)}), bf16[32,72,128]{2,1,0:T(8,128)(2,1)S(1)}, u32[]{:S(2)}, u32[]{:S(2)}) async-start(bf16[32,72,128]{2,1,0:T(8,128)(2,1)} %shard_map.87), calls=%async_computation.2 | async-start | bytes 1179648 | tf_op jit(solution)/shard_map/all_to_all | solution.py:48
  31.0 4.4 %collective-permute-start.2 = (bf16[32,256]{1,0:T(8,128)(2,1)S(1)}, bf16[32,256]{1,0:T(8,128)(2,1)S(1)}, u32[]{:S(2)}, u32[]{:S(2)}) collective-permute-start(bf16[32,256]{1,0:T(8,128)(2,1)S(1)} %get-tuple-element.363), channel_id=1, source_target_pairs={{0,64},{32,96},{64,0},{96,32},{1,65},{33,97},{65,1},{97,33},{2,66}... | collective-permute-start | bytes 49160 | tf_op jit(solution)/shard_map/ppermute | solution.py:58
  38.4 15.2 %all-to-all-start.5 = ((bf16[16,72,128]{2,1,0:T(8,128)(2,1)}), bf16[16,72,128]{2,1,0:T(8,128)(2,1)S(1)}, u32[]{:S(2)}, u32[]{:S(2)}) async-start(bf16[16,72,128]{2,1,0:T(8,128)(2,1)} %get-tuple-element.366), calls=%async_computation.5 | async-start | bytes 589824 | tf_op jit(solution)/shard_map/all_to_all | solution.py:54
  45.1 4.3 %collective-permute-start.5 = (f32[32,256]{1,0:T(8,128)S(1)}, f32[32,256]{1,0:T(8,128)S(1)}, u32[]{:S(2)}, u32[]{:S(2)}) collective-permute-start(f32[32,256]{1,0:T(8,128)S(1)} %get-tuple-element.365.refs_4_.refs_6_.refs_8_), channel_id=1, source_target_pairs={{0,64},{32,96},{64,0},{96,32},{1,65},{33,97},{65,1},{97,33},{2,66}... | collective-permute-start | bytes 98312 | tf_op jit(solution)/shard_map/ppermute | solution.py:58
  45.9 4.2 %collective-permute-start.4 = (f32[32,256]{1,0:T(8,128)S(1)}, f32[32,256]{1,0:T(8,128)S(1)}, u32[]{:S(2)}, u32[]{:S(2)}) collective-permute-start(f32[32,256]{1,0:T(8,128)S(1)} %get-tuple-element.365.refs_4_.refs_6_.refs_8_), channel_id=1, source_target_pairs={{0,32},{32,0},{64,96},{96,64},{1,33},{33,1},{65,97},{97,65},{2,34}... | collective-permute-start | bytes 98312 | tf_op jit(solution)/shard_map/ppermute | solution.py:58
  53.6 23.1 %all-to-all-start.4 = ((bf16[32,72,128]{2,1,0:T(8,128)(2,1)}), bf16[32,72,128]{2,1,0:T(8,128)(2,1)S(1)}, u32[]{:S(2)}, u32[]{:S(2)}) async-start(bf16[32,72,128]{2,1,0:T(8,128)(2,1)} %shard_map.90), calls=%async_computation.4 | async-start | bytes 1179648 | tf_op jit(solution)/shard_map/all_to_all | solution.py:48
  70.8 4.4 %collective-permute-start.9 = (bf16[32,256]{1,0:T(8,128)(2,1)S(1)}, bf16[32,256]{1,0:T(8,128)(2,1)S(1)}, u32[]{:S(2)}, u32[]{:S(2)}) collective-permute-start(bf16[32,256]{1,0:T(8,128)(2,1)S(1)} %get-tuple-element.369), channel_id=1, source_target_pairs={{0,64},{32,96},{64,0},{96,32},{1,65},{33,97},{65,1},{97,33},{2,66}... | collective-permute-start | bytes 49160 | tf_op jit(solution)/shard_map/ppermute | solution.py:58
  72.6 4.1 %collective-permute-start.10 = (bf16[32,256]{1,0:T(8,128)(2,1)S(1)}, bf16[32,256]{1,0:T(8,128)(2,1)S(1)}, u32[]{:S(2)}, u32[]{:S(2)}) collective-permute-start(bf16[32,256]{1,0:T(8,128)(2,1)S(1)} %get-tuple-element.370), channel_id=1, source_target_pairs={{0,96},{32,64},{64,32},{96,0},{1,97},{33,65},{65,33},{97,1},{2,98}... | collective-permute-start | bytes 49160 | tf_op jit(solution)/shard_map/ppermute | solution.py:58
  77.6 14.9 %all-to-all-start.7 = ((bf16[16,72,128]{2,1,0:T(8,128)(2,1)}), bf16[16,72,128]{2,1,0:T(8,128)(2,1)S(1)}, u32[]{:S(2)}, u32[]{:S(2)}) async-start(bf16[16,72,128]{2,1,0:T(8,128)(2,1)} %get-tuple-element.373), calls=%async_computation.7 | async-start | bytes 589824 | tf_op jit(solution)/shard_map/all_to_all | solution.py:54
  84.0 4.1 %collective-permute-start.13 = (f32[32,256]{1,0:T(8,128)S(1)}, f32[32,256]{1,0:T(8,128)S(1)}, u32[]{:S(2)}, u32[]{:S(2)}) collective-permute-start(f32[32,256]{1,0:T(8,128)S(1)} %get-tuple-element.372.refs_8_.refs_4_.refs_6_.refs_12_), channel_id=1, source_target_pairs={{0,96},{32,64},{64,32},{96,0},{1,97},{33,65},{65,33},{97,1},{2,98}... | collective-permute-start | bytes 98312 | tf_op jit(solution)/shard_map/ppermute | solution.py:58
  84.7 4.3 %collective-permute-start.12 = (f32[32,256]{1,0:T(8,128)S(1)}, f32[32,256]{1,0:T(8,128)S(1)}, u32[]{:S(2)}, u32[]{:S(2)}) collective-permute-start(f32[32,256]{1,0:T(8,128)S(1)} %get-tuple-element.372.refs_8_.refs_4_.refs_6_.refs_12_), channel_id=1, source_target_pairs={{0,64},{32,96},{64,0},{96,32},{1,65},{33,97},{65,1},{97,33},{2,66}... | collective-permute-start | bytes 98312 | tf_op jit(solution)/shard_map/ppermute | solution.py:58
  84.7 4.3 %collective-permute-start.11 = (f32[32,256]{1,0:T(8,128)S(1)}, f32[32,256]{1,0:T(8,128)S(1)}, u32[]{:S(2)}, u32[]{:S(2)}) collective-permute-start(f32[32,256]{1,0:T(8,128)S(1)} %get-tuple-element.372.refs_8_.refs_4_.refs_6_.refs_12_), channel_id=1, source_target_pairs={{0,32},{32,0},{64,96},{96,64},{1,33},{33,1},{65,97},{97,65},{2,34}... | collective-permute-start | bytes 98312 | tf_op jit(solution)/shard_map/ppermute | solution.py:58
  92.6 23.1 %all-to-all-start.6 = ((bf16[32,72,128]{2,1,0:T(8,128)(2,1)}), bf16[32,72,128]{2,1,0:T(8,128)(2,1)S(1)}, u32[]{:S(2)}, u32[]{:S(2)}) async-start(bf16[32,72,128]{2,1,0:T(8,128)(2,1)} %shard_map.93), calls=%async_computation.6 | async-start | bytes 1179648 | tf_op jit(solution)/shard_map/all_to_all | solution.py:48
  109.7 4.4 %collective-permute-start.16 = (bf16[32,256]{1,0:T(8,128)(2,1)S(1)}, bf16[32,256]{1,0:T(8,128)(2,1)S(1)}, u32[]{:S(2)}, u32[]{:S(2)}) collective-permute-start(bf16[32,256]{1,0:T(8,128)(2,1)S(1)} %get-tuple-element.376), channel_id=1, source_target_pairs={{0,64},{32,96},{64,0},{96,32},{1,65},{33,97},{65,1},{97,33},{2,66}... | collective-permute-start | bytes 49160 | tf_op jit(solution)/shard_map/ppermute | solution.py:58
  111.6 4.1 %collective-permute-start.17 = (bf16[32,256]{1,0:T(8,128)(2,1)S(1)}, bf16[32,256]{1,0:T(8,128)(2,1)S(1)}, u32[]{:S(2)}, u32[]{:S(2)}) collective-permute-start(bf16[32,256]{1,0:T(8,128)(2,1)S(1)} %get-tuple-element.377), channel_id=1, source_target_pairs={{0,96},{32,64},{64,32},{96,0},{1,97},{33,65},{65,33},{97,1},{2,98}... | collective-permute-start | bytes 49160 | tf_op jit(solution)/shard_map/ppermute | solution.py:58
  116.5 15.0 %all-to-all-start.9 = ((bf16[16,72,128]{2,1,0:T(8,128)(2,1)}), bf16[16,72,128]{2,1,0:T(8,128)(2,1)S(1)}, u32[]{:S(2)}, u32[]{:S(2)}) async-start(bf16[16,72,128]{2,1,0:T(8,128)(2,1)} %get-tuple-element.380), calls=%async_computation.9 | async-start | bytes 589824 | tf_op jit(solution)/shard_map/all_to_all | solution.py:54
  123.6 4.3 %collective-permute-start.19 = (f32[32,256]{1,0:T(8,128)S(1)}, f32[32,256]{1,0:T(8,128)S(1)}, u32[]{:S(2)}, u32[]{:S(2)}) collective-permute-start(f32[32,256]{1,0:T(8,128)S(1)} %get-tuple-element.379.refs_12_.refs_4_.refs_16_), channel_id=1, source_target_pairs={{0,64},{32,96},{64,0},{96,32},{1,65},{33,97},{65,1},{97,33},{2,66}... | collective-permute-start | bytes 98312 | tf_op jit(solution)/shard_map/ppermute | solution.py:58
  123.6 4.3 %collective-permute-start.18 = (f32[32,256]{1,0:T(8,128)S(1)}, f32[32,256]{1,0:T(8,128)S(1)}, u32[]{:S(2)}, u32[]{:S(2)}) collective-permute-start(f32[32,256]{1,0:T(8,128)S(1)} %get-tuple-element.379.refs_12_.refs_4_.refs_16_), channel_id=1, source_target_pairs={{0,32},{32,0},{64,96},{96,64},{1,33},{33,1},{65,97},{97,65},{2,34}... | collective-permute-start | bytes 98312 | tf_op jit(solution)/shard_map/ppermute | solution.py:58
  131.5 23.1 %all-to-all-start.8 = ((bf16[32,72,128]{2,1,0:T(8,128)(2,1)}), bf16[32,72,128]{2,1,0:T(8,128)(2,1)S(1)}, u32[]{:S(2)}, u32[]{:S(2)}) async-start(bf16[32,72,128]{2,1,0:T(8,128)(2,1)} %shard_map.96), calls=%async_computation.8 | async-start | bytes 1179648 | tf_op jit(solution)/shard_map/all_to_all | solution.py:48
  148.7 4.4 %collective-permute-start.23 = (bf16[32,256]{1,0:T(8,128)(2,1)S(1)}, bf16[32,256]{1,0:T(8,128)(2,1)S(1)}, u32[]{:S(2)}, u32[]{:S(2)}) collective-permute-start(bf16[32,256]{1,0:T(8,128)(2,1)S(1)} %get-tuple-element.383), channel_id=1, source_target_pairs={{0,64},{32,96},{64,0},{96,32},{1,65},{33,97},{65,1},{97,33},{2,66}... | collective-permute-start | bytes 49160 | tf_op jit(solution)/shard_map/ppermute | solution.py:58
  150.5 4.1 %collective-permute-start.24 = (bf16[32,256]{1,0:T(8,128)(2,1)S(1)}, bf16[32,256]{1,0:T(8,128)(2,1)S(1)}, u32[]{:S(2)}, u32[]{:S(2)}) collective-permute-start(bf16[32,256]{1,0:T(8,128)(2,1)S(1)} %get-tuple-element.384), channel_id=1, source_target_pairs={{0,96},{32,64},{64,32},{96,0},{1,97},{33,65},{65,33},{97,1},{2,98}... | collective-permute-start | bytes 49160 | tf_op jit(solution)/shard_map/ppermute | solution.py:58
  156.9 4.4 %collective-permute-start.26 = (f32[32,256]{1,0:T(8,128)S(1)}, f32[32,256]{1,0:T(8,128)S(1)}, u32[]{:S(2)}, u32[]{:S(2)}) collective-permute-start(f32[32,256]{1,0:T(8,128)S(1)} %get-tuple-element.386.refs_16_.refs_20_), channel_id=1, source_target_pairs={{0,64},{32,96},{64,0},{96,32},{1,65},{33,97},{65,1},{97,33},{2,66}... | collective-permute-start | bytes 98312 | tf_op jit(solution)/shard_map/ppermute | solution.py:58
  165.5 16.2 %all-to-all-start.10 = ((f32[16,48,128]{2,1,0:T(8,128)}), f32[16,48,128]{2,1,0:T(8,128)S(1)}, u32[]{:S(2)}, u32[]{:S(2)}) async-start(f32[16,48,128]{2,1,0:T(8,128)} %shard_map.100), calls=%async_computation.10 | async-start | bytes 786432 | tf_op jit(solution)/shard_map/all_to_all | solution.py:54
  (19 other events, 130.6 us)

commit v10 on v9

--- a/solution.py
+++ b/solution.py
@@ -33,7 +33,7 @@
         kernel,
         out_shape=out_shape,
         in_specs=[spec(space) for space in in_spaces],
-        out_specs=[spec(VMEM)] * len(out_shape),
+        out_specs=[spec(SMEM if one.dtype == jnp.int32 else VMEM) for one in out_shape],
         scratch_shapes=list(scratch),
         compiler_params=pltpu.CompilerParams(vmem_limit_bytes=limit_mib << 20),
         cost_estimate=pl.CostEstimate(flops=flops, bytes_accessed=1 << 20, transcendentals=0),
@@ -392,7 +392,7 @@
     known = ITERS - 2
     early, refs = refs[: 2 * known], refs[2 * known :]
     vectors = [refs[i * groups : (i + 1) * groups] for i in range(ITERS + 1)]
-    proj_ref, fact_ref, out_ref, fresh_ref, low, inv = refs[(ITERS + 1) * groups :]
+    proj_ref, fact_ref, out_ref, bad_ref, low, inv = refs[(ITERS + 1) * groups :]
     owners = parts_ref.shape[0]
     width, edge = vectors[0][0].shape
     group = lax.axis_index("grp")
@@ -413,7 +413,7 @@
     )
     kept = jnp.sum(jnp.where(on_diagonal, square, 0.0), 1, keepdims=True)
     bad = jnp.where(kept > FRESH * jnp.sum(square, 1, keepdims=True), 0.0, 1.0)
-    fresh_ref[...] = jnp.broadcast_to(jnp.max(bad, 0, keepdims=True), fresh_ref.shape)
+    bad_ref[0, 0] = jnp.max(bad).astype(jnp.int32)
     for j in range(known):
         proj_ref[j], fact_ref[j] = early[2 * j][...], early[2 * j + 1][...]
     for j in range(known, ITERS):
@@ -679,7 +679,7 @@
             shape(ITERS, width, ITERS * width),
             shape(ITERS, width, width),
             shape(width, row_count),
-            shape(EXTRA, LANES),
+            shape(1, 1, dtype=jnp.int32),
         ],
         [VMEM] * (4 + len(early) + len(flat)),
         (parts, coef, *state, *early, *flat),
@@ -687,7 +687,7 @@
         [pltpu.VMEM((total, total), F32), pltpu.VMEM((total, total), F32)],
     )
     inputs = (tiles, tile_rows, tile_cols, live_tiles, dual_shift, start_block)
-    return lax.cond(bad[0, 0] < 0.5, lambda: tuple(results), lambda: step_by_step(*inputs))
+    return lax.cond(bad[0, 0] == 0, lambda: tuple(results), lambda: step_by_step(*inputs))
 
 
 def solution(mesh):

time: 190 us -> 190 us (level)
  no operation moved by 1% of the time
where the time goes in v10:
time: 190 us; the launch traced here: 189 us
  starting transfers between devices  106 us (56%)
  Pallas kernels  46.2 us (24%)
  waiting for transfers between devices  33.2 us (17%)
  between operations  2.47 us (1%)
    pallas_call x20, Pallas kernels, call(): pl.pallas_call(kernel, out_shape=out_shape, in_specs=[spec(space) for spa...  46.2 us
    all_to_all x4, starting transfers between devices, exchange(): return lax.all_to_all(parts, axis, split_axis=0, concat_axis=0, tiled=True)  39.7 us
    all_to_all x5, starting transfers between devices, same_core(): lax.all_to_all(parts, 'row', 0, 0, axis_index_groups=groups, tiled=True)  34.5 us
    ppermute x29, starting transfers between devices, swapped(): lax.ppermute(value, axis, [(i, i ^ mask) for i in range(lax.axis_size(axi...  32.2 us
    ppermute x29, waiting for transfers between devices, swapped(): lax.ppermute(value, axis, [(i, i ^ mask) for i in range(lax.axis_size(axi...  28.5 us
    all_to_all x5, waiting for transfers between devices, same_core(): lax.all_to_all(parts, 'row', 0, 0, axis_index_groups=groups, tiled=True)  4.71 us
  transfers between devices with their start and end apart: 38, of which 24 were waited for; matrix products, arithmetic and copies ran while one was open for 0% of the time, Pallas kernels for 18%

profile of v10, /device:TPU:1, one launch (start us, length us, event | category | flops | bytes accessed | tf_op | source)
XLA Modules:
  0.0 188.8 jit_solution(746494385658214984)
XLA Ops:
  2.3 8.4 %all-to-all-start.3 = ((bf16[16,64,128]{2,1,0:T(8,128)(2,1)}), bf16[16,64,128]{2,1,0:T(8,128)(2,1)S(1)}, u32[]{:S(2)}, u32[]{:S(2)}) async-start(bf16[16,64,128]{2,1,0:T(8,128)(2,1)} %get-tuple-element.360), calls=%async_computation.3 | async-start | bytes 524288 | tf_op jit(solution)/shard_map/all_to_all | solution.py:54
  13.4 3.3 %shard_map.87 = bf16[32,72,128]{2,1,0:T(8,128)(2,1)} custom-call(s32[1,1,32]{2,1,0:T(1,128)S(1)} %copy-done.4, s32[1,1,32]{2,1,0:T(1,128)S(1)} %copy-done.3, s32[1,1]{1,0:T(1,128)S(6)} %copy.112.live_ref, bf16[12,256,256]{2,1,0:T(8,128)(2,1)S(1)} %shard_map.85.kept_ref, bf16[1,1,32,256,256]{4,3,2,1,0:T(8,128)(2,1)S(1)} %copy-done, ...), custom_call_target="tpu_custom_call" | custom-call | flops 134217728 | bytes 1048576 | tf_op jit(solution)/shard_map/pallas_call | solution.py:32
  18.3 6.7 %all-to-all-start.2 = ((bf16[32,72,128]{2,1,0:T(8,128)(2,1)}), bf16[32,72,128]{2,1,0:T(8,128)(2,1)S(1)}, u32[]{:S(2)}, u32[]{:S(2)}) async-start(bf16[32,72,128]{2,1,0:T(8,128)(2,1)} %shard_map.87), calls=%async_computation.2 | async-start | bytes 1179648 | tf_op jit(solution)/shard_map/all_to_all | solution.py:48
  26.6 3.0 %shard_map.88 = (f32[32,256]{1,0:T(8,128)S(1)}, bf16[32,256]{1,0:T(8,128)(2,1)S(1)}, bf16[32,256]{1,0:T(8,128)(2,1)S(1)}, bf16[32,256]{1,0:T(8,128)(2,1)S(1)}) custom-call(s32[1,1,32]{2,1,0:T(1,128)S(1)} %copy-done.4, s32[1,1,32]{2,1,0:T(1,128)S(1)} %copy-done.3, s32[1,1]{1,0:T(1,128)S(6)} %copy.112.live_ref, bf16[12,256,256]{2,1,0:T(8,128)(2,1)S(1)} %shard_map.85.kept_ref, ...), custom_call_target="tpu_custom_call" | custom-call | flops 134217728 | bytes 1048576 | tf_op jit(solution)/shard_map/pallas_call | solution.py:32
  31.0 2.6 %collective-permute-start.2 = (bf16[32,256]{1,0:T(8,128)(2,1)S(1)}, bf16[32,256]{1,0:T(8,128)(2,1)S(1)}, u32[]{:S(2)}, u32[]{:S(2)}) collective-permute-start(bf16[32,256]{1,0:T(8,128)(2,1)S(1)} %get-tuple-element.363), channel_id=1, source_target_pairs={{0,64},{32,96},{64,0},{96,32},{1,65},{33,97},{65,1},{97,33},{2,66}... | collective-permute-start | bytes 49160 | tf_op jit(solution)/shard_map/ppermute | solution.py:58
  38.4 6.7 %all-to-all-start.5 = ((bf16[16,72,128]{2,1,0:T(8,128)(2,1)}), bf16[16,72,128]{2,1,0:T(8,128)(2,1)S(1)}, u32[]{:S(2)}, u32[]{:S(2)}) async-start(bf16[16,72,128]{2,1,0:T(8,128)(2,1)} %get-tuple-element.366), calls=%async_computation.5 | async-start | bytes 589824 | tf_op jit(solution)/shard_map/all_to_all | solution.py:54
  45.9 2.5 %collective-permute-start.4 = (f32[32,256]{1,0:T(8,128)S(1)}, f32[32,256]{1,0:T(8,128)S(1)}, u32[]{:S(2)}, u32[]{:S(2)}) collective-permute-start(f32[32,256]{1,0:T(8,128)S(1)} %get-tuple-element.365.refs_4_.refs_6_.refs_8_), channel_id=1, source_target_pairs={{0,32},{32,0},{64,96},{96,64},{1,33},{33,1},{65,97},{97,65},{2,34}... | collective-permute-start | bytes 98312 | tf_op jit(solution)/shard_map/ppermute | solution.py:58
  50.0 3.5 %shard_map.90 = bf16[32,72,128]{2,1,0:T(8,128)(2,1)} custom-call(s32[1,1,32]{2,1,0:T(1,128)S(1)} %copy-done.4, s32[1,1,32]{2,1,0:T(1,128)S(1)} %copy-done.3, s32[1,1]{1,0:T(1,128)S(6)} %copy.112.live_ref, bf16[12,256,256]{2,1,0:T(8,128)(2,1)S(1)} %shard_map.85.kept_ref, bf16[1,1,32,256,256]{4,3,2,1,0:T(8,128)(2,1)} %tiles_ref.17, ...), custom_call_target="tpu_custom_call" | custom-call | flops 134217728 | bytes 1048576 | tf_op jit(solution)/shard_map/pallas_call | solution.py:32
  53.6 11.0 %all-to-all-start.4 = ((bf16[32,72,128]{2,1,0:T(8,128)(2,1)}), bf16[32,72,128]{2,1,0:T(8,128)(2,1)S(1)}, u32[]{:S(2)}, u32[]{:S(2)}) async-start(bf16[32,72,128]{2,1,0:T(8,128)(2,1)} %shard_map.90), calls=%async_computation.4 | async-start | bytes 1179648 | tf_op jit(solution)/shard_map/all_to_all | solution.py:48
  66.2 3.0 %shard_map.91 = (f32[32,256]{1,0:T(8,128)S(1)}, bf16[32,256]{1,0:T(8,128)(2,1)S(1)}, bf16[32,256]{1,0:T(8,128)(2,1)S(1)}, bf16[32,256]{1,0:T(8,128)(2,1)S(1)}, f32[32,128]{1,0:T(8,128)S(1)}) custom-call(s32[1,1,32]{2,1,0:T(1,128)S(1)} %copy-done.4, s32[1,1,32]{2,1,0:T(1,128)S(1)} %copy-done.3, s32[1,1]{1,0:T(1,128)S(6)} %copy.112.live_ref, ...), custom_call_target="tpu_custom_call" | custom-call | flops 134217728 | bytes 1048576 | tf_op jit(solution)/shard_map/pallas_call | solution.py:32
  77.6 6.4 %all-to-all-start.7 = ((bf16[16,72,128]{2,1,0:T(8,128)(2,1)}), bf16[16,72,128]{2,1,0:T(8,128)(2,1)S(1)}, u32[]{:S(2)}, u32[]{:S(2)}) async-start(bf16[16,72,128]{2,1,0:T(8,128)(2,1)} %get-tuple-element.373), calls=%async_computation.7 | async-start | bytes 589824 | tf_op jit(solution)/shard_map/all_to_all | solution.py:54
  84.7 2.6 %collective-permute-start.11 = (f32[32,256]{1,0:T(8,128)S(1)}, f32[32,256]{1,0:T(8,128)S(1)}, u32[]{:S(2)}, u32[]{:S(2)}) collective-permute-start(f32[32,256]{1,0:T(8,128)S(1)} %get-tuple-element.372.refs_8_.refs_4_.refs_6_.refs_12_), channel_id=1, source_target_pairs={{0,32},{32,0},{64,96},{96,64},{1,33},{33,1},{65,97},{97,65},{2,34}... | collective-permute-start | bytes 98312 | tf_op jit(solution)/shard_map/ppermute | solution.py:58
  89.0 3.5 %shard_map.93 = bf16[32,72,128]{2,1,0:T(8,128)(2,1)} custom-call(s32[1,1,32]{2,1,0:T(1,128)S(1)} %copy-done.4, s32[1,1,32]{2,1,0:T(1,128)S(1)} %copy-done.3, s32[1,1]{1,0:T(1,128)S(6)} %copy.112.live_ref, bf16[12,256,256]{2,1,0:T(8,128)(2,1)S(1)} %shard_map.85.kept_ref, bf16[1,1,32,256,256]{4,3,2,1,0:T(8,128)(2,1)} %tiles_ref.17, ...), custom_call_target="tpu_custom_call" | custom-call | flops 134217728 | bytes 1048576 | tf_op jit(solution)/shard_map/pallas_call | solution.py:32
  92.6 11.0 %all-to-all-start.6 = ((bf16[32,72,128]{2,1,0:T(8,128)(2,1)}), bf16[32,72,128]{2,1,0:T(8,128)(2,1)S(1)}, u32[]{:S(2)}, u32[]{:S(2)}) async-start(bf16[32,72,128]{2,1,0:T(8,128)(2,1)} %shard_map.93), calls=%async_computation.6 | async-start | bytes 1179648 | tf_op jit(solution)/shard_map/all_to_all | solution.py:48
  105.2 3.0 %shard_map.94 = (f32[32,256]{1,0:T(8,128)S(1)}, bf16[32,256]{1,0:T(8,128)(2,1)S(1)}, bf16[32,256]{1,0:T(8,128)(2,1)S(1)}, bf16[32,256]{1,0:T(8,128)(2,1)S(1)}, f32[32,128]{1,0:T(8,128)S(1)}) custom-call(s32[1,1,32]{2,1,0:T(1,128)S(1)} %copy-done.4, s32[1,1,32]{2,1,0:T(1,128)S(1)} %copy-done.3, s32[1,1]{1,0:T(1,128)S(6)} %copy.112.live_ref, ...), custom_call_target="tpu_custom_call" | custom-call | flops 134217728 | bytes 1048576 | tf_op jit(solution)/shard_map/pallas_call | solution.py:32
  116.5 6.4 %all-to-all-start.9 = ((bf16[16,72,128]{2,1,0:T(8,128)(2,1)}), bf16[16,72,128]{2,1,0:T(8,128)(2,1)S(1)}, u32[]{:S(2)}, u32[]{:S(2)}) async-start(bf16[16,72,128]{2,1,0:T(8,128)(2,1)} %get-tuple-element.380), calls=%async_computation.9 | async-start | bytes 589824 | tf_op jit(solution)/shard_map/all_to_all | solution.py:54
  123.6 2.6 %collective-permute-start.18 = (f32[32,256]{1,0:T(8,128)S(1)}, f32[32,256]{1,0:T(8,128)S(1)}, u32[]{:S(2)}, u32[]{:S(2)}) collective-permute-start(f32[32,256]{1,0:T(8,128)S(1)} %get-tuple-element.379.refs_12_.refs_4_.refs_16_), channel_id=1, source_target_pairs={{0,32},{32,0},{64,96},{96,64},{1,33},{33,1},{65,97},{97,65},{2,34}... | collective-permute-start | bytes 98312 | tf_op jit(solution)/shard_map/ppermute | solution.py:58
  127.9 3.6 %shard_map.96 = bf16[32,72,128]{2,1,0:T(8,128)(2,1)} custom-call(s32[1,1,32]{2,1,0:T(1,128)S(1)} %copy-done.4, s32[1,1,32]{2,1,0:T(1,128)S(1)} %copy-done.3, s32[1,1]{1,0:T(1,128)S(6)} %copy.112.live_ref, bf16[12,256,256]{2,1,0:T(8,128)(2,1)S(1)} %shard_map.85.kept_ref, bf16[1,1,32,256,256]{4,3,2,1,0:T(8,128)(2,1)} %tiles_ref.17, ...), custom_call_target="tpu_custom_call" | custom-call | flops 134217728 | bytes 1048576 | tf_op jit(solution)/shard_map/pallas_call | solution.py:32
  131.5 11.0 %all-to-all-start.8 = ((bf16[32,72,128]{2,1,0:T(8,128)(2,1)}), bf16[32,72,128]{2,1,0:T(8,128)(2,1)S(1)}, u32[]{:S(2)}, u32[]{:S(2)}) async-start(bf16[32,72,128]{2,1,0:T(8,128)(2,1)} %shard_map.96), calls=%async_computation.8 | async-start | bytes 1179648 | tf_op jit(solution)/shard_map/all_to_all | solution.py:48
  144.2 3.0 %shard_map.97 = (f32[32,256]{1,0:T(8,128)S(1)}, bf16[32,256]{1,0:T(8,128)(2,1)S(1)}, bf16[32,256]{1,0:T(8,128)(2,1)S(1)}, bf16[32,256]{1,0:T(8,128)(2,1)S(1)}, f32[32,128]{1,0:T(8,128)S(1)}) custom-call(s32[1,1,32]{2,1,0:T(1,128)S(1)} %copy-done.4, s32[1,1,32]{2,1,0:T(1,128)S(1)} %copy-done.3, s32[1,1]{1,0:T(1,128)S(6)} %copy.112.live_ref, ...), custom_call_target="tpu_custom_call" | custom-call | flops 134217728 | bytes 1048576 | tf_op jit(solution)/shard_map/pallas_call | solution.py:32
  158.8 2.4 %collective-permute-done.26.refs_18_.refs_22_ = f32[32,256]{1,0:T(8,128)S(1)} collective-permute-done((f32[32,256]{1,0:T(8,128)S(1)}, f32[32,256]{1,0:T(8,128)S(1)}, u32[]{:S(2)}, u32[]{:S(2)}) %collective-permute-start.26) | collective-permute-done | bytes 32800 | tf_op jit(solution)/shard_map/ppermute | solution.py:58
  165.5 6.6 %all-to-all-start.10 = ((f32[16,48,128]{2,1,0:T(8,128)}), f32[16,48,128]{2,1,0:T(8,128)S(1)}, u32[]{:S(2)}, u32[]{:S(2)}) async-start(f32[16,48,128]{2,1,0:T(8,128)} %shard_map.100), calls=%async_computation.10 | async-start | bytes 786432 | tf_op jit(solution)/shard_map/all_to_all | solution.py:54
  178.5 3.2 %all-to-all-done.10.parts_ref = f32[16,48,128]{2,1,0:T(8,128)S(1)} async-done(((f32[16,48,128]{2,1,0:T(8,128)}), f32[16,48,128]{2,1,0:T(8,128)S(1)}, u32[]{:S(2)}, u32[]{:S(2)}) %all-to-all-start.10) | async-done | bytes 393248 | tf_op jit(solution)/shard_map/all_to_all | solution.py:54
  181.7 6.1 %shard_map.104 = (f32[4,32,128]{2,1,0:T(8,128)}, f32[4,32,32]{2,1,0:T(8,128)}, f32[32,1024]{1,0:T(8,128)}, s32[1,1]{1,0:T(1,128)}) custom-call(f32[16,48,128]{2,1,0:T(8,128)S(1)} %all-to-all-done.10.parts_ref, f32[8,128]{1,0:T(8,128)S(1)} %get-tuple-element.378.refs_7_.coef_ref, f32[160,160]{1,0:T(8,128)S(1)} %get-tuple-element.394.old_low, ...), custom_call_target="tpu_custom_call" | custom-call | flops 2000000 | bytes 1048576 | tf_op jit(solution)/shard_map/pallas_call | solution.py:32
  (83 shorter events, 64.1 us)
Async XLA Ops:
  2.3 16.0 %all-to-all-start.3 = ((bf16[16,64,128]{2,1,0:T(8,128)(2,1)}), bf16[16,64,128]{2,1,0:T(8,128)(2,1)S(1)}, u32[]{:S(2)}, u32[]{:S(2)}) async-start(bf16[16,64,128]{2,1,0:T(8,128)(2,1)} %get-tuple-element.360), calls=%async_computation.3 | async-start | bytes 524288 | tf_op jit(solution)/shard_map/all_to_all | solution.py:54
  18.3 19.1 %all-to-all-start.2 = ((bf16[32,72,128]{2,1,0:T(8,128)(2,1)}), bf16[32,72,128]{2,1,0:T(8,128)(2,1)S(1)}, u32[]{:S(2)}, u32[]{:S(2)}) async-start(bf16[32,72,128]{2,1,0:T(8,128)(2,1)} %shard_map.87), calls=%async_computation.2 | async-start | bytes 1179648 | tf_op jit(solution)/shard_map/all_to_all | solution.py:48
  31.0 4.4 %collective-permute-start.2 = (bf16[32,256]{1,0:T(8,128)(2,1)S(1)}, bf16[32,256]{1,0:T(8,128)(2,1)S(1)}, u32[]{:S(2)}, u32[]{:S(2)}) collective-permute-start(bf16[32,256]{1,0:T(8,128)(2,1)S(1)} %get-tuple-element.363), channel_id=1, source_target_pairs={{0,64},{32,96},{64,0},{96,32},{1,65},{33,97},{65,1},{97,33},{2,66}... | collective-permute-start | bytes 49160 | tf_op jit(solution)/shard_map/ppermute | solution.py:58
  38.4 15.2 %all-to-all-start.5 = ((bf16[16,72,128]{2,1,0:T(8,128)(2,1)}), bf16[16,72,128]{2,1,0:T(8,128)(2,1)S(1)}, u32[]{:S(2)}, u32[]{:S(2)}) async-start(bf16[16,72,128]{2,1,0:T(8,128)(2,1)} %get-tuple-element.366), calls=%async_computation.5 | async-start | bytes 589824 | tf_op jit(solution)/shard_map/all_to_all | solution.py:54
  45.1 4.3 %collective-permute-start.5 = (f32[32,256]{1,0:T(8,128)S(1)}, f32[32,256]{1,0:T(8,128)S(1)}, u32[]{:S(2)}, u32[]{:S(2)}) collective-permute-start(f32[32,256]{1,0:T(8,128)S(1)} %get-tuple-element.365.refs_4_.refs_6_.refs_8_), channel_id=1, source_target_pairs={{0,64},{32,96},{64,0},{96,32},{1,65},{33,97},{65,1},{97,33},{2,66}... | collective-permute-start | bytes 98312 | tf_op jit(solution)/shard_map/ppermute | solution.py:58
  45.9 4.2 %collective-permute-start.4 = (f32[32,256]{1,0:T(8,128)S(1)}, f32[32,256]{1,0:T(8,128)S(1)}, u32[]{:S(2)}, u32[]{:S(2)}) collective-permute-start(f32[32,256]{1,0:T(8,128)S(1)} %get-tuple-element.365.refs_4_.refs_6_.refs_8_), channel_id=1, source_target_pairs={{0,32},{32,0},{64,96},{96,64},{1,33},{33,1},{65,97},{97,65},{2,34}... | collective-permute-start | bytes 98312 | tf_op jit(solution)/shard_map/ppermute | solution.py:58
  53.6 23.1 %all-to-all-start.4 = ((bf16[32,72,128]{2,1,0:T(8,128)(2,1)}), bf16[32,72,128]{2,1,0:T(8,128)(2,1)S(1)}, u32[]{:S(2)}, u32[]{:S(2)}) async-start(bf16[32,72,128]{2,1,0:T(8,128)(2,1)} %shard_map.90), calls=%async_computation.4 | async-start | bytes 1179648 | tf_op jit(solution)/shard_map/all_to_all | solution.py:48
  70.8 4.4 %collective-permute-start.9 = (bf16[32,256]{1,0:T(8,128)(2,1)S(1)}, bf16[32,256]{1,0:T(8,128)(2,1)S(1)}, u32[]{:S(2)}, u32[]{:S(2)}) collective-permute-start(bf16[32,256]{1,0:T(8,128)(2,1)S(1)} %get-tuple-element.369), channel_id=1, source_target_pairs={{0,64},{32,96},{64,0},{96,32},{1,65},{33,97},{65,1},{97,33},{2,66}... | collective-permute-start | bytes 49160 | tf_op jit(solution)/shard_map/ppermute | solution.py:58
  72.6 4.1 %collective-permute-start.10 = (bf16[32,256]{1,0:T(8,128)(2,1)S(1)}, bf16[32,256]{1,0:T(8,128)(2,1)S(1)}, u32[]{:S(2)}, u32[]{:S(2)}) collective-permute-start(bf16[32,256]{1,0:T(8,128)(2,1)S(1)} %get-tuple-element.370), channel_id=1, source_target_pairs={{0,96},{32,64},{64,32},{96,0},{1,97},{33,65},{65,33},{97,1},{2,98}... | collective-permute-start | bytes 49160 | tf_op jit(solution)/shard_map/ppermute | solution.py:58
  77.6 14.9 %all-to-all-start.7 = ((bf16[16,72,128]{2,1,0:T(8,128)(2,1)}), bf16[16,72,128]{2,1,0:T(8,128)(2,1)S(1)}, u32[]{:S(2)}, u32[]{:S(2)}) async-start(bf16[16,72,128]{2,1,0:T(8,128)(2,1)} %get-tuple-element.373), calls=%async_computation.7 | async-start | bytes 589824 | tf_op jit(solution)/shard_map/all_to_all | solution.py:54
  84.0 4.1 %collective-permute-start.13 = (f32[32,256]{1,0:T(8,128)S(1)}, f32[32,256]{1,0:T(8,128)S(1)}, u32[]{:S(2)}, u32[]{:S(2)}) collective-permute-start(f32[32,256]{1,0:T(8,128)S(1)} %get-tuple-element.372.refs_8_.refs_4_.refs_6_.refs_12_), channel_id=1, source_target_pairs={{0,96},{32,64},{64,32},{96,0},{1,97},{33,65},{65,33},{97,1},{2,98}... | collective-permute-start | bytes 98312 | tf_op jit(solution)/shard_map/ppermute | solution.py:58
  84.7 4.3 %collective-permute-start.12 = (f32[32,256]{1,0:T(8,128)S(1)}, f32[32,256]{1,0:T(8,128)S(1)}, u32[]{:S(2)}, u32[]{:S(2)}) collective-permute-start(f32[32,256]{1,0:T(8,128)S(1)} %get-tuple-element.372.refs_8_.refs_4_.refs_6_.refs_12_), channel_id=1, source_target_pairs={{0,64},{32,96},{64,0},{96,32},{1,65},{33,97},{65,1},{97,33},{2,66}... | collective-permute-start | bytes 98312 | tf_op jit(solution)/shard_map/ppermute | solution.py:58
  84.7 4.3 %collective-permute-start.11 = (f32[32,256]{1,0:T(8,128)S(1)}, f32[32,256]{1,0:T(8,128)S(1)}, u32[]{:S(2)}, u32[]{:S(2)}) collective-permute-start(f32[32,256]{1,0:T(8,128)S(1)} %get-tuple-element.372.refs_8_.refs_4_.refs_6_.refs_12_), channel_id=1, source_target_pairs={{0,32},{32,0},{64,96},{96,64},{1,33},{33,1},{65,97},{97,65},{2,34}... | collective-permute-start | bytes 98312 | tf_op jit(solution)/shard_map/ppermute | solution.py:58
  92.6 23.1 %all-to-all-start.6 = ((bf16[32,72,128]{2,1,0:T(8,128)(2,1)}), bf16[32,72,128]{2,1,0:T(8,128)(2,1)S(1)}, u32[]{:S(2)}, u32[]{:S(2)}) async-start(bf16[32,72,128]{2,1,0:T(8,128)(2,1)} %shard_map.93), calls=%async_computation.6 | async-start | bytes 1179648 | tf_op jit(solution)/shard_map/all_to_all | solution.py:48
  109.7 4.4 %collective-permute-start.16 = (bf16[32,256]{1,0:T(8,128)(2,1)S(1)}, bf16[32,256]{1,0:T(8,128)(2,1)S(1)}, u32[]{:S(2)}, u32[]{:S(2)}) collective-permute-start(bf16[32,256]{1,0:T(8,128)(2,1)S(1)} %get-tuple-element.376), channel_id=1, source_target_pairs={{0,64},{32,96},{64,0},{96,32},{1,65},{33,97},{65,1},{97,33},{2,66}... | collective-permute-start | bytes 49160 | tf_op jit(solution)/shard_map/ppermute | solution.py:58
  111.6 4.1 %collective-permute-start.17 = (bf16[32,256]{1,0:T(8,128)(2,1)S(1)}, bf16[32,256]{1,0:T(8,128)(2,1)S(1)}, u32[]{:S(2)}, u32[]{:S(2)}) collective-permute-start(bf16[32,256]{1,0:T(8,128)(2,1)S(1)} %get-tuple-element.377), channel_id=1, source_target_pairs={{0,96},{32,64},{64,32},{96,0},{1,97},{33,65},{65,33},{97,1},{2,98}... | collective-permute-start | bytes 49160 | tf_op jit(solution)/shard_map/ppermute | solution.py:58
  116.5 15.0 %all-to-all-start.9 = ((bf16[16,72,128]{2,1,0:T(8,128)(2,1)}), bf16[16,72,128]{2,1,0:T(8,128)(2,1)S(1)}, u32[]{:S(2)}, u32[]{:S(2)}) async-start(bf16[16,72,128]{2,1,0:T(8,128)(2,1)} %get-tuple-element.380), calls=%async_computation.9 | async-start | bytes 589824 | tf_op jit(solution)/shard_map/all_to_all | solution.py:54
  123.6 4.3 %collective-permute-start.19 = (f32[32,256]{1,0:T(8,128)S(1)}, f32[32,256]{1,0:T(8,128)S(1)}, u32[]{:S(2)}, u32[]{:S(2)}) collective-permute-start(f32[32,256]{1,0:T(8,128)S(1)} %get-tuple-element.379.refs_12_.refs_4_.refs_16_), channel_id=1, source_target_pairs={{0,64},{32,96},{64,0},{96,32},{1,65},{33,97},{65,1},{97,33},{2,66}... | collective-permute-start | bytes 98312 | tf_op jit(solution)/shard_map/ppermute | solution.py:58
  123.6 4.3 %collective-permute-start.18 = (f32[32,256]{1,0:T(8,128)S(1)}, f32[32,256]{1,0:T(8,128)S(1)}, u32[]{:S(2)}, u32[]{:S(2)}) collective-permute-start(f32[32,256]{1,0:T(8,128)S(1)} %get-tuple-element.379.refs_12_.refs_4_.refs_16_), channel_id=1, source_target_pairs={{0,32},{32,0},{64,96},{96,64},{1,33},{33,1},{65,97},{97,65},{2,34}... | collective-permute-start | bytes 98312 | tf_op jit(solution)/shard_map/ppermute | solution.py:58
  131.5 23.1 %all-to-all-start.8 = ((bf16[32,72,128]{2,1,0:T(8,128)(2,1)}), bf16[32,72,128]{2,1,0:T(8,128)(2,1)S(1)}, u32[]{:S(2)}, u32[]{:S(2)}) async-start(bf16[32,72,128]{2,1,0:T(8,128)(2,1)} %shard_map.96), calls=%async_computation.8 | async-start | bytes 1179648 | tf_op jit(solution)/shard_map/all_to_all | solution.py:48
  148.7 4.4 %collective-permute-start.23 = (bf16[32,256]{1,0:T(8,128)(2,1)S(1)}, bf16[32,256]{1,0:T(8,128)(2,1)S(1)}, u32[]{:S(2)}, u32[]{:S(2)}) collective-permute-start(bf16[32,256]{1,0:T(8,128)(2,1)S(1)} %get-tuple-element.383), channel_id=1, source_target_pairs={{0,64},{32,96},{64,0},{96,32},{1,65},{33,97},{65,1},{97,33},{2,66}... | collective-permute-start | bytes 49160 | tf_op jit(solution)/shard_map/ppermute | solution.py:58
  150.5 4.1 %collective-permute-start.24 = (bf16[32,256]{1,0:T(8,128)(2,1)S(1)}, bf16[32,256]{1,0:T(8,128)(2,1)S(1)}, u32[]{:S(2)}, u32[]{:S(2)}) collective-permute-start(bf16[32,256]{1,0:T(8,128)(2,1)S(1)} %get-tuple-element.384), channel_id=1, source_target_pairs={{0,96},{32,64},{64,32},{96,0},{1,97},{33,65},{65,33},{97,1},{2,98}... | collective-permute-start | bytes 49160 | tf_op jit(solution)/shard_map/ppermute | solution.py:58
  156.9 4.4 %collective-permute-start.26 = (f32[32,256]{1,0:T(8,128)S(1)}, f32[32,256]{1,0:T(8,128)S(1)}, u32[]{:S(2)}, u32[]{:S(2)}) collective-permute-start(f32[32,256]{1,0:T(8,128)S(1)} %get-tuple-element.386.refs_16_.refs_20_), channel_id=1, source_target_pairs={{0,64},{32,96},{64,0},{96,32},{1,65},{33,97},{65,1},{97,33},{2,66}... | collective-permute-start | bytes 98312 | tf_op jit(solution)/shard_map/ppermute | solution.py:58
  165.5 16.2 %all-to-all-start.10 = ((f32[16,48,128]{2,1,0:T(8,128)}), f32[16,48,128]{2,1,0:T(8,128)S(1)}, u32[]{:S(2)}, u32[]{:S(2)}) async-start(f32[16,48,128]{2,1,0:T(8,128)} %shard_map.100), calls=%async_computation.10 | async-start | bytes 786432 | tf_op jit(solution)/shard_map/all_to_all | solution.py:54
  (19 other events, 130.3 us)
